TPU v7x, 8 devices: a whole 2x2x1 slice. The times are simulated.
8 devices in a mesh: rep: 1 (over z), tp: 2 (over y), stage: 4 (over x, core).
Axes of the slice: x: 2, y: 2, z: 1, core: 2. Of those that a mesh axis runs over, the one named last changes fastest.
Arguments:
- inputs: bfloat16 [8, 2, 192, 1536], P('rep')
- targets: bfloat16 [8, 2, 192, 1536], P('rep')
- w_qkv: bfloat16 [4, 1536, 3, 16, 96], P(('rep', 'stage'), None, None, 'tp')
- w_out: bfloat16 [4, 16, 96, 1536], P(('rep', 'stage'), 'tp')
- w_up: bfloat16 [4, 1536, 6144], P(('rep', 'stage'), None, 'tp')
- w_down: bfloat16 [4, 6144, 1536], P(('rep', 'stage'), 'tp')
- gain_attn: bfloat16 [4, 1536], P(('rep', 'stage'))
- gain_mlp: bfloat16 [4, 1536], P(('rep', 'stage'))
Outputs:
- output 1: float32 [1], P('rep')
- output 2: bfloat16 [8, 2, 192, 1536], P('rep')
- output 3: float32 [4, 1536, 3, 16, 96], P(('rep', 'stage'), None, None, 'tp')
- output 4: float32 [4, 16, 96, 1536], P(('rep', 'stage'), 'tp')
- output 5: float32 [4, 1536, 6144], P(('rep', 'stage'), None, 'tp')
- output 6: float32 [4, 6144, 1536], P(('rep', 'stage'), 'tp')
- output 7: float32 [4, 1536], P(('rep', 'stage'))
- output 8: float32 [4, 1536], P(('rep', 'stage'))
All inputs are finite; a program needn't handle non-finite values.
Results may differ from a plain program's by a relative error of at most 0.02.
Values are sent between devices in bfloat16 or wider.
A program may use at most 1 GiB of HBM per device.

v0:
```python
import jax
import jax.numpy as jnp
from jax import lax
from jax.sharding import PartitionSpec as P

NORM_EPS = 1e-5


def rms_core(x_f32, gain_f32):
    inv_rms = lax.rsqrt(jnp.mean(x_f32 * x_f32, axis=-1, keepdims=True) + NORM_EPS)
    return x_f32 * inv_rms * gain_f32


def gelu_tanh(up_f32):
    return jax.nn.gelu(up_f32, approximate=True)


def attn_block(in_f32, w_qkv, w_out, gain_attn):
    head_dim = w_qkv.shape[-1]
    seq_len = in_f32.shape[1]
    normed_a = rms_core(in_f32, gain_attn.astype(jnp.float32)).astype(jnp.bfloat16)
    proj_qkv = jnp.einsum('bsd,dkhe->kbhse', normed_a, w_qkv, preferred_element_type=jnp.float32).astype(jnp.bfloat16)
    scores = jnp.einsum('bhqe,bhke->bhqk', proj_qkv[0], proj_qkv[1], preferred_element_type=jnp.float32) * (head_dim ** -0.5)
    q_pos = lax.broadcasted_iota(jnp.int32, (seq_len, seq_len), 0)
    k_pos = lax.broadcasted_iota(jnp.int32, (seq_len, seq_len), 1)
    attn_probs = jax.nn.softmax(jnp.where(k_pos <= q_pos, scores, -1e30), axis=-1)
    probs_bf = attn_probs.astype(jnp.bfloat16)
    context = jnp.einsum('bhqk,bhke->bhqe', probs_bf, proj_qkv[2], preferred_element_type=jnp.float32).astype(jnp.bfloat16)
    attn_part = jnp.einsum('bhse,hed->bsd', context, w_out, preferred_element_type=jnp.float32)
    mid_f32 = (in_f32 + lax.psum(attn_part, 'tp')).astype(jnp.bfloat16).astype(jnp.float32)
    return mid_f32, (normed_a, proj_qkv, attn_probs, probs_bf, context)


def mlp_front(mid_f32, w_up, gain_mlp):
    normed_m = rms_core(mid_f32, gain_mlp.astype(jnp.float32)).astype(jnp.bfloat16)
    up_f32 = jnp.einsum('bsd,df->bsf', normed_m, w_up, preferred_element_type=jnp.float32).astype(jnp.bfloat16).astype(jnp.float32)
    hidden_act = gelu_tanh(up_f32).astype(jnp.bfloat16)
    return normed_m, up_f32, hidden_act


def layer_forward(act_in, weights):
    w_qkv, w_out, w_up, w_down, gain_attn, gain_mlp = weights
    mid_f32, _ = attn_block(act_in.astype(jnp.float32), w_qkv, w_out, gain_attn)
    _, _, hidden_act = mlp_front(mid_f32, w_up, gain_mlp)
    down_part = jnp.einsum('bsf,fd->bsd', hidden_act, w_down, preferred_element_type=jnp.float32)
    return (mid_f32 + lax.psum(down_part, 'tp')).astype(jnp.bfloat16)


def layer_backward(act_in, grad_out, weights):
    w_qkv, w_out, w_up, w_down, gain_attn, gain_mlp = weights
    scale = w_qkv.shape[-1] ** -0.5
    in_f32 = act_in.astype(jnp.float32)
    mid_f32, (normed_a, proj_qkv, attn_probs, probs_bf, context) = attn_block(in_f32, w_qkv, w_out, gain_attn)
    normed_m, up_f32, hidden_act = mlp_front(mid_f32, w_up, gain_mlp)
    d_w_down = jnp.einsum('bsf,bsd->fd', hidden_act, grad_out, preferred_element_type=jnp.float32)
    d_act = jnp.einsum('bsd,fd->bsf', grad_out, w_down, preferred_element_type=jnp.float32).astype(jnp.bfloat16)
    _, gelu_pull = jax.vjp(gelu_tanh, up_f32)
    d_up = gelu_pull(d_act.astype(jnp.float32))[0].astype(jnp.bfloat16)
    d_w_up = jnp.einsum('bsd,bsf->df', normed_m, d_up, preferred_element_type=jnp.float32)
    d_normed_m = lax.psum(jnp.einsum('bsf,df->bsd', d_up, w_up, preferred_element_type=jnp.float32), 'tp').astype(jnp.bfloat16)
    _, norm_pull_m = jax.vjp(rms_core, mid_f32, gain_mlp.astype(jnp.float32))
    d_mid_norm, d_gain_mlp = norm_pull_m(d_normed_m.astype(jnp.float32))
    d_mid = (grad_out.astype(jnp.float32) + d_mid_norm).astype(jnp.bfloat16)
    d_w_out = jnp.einsum('bhse,bsd->hed', context, d_mid, preferred_element_type=jnp.float32)
    d_context = jnp.einsum('bsd,hed->bhse', d_mid, w_out, preferred_element_type=jnp.float32).astype(jnp.bfloat16)
    d_probs = jnp.einsum('bhqe,bhke->bhqk', d_context, proj_qkv[2], preferred_element_type=jnp.float32).astype(jnp.bfloat16).astype(jnp.float32)
    d_value = jnp.einsum('bhqk,bhqe->bhke', probs_bf, d_context, preferred_element_type=jnp.float32).astype(jnp.bfloat16)
    d_scores = attn_probs * (d_probs - jnp.sum(d_probs * attn_probs, axis=-1, keepdims=True)) * scale
    d_query = jnp.einsum('bhqk,bhke->bhqe', d_scores, proj_qkv[1].astype(jnp.float32), precision=lax.Precision.HIGHEST).astype(jnp.bfloat16)
    d_key = jnp.einsum('bhqk,bhqe->bhke', d_scores, proj_qkv[0].astype(jnp.float32), precision=lax.Precision.HIGHEST).astype(jnp.bfloat16)
    d_qkv = jnp.stack([d_query, d_key, d_value])
    d_w_qkv = jnp.einsum('bsd,kbhse->dkhe', normed_a, d_qkv, preferred_element_type=jnp.float32)
    d_normed_a = lax.psum(jnp.einsum('kbhse,dkhe->bsd', d_qkv, w_qkv, preferred_element_type=jnp.float32), 'tp').astype(jnp.bfloat16)
    _, norm_pull_a = jax.vjp(rms_core, in_f32, gain_attn.astype(jnp.float32))
    d_in_norm, d_gain_attn = norm_pull_a(d_normed_a.astype(jnp.float32))
    d_in = (d_mid.astype(jnp.float32) + d_in_norm).astype(jnp.bfloat16)
    return d_in, (d_w_qkv, d_w_out, d_w_up, d_w_down, d_gain_attn, d_gain_mlp)


def solution(mesh):
    stages = mesh.shape['stage']
    act_spec = P('rep', None, None, None)
    weight_specs = (
        P(('rep', 'stage'), None, None, 'tp', None),
        P(('rep', 'stage'), 'tp', None, None),
        P(('rep', 'stage'), None, 'tp'),
        P(('rep', 'stage'), 'tp', None),
        P(('rep', 'stage'), None),
        P(('rep', 'stage'), None),
    )

    def device_fn(inputs, targets, w_qkv, w_out, w_up, w_down, gain_attn, gain_mlp):
        weights = (w_qkv[0], w_out[0], w_up[0], w_down[0], gain_attn[0], gain_mlp[0])
        micro_count = inputs.shape[0]
        act_shape = inputs.shape[1:]
        stage_id = lax.axis_index('stage')
        num_slots = min(micro_count, 2 * stages - 1)
        total_ticks = micro_count + 2 * stages - 2
        norm_factor = 1.0 / (micro_count * act_shape[0] * act_shape[1] * act_shape[2])
        to_next = [(stage_idx, stage_idx + 1) for stage_idx in range(stages - 1)]
        to_prev = [(stage_idx + 1, stage_idx) for stage_idx in range(stages - 1)]
        is_first = stage_id == 0
        is_last = stage_id == stages - 1

        def tick(carry, tick_idx):
            from_prev, from_next, saved_inputs, grad_acc, dx_acc, loss_acc = carry
            fwd_micro = tick_idx - stage_id
            fwd_valid = (fwd_micro >= 0) & (fwd_micro < micro_count)
            fwd_index = jnp.clip(fwd_micro, 0, micro_count - 1)
            x_micro = lax.dynamic_index_in_dim(inputs, fwd_index, 0, keepdims=False)
            layer_in = jnp.where(is_first, x_micro, from_prev)
            layer_out = layer_forward(layer_in, weights)
            fwd_slot = fwd_index % num_slots
            old_slot = lax.dynamic_index_in_dim(saved_inputs, fwd_slot, 0, keepdims=False)
            saved_inputs = lax.dynamic_update_index_in_dim(saved_inputs, jnp.where(fwd_valid, layer_in, old_slot), fwd_slot, 0)
            bwd_micro = tick_idx - (2 * stages - 2) + stage_id
            bwd_valid = (bwd_micro >= 0) & (bwd_micro < micro_count)
            bwd_index = jnp.clip(bwd_micro, 0, micro_count - 1)
            stored_in = lax.dynamic_index_in_dim(saved_inputs, bwd_index % num_slots, 0, keepdims=False)
            y_micro = lax.dynamic_index_in_dim(targets, bwd_index, 0, keepdims=False)
            error_f32 = layer_out.astype(jnp.float32) - y_micro.astype(jnp.float32)
            seed_grad = (error_f32 * norm_factor).astype(jnp.bfloat16)
            grad_in = jnp.where(is_last, seed_grad, from_next)
            loss_acc = loss_acc + jnp.where(is_last & bwd_valid, 0.5 * jnp.sum(error_f32 * error_f32) * norm_factor, 0.0)
            grad_prev, layer_grads = layer_backward(stored_in, grad_in, weights)
            grad_acc = tuple(grad_sum + jnp.where(bwd_valid, grad_part, 0.0) for grad_sum, grad_part in zip(grad_acc, layer_grads))
            old_dx = lax.dynamic_index_in_dim(dx_acc, bwd_index, 0, keepdims=False)
            dx_acc = lax.dynamic_update_index_in_dim(dx_acc, jnp.where(is_first & bwd_valid, grad_prev, old_dx), bwd_index, 0)
            from_prev = lax.ppermute(layer_out, 'stage', to_next)
            from_next = lax.ppermute(grad_prev, 'stage', to_prev)
            return (from_prev, from_next, saved_inputs, grad_acc, dx_acc, loss_acc), None

        zero_act = jnp.zeros(act_shape, jnp.bfloat16)
        init_carry = (
            zero_act,
            zero_act,
            jnp.zeros((num_slots,) + act_shape, jnp.bfloat16),
            tuple(jnp.zeros(weight.shape, jnp.float32) for weight in weights),
            jnp.zeros(inputs.shape, jnp.bfloat16),
            jnp.zeros((), jnp.float32),
        )
        final_carry, _ = lax.scan(tick, init_carry, jnp.arange(total_ticks))
        grad_acc, dx_acc, loss_acc = final_carry[3], final_carry[4], final_carry[5]
        loss = lax.psum(loss_acc, 'stage').reshape(1)
        d_inputs = lax.psum(dx_acc, 'stage')
        return (loss, d_inputs) + tuple(grad_sum[None] for grad_sum in grad_acc)

    return jax.shard_map(device_fn, mesh=mesh, in_specs=(act_spec, act_spec) + weight_specs, out_specs=(P('rep'), act_spec) + weight_specs, check_vma=False)
```

profile of v0, /device:TPU:3, one launch (start us, length us, event | category | flops | bytes accessed | tf_op | source)
XLA Modules:
  0.0 6449.7 jit_solution(6152609451233520309)
XLA Ops:
  25.9 6235.9 %while.33 = (s32[]{:T(128)}, bf16[2,192,1536]{2,1,0:T(8,128)(2,1)}, bf16[2,192,1536]{2,1,0:T(8,128)(2,1)S(1)}, bf16[7,2,192,1536]{3,2,1,0:T(8,128)(2,1)}, f32[15...) while((s32[]{:T(128)}, bf16[2,192,1536]{2,1,0:T(8,128)(2,1)}, ...), condition=%wide.region_20.21_spmd.clone, body=%wide.region_0.20_spmd.clone.sunk | while | flops 42085761024 | bytes 644680640 | solution.py:142
  130.0 111.2 %all-reduce.13.cloned.1.call-done = (f32[2,192,1536]{2,1,0:T(8,128)}, f32[2,192,1536]{2,1,0:T(8,128)}) async-done(((f32[2,192,1536]{2,1,0:T(8,128)}, f32[2,192,1536]{2,1,0:T(8,128)}), (f32[2,192,1536]{2,1,0:T(8,128)}, f32[2,192,1536]{2,1,0:T(8,128)})) %all-reduce.13.cloned.1.call-update) | async-done | bytes 4718608 | tf_op jit(solution)/shard_map/while/body/eval_jaxpr/psum | solution.py:46
  276.6 56.4 all-reduce.14
  562.4 111.2 %all-reduce.13.cloned.1.call-done = (f32[2,192,1536]{2,1,0:T(8,128)}, f32[2,192,1536]{2,1,0:T(8,128)}) async-done(((f32[2,192,1536]{2,1,0:T(8,128)}, f32[2,192,1536]{2,1,0:T(8,128)}), (f32[2,192,1536]{2,1,0:T(8,128)}, f32[2,192,1536]{2,1,0:T(8,128)})) %all-reduce.13.cloned.1.call-update) | async-done | bytes 4718608 | tf_op jit(solution)/shard_map/while/body/eval_jaxpr/psum | solution.py:46
  709.0 56.2 all-reduce.14
  1009.0 111.2 %all-reduce.13.cloned.1.call-done = (f32[2,192,1536]{2,1,0:T(8,128)}, f32[2,192,1536]{2,1,0:T(8,128)}) async-done(((f32[2,192,1536]{2,1,0:T(8,128)}, f32[2,192,1536]{2,1,0:T(8,128)}), (f32[2,192,1536]{2,1,0:T(8,128)}, f32[2,192,1536]{2,1,0:T(8,128)})) %all-reduce.13.cloned.1.call-update) | async-done | bytes 4718608 | tf_op jit(solution)/shard_map/while/body/eval_jaxpr/psum | solution.py:46
  1155.8 56.2 all-reduce.14
  1455.8 111.2 %all-reduce.13.cloned.1.call-done = (f32[2,192,1536]{2,1,0:T(8,128)}, f32[2,192,1536]{2,1,0:T(8,128)}) async-done(((f32[2,192,1536]{2,1,0:T(8,128)}, f32[2,192,1536]{2,1,0:T(8,128)}), (f32[2,192,1536]{2,1,0:T(8,128)}, f32[2,192,1536]{2,1,0:T(8,128)})) %all-reduce.13.cloned.1.call-update) | async-done | bytes 4718608 | tf_op jit(solution)/shard_map/while/body/eval_jaxpr/psum | solution.py:46
  1602.4 56.4 all-reduce.14
  1902.4 111.1 %all-reduce.13.cloned.1.call-done = (f32[2,192,1536]{2,1,0:T(8,128)}, f32[2,192,1536]{2,1,0:T(8,128)}) async-done(((f32[2,192,1536]{2,1,0:T(8,128)}, f32[2,192,1536]{2,1,0:T(8,128)}), (f32[2,192,1536]{2,1,0:T(8,128)}, f32[2,192,1536]{2,1,0:T(8,128)})) %all-reduce.13.cloned.1.call-update) | async-done | bytes 4718608 | tf_op jit(solution)/shard_map/while/body/eval_jaxpr/psum | solution.py:46
  2048.9 56.2 all-reduce.14
  2123.2 55.0 all-reduce.15
  2348.9 111.2 %all-reduce.13.cloned.1.call-done = (f32[2,192,1536]{2,1,0:T(8,128)}, f32[2,192,1536]{2,1,0:T(8,128)}) async-done(((f32[2,192,1536]{2,1,0:T(8,128)}, f32[2,192,1536]{2,1,0:T(8,128)}), (f32[2,192,1536]{2,1,0:T(8,128)}, f32[2,192,1536]{2,1,0:T(8,128)})) %all-reduce.13.cloned.1.call-update) | async-done | bytes 4718608 | tf_op jit(solution)/shard_map/while/body/eval_jaxpr/psum | solution.py:46
  2495.7 56.2 all-reduce.14
  2795.7 111.2 %all-reduce.13.cloned.1.call-done = (f32[2,192,1536]{2,1,0:T(8,128)}, f32[2,192,1536]{2,1,0:T(8,128)}) async-done(((f32[2,192,1536]{2,1,0:T(8,128)}, f32[2,192,1536]{2,1,0:T(8,128)}), (f32[2,192,1536]{2,1,0:T(8,128)}, f32[2,192,1536]{2,1,0:T(8,128)})) %all-reduce.13.cloned.1.call-update) | async-done | bytes 4718608 | tf_op jit(solution)/shard_map/while/body/eval_jaxpr/psum | solution.py:46
  2942.3 56.4 all-reduce.14
  3242.3 111.1 %all-reduce.13.cloned.1.call-done = (f32[2,192,1536]{2,1,0:T(8,128)}, f32[2,192,1536]{2,1,0:T(8,128)}) async-done(((f32[2,192,1536]{2,1,0:T(8,128)}, f32[2,192,1536]{2,1,0:T(8,128)}), (f32[2,192,1536]{2,1,0:T(8,128)}, f32[2,192,1536]{2,1,0:T(8,128)})) %all-reduce.13.cloned.1.call-update) | async-done | bytes 4718608 | tf_op jit(solution)/shard_map/while/body/eval_jaxpr/psum | solution.py:46
  3388.9 56.2 all-reduce.14
  3688.9 111.2 %all-reduce.13.cloned.1.call-done = (f32[2,192,1536]{2,1,0:T(8,128)}, f32[2,192,1536]{2,1,0:T(8,128)}) async-done(((f32[2,192,1536]{2,1,0:T(8,128)}, f32[2,192,1536]{2,1,0:T(8,128)}), (f32[2,192,1536]{2,1,0:T(8,128)}, f32[2,192,1536]{2,1,0:T(8,128)})) %all-reduce.13.cloned.1.call-update) | async-done | bytes 4718608 | tf_op jit(solution)/shard_map/while/body/eval_jaxpr/psum | solution.py:46
  3835.7 56.2 all-reduce.14
  4135.7 111.2 %all-reduce.13.cloned.1.call-done = (f32[2,192,1536]{2,1,0:T(8,128)}, f32[2,192,1536]{2,1,0:T(8,128)}) async-done(((f32[2,192,1536]{2,1,0:T(8,128)}, f32[2,192,1536]{2,1,0:T(8,128)}), (f32[2,192,1536]{2,1,0:T(8,128)}, f32[2,192,1536]{2,1,0:T(8,128)})) %all-reduce.13.cloned.1.call-update) | async-done | bytes 4718608 | tf_op jit(solution)/shard_map/while/body/eval_jaxpr/psum | solution.py:46
  4282.3 56.4 all-reduce.14
  4582.3 111.1 %all-reduce.13.cloned.1.call-done = (f32[2,192,1536]{2,1,0:T(8,128)}, f32[2,192,1536]{2,1,0:T(8,128)}) async-done(((f32[2,192,1536]{2,1,0:T(8,128)}, f32[2,192,1536]{2,1,0:T(8,128)}), (f32[2,192,1536]{2,1,0:T(8,128)}, f32[2,192,1536]{2,1,0:T(8,128)})) %all-reduce.13.cloned.1.call-update) | async-done | bytes 4718608 | tf_op jit(solution)/shard_map/while/body/eval_jaxpr/psum | solution.py:46
  4728.8 56.2 all-reduce.14
  4803.1 55.0 all-reduce.15
  5028.8 111.2 %all-reduce.13.cloned.1.call-done = (f32[2,192,1536]{2,1,0:T(8,128)}, f32[2,192,1536]{2,1,0:T(8,128)}) async-done(((f32[2,192,1536]{2,1,0:T(8,128)}, f32[2,192,1536]{2,1,0:T(8,128)}), (f32[2,192,1536]{2,1,0:T(8,128)}, f32[2,192,1536]{2,1,0:T(8,128)})) %all-reduce.13.cloned.1.call-update) | async-done | bytes 4718608 | tf_op jit(solution)/shard_map/while/body/eval_jaxpr/psum | solution.py:46
  5175.6 56.2 all-reduce.14
  5475.6 111.2 %all-reduce.13.cloned.1.call-done = (f32[2,192,1536]{2,1,0:T(8,128)}, f32[2,192,1536]{2,1,0:T(8,128)}) async-done(((f32[2,192,1536]{2,1,0:T(8,128)}, f32[2,192,1536]{2,1,0:T(8,128)}), (f32[2,192,1536]{2,1,0:T(8,128)}, f32[2,192,1536]{2,1,0:T(8,128)})) %all-reduce.13.cloned.1.call-update) | async-done | bytes 4718608 | tf_op jit(solution)/shard_map/while/body/eval_jaxpr/psum | solution.py:46
  5622.2 56.4 all-reduce.14
  5922.2 111.1 %all-reduce.13.cloned.1.call-done = (f32[2,192,1536]{2,1,0:T(8,128)}, f32[2,192,1536]{2,1,0:T(8,128)}) async-done(((f32[2,192,1536]{2,1,0:T(8,128)}, f32[2,192,1536]{2,1,0:T(8,128)}), (f32[2,192,1536]{2,1,0:T(8,128)}, f32[2,192,1536]{2,1,0:T(8,128)})) %all-reduce.13.cloned.1.call-update) | async-done | bytes 4718608 | tf_op jit(solution)/shard_map/while/body/eval_jaxpr/psum | solution.py:46
  6068.8 56.2 all-reduce.14
  6275.5 158.3 %all-reduce.9.cloned.1.call-done = bf16[8,2,192,1536]{3,2,1,0:T(8,128)(2,1)} async-done(((bf16[8,2,192,1536]{3,2,1,0:T(8,128)(2,1)}), bf16[8,2,192,1536]{3,2,1,0:T(8,128)(2,1)}) %all-reduce.9.cloned.1.call-update) | async-done | bytes 9437200 | tf_op jit(solution)/shard_map/psum | solution.py:145
  (2374 shorter events, 3779.0 us)
Async XLA Ops:
  47.0 194.1 %all-reduce.13.cloned.1.call-start = ((), (), s32[]{:S(2)}) async-start(), calls=%async_computation.2 | async-start | bytes 9437184 | tf_op jit(solution)/shard_map/while/body/eval_jaxpr/psum | solution.py:46
  245.4 208.4 %collective-permute-start = (bf16[2,192,1536]{2,1,0:T(8,128)(2,1)}, bf16[2,192,1536]{2,1,0:T(8,128)(2,1)}, u32[]{:S(2)}, u32[]{:S(2)}) collective-permute-start(bf16[2,192,1536]{2,1,0:T(8,128)(2,1)} %get-tuple-element.641), channel_id=1, source_target_pairs={{0,1},{1,2},{2,3},{4,5},{5,6},{6,7}} | collective-permute-start | bytes 3538952 | tf_op jit(solution)/shard_map/while/body/eval_jaxpr/ppermute | solution.py:129
  454.0 89.1 %all-reduce.11.cloned.1.call-start = ((), (), s32[]{:S(2)}) async-start(), calls=%async_computation.1 | async-start | bytes 4718592 | tf_op jit(solution)/shard_map/while/body/eval_jaxpr/psum | solution.py:30
  475.1 198.4 %all-reduce.13.cloned.1.call-start = ((), (), s32[]{:S(2)}) async-start(), calls=%async_computation.2 | async-start | bytes 9437184 | tf_op jit(solution)/shard_map/while/body/eval_jaxpr/psum | solution.py:46
  677.8 222.6 %collective-permute-start = (bf16[2,192,1536]{2,1,0:T(8,128)(2,1)}, bf16[2,192,1536]{2,1,0:T(8,128)(2,1)}, u32[]{:S(2)}, u32[]{:S(2)}) collective-permute-start(bf16[2,192,1536]{2,1,0:T(8,128)(2,1)} %get-tuple-element.641), channel_id=1, source_target_pairs={{0,1},{1,2},{2,3},{4,5},{5,6},{6,7}} | collective-permute-start | bytes 3538952 | tf_op jit(solution)/shard_map/while/body/eval_jaxpr/ppermute | solution.py:129
  921.8 198.4 %all-reduce.13.cloned.1.call-start = ((), (), s32[]{:S(2)}) async-start(), calls=%async_computation.2 | async-start | bytes 9437184 | tf_op jit(solution)/shard_map/while/body/eval_jaxpr/psum | solution.py:46
  1124.4 222.6 %collective-permute-start = (bf16[2,192,1536]{2,1,0:T(8,128)(2,1)}, bf16[2,192,1536]{2,1,0:T(8,128)(2,1)}, u32[]{:S(2)}, u32[]{:S(2)}) collective-permute-start(bf16[2,192,1536]{2,1,0:T(8,128)(2,1)} %get-tuple-element.641), channel_id=1, source_target_pairs={{0,1},{1,2},{2,3},{4,5},{5,6},{6,7}} | collective-permute-start | bytes 3538952 | tf_op jit(solution)/shard_map/while/body/eval_jaxpr/ppermute | solution.py:129
  1368.5 198.4 %all-reduce.13.cloned.1.call-start = ((), (), s32[]{:S(2)}) async-start(), calls=%async_computation.2 | async-start | bytes 9437184 | tf_op jit(solution)/shard_map/while/body/eval_jaxpr/psum | solution.py:46
  1571.2 222.6 %collective-permute-start = (bf16[2,192,1536]{2,1,0:T(8,128)(2,1)}, bf16[2,192,1536]{2,1,0:T(8,128)(2,1)}, u32[]{:S(2)}, u32[]{:S(2)}) collective-permute-start(bf16[2,192,1536]{2,1,0:T(8,128)(2,1)} %get-tuple-element.641), channel_id=1, source_target_pairs={{0,1},{1,2},{2,3},{4,5},{5,6},{6,7}} | collective-permute-start | bytes 3538952 | tf_op jit(solution)/shard_map/while/body/eval_jaxpr/ppermute | solution.py:129
  1794.0 89.1 %all-reduce.11.cloned.1.call-start = ((), (), s32[]{:S(2)}) async-start(), calls=%async_computation.1 | async-start | bytes 4718592 | tf_op jit(solution)/shard_map/while/body/eval_jaxpr/psum | solution.py:30
  1815.1 198.4 %all-reduce.13.cloned.1.call-start = ((), (), s32[]{:S(2)}) async-start(), calls=%async_computation.2 | async-start | bytes 9437184 | tf_op jit(solution)/shard_map/while/body/eval_jaxpr/psum | solution.py:46
  2017.8 222.6 %collective-permute-start = (bf16[2,192,1536]{2,1,0:T(8,128)(2,1)}, bf16[2,192,1536]{2,1,0:T(8,128)(2,1)}, u32[]{:S(2)}, u32[]{:S(2)}) collective-permute-start(bf16[2,192,1536]{2,1,0:T(8,128)(2,1)} %get-tuple-element.641), channel_id=1, source_target_pairs={{0,1},{1,2},{2,3},{4,5},{5,6},{6,7}} | collective-permute-start | bytes 3538952 | tf_op jit(solution)/shard_map/while/body/eval_jaxpr/ppermute | solution.py:129
  2261.7 198.4 %all-reduce.13.cloned.1.call-start = ((), (), s32[]{:S(2)}) async-start(), calls=%async_computation.2 | async-start | bytes 9437184 | tf_op jit(solution)/shard_map/while/body/eval_jaxpr/psum | solution.py:46
  2464.3 222.6 %collective-permute-start = (bf16[2,192,1536]{2,1,0:T(8,128)(2,1)}, bf16[2,192,1536]{2,1,0:T(8,128)(2,1)}, u32[]{:S(2)}, u32[]{:S(2)}) collective-permute-start(bf16[2,192,1536]{2,1,0:T(8,128)(2,1)} %get-tuple-element.641), channel_id=1, source_target_pairs={{0,1},{1,2},{2,3},{4,5},{5,6},{6,7}} | collective-permute-start | bytes 3538952 | tf_op jit(solution)/shard_map/while/body/eval_jaxpr/ppermute | solution.py:129
  2708.5 198.4 %all-reduce.13.cloned.1.call-start = ((), (), s32[]{:S(2)}) async-start(), calls=%async_computation.2 | async-start | bytes 9437184 | tf_op jit(solution)/shard_map/while/body/eval_jaxpr/psum | solution.py:46
  2911.1 222.6 %collective-permute-start = (bf16[2,192,1536]{2,1,0:T(8,128)(2,1)}, bf16[2,192,1536]{2,1,0:T(8,128)(2,1)}, u32[]{:S(2)}, u32[]{:S(2)}) collective-permute-start(bf16[2,192,1536]{2,1,0:T(8,128)(2,1)} %get-tuple-element.641), channel_id=1, source_target_pairs={{0,1},{1,2},{2,3},{4,5},{5,6},{6,7}} | collective-permute-start | bytes 3538952 | tf_op jit(solution)/shard_map/while/body/eval_jaxpr/ppermute | solution.py:129
  3134.0 89.1 %all-reduce.11.cloned.1.call-start = ((), (), s32[]{:S(2)}) async-start(), calls=%async_computation.1 | async-start | bytes 4718592 | tf_op jit(solution)/shard_map/while/body/eval_jaxpr/psum | solution.py:30
  3155.1 198.4 %all-reduce.13.cloned.1.call-start = ((), (), s32[]{:S(2)}) async-start(), calls=%async_computation.2 | async-start | bytes 9437184 | tf_op jit(solution)/shard_map/while/body/eval_jaxpr/psum | solution.py:46
  3357.7 222.6 %collective-permute-start = (bf16[2,192,1536]{2,1,0:T(8,128)(2,1)}, bf16[2,192,1536]{2,1,0:T(8,128)(2,1)}, u32[]{:S(2)}, u32[]{:S(2)}) collective-permute-start(bf16[2,192,1536]{2,1,0:T(8,128)(2,1)} %get-tuple-element.641), channel_id=1, source_target_pairs={{0,1},{1,2},{2,3},{4,5},{5,6},{6,7}} | collective-permute-start | bytes 3538952 | tf_op jit(solution)/shard_map/while/body/eval_jaxpr/ppermute | solution.py:129
  3601.7 198.4 %all-reduce.13.cloned.1.call-start = ((), (), s32[]{:S(2)}) async-start(), calls=%async_computation.2 | async-start | bytes 9437184 | tf_op jit(solution)/shard_map/while/body/eval_jaxpr/psum | solution.py:46
  3804.3 222.6 %collective-permute-start = (bf16[2,192,1536]{2,1,0:T(8,128)(2,1)}, bf16[2,192,1536]{2,1,0:T(8,128)(2,1)}, u32[]{:S(2)}, u32[]{:S(2)}) collective-permute-start(bf16[2,192,1536]{2,1,0:T(8,128)(2,1)} %get-tuple-element.641), channel_id=1, source_target_pairs={{0,1},{1,2},{2,3},{4,5},{5,6},{6,7}} | collective-permute-start | bytes 3538952 | tf_op jit(solution)/shard_map/while/body/eval_jaxpr/ppermute | solution.py:129
  4048.4 198.4 %all-reduce.13.cloned.1.call-start = ((), (), s32[]{:S(2)}) async-start(), calls=%async_computation.2 | async-start | bytes 9437184 | tf_op jit(solution)/shard_map/while/body/eval_jaxpr/psum | solution.py:46
  4251.1 222.6 %collective-permute-start = (bf16[2,192,1536]{2,1,0:T(8,128)(2,1)}, bf16[2,192,1536]{2,1,0:T(8,128)(2,1)}, u32[]{:S(2)}, u32[]{:S(2)}) collective-permute-start(bf16[2,192,1536]{2,1,0:T(8,128)(2,1)} %get-tuple-element.641), channel_id=1, source_target_pairs={{0,1},{1,2},{2,3},{4,5},{5,6},{6,7}} | collective-permute-start | bytes 3538952 | tf_op jit(solution)/shard_map/while/body/eval_jaxpr/ppermute | solution.py:129
  4495.0 198.4 %all-reduce.13.cloned.1.call-start = ((), (), s32[]{:S(2)}) async-start(), calls=%async_computation.2 | async-start | bytes 9437184 | tf_op jit(solution)/shard_map/while/body/eval_jaxpr/psum | solution.py:46
  4697.6 222.6 %collective-permute-start = (bf16[2,192,1536]{2,1,0:T(8,128)(2,1)}, bf16[2,192,1536]{2,1,0:T(8,128)(2,1)}, u32[]{:S(2)}, u32[]{:S(2)}) collective-permute-start(bf16[2,192,1536]{2,1,0:T(8,128)(2,1)} %get-tuple-element.641), channel_id=1, source_target_pairs={{0,1},{1,2},{2,3},{4,5},{5,6},{6,7}} | collective-permute-start | bytes 3538952 | tf_op jit(solution)/shard_map/while/body/eval_jaxpr/ppermute | solution.py:129
  4941.6 198.4 %all-reduce.13.cloned.1.call-start = ((), (), s32[]{:S(2)}) async-start(), calls=%async_computation.2 | async-start | bytes 9437184 | tf_op jit(solution)/shard_map/while/body/eval_jaxpr/psum | solution.py:46
  5144.2 222.6 %collective-permute-start = (bf16[2,192,1536]{2,1,0:T(8,128)(2,1)}, bf16[2,192,1536]{2,1,0:T(8,128)(2,1)}, u32[]{:S(2)}, u32[]{:S(2)}) collective-permute-start(bf16[2,192,1536]{2,1,0:T(8,128)(2,1)} %get-tuple-element.641), channel_id=1, source_target_pairs={{0,1},{1,2},{2,3},{4,5},{5,6},{6,7}} | collective-permute-start | bytes 3538952 | tf_op jit(solution)/shard_map/while/body/eval_jaxpr/ppermute | solution.py:129
  5388.3 198.4 %all-reduce.13.cloned.1.call-start = ((), (), s32[]{:S(2)}) async-start(), calls=%async_computation.2 | async-start | bytes 9437184 | tf_op jit(solution)/shard_map/while/body/eval_jaxpr/psum | solution.py:46
  5591.0 222.6 %collective-permute-start = (bf16[2,192,1536]{2,1,0:T(8,128)(2,1)}, bf16[2,192,1536]{2,1,0:T(8,128)(2,1)}, u32[]{:S(2)}, u32[]{:S(2)}) collective-permute-start(bf16[2,192,1536]{2,1,0:T(8,128)(2,1)} %get-tuple-element.641), channel_id=1, source_target_pairs={{0,1},{1,2},{2,3},{4,5},{5,6},{6,7}} | collective-permute-start | bytes 3538952 | tf_op jit(solution)/shard_map/while/body/eval_jaxpr/ppermute | solution.py:129
  5834.9 198.4 %all-reduce.13.cloned.1.call-start = ((), (), s32[]{:S(2)}) async-start(), calls=%async_computation.2 | async-start | bytes 9437184 | tf_op jit(solution)/shard_map/while/body/eval_jaxpr/psum | solution.py:46
  6037.6 222.6 %collective-permute-start = (bf16[2,192,1536]{2,1,0:T(8,128)(2,1)}, bf16[2,192,1536]{2,1,0:T(8,128)(2,1)}, u32[]{:S(2)}, u32[]{:S(2)}) collective-permute-start(bf16[2,192,1536]{2,1,0:T(8,128)(2,1)} %get-tuple-element.641), channel_id=1, source_target_pairs={{0,1},{1,2},{2,3},{4,5},{5,6},{6,7}} | collective-permute-start | bytes 3538952 | tf_op jit(solution)/shard_map/while/body/eval_jaxpr/ppermute | solution.py:129
  6261.9 171.9 %all-reduce.9.cloned.1.call-start = ((), (), s32[]{:S(2)}) async-start(), calls=%async_computation | async-start | bytes 18874368 | tf_op jit(solution)/shard_map/psum | solution.py:145
  (769 other events, 8583.3 us)
Sparse Core Ops, SparseCore 0:
  47.1 63.5 all-reduce.10
  127.7 113.3 all-reduce.12
  475.3 67.8 all-reduce.10
  560.2 113.3 all-reduce.12
  921.9 67.7 all-reduce.10
  1006.7 113.3 all-reduce.12
  1368.6 67.8 all-reduce.10
  1453.5 113.3 all-reduce.12
  1815.2 67.8 all-reduce.10
  1900.1 113.3 all-reduce.12
  2261.8 67.7 all-reduce.10
  2346.7 113.3 all-reduce.12
  2708.6 67.8 all-reduce.10
  2793.4 113.3 all-reduce.12
  3155.2 67.8 all-reduce.10
  3240.1 113.3 all-reduce.12
  3601.8 67.7 all-reduce.10
  3686.6 113.3 all-reduce.12
  4048.5 67.8 all-reduce.10
  4133.4 113.3 all-reduce.12
  4495.1 67.8 all-reduce.10
  4580.0 113.3 all-reduce.12
  4941.7 67.7 all-reduce.10
  5026.5 113.3 all-reduce.12
  5388.5 67.8 all-reduce.10
  5473.3 113.3 all-reduce.12
  5835.1 67.8 all-reduce.10
  5919.9 113.3 all-reduce.12
Sparse Core Ops, SparseCore 1:
  6265.4 168.4 all-reduce.8
where the time goes:
time: 6460 us; the launch traced here: 6450 us
  waiting for transfers between devices  2430 us (38%)
  matrix products  1650 us (26%)
  blocking collectives  1570 us (24%)
  other arithmetic  415 us (6%)
  local copies, waits for them, and re-layouts  216 us (3%)
  starting transfers between devices  110 us (2%)
    psum x14, waiting for transfers between devices, layer_forward(): return (mid_f32 + lax.psum(down_part, 'tp')).astype(jnp.bfloat16)  1560 us
    psum x14, blocking collectives, layer_backward(): lax.psum(jnp.einsum('bsf,df->bsd', d_up, w_up, preferred_element_type=jnp...  788 us
    psum x14, blocking collectives, layer_backward(): lax.psum(jnp.einsum('kbhse,dkhe->bsd', d_qkv, w_qkv, preferred_element_ty...  768 us
    psum x14, waiting for transfers between devices, attn_block(): lax.psum(attn_part, 'tp')  718 us
    dot_general x28, matrix products, mlp_front(): jnp.einsum('bsd,df->bsf', normed_m, w_up, preferred_element_type=jnp.floa...  243 us
    dot_general x14, matrix products, layer_backward(): jnp.einsum('bsd,kbhse->dkhe', normed_a, d_qkv, preferred_element_type=jnp...  207 us
    dot_general x14, matrix products, layer_backward(): jnp.einsum('bsf,bsd->fd', hidden_act, grad_out, preferred_element_type=jn...  190 us
    dot_general x14, matrix products, layer_backward(): jnp.einsum('bsd,bsf->df', normed_m, d_up, preferred_element_type=jnp.floa...  186 us
  transfers between devices with their start and end apart: 57, of which 29 were waited for; matrix products, arithmetic and copies ran while one was open for 24% of the time, Pallas kernels for 0%

commit v1 on v0

v1 whole, which is shorter than its diff:
```python
import jax
import jax.numpy as jnp
from jax import lax
from jax.sharding import PartitionSpec as P

NORM_EPS = 1e-5
AX = ('tp', 'stage')
BF = jnp.bfloat16
F32 = jnp.float32

FWD = [(0, 4), (1, 5), (4, 6), (5, 7), (6, 2), (7, 3)]
BWD = [(b, a) for a, b in FWD]
R_SWAP = [(1, 4), (4, 1), (2, 7), (7, 2)]
CORE_SWAP = [(0, 1), (1, 0), (2, 3), (3, 2), (4, 5), (5, 4), (6, 7), (7, 6)]
L_TO_R = [(0, 1), (5, 4), (6, 7), (3, 2)]
R_TO_L = [(1, 0), (4, 5), (7, 6), (2, 3)]
L_ACROSS = [(0, 4), (5, 1), (6, 2), (3, 7)]


def move(value, perm):
    return lax.ppermute(value, AX, perm)


def inv_rms(x_f32):
    return lax.rsqrt(jnp.mean(x_f32 * x_f32, axis=-1, keepdims=True) + NORM_EPS)


def rms_core(x_f32, gain_f32):
    return x_f32 * inv_rms(x_f32) * gain_f32


def gelu_tanh(up_f32):
    return jax.nn.gelu(up_f32, approximate=True)


def dot(eq, a, b):
    return jnp.einsum(eq, a, b, preferred_element_type=F32)


def attn_scores(query, key):
    seq_len = query.shape[-2]
    scores = dot('bhqe,bhke->bhqk', query, key) * (query.shape[-1] ** -0.5)
    q_pos = lax.broadcasted_iota(jnp.int32, (seq_len, seq_len), 0)
    k_pos = lax.broadcasted_iota(jnp.int32, (seq_len, seq_len), 1)
    return jax.nn.softmax(jnp.where(k_pos <= q_pos, scores, -1e30), axis=-1)


def attn_forward(qkv):
    probs = attn_scores(qkv[0], qkv[1])
    return probs, dot('bhqk,bhke->bhqe', probs.astype(BF), qkv[2]).astype(BF)


def attn_backward(qkv, probs, d_context):
    scale = qkv.shape[-1] ** -0.5
    d_probs = dot('bhqe,bhke->bhqk', d_context, qkv[2]).astype(BF).astype(F32)
    d_value = dot('bhqk,bhqe->bhke', probs.astype(BF), d_context).astype(BF)
    d_scores = probs * (d_probs - jnp.sum(d_probs * probs, axis=-1, keepdims=True)) * scale
    d_query = jnp.einsum('bhqk,bhke->bhqe', d_scores, qkv[1].astype(F32), precision=lax.Precision.HIGHEST).astype(BF)
    d_key = jnp.einsum('bhqk,bhqe->bhke', d_scores, qkv[0].astype(F32), precision=lax.Precision.HIGHEST).astype(BF)
    return jnp.stack([d_query, d_key, d_value])


def home_forward(act, slots, gain_attn, gain_mlp):
    in_f32 = act.astype(F32)
    normed_a = rms_core(in_f32, gain_attn).astype(BF)
    total = in_f32
    saved_qkv = []
    part = None
    for w_qkv, w_out, _, _ in slots:
        qkv = dot('bsd,dkhe->kbhse', normed_a, w_qkv).astype(BF)
        _, context = attn_forward(qkv)
        term = dot('bhse,hed->bsd', context, w_out)
        part = term if part is None else part + term
        saved_qkv.append(qkv)
    mid = (in_f32 + part).astype(BF)
    normed_m = rms_core(mid.astype(F32), gain_mlp).astype(BF)
    part = None
    saved_up = []
    for _, _, w_up, w_down in slots:
        up = dot('bsd,df->bsf', normed_m, w_up).astype(BF)
        hidden = gelu_tanh(up.astype(F32)).astype(BF)
        term = dot('bsf,fd->bsd', hidden, w_down)
        part = term if part is None else part + term
        saved_up.append(up)
    out = (mid.astype(F32) + part).astype(BF)
    return out, (act, mid, saved_qkv, saved_up)


def norm_backward(x_f32, gain, d_normed):
    _, pull = jax.vjp(rms_core, x_f32, gain)
    return pull(d_normed)


def home_backward(saved, grad_out, slots, gain_attn, gain_mlp):
    act, mid, saved_qkv, saved_up = saved
    part = None
    for (_, _, w_up, w_down), up in zip(slots, saved_up):
        d_act = dot('bsd,fd->bsf', grad_out, w_down).astype(BF)
        _, pull = jax.vjp(gelu_tanh, up.astype(F32))
        d_up = pull(d_act.astype(F32))[0].astype(BF)
        term = dot('bsf,df->bsd', d_up, w_up)
        part = term if part is None else part + term
    d_mid_norm, d_gain_mlp = norm_backward(mid.astype(F32), gain_mlp, part.astype(BF).astype(F32))
    d_mid = (grad_out.astype(F32) + d_mid_norm).astype(BF)
    part = None
    for (w_qkv, w_out, _, _), qkv in zip(slots, saved_qkv):
        d_context = dot('bsd,hed->bhse', d_mid, w_out).astype(BF)
        probs = attn_scores(qkv[0], qkv[1])
        d_qkv = attn_backward(qkv, probs, d_context)
        term = dot('kbhse,dkhe->bsd', d_qkv, w_qkv)
        part = term if part is None else part + term
    d_in_norm, d_gain_attn = norm_backward(act.astype(F32), gain_attn, part.astype(BF).astype(F32))
    d_in = (d_mid.astype(F32) + d_in_norm).astype(BF)
    return d_in, d_mid, d_gain_attn, d_gain_mlp


def owner_grads(act, mid, d_mid, grad_out, weights):
    w_qkv, w_out, w_up, w_down, gain_attn, gain_mlp = weights
    normed_a = rms_core(act.astype(F32), gain_attn).astype(BF)
    qkv = dot('bsd,dkhe->kbhse', normed_a, w_qkv).astype(BF)
    probs, context = attn_forward(qkv)
    d_w_out = dot('bhse,bsd->hed', context, d_mid)
    d_context = dot('bsd,hed->bhse', d_mid, w_out).astype(BF)
    d_qkv = attn_backward(qkv, probs, d_context)
    d_w_qkv = dot('bsd,kbhse->dkhe', normed_a, d_qkv)
    normed_m = rms_core(mid.astype(F32), gain_mlp).astype(BF)
    up_f32 = dot('bsd,df->bsf', normed_m, w_up).astype(BF).astype(F32)
    hidden = gelu_tanh(up_f32).astype(BF)
    d_w_down = dot('bsf,bsd->fd', hidden, grad_out)
    d_act = dot('bsd,fd->bsf', grad_out, w_down).astype(BF)
    _, pull = jax.vjp(gelu_tanh, up_f32)
    d_up = pull(d_act.astype(F32))[0].astype(BF)
    d_w_up = dot('bsd,bsf->df', normed_m, d_up)
    return d_w_qkv, d_w_out, d_w_up, d_w_down


def solution(mesh):
    act_spec = P('rep', None, None, None)
    weight_specs = (
        P(('rep', 'stage'), None, None, 'tp', None),
        P(('rep', 'stage'), 'tp', None, None),
        P(('rep', 'stage'), None, 'tp'),
        P(('rep', 'stage'), 'tp', None),
        P(('rep', 'stage'), None),
        P(('rep', 'stage'), None),
    )

    def device_fn(inputs, targets, w_qkv, w_out, w_up, w_down, gain_attn, gain_mlp):
        micro_count, _, seq_len, width = inputs.shape
        norm_factor = 1.0 / (inputs.size)
        stage = lax.axis_index('stage')
        tp = lax.axis_index('tp')
        x_pos, core = stage // 2, stage % 2
        home = jnp.where(x_pos == 0, tp, 3 - tp)
        is_l = stage == home
        is_first, is_last = home == 0, home == 3
        own = (w_qkv[0], w_out[0], w_up[0], w_down[0])
        own_gains = (gain_attn[0].astype(F32), gain_mlp[0].astype(F32))

        slot_x, slot_y = [], []
        for w in own:
            held = jnp.where(is_l, w, move(w, R_SWAP))
            slot_x.append(held)
            slot_y.append(move(held, CORE_SWAP))
        slots = (tuple(slot_x), tuple(slot_y))
        gains = jnp.stack(own_gains)
        gains = jnp.where(is_l, gains, move(gains, L_TO_R))
        g_attn, g_mlp = gains[0], gains[1]

        x_core = lax.dynamic_slice_in_dim(inputs, core, 1, 1)
        x_other = lax.dynamic_slice_in_dim(inputs, 1 - core, 1, 1)
        y_core = lax.dynamic_slice_in_dim(targets, core, 1, 1)

        ticks = micro_count + 6

        saved, outs, arrived = [], [], []
        for t in range(ticks):
            recv = arrived[t - 2] if t >= 2 else jnp.zeros((1, seq_len, width), BF)
            act = jnp.where(is_first, x_core[t], recv) if t < micro_count else recv
            out, keep = home_forward(act, slots, g_attn, g_mlp)
            saved.append(keep)
            outs.append(out)
            arrived.append(move(out, FWD))

        def aligned(values, m):
            result = values[m]
            for pos in (1, 2, 3):
                result = jnp.where(home == pos, values[m + 2 * pos], result)
            return result

        loss_acc = jnp.zeros((), F32)
        seeds = []
        for m in range(micro_count):
            error = outs[m + 6].astype(F32) - y_core[m].astype(F32)
            seeds.append((error * norm_factor).astype(BF))
            loss_acc = loss_acc + 0.5 * jnp.sum(error * error) * norm_factor
        loss_acc = jnp.where(is_last, loss_acc, 0.0)

        grads = [None] * ticks
        prevs = [None] * ticks
        mids = [None] * ticks
        back = [None] * ticks
        dga = jnp.zeros((width,), F32)
        dgm = jnp.zeros((width,), F32)
        for t in reversed(range(ticks)):
            recv = back[t + 2] if t + 2 < ticks else jnp.zeros((1, seq_len, width), BF)
            grad = jnp.where(is_last, seeds[t - 6], recv) if t >= 6 else recv
            prev, d_mid, dga_t, dgm_t = home_backward(saved[t], grad, slots, g_attn, g_mlp)
            valid = (t >= 2 * home) & (t < 2 * home + micro_count)
            dga = dga + jnp.where(valid, dga_t, 0.0)
            dgm = dgm + jnp.where(valid, dgm_t, 0.0)
            grads[t], prevs[t], mids[t] = grad, prev, d_mid
            back[t] = move(prev, BWD)

        acts = [s[0] for s in saved]
        hs = [s[1] for s in saved]
        is_4 = (home == 1) & jnp.logical_not(is_l)
        is_2 = (home == 3) & jnp.logical_not(is_l)
        gather_rows = {k: [] for k in ('a', 'h', 'd', 'g')}
        for m in range(micro_count):
            def both(value):
                r1 = move(value, L_ACROSS + R_TO_L)
                r2 = move(value, R_SWAP)
                return jnp.where(is_l, value, r1), jnp.where(is_l, r1, r2)
            gather_rows['h'].append(both(aligned(hs, m)))
            gather_rows['d'].append(both(aligned(mids, m)))
            a_m, o_m = aligned(acts, m), aligned(outs, m)
            r1 = move(a_m, R_TO_L + [(6, 2)])
            r2 = move(jnp.where(is_l, o_m, a_m), [(7, 2), (0, 1), (6, 7)])
            same = jnp.where(is_l, a_m, jnp.where(is_4, x_core[m], jnp.where(is_2, r1, o_m)))
            other = jnp.where(is_l, r1, jnp.where(is_4, x_other[m], r2))
            gather_rows['a'].append((same, other))
            g_m, p_m = aligned(grads, m), aligned(prevs, m)
            r1 = move(g_m, R_TO_L + [(5, 1), (3, 7)])
            r2 = move(jnp.where(is_l, p_m, g_m), [(4, 1), (2, 7), (5, 4), (3, 2)])
            same = jnp.where(is_l, g_m, jnp.where(is_4 | is_2, p_m, r1))
            other = jnp.where(is_l, r1, r2)
            gather_rows['g'].append((same, other))
        rows = {k: jnp.concatenate([p[0] for p in v] + [p[1] for p in v], 0) for k, v in gather_rows.items()}
        weight_grads = owner_grads(rows['a'], rows['h'], rows['d'], rows['g'], own + own_gains)

        layer_ids = jnp.arange(4)
        gain_sums = jnp.where((layer_ids == home)[:, None, None], jnp.stack([dga, dgm])[None], 0.0)
        gain_sums, loss = lax.psum((gain_sums, loss_acc), AX)
        mine = jnp.sum(jnp.where((layer_ids == stage)[:, None, None], gain_sums, 0.0), 0)

        dx = jnp.stack([prevs[m] for m in range(micro_count)])
        at_b = move(dx, [(0, 4), (1, 5)])
        at_d = move(dx, [(0, 2), (1, 3)])
        at_c = move(at_b, [(4, 6), (5, 7)])
        dx = jnp.where(home == 0, dx, jnp.where(home == 1, at_b, jnp.where(home == 2, at_c, at_d)))
        other = move(dx, CORE_SWAP)
        d_inputs = jnp.concatenate([jnp.where(core == 0, dx, other), jnp.where(core == 0, other, dx)], 1)
        return (loss.reshape(1), d_inputs) + tuple(g[None] for g in weight_grads) + (mine[0][None], mine[1][None])

    return jax.shard_map(device_fn, mesh=mesh, in_specs=(act_spec, act_spec) + weight_specs, out_specs=(P('rep'), act_spec) + weight_specs, check_vma=False)
```

time: 6460 us -> 2890 us (0.45)
  the two profiles are of different devices: /device:TPU:3 before, /device:TPU:5 now
where the time goes in v1:
time: 2890 us; the launch traced here: 2880 us
  matrix products  1720 us (60%)
  starting transfers between devices  592 us (20%)
  other arithmetic  222 us (8%)
  waiting for transfers between devices  219 us (8%)
  local copies, waits for them, and re-layouts  72.4 us (3%)
  blocking collectives  32.6 us (1%)
    dot_general x263, matrix products, dot(): return jnp.einsum(eq, a, b, preferred_element_type=F32)  1500 us
    ppermute x101, starting transfers between devices, move(): return lax.ppermute(value, AX, perm)  592 us
    ppermute x101, waiting for transfers between devices, move(): return lax.ppermute(value, AX, perm)  219 us
    dot_general x29, matrix products, attn_backward(): jnp.einsum('bhqk,bhke->bhqe', d_scores, qkv[1].astype(F32), precision=lax...  84.1 us
    sub x28, matrix products, attn_scores(): return jax.nn.softmax(jnp.where(k_pos <= q_pos, scores, -1e+30), axis=-1)  72.7 us
    unnamed x1179, local copies, waits for them, and re-layouts  70.3 us
    dot_general x29, matrix products, attn_backward(): jnp.einsum('bhqk,bhqe->bhke', d_scores, qkv[0].astype(F32), precision=lax...  60.8 us
  transfers between devices with their start and end apart: 101, of which 29 were waited for; matrix products, arithmetic and copies ran while one was open for 52% of the time, Pallas kernels for 0%

profile of v1, /device:TPU:5, one launch (start us, length us, event | category | flops | bytes accessed | tf_op | source)
XLA Modules:
  0.0 2875.0 jit_solution(17273277706414794497)
XLA Ops:
  25.4 166.5 %collective-permute-start.3 = (bf16[1536,3,8,96]{0,3,2,1:T(8,128)(2,1)}, bf16[1536,3,8,96]{0,3,2,1:T(8,128)(2,1)}, u32[]{:S(2)}, u32[]{:S(2)}) collective-permute-start(bf16[1536,3,8,96]{0,3,2,1:T(8,128)(2,1)} %broadcast_select_fusion.2), channel_id=1, source_target_pairs={{0,1},{1,0},{2,3},{3,2},{4,5},{5,4},{6,7},{7,6}} | collective-permute-start | bytes 21233672 | tf_op jit(solution)/shard_map/ppermute | solution.py:21
  214.6 83.3 %collective-permute-start.8 = (bf16[3072,1536]{1,0:T(8,128)(2,1)}, bf16[3072,1536]{1,0:T(8,128)(2,1)}, u32[]{:S(2)}, u32[]{:S(2)}) collective-permute-start(bf16[3072,1536]{1,0:T(8,128)(2,1)} %broadcast_select_fusion), channel_id=1, source_target_pairs={{0,1},{1,0},{2,3},{3,2},{4,5},{5,4},{6,7},{7,6}} | collective-permute-start | bytes 28311560 | tf_op jit(solution)/shard_map/ppermute | solution.py:21
  1077.7 14.9 fusion.1357
  1234.3 15.1 fusion.1356
  1333.7 15.0 fusion.1353
  1362.4 15.1 fusion.1354
  1473.6 14.9 fusion.1348
  1515.6 14.8 fusion.1004
  1636.9 14.9 fusion.1008
  1730.0 58.5 %collective-permute-start.59 = (bf16[1,192,1536]{2,1,0:T(8,128)(2,1)}, bf16[1,192,1536]{2,1,0:T(8,128)(2,1)}, u32[]{:S(2)}, u32[]{:S(2)}) collective-permute-start(bf16[1,192,1536]{2,1,0:T(8,128)(2,1)} %get-tuple-element.114), channel_id=1, source_target_pairs={{0,4},{5,1},{6,2},{3,7},{1,0},{4,5},{7,6},{2,3}} | collective-permute-start | bytes 1769480 | tf_op jit(solution)/shard_map/ppermute | solution.py:21
  1805.7 36.2 %convert_bitcast_fusion = bf16[3,16,8,192,96]{4,3,2,0,1:T(8,128)(2,1)} fusion(bf16[16,192,1536]{2,1,0:T(8,128)(2,1)S(1)} %fusion.1507, f32[1536]{0:T(1024)S(1)} %copy-done.305, f32[16,192]{1,0:T(8,128)S(1)} %add_rsqrt_fusion.1, bf16[1,1536,3,8,96]{1,4,3,2,0:T(8,128)(2,1)} %param.10), kind=kOutput, calls=%fused_computation.70 | convolution fusion | flops 21769224192 | bytes 30689280 | tf_op jit(solution)/shard_map/bsd,dkhe->kbhse/dot_general | solution.py:37
  1841.9 16.9 fusion.103
  1858.8 26.1 fusion.2340
  1884.9 14.8 fusion.1346
  1899.7 14.7 fusion.327
  1914.5 15.2 fusion.1350
  2001.3 15.1 collective-permute-done.26
  2053.5 14.9 fusion.1016
  2135.6 32.6 %all-reduce = (f32[1]{0:T(128)}, f32[4,2,1536]{2,0,1:T(4,128)S(1)}) all-reduce(f32[1]{0:T(128)} %bitcast.324, f32[4,2,1536]{2,0,1:T(4,128)S(1)} %broadcast_select_fusion.30), channel_id=1, replica_groups=mesh['rep'=1,'tp'=2,'stage'=4] {'tp','stage'}, use_global_device_ids=true, to_apply=%region_92.93 | all-reduce | flops 12289 | bytes 98312 | tf_op jit(solution)/shard_map/psum | solution.py:244
  2207.3 37.8 %collective-permute-start.92 = (bf16[1,192,1536]{2,1,0:T(8,128)(2,1)}, bf16[1,192,1536]{2,1,0:T(8,128)(2,1)}, u32[]{:S(2)}, u32[]{:S(2)}) collective-permute-start(bf16[1,192,1536]{2,1,0:T(8,128)(2,1)} %get-tuple-element.82), channel_id=1, source_target_pairs={{1,0},{4,5},{7,6},{2,3},{5,1},{3,7}} | collective-permute-start | bytes 1769480 | tf_op jit(solution)/shard_map/ppermute | solution.py:21
  2267.8 22.4 fusion.40
  2290.2 30.0 %convert_bitcast_fusion.2 = bf16[1,16,8,192,96]{4,3,2,1,0:T(8,128)(2,1)} fusion(bf16[3,16,8,192,96]{4,3,2,0,1:T(8,128)(2,1)} %convert_bitcast_fusion, bf16[16,8,192,192]{2,3,1,0:T(8,128)(2,1)} %get-tuple-element.404, f32[16,8,192]{2,1,0:T(8,128)S(1)} %get-tuple-element.164, f32[16,8,192,192]{2,3,1,0:T(8,128)} %get-tuple-element.403, ...), kind=kOutput, calls=%fused_computation.113 | convolution fusion | flops 5461770240 | bytes 48955392 | tf_op jit(solution)/shard_map/bhqk,bhqe->bhke/dot_general | solution.py:59
  2320.2 35.0 %convert_bitcast_fusion.3 = bf16[1,16,8,192,96]{4,3,2,1,0:T(8,128)(2,1)} fusion(bf16[3,16,8,192,96]{4,3,2,0,1:T(8,128)(2,1)} %convert_bitcast_fusion, bf16[16,8,192,192]{2,3,1,0:T(8,128)(2,1)} %get-tuple-element.404, f32[16,8,192]{2,1,0:T(8,128)S(1)} %get-tuple-element.164, f32[16,8,192,192]{2,3,1,0:T(8,128)} %get-tuple-element.403, ...), kind=kOutput, calls=%fused_computation.114 | convolution fusion | flops 5461770240 | bytes 48955392 | tf_op jit(solution)/shard_map/bhqk,bhke->bhqe/dot_general | solution.py:58
  2417.1 39.0 %collective-permute-start.85 = (bf16[1,192,1536]{2,1,0:T(8,128)(2,1)}, bf16[1,192,1536]{2,1,0:T(8,128)(2,1)}, u32[]{:S(2)}, u32[]{:S(2)}) collective-permute-start(bf16[1,192,1536]{2,1,0:T(8,128)(2,1)} %get-tuple-element.110), channel_id=1, source_target_pairs={{1,0},{4,5},{7,6},{2,3},{5,1},{3,7}} | collective-permute-start | bytes 1769480 | tf_op jit(solution)/shard_map/ppermute | solution.py:21
  2468.9 35.5 %fusion.93 = f32[1,1536,3,8,96]{1,4,3,2,0:T(8,128)} fusion(bf16[1,16,8,192,96]{4,3,2,1,0:T(8,128)(2,1)} %convert_bitcast_fusion.1, bf16[1,16,8,192,96]{4,3,2,1,0:T(8,128)(2,1)} %convert_bitcast_fusion.2, bf16[1,16,8,192,96]{4,3,2,1,0:T(8,128)(2,1)} %convert_bitcast_fusion.3, f32[1536]{0:T(1024)S(1)} %copy-done.306, f32[16,192]{1,0:T(8,128)S(1)} %copy-done.248, ...), kind=kOutput, calls=%fused_computation.103 | convolution fusion | flops 21804613632 | bytes 37767168 | tf_op jit(solution)/shard_map/bsd,kbhse->dkhe/dot_general | solution.py:37
  2504.4 37.7 %convolution_convert_fusion = bf16[16,192,3072]{2,1,0:T(8,128)(2,1)} fusion(bf16[1,1536,3072]{2,1,0:T(8,128)(2,1)} %param.12, bf16[16,192,1536]{2,1,0:T(8,128)(2,1)} %copy-done.26, f32[1536]{0:T(1024)S(1)} %copy-done.303, f32[16,192]{1,0:T(8,128)S(1)} %copy-done.249), kind=kOutput, calls=%fused_computation.87 | convolution fusion | flops 29019340800 | bytes 37767168 | tf_op jit(solution)/shard_map/bsd,df->bsf/dot_general | solution.py:37
  2616.0 60.4 %fusion.2621 = bf16[16,192,3072]{2,1,0:T(8,128)(2,1)} fusion(bf16[16,192,3072]{2,1,0:T(8,128)(2,1)} %convolution_convert_fusion, bf16[1,3072,1536]{2,1,0:T(8,128)(2,1)} %param.13, bf16[16,192,1536]{2,1,0:T(8,128)(2,1)} %select_dynamic-update-slice_fusion), kind=kOutput, calls=%fused_computation.38.clone.clone.clone.clone.2 | convolution fusion | flops 29198647296 | bytes 56623104 | tf_op jit(solution)/shard_map/bsd,fd->bsf/dot_general | solution.py:37
  2676.4 36.2 %collective-permute-done.33 = bf16[8,1,192,1536]{3,2,1,0:T(8,128)(2,1)} collective-permute-done((bf16[8,1,192,1536]{3,2,1,0:T(8,128)(2,1)}, bf16[8,1,192,1536]{3,2,1,0:T(8,128)(2,1)}, u32[]{:S(2)}, u32[]{:S(2)}) %collective-permute-start.33) | collective-permute-done | bytes 4718624 | tf_op jit(solution)/shard_map/ppermute | solution.py:21
  2716.0 42.4 %fusion.67 = f32[1,3072,1536]{2,1,0:T(8,128)} fusion(bf16[16,192,1536]{2,1,0:T(8,128)(2,1)} %select_dynamic-update-slice_fusion, bf16[16,192,3072]{2,1,0:T(8,128)(2,1)} %convolution_convert_fusion), kind=kOutput, calls=%fused_computation.76 | convolution fusion | flops 29085401088 | bytes 47185920 | tf_op jit(solution)/shard_map/bsf,bsd->fd/dot_general | solution.py:37
  2758.4 16.8 fusion.104
  2775.2 38.8 %collective-permute-done.34 = bf16[8,1,192,1536]{3,2,1,0:T(8,128)(2,1)} collective-permute-done((bf16[8,1,192,1536]{3,2,1,0:T(8,128)(2,1)}, bf16[8,1,192,1536]{3,2,1,0:T(8,128)(2,1)}, u32[]{:S(2)}, u32[]{:S(2)}) %collective-permute-start.34) | collective-permute-done | bytes 4718624 | tf_op jit(solution)/shard_map/ppermute | solution.py:21
  2822.6 39.5 %fusion.64 = f32[1,1536,3072]{2,1,0:T(8,128)} fusion(bf16[16,192,1536]{2,1,0:T(8,128)(2,1)} %copy-done.26, f32[1536]{0:T(1024)S(1)} %copy-done.304, f32[16,192]{1,0:T(8,128)S(1)} %copy-done.250, bf16[16,192,3072]{2,1,0:T(8,128)(2,1)} %fusion.2621), kind=kOutput, calls=%fused_computation.75 | convolution fusion | flops 29009903616 | bytes 47204352 | tf_op jit(solution)/shard_map/bsd,bsf->df/dot_general | solution.py:37
  (1900 shorter events, 1788.5 us)
Async XLA Ops:
  0.6 191.3 %collective-permute-start.5 = (bf16[1536,3072]{1,0:T(8,128)(2,1)}, bf16[1536,3072]{1,0:T(8,128)(2,1)}, u32[]{:S(2)}, u32[]{:S(2)}) collective-permute-start(bf16[1536,3072]{1,0:T(8,128)(2,1)} %bitcast.3000), channel_id=1, source_target_pairs={{1,4},{4,1},{2,7},{7,2}} | collective-permute-start | bytes 28311560 | tf_op jit(solution)/shard_map/ppermute | solution.py:21
  8.5 196.6 %collective-permute-start.6 = (bf16[3072,1536]{1,0:T(8,128)(2,1)}, bf16[3072,1536]{1,0:T(8,128)(2,1)}, u32[]{:S(2)}, u32[]{:S(2)}) collective-permute-start(bf16[3072,1536]{1,0:T(8,128)(2,1)} %bitcast.3001), channel_id=1, source_target_pairs={{1,4},{4,1},{2,7},{7,2}} | collective-permute-start | bytes 28311560 | tf_op jit(solution)/shard_map/ppermute | solution.py:21
  12.8 285.9 %collective-permute-start.2 = (bf16[8,96,1536]{2,1,0:T(8,128)(2,1)}, bf16[8,96,1536]{2,1,0:T(8,128)(2,1)}, u32[]{:S(2)}, u32[]{:S(2)}) collective-permute-start(bf16[8,96,1536]{2,1,0:T(8,128)(2,1)} %bitcast.3027), channel_id=1, source_target_pairs={{1,4},{4,1},{2,7},{7,2}} | collective-permute-start | bytes 7077896 | tf_op jit(solution)/shard_map/ppermute | solution.py:21
  15.6 282.4 %collective-permute-start.1 = (f32[2,1536]{1,0:T(2,128)S(1)}, f32[2,1536]{1,0:T(2,128)S(1)}, u32[]{:S(2)}, u32[]{:S(2)}) collective-permute-start(f32[2,1536]{1,0:T(2,128)S(1)} %maximum_convert_fusion), channel_id=1, source_target_pairs={{0,1},{5,4},{6,7},{3,2}} | collective-permute-start | bytes 36872 | tf_op jit(solution)/shard_map/ppermute | solution.py:21
  25.4 303.9 %collective-permute-start.3 = (bf16[1536,3,8,96]{0,3,2,1:T(8,128)(2,1)}, bf16[1536,3,8,96]{0,3,2,1:T(8,128)(2,1)}, u32[]{:S(2)}, u32[]{:S(2)}) collective-permute-start(bf16[1536,3,8,96]{0,3,2,1:T(8,128)(2,1)} %broadcast_select_fusion.2), channel_id=1, source_target_pairs={{0,1},{1,0},{2,3},{3,2},{4,5},{5,4},{6,7},{7,6}} | collective-permute-start | bytes 21233672 | tf_op jit(solution)/shard_map/ppermute | solution.py:21
  201.2 176.1 %collective-permute-start.7 = (bf16[1536,3072]{1,0:T(8,128)(2,1)}, bf16[1536,3072]{1,0:T(8,128)(2,1)}, u32[]{:S(2)}, u32[]{:S(2)}) collective-permute-start(bf16[1536,3072]{1,0:T(8,128)(2,1)} %broadcast_select_fusion.1), channel_id=1, source_target_pairs={{0,1},{1,0},{2,3},{3,2},{4,5},{5,4},{6,7},{7,6}} | collective-permute-start | bytes 28311560 | tf_op jit(solution)/shard_map/ppermute | solution.py:21
  214.6 168.5 %collective-permute-start.8 = (bf16[3072,1536]{1,0:T(8,128)(2,1)}, bf16[3072,1536]{1,0:T(8,128)(2,1)}, u32[]{:S(2)}, u32[]{:S(2)}) collective-permute-start(bf16[3072,1536]{1,0:T(8,128)(2,1)} %broadcast_select_fusion), channel_id=1, source_target_pairs={{0,1},{1,0},{2,3},{3,2},{4,5},{5,4},{6,7},{7,6}} | collective-permute-start | bytes 28311560 | tf_op jit(solution)/shard_map/ppermute | solution.py:21
  1316.5 391.4 %collective-permute-start.38 = (bf16[1,192,1536]{2,1,0:T(8,128)(2,1)}, bf16[1,192,1536]{2,1,0:T(8,128)(2,1)}, u32[]{:S(2)}, u32[]{:S(2)}) collective-permute-start(bf16[1,192,1536]{2,1,0:T(8,128)(2,1)} %get-tuple-element.148), channel_id=1, source_target_pairs={{1,0},{4,5},{7,6},{2,3},{6,2}} | collective-permute-start | bytes 1769480 | tf_op jit(solution)/shard_map/ppermute | solution.py:21
  1317.8 407.9 %collective-permute-start.46 = (bf16[1,192,1536]{2,1,0:T(8,128)(2,1)}, bf16[1,192,1536]{2,1,0:T(8,128)(2,1)}, u32[]{:S(2)}, u32[]{:S(2)}) collective-permute-start(bf16[1,192,1536]{2,1,0:T(8,128)(2,1)} %get-tuple-element.146), channel_id=1, source_target_pairs={{7,2},{0,1},{6,7}} | collective-permute-start | bytes 1769480 | tf_op jit(solution)/shard_map/ppermute | solution.py:21
  1319.3 391.5 %collective-permute-start.39 = (bf16[1,192,1536]{2,1,0:T(8,128)(2,1)}, bf16[1,192,1536]{2,1,0:T(8,128)(2,1)}, u32[]{:S(2)}, u32[]{:S(2)}) collective-permute-start(bf16[1,192,1536]{2,1,0:T(8,128)(2,1)} %get-tuple-element.188), channel_id=1, source_target_pairs={{1,0},{4,5},{7,6},{2,3},{6,2}} | collective-permute-start | bytes 1769480 | tf_op jit(solution)/shard_map/ppermute | solution.py:21
  1457.6 258.6 %collective-permute-start.41 = (bf16[1,192,1536]{2,1,0:T(8,128)(2,1)}, bf16[1,192,1536]{2,1,0:T(8,128)(2,1)}, u32[]{:S(2)}, u32[]{:S(2)}) collective-permute-start(bf16[1,192,1536]{2,1,0:T(8,128)(2,1)} %get-tuple-element.185), channel_id=1, source_target_pairs={{1,0},{4,5},{7,6},{2,3},{6,2}} | collective-permute-start | bytes 1769480 | tf_op jit(solution)/shard_map/ppermute | solution.py:21
  1623.5 82.6 %collective-permute-start.37 = (bf16[1,192,1536]{2,1,0:T(8,128)(2,1)}, bf16[1,192,1536]{2,1,0:T(8,128)(2,1)}, u32[]{:S(2)}, u32[]{:S(2)}) collective-permute-start(bf16[1,192,1536]{2,1,0:T(8,128)(2,1)} %get-tuple-element.203), channel_id=1, source_target_pairs={{1,0},{4,5},{7,6},{2,3},{6,2}} | collective-permute-start | bytes 1769480 | tf_op jit(solution)/shard_map/ppermute | solution.py:21
  1716.2 72.7 %collective-permute-start.49 = (bf16[1,192,1536]{2,1,0:T(8,128)(2,1)S(1)}, bf16[1,192,1536]{2,1,0:T(8,128)(2,1)S(1)}, u32[]{:S(2)}, u32[]{:S(2)}) collective-permute-start(bf16[1,192,1536]{2,1,0:T(8,128)(2,1)S(1)} %copy-done.394), channel_id=1, source_target_pairs={{7,2},{0,1},{6,7}} | collective-permute-start | bytes 1769480 | tf_op jit(solution)/shard_map/ppermute | solution.py:21
  1722.5 74.0 %collective-permute-start.51 = (bf16[1,192,1536]{2,1,0:T(8,128)(2,1)S(1)}, bf16[1,192,1536]{2,1,0:T(8,128)(2,1)S(1)}, u32[]{:S(2)}, u32[]{:S(2)}) collective-permute-start(bf16[1,192,1536]{2,1,0:T(8,128)(2,1)S(1)} %copy-done.393), channel_id=1, source_target_pairs={{7,2},{0,1},{6,7}} | collective-permute-start | bytes 1769480 | tf_op jit(solution)/shard_map/ppermute | solution.py:21
  1725.7 66.0 %collective-permute-start.50 = (bf16[1,192,1536]{2,1,0:T(8,128)(2,1)S(1)}, bf16[1,192,1536]{2,1,0:T(8,128)(2,1)S(1)}, u32[]{:S(2)}, u32[]{:S(2)}) collective-permute-start(bf16[1,192,1536]{2,1,0:T(8,128)(2,1)S(1)} %copy-done.226), channel_id=1, source_target_pairs={{7,2},{0,1},{6,7}} | collective-permute-start | bytes 1769480 | tf_op jit(solution)/shard_map/ppermute | solution.py:21
  1728.0 70.7 %collective-permute-start.52 = (bf16[1,192,1536]{2,1,0:T(8,128)(2,1)S(1)}, bf16[1,192,1536]{2,1,0:T(8,128)(2,1)S(1)}, u32[]{:S(2)}, u32[]{:S(2)}) collective-permute-start(bf16[1,192,1536]{2,1,0:T(8,128)(2,1)S(1)} %copy-done.225), channel_id=1, source_target_pairs={{7,2},{0,1},{6,7}} | collective-permute-start | bytes 1769480 | tf_op jit(solution)/shard_map/ppermute | solution.py:21
  1730.0 469.9 %collective-permute-start.59 = (bf16[1,192,1536]{2,1,0:T(8,128)(2,1)}, bf16[1,192,1536]{2,1,0:T(8,128)(2,1)}, u32[]{:S(2)}, u32[]{:S(2)}) collective-permute-start(bf16[1,192,1536]{2,1,0:T(8,128)(2,1)} %get-tuple-element.114), channel_id=1, source_target_pairs={{0,4},{5,1},{6,2},{3,7},{1,0},{4,5},{7,6},{2,3}} | collective-permute-start | bytes 1769480 | tf_op jit(solution)/shard_map/ppermute | solution.py:21
  1788.9 464.0 %collective-permute-start.67 = (bf16[1,192,1536]{2,1,0:T(8,128)(2,1)}, bf16[1,192,1536]{2,1,0:T(8,128)(2,1)}, u32[]{:S(2)}, u32[]{:S(2)}) collective-permute-start(bf16[1,192,1536]{2,1,0:T(8,128)(2,1)} %get-tuple-element.114), channel_id=1, source_target_pairs={{1,4},{4,1},{2,7},{7,2}} | collective-permute-start | bytes 1769480 | tf_op jit(solution)/shard_map/ppermute | solution.py:21
  1791.7 410.2 %collective-permute-start.60 = (bf16[1,192,1536]{2,1,0:T(8,128)(2,1)}, bf16[1,192,1536]{2,1,0:T(8,128)(2,1)}, u32[]{:S(2)}, u32[]{:S(2)}) collective-permute-start(bf16[1,192,1536]{2,1,0:T(8,128)(2,1)} %get-tuple-element.112), channel_id=1, source_target_pairs={{0,4},{5,1},{6,2},{3,7},{1,0},{4,5},{7,6},{2,3}} | collective-permute-start | bytes 1769480 | tf_op jit(solution)/shard_map/ppermute | solution.py:21
  1796.5 88.4 %collective-permute-start.25 = (bf16[1,192,1536]{2,1,0:T(8,128)(2,1)}, bf16[1,192,1536]{2,1,0:T(8,128)(2,1)S(1)}, u32[]{:S(2)}, u32[]{:S(2)}) collective-permute-start(bf16[1,192,1536]{2,1,0:T(8,128)(2,1)} %get-tuple-element.95), channel_id=1, source_target_pairs={{4,0},{5,1},{6,4},{7,5},{2,6},{3,7}} | collective-permute-start | bytes 1769480 | tf_op jit(solution)/shard_map/ppermute | solution.py:21
  1798.8 115.7 %collective-permute-start.31 = (bf16[1,192,1536]{2,1,0:T(8,128)(2,1)S(1)}, bf16[1,192,1536]{2,1,0:T(8,128)(2,1)S(1)}, u32[]{:S(2)}, u32[]{:S(2)}) collective-permute-start(bf16[1,192,1536]{2,1,0:T(8,128)(2,1)S(1)} %get-tuple-element.91), channel_id=1, source_target_pairs={{4,0},{5,1},{6,4},{7,5},{2,6},{3,7}} | collective-permute-start | bytes 1769480 | tf_op jit(solution)/shard_map/ppermute | solution.py:21
  2189.4 65.0 %collective-permute-start.68 = (bf16[1,192,1536]{2,1,0:T(8,128)(2,1)}, bf16[1,192,1536]{2,1,0:T(8,128)(2,1)S(1)}, u32[]{:S(2)}, u32[]{:S(2)}) collective-permute-start(bf16[1,192,1536]{2,1,0:T(8,128)(2,1)} %get-tuple-element.112), channel_id=1, source_target_pairs={{1,4},{4,1},{2,7},{7,2}} | collective-permute-start | bytes 1769480 | tf_op jit(solution)/shard_map/ppermute | solution.py:21
  2195.7 378.1 %collective-permute-start.91 = (bf16[1,192,1536]{2,1,0:T(8,128)(2,1)}, bf16[1,192,1536]{2,1,0:T(8,128)(2,1)}, u32[]{:S(2)}, u32[]{:S(2)}) collective-permute-start(bf16[1,192,1536]{2,1,0:T(8,128)(2,1)} %get-tuple-element.86), channel_id=1, source_target_pairs={{1,0},{4,5},{7,6},{2,3},{5,1},{3,7}} | collective-permute-start | bytes 1769480 | tf_op jit(solution)/shard_map/ppermute | solution.py:21
  2207.3 373.8 %collective-permute-start.92 = (bf16[1,192,1536]{2,1,0:T(8,128)(2,1)}, bf16[1,192,1536]{2,1,0:T(8,128)(2,1)}, u32[]{:S(2)}, u32[]{:S(2)}) collective-permute-start(bf16[1,192,1536]{2,1,0:T(8,128)(2,1)} %get-tuple-element.82), channel_id=1, source_target_pairs={{1,0},{4,5},{7,6},{2,3},{5,1},{3,7}} | collective-permute-start | bytes 1769480 | tf_op jit(solution)/shard_map/ppermute | solution.py:21
  2245.2 366.7 %collective-permute-start.99 = (bf16[1,192,1536]{2,1,0:T(8,128)(2,1)}, bf16[1,192,1536]{2,1,0:T(8,128)(2,1)}, u32[]{:S(2)}, u32[]{:S(2)}) collective-permute-start(bf16[1,192,1536]{2,1,0:T(8,128)(2,1)} %get-tuple-element.84), channel_id=1, source_target_pairs={{4,1},{2,7},{5,4},{3,2}} | collective-permute-start | bytes 1769480 | tf_op jit(solution)/shard_map/ppermute | solution.py:21
  2252.9 114.9 %collective-permute-start.69 = (bf16[1,192,1536]{2,1,0:T(8,128)(2,1)}, bf16[1,192,1536]{2,1,0:T(8,128)(2,1)}, u32[]{:S(2)}, u32[]{:S(2)}) collective-permute-start(bf16[1,192,1536]{2,1,0:T(8,128)(2,1)} %get-tuple-element.197), channel_id=1, source_target_pairs={{0,4},{5,1},{6,2},{3,7},{1,0},{4,5},{7,6},{2,3}} | collective-permute-start | bytes 1769480 | tf_op jit(solution)/shard_map/ppermute | solution.py:21
  2254.4 116.2 %collective-permute-start.70 = (bf16[1,192,1536]{2,1,0:T(8,128)(2,1)}, bf16[1,192,1536]{2,1,0:T(8,128)(2,1)}, u32[]{:S(2)}, u32[]{:S(2)}) collective-permute-start(bf16[1,192,1536]{2,1,0:T(8,128)(2,1)} %get-tuple-element.193), channel_id=1, source_target_pairs={{0,4},{5,1},{6,2},{3,7},{1,0},{4,5},{7,6},{2,3}} | collective-permute-start | bytes 1769480 | tf_op jit(solution)/shard_map/ppermute | solution.py:21
  2417.1 125.0 %collective-permute-start.85 = (bf16[1,192,1536]{2,1,0:T(8,128)(2,1)}, bf16[1,192,1536]{2,1,0:T(8,128)(2,1)}, u32[]{:S(2)}, u32[]{:S(2)}) collective-permute-start(bf16[1,192,1536]{2,1,0:T(8,128)(2,1)} %get-tuple-element.110), channel_id=1, source_target_pairs={{1,0},{4,5},{7,6},{2,3},{5,1},{3,7}} | collective-permute-start | bytes 1769480 | tf_op jit(solution)/shard_map/ppermute | solution.py:21
  2456.3 90.3 %collective-permute-start.86 = (bf16[1,192,1536]{2,1,0:T(8,128)(2,1)}, bf16[1,192,1536]{2,1,0:T(8,128)(2,1)}, u32[]{:S(2)}, u32[]{:S(2)}) collective-permute-start(bf16[1,192,1536]{2,1,0:T(8,128)(2,1)} %get-tuple-element.106), channel_id=1, source_target_pairs={{1,0},{4,5},{7,6},{2,3},{5,1},{3,7}} | collective-permute-start | bytes 1769480 | tf_op jit(solution)/shard_map/ppermute | solution.py:21
  2604.9 107.7 %collective-permute-start.33 = (bf16[8,1,192,1536]{3,2,1,0:T(8,128)(2,1)}, bf16[8,1,192,1536]{3,2,1,0:T(8,128)(2,1)}, u32[]{:S(2)}, u32[]{:S(2)}) collective-permute-start(bf16[8,1,192,1536]{3,2,1,0:T(8,128)(2,1)} %bitcast_dynamic-update-slice_fusion), channel_id=1, source_target_pairs={{0,4},{1,5}} | collective-permute-start | bytes 14155784 | tf_op jit(solution)/shard_map/ppermute | solution.py:21
  2607.1 168.1 %collective-permute-start.35 = (bf16[8,1,192,1536]{3,2,1,0:T(8,128)(2,1)}, bf16[8,1,192,1536]{3,2,1,0:T(8,128)(2,1)}, u32[]{:S(2)}, u32[]{:S(2)}) collective-permute-start(bf16[8,1,192,1536]{3,2,1,0:T(8,128)(2,1)} %bitcast_dynamic-update-slice_fusion), channel_id=1, source_target_pairs={{0,2},{1,3}} | collective-permute-start | bytes 14155784 | tf_op jit(solution)/shard_map/ppermute | solution.py:21
  2712.6 101.4 %collective-permute-start.34 = (bf16[8,1,192,1536]{3,2,1,0:T(8,128)(2,1)}, bf16[8,1,192,1536]{3,2,1,0:T(8,128)(2,1)}, u32[]{:S(2)}, u32[]{:S(2)}) collective-permute-start(bf16[8,1,192,1536]{3,2,1,0:T(8,128)(2,1)} %collective-permute-done.33), channel_id=1, source_target_pairs={{4,6},{5,7}} | collective-permute-start | bytes 14155784 | tf_op jit(solution)/shard_map/ppermute | solution.py:21
  (655 other events, 9474.4 us)

commit v2 on v1

v2 whole, which is shorter than its diff:
```python
import functools

import jax
import jax.numpy as jnp
from jax import lax
from jax.experimental import pallas as pl
from jax.experimental.pallas import tpu as pltpu
from jax.sharding import PartitionSpec as P

NORM_EPS = 1e-5
AX = ('tp', 'stage')
BF = jnp.bfloat16
F32 = jnp.float32
MESH = pl.DeviceIdType.MESH
ANY = pl.ANY

R_SWAP = [(1, 4), (4, 1), (2, 7), (7, 2)]
CORE_SWAP = [(0, 1), (1, 0), (2, 3), (3, 2), (4, 5), (5, 4), (6, 7), (7, 6)]
L_TO_R = [(0, 1), (5, 4), (6, 7), (3, 2)]

GELU_A = 0.7978845608028654
GELU_B = 0.044715
CHUNK = 1024
SUB = 256
DEPTH = 3
HEAD_PAD = 128


def move(value, perm):
    return lax.ppermute(value, AX, perm)


def rms_core(x_f32, gain_f32):
    inv_rms = lax.rsqrt(jnp.mean(x_f32 * x_f32, axis=-1, keepdims=True) + NORM_EPS)
    return x_f32 * inv_rms * gain_f32


def gelu_tanh(up_f32):
    return jax.nn.gelu(up_f32, approximate=True)


def dot(eq, a, b):
    return jnp.einsum(eq, a, b, preferred_element_type=F32)


def mm(a, b):
    return lax.dot_general(a, b, (((1,), (0,)), ((), ())), preferred_element_type=F32)


def mm_nt(a, b):
    return lax.dot_general(a, b, (((1,), (1,)), ((), ())), preferred_element_type=F32)


def mm_tn(a, b):
    return lax.dot_general(a, b, (((0,), (0,)), ((), ())), preferred_element_type=F32)


class Place:
    def __init__(self):
        self.tp = lax.axis_index('tp')
        self.stage = lax.axis_index('stage')
        self.core = self.stage % 2
        self.x_pos = self.stage // 2
        self.home = self.x_pos * (3 - 2 * self.tp) + self.tp
        self.is_l = self.stage == self.home
        self.sib = self.stage + 1 - 2 * self.core

    def at(self, tp, stage):
        return {'tp': tp, 'stage': stage}

    @property
    def sibling(self):
        return self.at(self.tp, self.sib)

    @property
    def across(self):
        return self.at(1 - self.tp, self.stage)

    @property
    def across_other(self):
        return self.at(1 - self.tp, self.sib)

    def chain(self, delta):
        there = self.home + delta
        x_pos = there // 2
        tp = there % 2 + x_pos * (1 - 2 * (there % 2))
        return self.at(tp, 2 * x_pos + self.core)


def entry_barrier(place):
    barrier = pltpu.get_barrier_semaphore()
    for d_tp in (0, 1):
        for d_stage in range(4):
            if d_tp or d_stage:
                tp = place.tp + d_tp - 2 * d_tp * place.tp
                stage = (place.stage + d_stage) % 4
                pl.semaphore_signal(barrier, inc=1, device_id=place.at(tp, stage), device_id_type=MESH)
    pl.semaphore_wait(barrier, 7)


def remote(src, dst, send_sem, recv_sem, device_id):
    return pltpu.make_async_remote_copy(src_ref=src, dst_ref=dst, send_sem=send_sem, recv_sem=recv_sem, device_id=device_id, device_id_type=MESH)


class Stream:
    def __init__(self, buf, sem, parts, total):
        self.buf, self.sem, self.parts, self.total = buf, sem, parts, total
        self.per_tick = sum(p[1] for p in parts)

    def view(self, ref, axis, index):
        where = pl.ds(pl.multiple_of(index * CHUNK, CHUNK), CHUNK)
        return ref.at[where, :] if axis == 0 else ref.at[:, where]

    def start(self, seq):
        @pl.when(seq < self.total)
        def _():
            j = seq % self.per_tick
            slot = seq % DEPTH
            base = 0
            for ref, chunks, axis in self.parts:
                low = base

                @pl.when((j >= low) & (j < low + chunks))
                def _(ref=ref, low=low, axis=axis):
                    pltpu.make_async_copy(self.view(ref, axis, j - low), self.buf.at[slot], self.sem.at[slot]).start()
                base += chunks

    def prime(self):
        for seq in range(DEPTH):
            self.start(jnp.int32(seq))

    def wait(self, seq):
        ref, _, axis = self.parts[0]
        slot = seq % DEPTH
        pltpu.make_async_copy(self.view(ref, axis, 0), self.buf.at[slot], self.sem.at[slot]).wait()
        return self.buf.at[slot]


def rows_loop(total, step, body):
    def run(i, carry):
        body(pl.ds(pl.multiple_of(i * step, step), step))
        return carry
    lax.fori_loop(0, total // step, run, 0)


def norm_rows(src, gain_row, dst, total):
    def body(rows):
        v = src[rows, :].astype(F32)
        inv = lax.rsqrt(jnp.mean(v * v, axis=-1, keepdims=True) + NORM_EPS)
        dst[rows, :] = (v * inv * gain_row).astype(BF)
    rows_loop(total, 32, body)


def gelu_gate(u):
    u2 = u * u
    t = jnp.tanh(u * (GELU_A + (GELU_A * GELU_B) * u2))
    return 0.5 * t + 0.5, u2


def causal_probs(q, k, scale):
    s = mm_nt(q, k) * scale
    q_pos = lax.broadcasted_iota(jnp.int32, s.shape, 0)
    k_pos = lax.broadcasted_iota(jnp.int32, s.shape, 1)
    s = jnp.where(k_pos <= q_pos, s, -1e30)
    e = jnp.exp(s - jnp.max(s, axis=-1, keepdims=True))
    return e * (1.0 / jnp.sum(e, axis=-1, keepdims=True))


def lanes(offset, size):
    return pl.ds(pl.multiple_of(offset, 128), size)


def forward_kernel(dims, x_ref, wqx, wqy, wox, woy, wux, wuy, wdx, wdy, gains,
                   a_s, h_s, out_s, qkv_s, u_s, oh_same, oh_other, oa_same, oa_other,
                   abuf, hbuf, obuf, nbuf, qkvbuf, ubuf, zbuf, ctxbuf, acc, wn, wk,
                   act_sem, hop_send, save_sem, stream_n, stream_k, os_sem, oo_sem, as_sem, ao_sem, send_sems, big_sem):
    micro, seq, width, heads, head_dim, ffn = dims
    place = Place()
    is_first, is_last = place.home == 0, place.home == 3
    home02 = (place.home == 0) | (place.home == 2)
    is_r = jnp.logical_not(place.is_l)
    half = heads // 2 * HEAD_PAD
    qkv_cols = 6 * half
    entry_barrier(place)
    sn = Stream(wn, stream_n, [(wqx, 3, 1), (wqy, 3, 1), (wux, 3, 1), (wuy, 3, 1)], micro * 12)
    sk = Stream(wk, stream_k, [(wox, 1, 0), (woy, 1, 0), (wdx, 3, 0), (wdy, 3, 0)], micro * 8)

    @pl.when(is_first)
    def _():
        for m in range(micro):
            pltpu.make_async_copy(x_ref.at[m], abuf.at[m], act_sem.at[m]).start()
    sn.prime()
    sk.prime()

    def big_copies(m):
        return (pltpu.make_async_copy(qkvbuf, qkv_s.at[m], big_sem.at[0]), pltpu.make_async_copy(ubuf, u_s.at[m], big_sem.at[1]))

    def tick(m, carry):
        act, mid, out = abuf.at[m], hbuf.at[m], obuf.at[m]
        pltpu.make_async_copy(x_ref.at[m], act, act_sem.at[m]).wait()
        pltpu.make_async_copy(act, a_s.at[m], save_sem.at[0]).start()

        @pl.when(place.is_l)
        def _():
            pltpu.make_async_copy(act, oa_same.at[m], as_sem).start()

        @pl.when(is_r)
        def _():
            remote(act, oa_other.at[m], send_sems.at[0], ao_sem, place.sibling).start()

        @pl.when((place.home == 2) & place.is_l)
        def _():
            remote(act, oa_same.at[m], send_sems.at[1], as_sem, place.across).start()

        @pl.when((place.home == 2) & is_r)
        def _():
            remote(act, oa_other.at[m], send_sems.at[1], ao_sem, place.across_other).start()

        norm_rows(act, gains[0:1, :], nbuf, seq)

        @pl.when(m > 0)
        def _():
            big_copies(m)[0].wait()

        def qkv_step(j, c):
            w = sn.wait(m * 12 + j)
            for n in range(0, CHUNK, SUB):
                qkvbuf[:, lanes(j * CHUNK + n, SUB)] = mm(nbuf[...], w[:, n:n + SUB]).astype(BF)
            sn.start(m * 12 + j + DEPTH)
            return c
        lax.fori_loop(0, 6, qkv_step, 0)
        big_copies(m)[0].start()

        def head_step(i, c):
            for r in range(4):
                base = (i // 2) * (3 * half) + ((i % 2) * 4 + r) * HEAD_PAD
                q = qkvbuf[:, lanes(base, HEAD_PAD)]
                k = qkvbuf[:, lanes(base + half, HEAD_PAD)]
                v = qkvbuf[:, lanes(base + 2 * half, HEAD_PAD)]
                probs = causal_probs(q, k, head_dim ** -0.5).astype(BF)
                ctxbuf[:, lanes((i * 4 + r) * HEAD_PAD, HEAD_PAD)] = mm(probs, v).astype(BF)
            return c
        lax.fori_loop(0, heads // 4, head_step, 0)

        w0, w1 = sk.wait(m * 8), sk.wait(m * 8 + 1)
        for n in range(0, width, SUB):
            total = mm(ctxbuf[:, 0:half], w0[:, n:n + SUB]) + mm(ctxbuf[:, half:2 * half], w1[:, n:n + SUB])
            mid[:, n:n + SUB] = (act[:, n:n + SUB].astype(F32) + total).astype(BF)
        sk.start(m * 8 + DEPTH)
        sk.start(m * 8 + 1 + DEPTH)
        pltpu.make_async_copy(mid, h_s.at[m], save_sem.at[1]).start()

        norm_rows(mid, gains[1:2, :], nbuf, seq)

        @pl.when(place.is_l)
        def _():
            pltpu.make_async_copy(mid, oh_same.at[m], os_sem).start()
            remote(mid, oh_same.at[m], send_sems.at[2], os_sem, place.across).start()

        @pl.when(is_r)
        def _():
            remote(mid, oh_other.at[m], send_sems.at[2], oo_sem, place.sibling).start()
            remote(mid, oh_other.at[m], send_sems.at[3], oo_sem, place.across_other).start()

        @pl.when(m > 0)
        def _():
            big_copies(m)[1].wait()

        acc[...] = jnp.zeros_like(acc)

        def mlp_step(j, c):
            w = sn.wait(m * 12 + 6 + j)
            for n in range(0, CHUNK, SUB):
                u = mm(nbuf[...], w[:, n:n + SUB]).astype(BF)
                ubuf[:, lanes(j * CHUNK + n, SUB)] = u
                uf = u.astype(F32)
                zbuf[:, n:n + SUB] = (uf * gelu_gate(uf)[0]).astype(BF)
            sn.start(m * 12 + 6 + j + DEPTH)
            w2 = sk.wait(m * 8 + 2 + j)
            for n in range(0, width, SUB):
                acc[:, n:n + SUB] += mm(zbuf[...], w2[:, n:n + SUB])
            sk.start(m * 8 + 2 + j + DEPTH)
            return c
        lax.fori_loop(0, 6, mlp_step, 0)
        big_copies(m)[1].start()

        def finish(rows):
            out[rows, :] = (mid[rows, :].astype(F32) + acc[rows, :]).astype(BF)
        rows_loop(seq, 32, finish)

        @pl.when(jnp.logical_not(is_last))
        def _():
            remote(out, abuf.at[m], hop_send, act_sem.at[m], place.chain(1)).start()
        pltpu.make_async_copy(out, out_s.at[m], save_sem.at[2]).start()

        @pl.when(home02 & place.is_l)
        def _():
            remote(out, oa_other.at[m], send_sems.at[4], ao_sem, place.sibling).start()

        @pl.when(home02 & is_r)
        def _():
            pltpu.make_async_copy(out, oa_same.at[m], as_sem).start()
        return carry

    lax.fori_loop(0, micro, tick, 0)

    for copy in big_copies(micro - 1):
        copy.wait()
    for buf, dst, index in ((abuf, a_s, 0), (hbuf, h_s, 1), (obuf, out_s, 2)):
        pltpu.make_async_copy(buf, dst, save_sem.at[index]).wait()

    def sent(buf, sem):
        remote(buf, a_s, sem, act_sem.at[0], place.sibling).wait_send()

    def got(dst, sem):
        pltpu.make_async_copy(dst, dst, sem).wait()

    sent(hbuf, send_sems.at[2])

    @pl.when(is_r)
    def _():
        sent(abuf, send_sems.at[0])
        sent(hbuf, send_sems.at[3])

    @pl.when(place.home == 2)
    def _():
        sent(abuf, send_sems.at[1])

    @pl.when(home02 & place.is_l)
    def _():
        sent(obuf, send_sems.at[4])

    @pl.when(jnp.logical_not(is_last))
    def _():
        sent(obuf, hop_send)
    got(oh_same, os_sem)
    got(oh_other, oo_sem)

    @pl.when(place.is_l | (place.home != 1))
    def _():
        got(oa_same, as_sem)
        got(oa_other, ao_sem)


def backward_kernel(dims, seed_ref, a_ref, h_ref, qkv_ref, u_ref, wdx, wdy, wox, woy, wux, wuy, wqx, wqy, gains,
                    dx_s, od_same, od_other, og_same, og_other, dgain,
                    gbuf, dbuf, pbuf, accg, qkvbuf, ubuf, habuf, dupbuf, dctxbuf, dqkvbuf, acc, wn, wk,
                    act_sem, hop_send, save_sem, stream_n, stream_k, load_sem, os_sem, oo_sem, gs_sem, go_sem, send_sems):
    micro, seq, width, heads, head_dim, ffn = dims
    place = Place()
    is_first, is_last = place.home == 0, place.home == 3
    home13 = (place.home == 1) | (place.home == 3)
    is_r = jnp.logical_not(place.is_l)
    half = heads // 2 * HEAD_PAD
    scale = head_dim ** -0.5
    entry_barrier(place)
    sn = Stream(wn, stream_n, [(wdx, 3, 1), (wdy, 3, 1), (wox, 1, 1), (woy, 1, 1)], micro * 8)
    sk = Stream(wk, stream_k, [(wux, 3, 0), (wuy, 3, 0), (wqx, 3, 0), (wqy, 3, 0)], micro * 12)

    @pl.when(is_last)
    def _():
        for m in range(micro):
            pltpu.make_async_copy(seed_ref.at[m], gbuf.at[m], act_sem.at[m]).start()

    def loads(i):
        m = micro - 1 - i
        slot = i % 2
        return (pltpu.make_async_copy(u_ref.at[m], ubuf.at[slot], load_sem.at[0, slot]),
                pltpu.make_async_copy(qkv_ref.at[m], qkvbuf.at[slot], load_sem.at[1, slot]),
                pltpu.make_async_copy(h_ref.at[m], habuf.at[slot, 0], load_sem.at[2, slot]),
                pltpu.make_async_copy(a_ref.at[m], habuf.at[slot, 1], load_sem.at[3, slot]))

    sn.prime()
    sk.prime()
    for copy in loads(0):
        copy.start()
    accg[...] = jnp.zeros_like(accg)

    def norm_back(index, x, dn, base, dst, gain_row):
        def body(rows):
            xf = x[rows, :].astype(F32)
            dy = dn[rows, :].astype(BF).astype(F32)
            inv = lax.rsqrt(jnp.mean(xf * xf, axis=-1, keepdims=True) + NORM_EPS)
            xn = xf * inv
            accg[index] += jnp.sum((dy * xn).reshape(4, 8, width), axis=0)
            dyg = dy * gain_row
            dx = inv * (dyg - xn * jnp.mean(dyg * xn, axis=-1, keepdims=True))
            dst[rows, :] = (base[rows, :].astype(F32) + dx).astype(BF)
        rows_loop(seq, 32, body)

    def tick(i, carry):
        m = micro - 1 - i
        slot = i % 2
        grad, dmid, prev = gbuf.at[m], dbuf.at[m], pbuf.at[m]
        u_now, qkv_now, h_now, a_now = ubuf.at[slot], qkvbuf.at[slot], habuf.at[slot, 0], habuf.at[slot, 1]

        @pl.when(i + 1 < micro)
        def _():
            for copy in loads(i + 1):
                copy.start()
        pltpu.make_async_copy(seed_ref.at[m], grad, act_sem.at[m]).wait()

        @pl.when(place.is_l)
        def _():
            pltpu.make_async_copy(grad, og_same.at[m], gs_sem).start()

        @pl.when(is_r)
        def _():
            remote(grad, og_other.at[m], send_sems.at[0], go_sem, place.sibling).start()

        @pl.when(home13 & place.is_l)
        def _():
            remote(grad, og_same.at[m], send_sems.at[1], gs_sem, place.across).start()

        @pl.when(home13 & is_r)
        def _():
            remote(grad, og_other.at[m], send_sems.at[1], go_sem, place.across_other).start()

        for copy in loads(i)[:1]:
            copy.wait()
        acc[...] = jnp.zeros_like(acc)

        def mlp_step(j, c):
            w = sn.wait(i * 8 + j)
            for n in range(0, CHUNK, SUB):
                dz = mm(grad[...], w[:, n:n + SUB]).astype(BF).astype(F32)
                u = u_now[:, lanes(j * CHUNK + n, SUB)].astype(F32)
                gate, u2 = gelu_gate(u)
                slope = gate + u * gate * (1.0 - gate) * (2.0 * GELU_A + (6.0 * GELU_A * GELU_B) * u2)
                dupbuf[:, n:n + SUB] = (dz * slope).astype(BF)
            sn.start(i * 8 + j + DEPTH)
            w2 = sk.wait(i * 12 + j)
            for n in range(0, width, SUB):
                acc[:, n:n + SUB] += mm(dupbuf[...], w2[:, n:n + SUB])
            sk.start(i * 12 + j + DEPTH)
            return c
        lax.fori_loop(0, 6, mlp_step, 0)

        for copy in loads(i)[1:]:
            copy.wait()
        norm_back(1, h_now, acc, grad, dmid, gains[1:2, :])

        for c in range(2):
            w = sn.wait(i * 8 + 6 + c)
            for n in range(0, CHUNK, SUB):
                dctxbuf[:, c * CHUNK + n:c * CHUNK + n + SUB] = mm(dmid[...], w[:, n:n + SUB]).astype(BF)
            sn.start(i * 8 + 6 + c + DEPTH)

        @pl.when(place.is_l)
        def _():
            pltpu.make_async_copy(dmid, od_same.at[m], os_sem).start()
            remote(dmid, od_same.at[m], send_sems.at[2], os_sem, place.across).start()

        @pl.when(is_r)
        def _():
            remote(dmid, od_other.at[m], send_sems.at[2], oo_sem, place.sibling).start()
            remote(dmid, od_other.at[m], send_sems.at[3], oo_sem, place.across_other).start()

        def head_step(t, c):
            for r in range(2):
                base = (t // 4) * (3 * half) + ((t % 4) * 2 + r) * HEAD_PAD
                q = qkv_now[:, lanes(base, HEAD_PAD)]
                k = qkv_now[:, lanes(base + half, HEAD_PAD)]
                v = qkv_now[:, lanes(base + 2 * half, HEAD_PAD)]
                dc = dctxbuf[:, lanes((t * 2 + r) * HEAD_PAD, HEAD_PAD)]
                probs = causal_probs(q, k, scale)
                dp = mm_nt(dc, v).astype(BF).astype(F32)
                ds = probs * (dp - jnp.sum(dp * probs, axis=-1, keepdims=True)) * scale
                dv = mm_tn(probs.astype(BF), dc)
                hi = ds.astype(BF)
                rest = ds - hi.astype(F32)
                lo = rest.astype(BF)
                tail = (rest - lo.astype(F32)).astype(BF)
                dq = mm(hi, k) + (mm(lo, k) + mm(tail, k))
                dk = mm_tn(hi, q) + (mm_tn(lo, q) + mm_tn(tail, q))
                dqkvbuf[:, lanes(base, HEAD_PAD)] = dq.astype(BF)
                dqkvbuf[:, lanes(base + half, HEAD_PAD)] = dk.astype(BF)
                dqkvbuf[:, lanes(base + 2 * half, HEAD_PAD)] = dv.astype(BF)
            return c
        lax.fori_loop(0, heads // 2, head_step, 0)

        acc[...] = jnp.zeros_like(acc)

        def qkv_step(j, c):
            w2 = sk.wait(i * 12 + 6 + j)
            for n in range(0, width, SUB):
                acc[:, n:n + SUB] += mm(dqkvbuf[:, lanes(j * CHUNK, CHUNK)], w2[:, n:n + SUB])
            sk.start(i * 12 + 6 + j + DEPTH)
            return c
        lax.fori_loop(0, 6, qkv_step, 0)
        norm_back(0, a_now, acc, dmid, prev, gains[0:1, :])

        @pl.when(jnp.logical_not(is_first))
        def _():
            remote(prev, gbuf.at[m], hop_send, act_sem.at[m], place.chain(-1)).start()
        pltpu.make_async_copy(prev, dx_s.at[m], save_sem).start()

        @pl.when(home13 & place.is_l)
        def _():
            remote(prev, og_other.at[m], send_sems.at[4], go_sem, place.sibling).start()

        @pl.when(home13 & is_r)
        def _():
            pltpu.make_async_copy(prev, og_same.at[m], gs_sem).start()
        return carry

    lax.fori_loop(0, micro, tick, 0)
    dgain[...] = accg[...]
    pltpu.make_async_copy(pbuf, dx_s, save_sem).wait()

    def sent(buf, sem):
        remote(buf, dx_s, sem, act_sem.at[0], place.sibling).wait_send()

    def got(dst, sem):
        pltpu.make_async_copy(dst, dst, sem).wait()

    sent(dbuf, send_sems.at[2])

    @pl.when(is_r)
    def _():
        sent(gbuf, send_sems.at[0])
        sent(dbuf, send_sems.at[3])

    @pl.when(home13)
    def _():
        sent(gbuf, send_sems.at[1])

    @pl.when(home13 & place.is_l)
    def _():
        sent(pbuf, send_sems.at[4])

    @pl.when(jnp.logical_not(is_first))
    def _():
        sent(pbuf, hop_send)
    got(od_same, os_sem)
    got(od_other, oo_sem)
    got(og_same, gs_sem)
    got(og_other, go_sem)


def bf(*shape):
    return jax.ShapeDtypeStruct(shape, BF)


def forward_phase(dims, x, weights, gains):
    micro, seq, width, heads, head_dim, ffn = dims
    half = heads // 2 * HEAD_PAD
    act = bf(micro, seq, width)
    vmem, dma = pltpu.VMEM, pltpu.SemaphoreType.DMA
    return pl.pallas_call(
        functools.partial(forward_kernel, dims),
        out_shape=(act, act, act, bf(micro, seq, 6 * half), bf(micro, seq, ffn), act, act, act, act),
        in_specs=[pl.BlockSpec(memory_space=ANY)] * 9 + [pl.BlockSpec(memory_space=vmem)],
        out_specs=(pl.BlockSpec(memory_space=ANY),) * 9,
        scratch_shapes=[
            vmem((micro, seq, width), BF), vmem((micro, seq, width), BF), vmem((micro, seq, width), BF),
            vmem((seq, width), BF), vmem((seq, 6 * half), BF), vmem((seq, ffn), BF), vmem((seq, CHUNK), BF), vmem((seq, 2 * half), BF),
            vmem((seq, width), F32), vmem((DEPTH, width, CHUNK), BF), vmem((DEPTH, CHUNK, width), BF),
            dma((micro,)), dma(()), dma((3,)), dma((DEPTH,)), dma((DEPTH,)), dma(()), dma(()), dma(()), dma(()), dma((5,)), dma((2,)),
        ],
        compiler_params=pltpu.CompilerParams(collective_id=0, has_side_effects=True, vmem_limit_bytes=60 * 1024 * 1024),
        name='forward_phase',
    )(x, *weights, gains)


def backward_phase(dims, seeds, acts, mids, qkv, ups, weights, gains):
    micro, seq, width, heads, head_dim, ffn = dims
    half = heads // 2 * HEAD_PAD
    act = bf(micro, seq, width)
    vmem, dma = pltpu.VMEM, pltpu.SemaphoreType.DMA
    return pl.pallas_call(
        functools.partial(backward_kernel, dims),
        out_shape=(act, act, act, act, act, jax.ShapeDtypeStruct((2, 8, width), F32)),
        in_specs=[pl.BlockSpec(memory_space=ANY)] * 13 + [pl.BlockSpec(memory_space=vmem)],
        out_specs=(pl.BlockSpec(memory_space=ANY),) * 5 + (pl.BlockSpec(memory_space=vmem),),
        scratch_shapes=[
            vmem((micro, seq, width), BF), vmem((micro, seq, width), BF), vmem((micro, seq, width), BF),
            vmem((2, 8, width), F32), vmem((2, seq, 6 * half), BF), vmem((2, seq, ffn), BF), vmem((2, 2, seq, width), BF),
            vmem((seq, CHUNK), BF), vmem((seq, 2 * half), BF), vmem((seq, 6 * half), BF), vmem((seq, width), F32),
            vmem((DEPTH, width, CHUNK), BF), vmem((DEPTH, CHUNK, width), BF),
            dma((micro,)), dma(()), dma(()), dma((DEPTH,)), dma((DEPTH,)), dma((4, 2)), dma(()), dma(()), dma(()), dma(()), dma((5,)),
        ],
        compiler_params=pltpu.CompilerParams(collective_id=1, has_side_effects=True, vmem_limit_bytes=62 * 1024 * 1024),
        name='backward_phase',
    )(seeds, acts, mids, qkv, ups, *weights, gains)


def attn_scores(query, key):
    seq_len = query.shape[-2]
    scores = dot('bhqe,bhke->bhqk', query, key) * (query.shape[-1] ** -0.5)
    q_pos = lax.broadcasted_iota(jnp.int32, (seq_len, seq_len), 0)
    k_pos = lax.broadcasted_iota(jnp.int32, (seq_len, seq_len), 1)
    return jax.nn.softmax(jnp.where(k_pos <= q_pos, scores, -1e30), axis=-1)


def attn_backward(qkv, probs, d_context):
    scale = qkv.shape[-1] ** -0.5
    d_probs = dot('bhqe,bhke->bhqk', d_context, qkv[2]).astype(BF).astype(F32)
    d_value = dot('bhqk,bhqe->bhke', probs.astype(BF), d_context).astype(BF)
    d_scores = probs * (d_probs - jnp.sum(d_probs * probs, axis=-1, keepdims=True)) * scale
    d_query = jnp.einsum('bhqk,bhke->bhqe', d_scores, qkv[1].astype(F32), precision=lax.Precision.HIGHEST).astype(BF)
    d_key = jnp.einsum('bhqk,bhqe->bhke', d_scores, qkv[0].astype(F32), precision=lax.Precision.HIGHEST).astype(BF)
    return jnp.stack([d_query, d_key, d_value])


def owner_grads(act, mid, d_mid, grad_out, weights):
    w_qkv, w_out, w_up, w_down, gain_attn, gain_mlp = weights
    normed_a = rms_core(act.astype(F32), gain_attn).astype(BF)
    qkv = dot('bsd,dkhe->kbhse', normed_a, w_qkv).astype(BF)
    probs = attn_scores(qkv[0], qkv[1])
    context = dot('bhqk,bhke->bhqe', probs.astype(BF), qkv[2]).astype(BF)
    d_w_out = dot('bhse,bsd->hed', context, d_mid)
    d_context = dot('bsd,hed->bhse', d_mid, w_out).astype(BF)
    d_qkv = attn_backward(qkv, probs, d_context)
    d_w_qkv = dot('bsd,kbhse->dkhe', normed_a, d_qkv)
    normed_m = rms_core(mid.astype(F32), gain_mlp).astype(BF)
    up_f32 = dot('bsd,df->bsf', normed_m, w_up).astype(BF).astype(F32)
    hidden = gelu_tanh(up_f32).astype(BF)
    d_w_down = dot('bsf,bsd->fd', hidden, grad_out)
    d_act = dot('bsd,fd->bsf', grad_out, w_down).astype(BF)
    _, pull = jax.vjp(gelu_tanh, up_f32)
    d_up = pull(d_act.astype(F32))[0].astype(BF)
    d_w_up = dot('bsd,bsf->df', normed_m, d_up)
    return d_w_qkv, d_w_out, d_w_up, d_w_down


def pad_qkv(w):
    pad = HEAD_PAD - w.shape[-1]
    return jnp.pad(w, ((0, 0), (0, 0), (0, 0), (0, pad))).reshape(w.shape[0], -1)


def pad_out(w):
    pad = HEAD_PAD - w.shape[1]
    return jnp.pad(w, ((0, 0), (0, pad), (0, 0))).reshape(-1, w.shape[2])


def solution(mesh):
    act_spec = P('rep', None, None, None)
    weight_specs = (
        P(('rep', 'stage'), None, None, 'tp', None),
        P(('rep', 'stage'), 'tp', None, None),
        P(('rep', 'stage'), None, 'tp'),
        P(('rep', 'stage'), 'tp', None),
        P(('rep', 'stage'), None),
        P(('rep', 'stage'), None),
    )

    def device_fn(inputs, targets, w_qkv, w_out, w_up, w_down, gain_attn, gain_mlp):
        micro_count, _, seq_len, width = inputs.shape
        dims = (micro_count, seq_len, width, 2 * w_out.shape[1], w_out.shape[2], 2 * w_up.shape[2])
        norm_factor = 1.0 / (inputs.size)
        stage = lax.axis_index('stage')
        tp = lax.axis_index('tp')
        x_pos, core = stage // 2, stage % 2
        home = jnp.where(x_pos == 0, tp, 3 - tp)
        is_l = stage == home
        is_last = home == 3
        own = (w_qkv[0], w_out[0], w_up[0], w_down[0])
        own_gains = (gain_attn[0].astype(F32), gain_mlp[0].astype(F32))

        slots = []
        for w in own:
            held = jnp.where(is_l, w, move(w, R_SWAP))
            slots.append((held, move(held, CORE_SWAP)))
        gains = jnp.stack(own_gains)
        gains = jnp.where(is_l, gains, move(gains, L_TO_R))
        wq = [pad_qkv(w) for w in slots[0]]
        wo = [pad_out(w) for w in slots[1]]
        wu, wd = slots[2], slots[3]

        x_core = lax.dynamic_index_in_dim(inputs, core, 1, keepdims=False)
        x_other = lax.dynamic_index_in_dim(inputs, 1 - core, 1, keepdims=False)
        y_core = lax.dynamic_index_in_dim(targets, core, 1, keepdims=False)

        acts, mids, outs, qkv, ups, oh_same, oh_other, oa_same, oa_other = forward_phase(dims, x_core, (*wq, *wo, *wu, *wd), gains)
        error = outs.astype(F32) - y_core.astype(F32)
        seeds = (error * norm_factor).astype(BF)
        loss = jnp.where(is_last, 0.5 * jnp.sum(error * error) * norm_factor, 0.0)

        turned = [w.T for w in (*wd, *wo, *wu, *wq)]
        dx, od_same, od_other, og_same, og_other, gain_sum = backward_phase(dims, seeds, acts, mids, qkv, ups, turned, gains)

        is_4 = (home == 1) & jnp.logical_not(is_l)
        both = lambda same, other: jnp.concatenate([same, other], 0)
        rows_a = both(jnp.where(is_4, x_core, oa_same), jnp.where(is_4, x_other, oa_other))
        weight_grads = owner_grads(rows_a, both(oh_same, oh_other), both(od_same, od_other), both(og_same, og_other), own + own_gains)

        layer_ids = jnp.arange(4)
        gain_sums = jnp.where((layer_ids == home)[:, None, None], jnp.sum(gain_sum, 1)[None], 0.0)
        gain_sums, loss = lax.psum((gain_sums, loss), AX)
        mine = jnp.sum(jnp.where((layer_ids == stage)[:, None, None], gain_sums, 0.0), 0)

        dx = dx[:, None]
        at_b = move(dx, [(0, 4), (1, 5)])
        at_d = move(dx, [(0, 2), (1, 3)])
        at_c = move(at_b, [(4, 6), (5, 7)])
        dx = jnp.where(home == 0, dx, jnp.where(home == 1, at_b, jnp.where(home == 2, at_c, at_d)))
        other = move(dx, CORE_SWAP)
        d_inputs = jnp.concatenate([jnp.where(core == 0, dx, other), jnp.where(core == 0, other, dx)], 1)
        return (loss.reshape(1), d_inputs) + tuple(g[None] for g in weight_grads) + (mine[0][None], mine[1][None])

    return jax.shard_map(device_fn, mesh=mesh, in_specs=(act_spec, act_spec) + weight_specs, out_specs=(P('rep'), act_spec) + weight_specs, check_vma=False)
```

time: 2890 us -> 1860 us (0.64)
  the two profiles are of different devices: /device:TPU:5 before, /device:TPU:3 now
where the time goes in v2:
time: 1860 us
  Pallas kernels  733 us (39%)
  matrix products  375 us (20%)
  starting transfers between devices  299 us (16%)
  local copies, waits for them, and re-layouts  159 us (9%)
  blocking collectives  122 us (7%)
  other arithmetic  109 us (6%)
  waiting for transfers between devices  56.6 us (3%)
    pallas_call x1, Pallas kernels, forward_phase(): pl.pallas_call(functools.partial(forward_kernel, dims), out_shape=(act, a...  411 us
    pallas_call x1, Pallas kernels, backward_phase(): pl.pallas_call(functools.partial(backward_kernel, dims), out_shape=(act,...  322 us
    dot_general x11, matrix products, dot(): return jnp.einsum(eq, a, b, preferred_element_type=F32)  310 us
    ppermute x13, starting transfers between devices, move(): return lax.ppermute(value, AX, perm)  299 us
    psum x1, blocking collectives, device_fn(): gain_sums, loss = lax.psum((gain_sums, loss), AX)  122 us
    ppermute x13, waiting for transfers between devices, move(): return lax.ppermute(value, AX, perm)  56.6 us
    unnamed x63, local copies, waits for them, and re-layouts  41.8 us
  transfers between devices with their start and end apart: 13, of which 1 were waited for; matrix products, arithmetic and copies ran while one was open for 17% of the time, Pallas kernels for 0%

profile of v2, /device:TPU:3, one launch (start us, length us, event | category | flops | bytes accessed | tf_op | source)
XLA Modules:
  0.0 1855.1 jit_solution(12810821575347796169)
XLA Ops:
  0.6 12.6 copy.36
  17.5 12.6 copy.37
  38.0 10.8 broadcast_select_fusion.1
  48.8 82.4 %collective-permute-start.5 = (bf16[1536,3072]{0,1:T(8,128)(2,1)}, bf16[1536,3072]{0,1:T(8,128)(2,1)}, u32[]{:S(2)}, u32[]{:S(2)}) collective-permute-start(bf16[1536,3072]{0,1:T(8,128)(2,1)} %broadcast_select_fusion.1), channel_id=1, source_target_pairs={{0,1},{1,0},{2,3},{3,2},{4,5},{5,4},{6,7},{7,6}} | collective-permute-start | bytes 28311560 | tf_op jit(solution)/shard_map/ppermute | solution.py:30
  135.8 94.6 %collective-permute-start.7 = (bf16[3072,1536]{0,1:T(8,128)(2,1)}, bf16[3072,1536]{0,1:T(8,128)(2,1)}, u32[]{:S(2)}, u32[]{:S(2)}) collective-permute-start(bf16[3072,1536]{0,1:T(8,128)(2,1)} %broadcast_select_fusion), channel_id=1, source_target_pairs={{0,1},{1,0},{2,3},{3,2},{4,5},{5,4},{6,7},{7,6}} | collective-permute-start | bytes 28311560 | tf_op jit(solution)/shard_map/ppermute | solution.py:30
  237.1 68.5 %collective-permute-start.1 = (bf16[1536,3,8,96]{0,3,2,1:T(8,128)(2,1)}, bf16[1536,3,8,96]{0,3,2,1:T(8,128)(2,1)}, u32[]{:S(2)}, u32[]{:S(2)}) collective-permute-start(bf16[1536,3,8,96]{0,3,2,1:T(8,128)(2,1)} %broadcast_select_fusion.2), channel_id=1, source_target_pairs={{0,1},{1,0},{2,3},{3,2},{4,5},{5,4},{6,7},{7,6}} | collective-permute-start | bytes 21233672 | tf_op jit(solution)/shard_map/ppermute | solution.py:30
  308.1 29.3 %collective-permute-start.3 = (bf16[8,96,1536]{2,1,0:T(8,128)(2,1)}, bf16[8,96,1536]{2,1,0:T(8,128)(2,1)}, u32[]{:S(2)}, u32[]{:S(2)}) collective-permute-start(bf16[8,96,1536]{2,1,0:T(8,128)(2,1)} %broadcast_select_fusion.6), channel_id=1, source_target_pairs={{0,1},{1,0},{2,3},{3,2},{4,5},{5,4},{6,7},{7,6}} | collective-permute-start | bytes 7077896 | tf_op jit(solution)/shard_map/ppermute | solution.py:30
  368.6 12.6 copy.38.wqx
  381.2 12.7 copy.42.wux
  393.9 12.6 copy.44.wdx
  414.3 12.6 copy.39.wqy
  426.9 12.6 copy.43.wuy
  439.6 12.6 copy.45.wdy
  452.2 410.6 %forward_phase.1 = (bf16[8,192,1536]{2,1,0:T(8,128)(2,1)}, bf16[8,192,1536]{2,1,0:T(8,128)(2,1)}, bf16[8,192,1536]{2,1,0:T(8,128)(2,1)}, bf16[8,192,6144]{2,1,0:...) custom-call(bf16[8,192,1536]{2,1,0:T(8,128)(2,1)} %dynamic-slice_bit, ...), custom_call_target="tpu_custom_call" | custom-call | tf_op jit(solution)/shard_map/forward_phase/pallas_call | solution.py:550
  868.7 36.8 %convolution_convert_fusion = bf16[16,192,3072]{2,1,0:T(8,128)(2,1)} fusion(bf16[1,1536,3072]{2,1,0:T(8,128)(2,1)} %param.12, f32[1536]{0:T(1024)S(1)} %convert_reduce_fusion, f32[16,192]{1,0:T(8,128)S(1)} %add_rsqrt_fusion, bf16[8,192,1536]{2,1,0:T(8,128)(2,1)} %get-tuple-element.34, bf16[8,192,1536]{2,1,0:T(8,128)(2,1)S(1)} %bitcast.155), kind=kOutput, calls=%fused_computation.59 | convolution fusion | flops 29024059392 | bytes 37767168 | tf_op jit(solution)/shard_map/bsd,df->bsf/dot_general | solution.py:43
  910.4 9.2 multiply_convert_fusion
  919.5 322.0 %backward_phase.1 = (bf16[8,192,1536]{2,1,0:T(8,128)(2,1)}, bf16[8,192,1536]{2,1,0:T(8,128)(2,1)}, bf16[8,192,1536]{2,1,0:T(8,128)(2,1)}, bf16[8,192,1536]{2,1,0...) custom-call(bf16[8,192,1536]{2,1,0:T(8,128)(2,1)} %get-tuple-element.58.seed_ref, ...), custom_call_target="tpu_custom_call" | custom-call | tf_op jit(solution)/shard_map/backward_phase/pallas_call | solution.py:571
  1256.3 13.6 fusion.81
  1283.9 36.2 %convert_bitcast_fusion = bf16[3,16,8,192,96]{4,3,2,0,1:T(8,128)(2,1)} fusion(f32[1536]{0:T(1024)S(1)} %copy-done.13, f32[16,192]{1,0:T(8,128)S(1)} %add_rsqrt_fusion.1, bf16[1,1536,3,8,96]{1,4,3,2,0:T(8,128)(2,1)} %param.10, bf16[8,192,1536]{2,1,0:T(8,128)(2,1)S(1)} %get-tuple-element.67, bf16[8,192,1536]{2,1,0:T(8,128)(2,1)} %get-tuple-element.68), kind=kOutput, calls=%fused_computation.42 | convolution fusion | flops 21783379968 | bytes 30689280 | tf_op jit(solution)/shard_map/bsd,dkhe->kbhse/dot_general | solution.py:43
  1320.1 17.1 fusion.75
  1337.1 25.0 %fusion.119 = (f32[16,8,192]{2,1,0:T(8,128)S(1)}, f32[16,8,192,192]{2,3,1,0:T(8,128)}) fusion(f32[16,8,192,192]{2,3,1,0:T(8,128)} %fusion.75, pred[192,192]{0,1:T(8,128)(4,1)S(1)} %copy-done.9), kind=kOutput, calls=%fused_computation.138 | output fusion | flops 28311744 | bytes 37883904 | tf_op jit(solution)/shard_map/sub | solution.py:593
  1362.1 22.4 %fusion.12 = (f32[16,8,192]{2,1,0:T(8,128)S(1)}, bf16[16,8,192,192]{2,3,1,0:T(8,128)(2,1)}, bf16[16,8,192,192]{2,3,1,0:T(8,128)(2,1)}) fusion(f32[16,8,192,192]{2,3,1,0:T(8,128)} %get-tuple-element.65, f32[16,8,192]{2,1,0:T(8,128)S(1)} %get-tuple-element.64, bf16[3,16,8,192,96]{4,3,2,0,1:T(8,128)(2,1)} %convert_bitcast_fusion, ...), kind=kOutput, calls=%fused_computation.20 | convolution fusion | flops 934256640 | bytes 56819712 | tf_op jit(solution)/shard_map/bhqe,bhke->bhqk/dot_general | solution.py:43
  1384.5 34.8 %convert_bitcast_fusion.3 = bf16[1,16,8,192,96]{4,3,2,1,0:T(8,128)(2,1)} fusion(bf16[3,16,8,192,96]{4,3,2,0,1:T(8,128)(2,1)} %convert_bitcast_fusion, bf16[16,8,192,192]{2,3,1,0:T(8,128)(2,1)} %get-tuple-element.66, f32[16,8,192]{2,1,0:T(8,128)S(1)} %get-tuple-element.56, f32[16,8,192,192]{2,3,1,0:T(8,128)} %get-tuple-element.65, ...), kind=kOutput, calls=%fused_computation.91 | convolution fusion | flops 5461770240 | bytes 48955392 | tf_op jit(solution)/shard_map/bhqk,bhke->bhqe/dot_general | solution.py:601
  1419.4 30.4 %convert_bitcast_fusion.2 = bf16[1,16,8,192,96]{4,3,2,1,0:T(8,128)(2,1)} fusion(bf16[3,16,8,192,96]{4,3,2,0,1:T(8,128)(2,1)} %convert_bitcast_fusion, bf16[16,8,192,192]{2,3,1,0:T(8,128)(2,1)} %get-tuple-element.66, f32[16,8,192]{2,1,0:T(8,128)S(1)} %get-tuple-element.56, f32[16,8,192,192]{2,3,1,0:T(8,128)} %get-tuple-element.65, ...), kind=kOutput, calls=%fused_computation.90 | convolution fusion | flops 5461770240 | bytes 48955392 | tf_op jit(solution)/shard_map/bhqk,bhqe->bhke/dot_general | solution.py:602
  1453.9 37.0 %fusion.53 = bf16[16,192,3072]{2,1,0:T(8,128)(2,1)} fusion(bf16[16,192,1536]{2,1,0:T(8,128)(2,1)} %get-tuple-element.70, bf16[1,3072,1536]{2,1,0:T(8,128)(2,1)} %param.13), kind=kOutput, calls=%fused_computation.65 | convolution fusion | flops 28991029248 | bytes 37748736 | tf_op jit(solution)/shard_map/bsd,fd->bsf/dot_general | solution.py:43
  1490.9 12.5 convert_bitcast_fusion.1
  1504.7 33.0 %fusion.65 = f32[1,1536,3,8,96]{1,4,3,2,0:T(8,128)} fusion(bf16[1,16,8,192,96]{4,3,2,1,0:T(8,128)(2,1)} %convert_bitcast_fusion.1, bf16[1,16,8,192,96]{4,3,2,1,0:T(8,128)(2,1)} %convert_bitcast_fusion.2, bf16[1,16,8,192,96]{4,3,2,1,0:T(8,128)(2,1)} %convert_bitcast_fusion.3, f32[1536]{0:T(1024)S(1)} %copy-done.14, f32[16,192]{1,0:T(8,128)S(1)} %copy-done.12, ...), kind=kOutput, calls=%fused_computation.80 | convolution fusion | flops 21818769408 | bytes 37767168 | tf_op jit(solution)/shard_map/bsd,kbhse->dkhe/dot_general | solution.py:43
  1537.8 41.6 %fusion.36 = f32[1,1536,3072]{2,1,0:T(8,128)} fusion(bf16[16,192,3072]{2,1,0:T(8,128)(2,1)} %convolution_convert_fusion, bf16[16,192,3072]{2,1,0:T(8,128)(2,1)} %fusion.53, bf16[16,192,1536]{2,1,0:T(8,128)(2,1)S(1)} %copy-done.3), kind=kOutput, calls=%fused_computation.47 | convolution fusion | flops 29198647296 | bytes 66060288 | tf_op jit(solution)/shard_map/bsd,bsf->df/dot_general | solution.py:43
  1582.2 42.6 %fusion.39 = f32[1,3072,1536]{2,1,0:T(8,128)} fusion(bf16[16,192,1536]{2,1,0:T(8,128)(2,1)} %get-tuple-element.70, bf16[16,192,3072]{2,1,0:T(8,128)(2,1)} %convolution_convert_fusion), kind=kOutput, calls=%fused_computation.48 | convolution fusion | flops 29085401088 | bytes 47185920 | tf_op jit(solution)/shard_map/bsf,bsd->fd/dot_general | solution.py:43
  1624.8 56.6 %collective-permute-done.11 = bf16[8,1,192,1536]{3,2,0,1:T(8,128)(2,1)} collective-permute-done((bf16[8,1,192,1536]{3,2,0,1:T(8,128)(2,1)}, bf16[8,1,192,1536]{3,2,0,1:T(8,128)(2,1)}, u32[]{:S(2)}, u32[]{:S(2)}) %collective-permute-start.11) | collective-permute-done | bytes 4718624 | tf_op jit(solution)/shard_map/ppermute | solution.py:30
  1690.7 122.0 %all-reduce.4 = (f32[1]{0:T(128)}, f32[4,2,1536]{2,0,1:T(4,128)S(1)}) all-reduce(f32[1]{0:T(128)} %bitcast.10, f32[4,2,1536]{2,0,1:T(4,128)S(1)} %broadcast_select_fusion.7), channel_id=1, replica_groups=mesh['rep'=1,'tp'=2,'stage'=4] {'tp','stage'}, use_global_device_ids=true, to_apply=%region_1.2 | all-reduce | flops 12289 | bytes 98312 | tf_op jit(solution)/shard_map/psum | solution.py:690
  1813.4 16.8 fusion.76
  (118 shorter events, 146.5 us)
Async XLA Ops:
  13.2 24.7 %collective-permute-start.4 = (bf16[1536,3072]{0,1:T(8,128)(2,1)}, bf16[1536,3072]{0,1:T(8,128)(2,1)}, u32[]{:S(2)}, u32[]{:S(2)}) collective-permute-start(bf16[1536,3072]{0,1:T(8,128)(2,1)} %bitcast.147), channel_id=1, source_target_pairs={{1,4},{4,1},{2,7},{7,2}} | collective-permute-start | bytes 28311560 | tf_op jit(solution)/shard_map/ppermute | solution.py:30
  30.1 101.0 %collective-permute-start.6 = (bf16[3072,1536]{0,1:T(8,128)(2,1)}, bf16[3072,1536]{0,1:T(8,128)(2,1)}, u32[]{:S(2)}, u32[]{:S(2)}) collective-permute-start(bf16[3072,1536]{0,1:T(8,128)(2,1)} %bitcast.144), channel_id=1, source_target_pairs={{1,4},{4,1},{2,7},{7,2}} | collective-permute-start | bytes 28311560 | tf_op jit(solution)/shard_map/ppermute | solution.py:30
  34.4 196.0 %collective-permute-start = (bf16[1536,3,8,96]{0,3,2,1:T(8,128)(2,1)}, bf16[1536,3,8,96]{0,3,2,1:T(8,128)(2,1)}, u32[]{:S(2)}, u32[]{:S(2)}) collective-permute-start(bf16[1536,3,8,96]{0,3,2,1:T(8,128)(2,1)} %bitcast.158), channel_id=1, source_target_pairs={{1,4},{4,1},{2,7},{7,2}} | collective-permute-start | bytes 21233672 | tf_op jit(solution)/shard_map/ppermute | solution.py:30
  37.9 93.2 %slice-start = ((s8[9437184]{0:T(1024)(128)(4,1)}), s8[1048576]{0:T(1024)(128)(4,1)S(1)}, s32[]{:S(2)}) async-start(s8[9437184]{0:T(1024)(128)(4,1)} %bitcast.145), calls=%async_computation | async-start | bytes 2097152
  37.9 93.2 %slice-start.1 = ((s8[9437184]{0:T(1024)(128)(4,1)}), s8[4194304]{0:T(1024)(128)(4,1)S(1)}, s32[]{:S(2)}) async-start(s8[9437184]{0:T(1024)(128)(4,1)} %bitcast.145), calls=%async_computation.1 | async-start | bytes 8388608
  38.0 93.2 %slice-start.2 = ((s8[9437184]{0:T(1024)(128)(4,1)}), s8[4194304]{0:T(1024)(128)(4,1)S(1)}, s32[]{:S(2)}) async-start(s8[9437184]{0:T(1024)(128)(4,1)} %bitcast.145), calls=%async_computation.2 | async-start | bytes 8388608
  48.8 378.2 %collective-permute-start.5 = (bf16[1536,3072]{0,1:T(8,128)(2,1)}, bf16[1536,3072]{0,1:T(8,128)(2,1)}, u32[]{:S(2)}, u32[]{:S(2)}) collective-permute-start(bf16[1536,3072]{0,1:T(8,128)(2,1)} %broadcast_select_fusion.1), channel_id=1, source_target_pairs={{0,1},{1,0},{2,3},{3,2},{4,5},{5,4},{6,7},{7,6}} | collective-permute-start | bytes 28311560 | tf_op jit(solution)/shard_map/ppermute | solution.py:30
  135.8 169.8 %copy-start.4 = (bf16[1,8,96,1536]{3,2,1,0:T(8,128)(2,1)S(1)}, bf16[1,8,96,1536]{3,2,1,0:T(8,128)(2,1)}, u32[]{:S(2)}) copy-start(bf16[1,8,96,1536]{3,2,1,0:T(8,128)(2,1)} %param.11) | copy-start | bytes 7077892
  135.8 201.6 %copy-start.7 = (bf16[1,1536]{1,0:T(2,128)(2,1)S(1)}, bf16[1,1536]{1,0:T(2,128)(2,1)}, u32[]{:S(2)}) copy-start(bf16[1,1536]{1,0:T(2,128)(2,1)} %param.15) | copy-start | bytes 9220
  135.8 201.6 %copy-start.8 = (bf16[1,1536]{1,0:T(2,128)(2,1)S(1)}, bf16[1,1536]{1,0:T(2,128)(2,1)}, u32[]{:S(2)}) copy-start(bf16[1,1536]{1,0:T(2,128)(2,1)} %param.14) | copy-start | bytes 9220
  135.8 303.8 %collective-permute-start.7 = (bf16[3072,1536]{0,1:T(8,128)(2,1)}, bf16[3072,1536]{0,1:T(8,128)(2,1)}, u32[]{:S(2)}, u32[]{:S(2)}) collective-permute-start(bf16[3072,1536]{0,1:T(8,128)(2,1)} %broadcast_select_fusion), channel_id=1, source_target_pairs={{0,1},{1,0},{2,3},{3,2},{4,5},{5,4},{6,7},{7,6}} | collective-permute-start | bytes 28311560 | tf_op jit(solution)/shard_map/ppermute | solution.py:30
  237.1 169.5 %collective-permute-start.1 = (bf16[1536,3,8,96]{0,3,2,1:T(8,128)(2,1)}, bf16[1536,3,8,96]{0,3,2,1:T(8,128)(2,1)}, u32[]{:S(2)}, u32[]{:S(2)}) collective-permute-start(bf16[1536,3,8,96]{0,3,2,1:T(8,128)(2,1)} %broadcast_select_fusion.2), channel_id=1, source_target_pairs={{0,1},{1,0},{2,3},{3,2},{4,5},{5,4},{6,7},{7,6}} | collective-permute-start | bytes 21233672 | tf_op jit(solution)/shard_map/ppermute | solution.py:30
  305.6 0.8 collective-permute-start.2
  308.1 44.5 %collective-permute-start.3 = (bf16[8,96,1536]{2,1,0:T(8,128)(2,1)}, bf16[8,96,1536]{2,1,0:T(8,128)(2,1)}, u32[]{:S(2)}, u32[]{:S(2)}) collective-permute-start(bf16[8,96,1536]{2,1,0:T(8,128)(2,1)} %broadcast_select_fusion.6), channel_id=1, source_target_pairs={{0,1},{1,0},{2,3},{3,2},{4,5},{5,4},{6,7},{7,6}} | collective-permute-start | bytes 7077896 | tf_op jit(solution)/shard_map/ppermute | solution.py:30
  337.4 9.3 collective-permute-start.8
  349.2 19.4 %copy-start = (bf16[8,128,1536]{2,1,0:T(8,128)(2,1)}, bf16[8,128,1536]{2,1,0:T(8,128)(2,1)S(1)}, u32[]{:S(2)}) copy-start(bf16[8,128,1536]{2,1,0:T(8,128)(2,1)S(1)} %pad.16) | copy-start | bytes 9437188
  868.7 36.9 %copy-start.2 = (bf16[8,192,1536]{2,1,0:T(8,128)(2,1)S(1)}, bf16[8,192,1536]{2,1,0:T(8,128)(2,1)}, u32[]{:S(2)}) copy-start(bf16[8,192,1536]{2,1,0:T(8,128)(2,1)} %get-tuple-element.34) | copy-start | bytes 14155780
  1249.3 20.6 %slice-start.3 = ((s8[9437184]{0:T(1024)(128)(4,1)}), s8[1048576]{0:T(1024)(128)(4,1)S(1)}, s32[]{:S(2)}) async-start(s8[9437184]{0:T(1024)(128)(4,1)} %bitcast.152), calls=%async_computation.3 | async-start | bytes 2097152
  1256.3 13.6 slice-start.4
  1256.3 13.6 slice-start.5
  1320.1 17.1 copy-start.9
  1449.7 129.7 %collective-permute-start.9 = (bf16[8,1,192,1536]{3,2,0,1:T(8,128)(2,1)}, bf16[8,1,192,1536]{3,2,0,1:T(8,128)(2,1)}, u32[]{:S(2)}, u32[]{:S(2)}) collective-permute-start(bf16[8,1,192,1536]{3,2,0,1:T(8,128)(2,1)} %bitcast.161), channel_id=1, source_target_pairs={{0,4},{1,5}} | collective-permute-start | bytes 14155784 | tf_op jit(solution)/shard_map/ppermute | solution.py:30
  1452.6 228.8 %collective-permute-start.11 = (bf16[8,1,192,1536]{3,2,0,1:T(8,128)(2,1)}, bf16[8,1,192,1536]{3,2,0,1:T(8,128)(2,1)}, u32[]{:S(2)}, u32[]{:S(2)}) collective-permute-start(bf16[8,1,192,1536]{3,2,0,1:T(8,128)(2,1)} %bitcast.162), channel_id=1, source_target_pairs={{0,2},{1,3}} | collective-permute-start | bytes 14155784 | tf_op jit(solution)/shard_map/ppermute | solution.py:30
  1490.9 12.5 copy-start.6
  1490.9 13.8 copy-start.12
  1490.9 13.8 copy-start.14
  1504.7 33.0 %copy-start.3 = (bf16[16,192,1536]{2,1,0:T(8,128)(2,1)S(1)}, bf16[16,192,1536]{2,1,0:T(8,128)(2,1)}, u32[]{:S(2)}) copy-start(bf16[16,192,1536]{2,1,0:T(8,128)(2,1)} %fusion.132) | copy-start | bytes 28311556
  1579.4 102.0 %collective-permute-start.10 = (bf16[8,1,192,1536]{3,2,0,1:T(8,128)(2,1)}, bf16[8,1,192,1536]{3,2,0,1:T(8,128)(2,1)}, u32[]{:S(2)}, u32[]{:S(2)}) collective-permute-start(bf16[8,1,192,1536]{3,2,0,1:T(8,128)(2,1)} %collective-permute-done.9), channel_id=1, source_target_pairs={{4,6},{5,7}} | collective-permute-start | bytes 14155784 | tf_op jit(solution)/shard_map/ppermute | solution.py:30
  1624.8 65.8 %copy-start.10 = (f32[2,1536]{1,0:T(2,128)S(1)}, f32[2,1536]{1,0:T(2,128)}, u32[]{:S(2)}) copy-start(f32[2,1536]{1,0:T(2,128)} %reduce_sum.68) | copy-start | bytes 36868
  1624.8 65.8 %copy-start.16 = (pred[4]{0:T(512)(128)(4,1)S(1)}, pred[4]{0:T(512)(128)(4,1)}, u32[]{:S(2)}) copy-start(pred[4]{0:T(512)(128)(4,1)} %iota_compare_fusion.1) | copy-start | bytes 16
  1624.8 187.9 %copy-start.15 = (pred[4]{0:T(512)(128)(4,1)S(1)}, pred[4]{0:T(512)(128)(4,1)}, u32[]{:S(2)}) copy-start(pred[4]{0:T(512)(128)(4,1)} %iota_compare_fusion.2) | copy-start | bytes 16
  1688.0 142.2 %collective-permute-start.12 = (bf16[8,1,192,1536]{3,2,0,1:T(8,128)(2,1)}, bf16[8,1,192,1536]{3,2,0,1:T(8,128)(2,1)}, u32[]{:S(2)}, u32[]{:S(2)}) collective-permute-start(bf16[8,1,192,1536]{3,2,0,1:T(8,128)(2,1)} %select_select_fusion), channel_id=1, source_target_pairs={{0,1},{1,0},{2,3},{3,2},{4,5},{5,4},{6,7},{7,6}} | collective-permute-start | bytes 14155784 | tf_op jit(solution)/shard_map/ppermute | solution.py:30
  (10 other events, 52.6 us)

commit v3 on v2

v3 whole, which is shorter than its diff:
```python
import functools

import jax
import jax.numpy as jnp
from jax import lax
from jax.experimental import pallas as pl
from jax.experimental.pallas import tpu as pltpu
from jax.sharding import PartitionSpec as P

NORM_EPS = 1e-5
AX = ('tp', 'stage')
BF = jnp.bfloat16
F32 = jnp.float32
MESH = pl.DeviceIdType.MESH
ANY = pl.ANY

R_SWAP = [(1, 4), (4, 1), (2, 7), (7, 2)]
CORE_SWAP = [(0, 1), (1, 0), (2, 3), (3, 2), (4, 5), (5, 4), (6, 7), (7, 6)]
L_TO_R = [(0, 1), (5, 4), (6, 7), (3, 2)]

GELU_A = 0.7978845608028654
GELU_B = 0.044715
CHUNK = 1024
SUB = 256
DEPTH = 3
KDEPTH = 2
HEAD_PAD = 128


def move(value, perm):
    return lax.ppermute(value, AX, perm)


def rms_core(x_f32, gain_f32):
    inv_rms = lax.rsqrt(jnp.mean(x_f32 * x_f32, axis=-1, keepdims=True) + NORM_EPS)
    return x_f32 * inv_rms * gain_f32


def gelu_tanh(up_f32):
    return jax.nn.gelu(up_f32, approximate=True)


def dot(eq, a, b):
    return jnp.einsum(eq, a, b, preferred_element_type=F32)


def mm(a, b):
    return lax.dot_general(a, b, (((1,), (0,)), ((), ())), preferred_element_type=F32)


def mm_nt(a, b):
    return lax.dot_general(a, b, (((1,), (1,)), ((), ())), preferred_element_type=F32)


def mm_tn(a, b):
    return lax.dot_general(a, b, (((0,), (0,)), ((), ())), preferred_element_type=F32)


class Place:
    def __init__(self):
        self.tp = lax.axis_index('tp')
        self.stage = lax.axis_index('stage')
        self.core = self.stage % 2
        self.x_pos = self.stage // 2
        self.home = self.x_pos * (3 - 2 * self.tp) + self.tp
        self.is_l = self.stage == self.home
        self.sib = self.stage + 1 - 2 * self.core

    def at(self, tp, stage):
        return {'tp': tp, 'stage': stage}

    @property
    def sibling(self):
        return self.at(self.tp, self.sib)

    @property
    def across(self):
        return self.at(1 - self.tp, self.stage)

    @property
    def across_other(self):
        return self.at(1 - self.tp, self.sib)

    def others(self, src, dst, send_sems, recv_sem):
        copies = []
        for d_tp in (0, 1):
            for d_stage in range(4):
                if d_tp or d_stage:
                    there = self.at(self.tp + d_tp - 2 * d_tp * self.tp, (self.stage + d_stage) % 4)
                    copies.append(remote(src, dst, send_sems.at[len(copies)], recv_sem, there))
        return copies

    def chain(self, delta):
        there = self.home + delta
        x_pos = there // 2
        tp = there % 2 + x_pos * (1 - 2 * (there % 2))
        return self.at(tp, 2 * x_pos + self.core)


def entry_barrier(place):
    barrier = pltpu.get_barrier_semaphore()
    for d_tp in (0, 1):
        for d_stage in range(4):
            if d_tp or d_stage:
                tp = place.tp + d_tp - 2 * d_tp * place.tp
                stage = (place.stage + d_stage) % 4
                pl.semaphore_signal(barrier, inc=1, device_id=place.at(tp, stage), device_id_type=MESH)
    pl.semaphore_wait(barrier, 7)


def remote(src, dst, send_sem, recv_sem, device_id):
    return pltpu.make_async_remote_copy(src_ref=src, dst_ref=dst, send_sem=send_sem, recv_sem=recv_sem, device_id=device_id, device_id_type=MESH)


def rows_loop(total, step, body):
    def run(i, carry):
        body(pl.ds(pl.multiple_of(i * step, step), step))
        return carry
    lax.fori_loop(0, total // step, run, 0)


def norm_rows(src, gain_row, dst, total):
    def body(rows):
        v = src[rows, :].astype(F32)
        inv = lax.rsqrt(jnp.mean(v * v, axis=-1, keepdims=True) + NORM_EPS)
        dst[rows, :] = (v * inv * gain_row).astype(BF)
    rows_loop(total, 32, body)


def gelu_gate(u):
    u2 = u * u
    t = jnp.tanh(u * (GELU_A + (GELU_A * GELU_B) * u2))
    return 0.5 * t + 0.5, u2


def causal_probs(q, k, scale):
    s = mm_nt(q, k) * scale
    q_pos = lax.broadcasted_iota(jnp.int32, s.shape, 0)
    k_pos = lax.broadcasted_iota(jnp.int32, s.shape, 1)
    s = jnp.where(k_pos <= q_pos, s, -1e30)
    e = jnp.exp(s - jnp.max(s, axis=-1, keepdims=True))
    return e * (1.0 / jnp.sum(e, axis=-1, keepdims=True))


def lanes(offset, size):
    return pl.ds(pl.multiple_of(offset, 128), size)


class Stream:
    def __init__(self, buf, sem, depth, parts, total, by_heads):
        self.buf, self.sem, self.depth, self.parts, self.total, self.by_heads = buf, sem, depth, parts, total, by_heads
        self.per_tick = sum(p[1] for p in parts)

    def copy_in(self, ref, index, slot):
        if not self.by_heads:
            where = pl.ds(pl.multiple_of(index * CHUNK, CHUNK), CHUNK)
            pltpu.make_async_copy(ref.at[:, where], self.buf.at[slot], self.sem.at[slot]).start()
            return
        for r in range(8):
            rows = pl.ds(pl.multiple_of(index * 768 + r * 96, 96), 96)
            pltpu.make_async_copy(ref.at[rows, :], self.buf.at[slot, r * 128:r * 128 + 96, :], self.sem.at[slot]).start()

    def start(self, seq):
        @pl.when(seq < self.total)
        def _():
            j = seq % self.per_tick
            slot = seq % self.depth
            base = 0
            for choices, chunks in self.parts:
                for condition, ref in choices:
                    here = (j >= base) & (j < base + chunks)
                    here = here if condition is None else here & condition

                    @pl.when(here)
                    def _(ref=ref, low=base):
                        self.copy_in(ref, j - low, slot)
                base += chunks

    def prime(self):
        for seq in range(self.depth):
            self.start(jnp.int32(seq))

    def wait(self, seq):
        slot = seq % self.depth
        ref = self.parts[0][0][0][1]
        if self.by_heads:
            pltpu.make_async_copy(ref.at[0:768, :], self.buf.at[slot, 0:768, :], self.sem.at[slot]).wait()
        else:
            pltpu.make_async_copy(ref.at[:, 0:CHUNK], self.buf.at[slot], self.sem.at[slot]).wait()
        return self.buf.at[slot]


PIECES = [(0, 0, 0), (0, 0, 1), (0, 0, 2), (1, 0, 0), (2, 1, 0), (2, 1, 1), (2, 1, 2), (2, 1, 3), (3, 0, 0), (3, 0, 1), (3, 0, 2), (3, 0, 3)]


def piece(ref, axis, index):
    return ref.at[index * 768:(index + 1) * 768, :] if axis == 0 else ref.at[:, index * 768:(index + 1) * 768]


def weight_phase(place, is_r, own, near, far, turned, wn, wk, send_sem, y_send, d_send, near_sem, far_sem, load_sem, store_sem):
    wk[...] = jnp.zeros_like(wk)

    @pl.when(place.is_l)
    def _():
        for i in range(4):
            remote(own[i], near[i], send_sem.at[i], near_sem.at[i], place.sibling).start()

    @pl.when(is_r)
    def _():
        for c, (i, axis, index) in enumerate(PIECES):
            remote(piece(own[i], axis, index), piece(far[i], axis, index), y_send.at[i], far_sem.at[c], place.across_other).start()

    def load(i, refs, t, slot):
        for condition, ref in refs:
            def go(ref=ref):
                if i < 2:
                    for r in range(2):
                        rows = pl.ds(pl.multiple_of(t * 192 + r * 96, 96), 96)
                        pltpu.make_async_copy(ref.at[rows, :], wk.at[0, pl.ds(slot * 256 + r * 128, 96), :], load_sem.at[slot]).start()
                elif i == 2:
                    pltpu.make_async_copy(ref.at[:, lanes(t * 256, 256)], wn.at[slot, :, 0:256], load_sem.at[slot]).start()
                else:
                    rows = pl.ds(pl.multiple_of(t * 256, 256), 256)
                    pltpu.make_async_copy(ref.at[rows, :], wk.at[0, pl.ds(512 + slot * 256, 256), :], load_sem.at[slot]).start()
            if condition is None:
                go()
            else:
                pl.when(condition)(go)

    def loaded(i, refs, slot):
        ref = refs[0][1]
        if i < 2:
            pltpu.make_async_copy(ref.at[0:192, :], wk.at[0, 0:192, :], load_sem.at[slot]).wait()
        elif i == 2:
            pltpu.make_async_copy(ref.at[:, 0:256], wn.at[slot, :, 0:256], load_sem.at[slot]).wait()
        else:
            pltpu.make_async_copy(ref.at[0:256, :], wk.at[0, 512:768, :], load_sem.at[slot]).wait()

    def store(i, dst, t, slot):
        if i == 2:
            rows = pl.ds(pl.multiple_of(t * 256, 256), 256)
            return pltpu.make_async_copy(wk.at[1, pl.ds(slot * 256, 256), :], dst.at[rows, :], store_sem.at[slot])
        return pltpu.make_async_copy(wn.at[slot, :, 256:512], dst.at[:, lanes(t * 256, 256)], store_sem.at[slot])

    def turn(i, refs, dst, first, count):
        load(i, refs, first, 0)

        def step(n, c):
            slot = n % 2

            @pl.when(n + 1 < count)
            def _():
                load(i, refs, first + n + 1, 1 - slot)
            loaded(i, refs, slot)

            @pl.when(n >= 2)
            def _():
                store(i, dst, first + n - 2, slot).wait()
            for b in range(6):
                cut = slice(b * 256, b * 256 + 256)
                if i == 2:
                    wk[1, pl.ds(pl.multiple_of(slot * 256, 256), 256), cut] = wn[slot, cut, 0:256].T
                else:
                    base = 0 if i < 2 else 512
                    wn[slot, cut, 256:512] = wk[0, pl.ds(pl.multiple_of(base + slot * 256, 256), 256), cut].T
            store(i, dst, first + n, slot).start()
            return c
        lax.fori_loop(0, count, step, 0)
        for n in (count - 2, count - 1):
            store(i, dst, first + n, n % 2).wait()

    counts = (12, 4, 12, 12)
    for i in range(4):
        @pl.when(is_r)
        def _(i=i):
            remote(near[i], near[i], send_sem.at[i], near_sem.at[i], place.sibling).wait_recv()
        turn(i, [(place.is_l, own[i]), (is_r, near[i])], turned[i][0], 0, counts[i])
    done = [0, 0, 0, 0]
    for c, (i, axis, index) in enumerate(PIECES):
        view = piece(far[i], axis, index)
        remote(view, view, d_send.at[i], far_sem.at[c], place.sibling).wait_recv()

        @pl.when(is_r)
        def _(i=i, c=c, view=view):
            remote(view, view, d_send.at[i], far_sem.at[c], place.sibling).start()
        count = 4 if i < 2 else 3
        turn(i, [(None, far[i])], turned[i][1], done[i], count)
        done[i] += count

    @pl.when(place.is_l)
    def _():
        for i in range(4):
            remote(own[i], near[i], send_sem.at[i], near_sem.at[i], place.sibling).wait_send()

    @pl.when(is_r)
    def _():
        for i in range(4):
            remote(own[i], far[i], y_send.at[i], far_sem.at[0], place.across_other).wait_send()
            remote(far[i], far[i], d_send.at[i], far_sem.at[0], place.sibling).wait_send()


def step_kernel(dims, x_ref, y_ref, wq, wo, wu, wd, own_gains,
                a_s, h_s, m_s, qkv_s, u_s, dx_s, oh_same, oh_other, oa_same, oa_other, od_same, od_other, og_same, og_other,
                dg_same, dg_other, loss_all, nq, no, nu, nd, fq, fo, fu, fd, tq0, to0, tu0, td0, tq1, to1, tu1, td1,
                abuf, gbuf, hbuf, obuf, nbuf, ybuf, qkvbuf, ubuf, habuf, zbuf, ctxbuf, dqkvbuf, acc, accg, lossbuf, losstile, gains, wres, wn, wk,
                send_sem, y_send, d_send, near_sem, far_sem, t_load, t_store,
                act_sem, grad_sem, hop_f, hop_b, keep_sem, back_sem, save_sem, stream_n, stream_k, res_sem, big_sem, load_sem, y_sem,
                os_sem, oo_sem, as_sem, ao_sem, ds_sem, do_sem, gs_sem, go_sem, bulk, gain_sem, tiny, loss_send):
    micro, seq, width, heads, head_dim, ffn = dims
    place = Place()
    is_first, is_last = place.home == 0, place.home == 3
    home02 = (place.home == 0) | (place.home == 2)
    home13 = jnp.logical_not(home02)
    is_r = jnp.logical_not(place.is_l)
    half = heads // 2 * HEAD_PAD
    scale = head_dim ** -0.5
    norm_factor = 1.0 / (micro * 2 * seq * width)
    own, near, far = (wq, wo, wu, wd), (nq, no, nu, nd), (fq, fo, fu, fd)
    turned = ((tq0, tq1), (to0, to1), (tu0, tu1), (td0, td1))
    entry_barrier(place)

    @pl.when(place.is_l)
    def _():
        pltpu.make_async_copy(own_gains, gains, gain_sem.at[0]).start()
        remote(own_gains, gains, gain_sem.at[1], gain_sem.at[0], place.sibling).start()

    @pl.when(is_first)
    def _():
        for m in range(micro):
            pltpu.make_async_copy(x_ref.at[m, place.core], abuf.at[m], act_sem.at[m]).start()
    weight_phase(place, is_r, own, near, far, turned, wn, wk, send_sem, y_send, d_send, near_sem, far_sem, t_load, t_store)
    pltpu.make_async_copy(own_gains, gains, gain_sem.at[0]).wait()

    @pl.when(place.is_l)
    def _():
        remote(own_gains, gains, gain_sem.at[1], gain_sem.at[0], place.sibling).wait_send()

    def near_of(i):
        return [(place.is_l, own[i]), (is_r, near[i])]

    def resident(choices_of_half, start):
        for c in range(6):
            for condition, ref in choices_of_half[c // 3]:
                copy = pltpu.make_async_copy(ref.at[(c % 3) * CHUNK:(c % 3 + 1) * CHUNK, :], wres.at[c], res_sem.at[c])
                if condition is None:
                    copy.start()
                else:
                    pl.when(condition)(copy.start)

    def resident_ready(j):
        pltpu.make_async_copy(wd.at[0:CHUNK, :], wres.at[j], res_sem.at[j]).wait()

    def saved(dst, index):
        return pltpu.make_async_copy(hbuf, dst, save_sem.at[index])

    sn = Stream(wn, stream_n, DEPTH, [([(None, tq0)], 3), ([(None, tq1)], 3), (near_of(2), 3), ([(None, fu)], 3)], micro * 12, False)
    sk = Stream(wk, stream_k, KDEPTH, [(near_of(1), 1), ([(None, fo)], 1)], micro * 2, True)
    sn.prime()
    sk.prime()
    resident((near_of(3), [(None, fd)]), True)
    lossbuf[...] = jnp.zeros_like(lossbuf)

    def qkv_out(m):
        return pltpu.make_async_copy(qkvbuf.at[0], qkv_s.at[m], big_sem.at[0])

    def up_out(m):
        return pltpu.make_async_copy(ubuf.at[0], u_s.at[m], big_sem.at[1])

    def act_out(m):
        return pltpu.make_async_copy(abuf.at[m], a_s.at[m], save_sem.at[2])

    def hop_forward(m):
        return remote(obuf.at[m % 2], abuf.at[m], hop_f.at[m % 2], act_sem.at[m], place.chain(1))

    def near_hand(src, dst_far, dst_own, sem, recv_sem):
        return (lambda: remote(src, dst_far, sem, recv_sem, place.sibling)), (lambda: pltpu.make_async_copy(src, dst_own, sem))

    def hand_out(m):
        return near_hand(obuf.at[m % 2], oa_other.at[m], oa_same.at[m], keep_sem.at[m % 2], ao_sem)

    def both_kinds(condition, copies, start):
        far_copy, own_copy = copies

        @pl.when(condition & place.is_l)
        def _():
            far_copy().start() if start else far_copy().wait_send()

        @pl.when(condition & is_r)
        def _():
            own_copy().start() if start else own_copy().wait()

    def forward_tick(m, carry):
        act, mid, out = abuf.at[m], hbuf, obuf.at[m % 2]
        pltpu.make_async_copy(x_ref.at[m, place.core], act, act_sem.at[m]).wait()
        act_out(m).start()

        @pl.when(place.is_l)
        def _():
            pltpu.make_async_copy(act, oa_same.at[m], as_sem).start()

        @pl.when(is_last)
        def _():
            pltpu.make_async_copy(y_ref.at[m, place.core], ybuf, y_sem).start()
        norm_rows(act, gains[0:1, :], nbuf, seq)

        @pl.when(m > 0)
        def _():
            qkv_out(m).wait()

        def qkv_step(j, c):
            w = sn.wait(m * 12 + j)
            for n in range(0, CHUNK, SUB):
                qkvbuf[0, :, lanes(j * CHUNK + n, SUB)] = mm(nbuf[...], w[:, n:n + SUB]).astype(BF)
            sn.start(m * 12 + j + DEPTH)
            return c
        lax.fori_loop(0, 6, qkv_step, 0)
        qkv_out(m).start()
        act_out(m).wait()

        @pl.when(is_r)
        def _():
            remote(a_s.at[m], oa_other.at[m], bulk.at[0], ao_sem, place.sibling).start()

        def head_step(i, c):
            for r in range(4):
                base = (i // 2) * (3 * half) + ((i % 2) * 4 + r) * HEAD_PAD
                q = qkvbuf[0, :, lanes(base, HEAD_PAD)]
                k = qkvbuf[0, :, lanes(base + half, HEAD_PAD)]
                v = qkvbuf[0, :, lanes(base + 2 * half, HEAD_PAD)]
                probs = causal_probs(q, k, scale).astype(BF)
                ctxbuf[:, lanes((i * 4 + r) * HEAD_PAD, HEAD_PAD)] = mm(probs, v).astype(BF)
            return c
        lax.fori_loop(0, heads // 4, head_step, 0)

        w0, w1 = sk.wait(m * 2), sk.wait(m * 2 + 1)
        for n in range(0, width, SUB):
            total = mm(ctxbuf[:, 0:half], w0[:, n:n + SUB]) + mm(ctxbuf[:, half:2 * half], w1[:, n:n + SUB])
            mid[:, n:n + SUB] = (act[:, n:n + SUB].astype(F32) + total).astype(BF)
        sk.start(m * 2 + KDEPTH)
        sk.start(m * 2 + 1 + KDEPTH)
        saved(h_s.at[m], 0).start()

        @pl.when(place.is_l)
        def _():
            saved(oh_same.at[m], 1).start()
        norm_rows(mid, gains[1:2, :], nbuf, seq)

        @pl.when(m > 0)
        def _():
            up_out(m).wait()
        acc[...] = jnp.zeros_like(acc)

        def mlp_step(j, c):
            w = sn.wait(m * 12 + 6 + j)
            for n in range(0, CHUNK, SUB):
                u = mm(nbuf[...], w[:, n:n + SUB]).astype(BF)
                ubuf[0, :, lanes(j * CHUNK + n, SUB)] = u
                uf = u.astype(F32)
                zbuf[:, n:n + SUB] = (uf * gelu_gate(uf)[0]).astype(BF)
            sn.start(m * 12 + 6 + j + DEPTH)

            @pl.when(m == 0)
            def _():
                resident_ready(j)
            for n in range(0, width, SUB):
                acc[:, n:n + SUB] += mm(zbuf[...], wres[j, :, n:n + SUB])
            return c
        lax.fori_loop(0, 6, mlp_step, 0)
        up_out(m).start()

        @pl.when((m > 1) & jnp.logical_not(is_last))
        def _():
            hop_forward(m).wait_send()

        both_kinds((m > 1) & home02, hand_out(m), False)

        def finish(rows):
            out[rows, :] = (mid[rows, :].astype(F32) + acc[rows, :]).astype(BF)
        rows_loop(seq, 32, finish)

        @pl.when(jnp.logical_not(is_last))
        def _():
            hop_forward(m).start()

        both_kinds(home02, hand_out(m), True)

        @pl.when(is_last)
        def _():
            pltpu.make_async_copy(y_ref.at[m, place.core], ybuf, y_sem).wait()

            def seed(rows):
                error = out[rows, :].astype(F32) - ybuf[rows, :].astype(F32)
                gbuf[m, rows, :] = (error * norm_factor).astype(BF)
                lossbuf[...] += jnp.sum((error * error).reshape(4, 8, width), axis=0)
            rows_loop(seq, 32, seed)

        saved(h_s.at[m], 0).wait()

        @pl.when(place.is_l)
        def _():
            saved(oh_same.at[m], 1).wait()
            remote(h_s.at[m], oh_same.at[m], bulk.at[2], os_sem, place.across).start()

        @pl.when(is_r)
        def _():
            remote(h_s.at[m], oh_other.at[m], bulk.at[2], oo_sem, place.sibling).start()
            remote(h_s.at[m], oh_other.at[m], bulk.at[3], oo_sem, place.across_other).start()

        @pl.when(is_last & place.is_l)
        def _():
            remote(gbuf.at[m], og_same.at[m], bulk.at[4], gs_sem, place.across).start()

        @pl.when(is_last & is_r)
        def _():
            remote(gbuf.at[m], og_other.at[m], bulk.at[4], go_sem, place.across_other).start()
        return carry

    lax.fori_loop(0, micro, forward_tick, 0)

    @pl.when(is_last)
    def _():
        total = lossbuf[:, 0:128]
        for n in range(128, width, 128):
            total = total + lossbuf[:, n:n + 128]
        losstile[...] = total
        pltpu.make_async_copy(losstile, loss_all.at[place.core], tiny.at[5]).start()
        for index, copy in enumerate(place.others(losstile, loss_all.at[place.core], loss_send, tiny.at[5])):
            copy.start()
    for copy in (qkv_out(micro - 1), up_out(micro - 1)):
        copy.wait()

    @pl.when(jnp.logical_not(is_last))
    def _():
        for m in (micro - 2, micro - 1):
            hop_forward(m).wait_send()
    for m in (micro - 2, micro - 1):
        both_kinds(home02, hand_out(m), False)

    bn = Stream(wn, stream_n, DEPTH, [([(None, td0)], 3), ([(None, td1)], 3), ([(None, to0)], 1), ([(None, to1)], 1)], micro * 8, False)
    bk = Stream(wk, stream_k, KDEPTH, [(near_of(0), 3), ([(None, fq)], 3)], micro * 6, True)
    bn.prime()
    bk.prime()
    resident(([(None, tu0)], [(None, tu1)]), True)

    def loads(i):
        m = micro - 1 - i
        slot = i % 2
        return (pltpu.make_async_copy(u_s.at[m], ubuf.at[slot], load_sem.at[0, slot]),
                pltpu.make_async_copy(qkv_s.at[m], qkvbuf.at[slot], load_sem.at[1, slot]),
                pltpu.make_async_copy(h_s.at[m], habuf.at[slot, 0], load_sem.at[2, slot]),
                pltpu.make_async_copy(a_s.at[m], habuf.at[slot, 1], load_sem.at[3, slot]))

    for copy in loads(0):
        copy.start()
    accg[...] = jnp.zeros_like(accg)

    def norm_back(index, x, base, dst, gain_row):
        def body(rows):
            xf = x[rows, :].astype(F32)
            dy = acc[rows, :].astype(BF).astype(F32)
            inv = lax.rsqrt(jnp.mean(xf * xf, axis=-1, keepdims=True) + NORM_EPS)
            xn = xf * inv
            accg[index] += jnp.sum((dy * xn).reshape(4, 8, width), axis=0)
            dyg = dy * gain_row
            dx = inv * (dyg - xn * jnp.mean(dyg * xn, axis=-1, keepdims=True))
            dst[rows, :] = (base[rows, :].astype(F32) + dx).astype(BF)
        rows_loop(seq, 32, body)

    def hop_back(i):
        m = micro - 1 - i
        return remote(obuf.at[i % 2], gbuf.at[m], hop_b.at[i % 2], grad_sem.at[m], place.chain(-1))

    def hand_back(i):
        m = micro - 1 - i
        return near_hand(obuf.at[i % 2], og_other.at[m], og_same.at[m], back_sem.at[i % 2], go_sem)

    def keep_dx(i):
        return pltpu.make_async_copy(obuf.at[i % 2], dx_s.at[micro - 1 - i], back_sem.at[i % 2])

    def back_ready(i):
        both_kinds((i > 1) & home13, hand_back(i), False)

        @pl.when((i > 1) & is_first)
        def _():
            keep_dx(i).wait()

        @pl.when((i > 1) & jnp.logical_not(is_first))
        def _():
            hop_back(i).wait_send()

    def backward_tick(i, carry):
        m = micro - 1 - i
        slot = i % 2
        grad, dmid, prev = gbuf.at[m], hbuf, obuf.at[slot]
        u_now, qkv_now, h_now, a_now = ubuf.at[slot], qkvbuf.at[slot], habuf.at[slot, 0], habuf.at[slot, 1]

        @pl.when(i + 1 < micro)
        def _():
            for copy in loads(i + 1):
                copy.start()

        @pl.when(jnp.logical_not(is_last))
        def _():
            remote(grad, grad, hop_b.at[slot], grad_sem.at[m], place.sibling).wait_recv()

        @pl.when(place.is_l)
        def _():
            pltpu.make_async_copy(grad, og_same.at[m], gs_sem).start()

        @pl.when(is_r)
        def _():
            remote(grad, og_other.at[m], bulk.at[5], go_sem, place.sibling).start()
        load_u, load_qkv, load_h, load_a = loads(i)
        load_u.wait()
        acc[...] = jnp.zeros_like(acc)

        def mlp_step(j, c):
            w = bn.wait(i * 8 + j)
            for n in range(0, CHUNK, SUB):
                dz = mm(grad[...], w[:, n:n + SUB]).astype(BF).astype(F32)
                u = u_now[:, lanes(j * CHUNK + n, SUB)].astype(F32)
                gate, u2 = gelu_gate(u)
                slope = gate + u * gate * (1.0 - gate) * (2.0 * GELU_A + (6.0 * GELU_A * GELU_B) * u2)
                zbuf[:, n:n + SUB] = (dz * slope).astype(BF)
            bn.start(i * 8 + j + DEPTH)

            @pl.when(i == 0)
            def _():
                resident_ready(j)
            for n in range(0, width, SUB):
                acc[:, n:n + SUB] += mm(zbuf[...], wres[j, :, n:n + SUB])
            return c
        lax.fori_loop(0, 6, mlp_step, 0)
        load_h.wait()
        norm_back(1, h_now, grad, dmid, gains[1:2, :])

        @pl.when(place.is_l)
        def _():
            saved(od_same.at[m], 0).start()

        @pl.when(is_r)
        def _():
            saved(m_s.at[m], 0).start()
        for c in range(2):
            w = bn.wait(i * 8 + 6 + c)
            for n in range(0, CHUNK, SUB):
                ctxbuf[:, c * CHUNK + n:c * CHUNK + n + SUB] = mm(dmid[...], w[:, n:n + SUB]).astype(BF)
            bn.start(i * 8 + 6 + c + DEPTH)
        load_qkv.wait()

        def head_step(t, c):
            for r in range(2):
                base = (t // 4) * (3 * half) + ((t % 4) * 2 + r) * HEAD_PAD
                q = qkv_now[:, lanes(base, HEAD_PAD)]
                k = qkv_now[:, lanes(base + half, HEAD_PAD)]
                v = qkv_now[:, lanes(base + 2 * half, HEAD_PAD)]
                dc = ctxbuf[:, lanes((t * 2 + r) * HEAD_PAD, HEAD_PAD)]
                probs = causal_probs(q, k, scale)
                dp = mm_nt(dc, v).astype(BF).astype(F32)
                ds = probs * (dp - jnp.sum(dp * probs, axis=-1, keepdims=True)) * scale
                dv = mm_tn(probs.astype(BF), dc)
                hi = ds.astype(BF)
                rest = ds - hi.astype(F32)
                lo = rest.astype(BF)
                tail = (rest - lo.astype(F32)).astype(BF)
                dq = mm(hi, k) + (mm(lo, k) + mm(tail, k))
                dk = mm_tn(hi, q) + (mm_tn(lo, q) + mm_tn(tail, q))
                dqkvbuf[:, lanes(base, HEAD_PAD)] = dq.astype(BF)
                dqkvbuf[:, lanes(base + half, HEAD_PAD)] = dk.astype(BF)
                dqkvbuf[:, lanes(base + 2 * half, HEAD_PAD)] = dv.astype(BF)
            return c
        lax.fori_loop(0, heads // 2, head_step, 0)
        acc[...] = jnp.zeros_like(acc)

        def qkv_step(j, c):
            w = bk.wait(i * 6 + j)
            for n in range(0, width, SUB):
                acc[:, n:n + SUB] += mm(dqkvbuf[:, lanes(j * CHUNK, CHUNK)], w[:, n:n + SUB])
            bk.start(i * 6 + j + KDEPTH)
            return c
        lax.fori_loop(0, 6, qkv_step, 0)
        load_a.wait()
        back_ready(i)
        norm_back(0, a_now, dmid, prev, gains[0:1, :])

        @pl.when(jnp.logical_not(is_first))
        def _():
            hop_back(i).start()

        @pl.when(is_first)
        def _():
            keep_dx(i).start()
        both_kinds(home13, hand_back(i), True)

        @pl.when(place.is_l)
        def _():
            saved(od_same.at[m], 0).wait()
            remote(od_same.at[m], od_same.at[m], bulk.at[6], ds_sem, place.across).start()

        @pl.when(is_r)
        def _():
            saved(m_s.at[m], 0).wait()
            remote(m_s.at[m], od_other.at[m], bulk.at[6], do_sem, place.sibling).start()
            remote(m_s.at[m], od_other.at[m], bulk.at[7], do_sem, place.across_other).start()

        @pl.when((place.home == 2) & place.is_l)
        def _():
            remote(a_s.at[m], oa_same.at[m], bulk.at[8], as_sem, place.across).start()

        @pl.when((place.home == 2) & is_r)
        def _():
            remote(a_s.at[m], oa_other.at[m], bulk.at[8], ao_sem, place.across_other).start()
        return carry

    lax.fori_loop(0, micro, backward_tick, 0)

    @pl.when((place.home == 1) & place.is_l)
    def _():
        for m in reversed(range(micro)):
            remote(gbuf.at[m], og_same.at[m], bulk.at[4], gs_sem, place.across).start()

    @pl.when((place.home == 1) & is_r)
    def _():
        for m in reversed(range(micro)):
            remote(gbuf.at[m], og_other.at[m], bulk.at[4], go_sem, place.across_other).start()

    @pl.when(place.is_l)
    def _():
        pltpu.make_async_copy(accg, dg_same, tiny.at[0]).start()
        remote(accg, dg_same, tiny.at[1], tiny.at[0], place.across).start()

    @pl.when(is_r)
    def _():
        remote(accg, dg_other, tiny.at[1], tiny.at[4], place.sibling).start()
        remote(accg, dg_other, tiny.at[2], tiny.at[4], place.across_other).start()

    for i in (micro - 2, micro - 1):
        back_ready(jnp.int32(i))

    def sent(buf, sem):
        remote(buf, a_s, sem, ao_sem, place.sibling).wait_send()

    def got(dst, sem):
        pltpu.make_async_copy(dst, dst, sem).wait()

    sent(h_s, bulk.at[2])
    sent(m_s, bulk.at[6])

    @pl.when(is_r)
    def _():
        sent(a_s, bulk.at[0])
        sent(h_s, bulk.at[3])
        sent(gbuf, bulk.at[5])
        sent(m_s, bulk.at[7])
        remote(accg, dg_other, tiny.at[2], tiny.at[4], place.sibling).wait_send()

    @pl.when(home13)
    def _():
        sent(gbuf, bulk.at[4])

    @pl.when(place.home == 2)
    def _():
        sent(a_s, bulk.at[8])

    @pl.when(is_last)
    def _():
        for copy in place.others(losstile, loss_all.at[place.core], loss_send, tiny.at[5]):
            copy.wait_send()
    remote(accg, dg_other, tiny.at[1], tiny.at[4], place.sibling).wait_send()
    got(oh_other, oo_sem)
    got(od_other, do_sem)
    got(og_other, go_sem)
    got(dg_same, tiny.at[0])
    got(dg_other, tiny.at[4])
    got(loss_all, tiny.at[5])

    @pl.when(is_r)
    def _():
        got(oh_same, os_sem)
        got(od_same, ds_sem)

    @pl.when(place.is_l | home02)
    def _():
        got(og_same, gs_sem)

    @pl.when(place.is_l | (place.home == 3))
    def _():
        got(oa_same, as_sem)

    @pl.when(place.is_l | (place.home != 1))
    def _():
        got(oa_other, ao_sem)


def step_phase(dims, x, y, own, own_gains):
    micro, seq, width, heads, head_dim, ffn = dims
    half = heads // 2 * HEAD_PAD
    act = (micro, seq, width)
    raw = [(heads // 2 * 3 * head_dim, width), (heads // 2 * head_dim, width), (width, ffn // 2), (ffn // 2, width)]
    turned = [(width, 3 * half), (width, half), (ffn // 2, width), (width, ffn // 2)]
    outs = [act, act, act, (micro, seq, 6 * half), (micro, seq, ffn), act] + [act] * 8
    out_shape = [jax.ShapeDtypeStruct(s, BF) for s in outs]
    out_shape += [jax.ShapeDtypeStruct(s, F32) for s in ((2, 8, width), (2, 8, width), (2, 8, 128))]
    out_shape += [jax.ShapeDtypeStruct(s, BF) for s in raw + raw + turned + turned]
    any_spec = pl.BlockSpec(memory_space=ANY)
    vmem, dma = pltpu.VMEM, pltpu.SemaphoreType.DMA
    scratch = [
        vmem(act, BF), vmem(act, BF), vmem((seq, width), BF), vmem((2, seq, width), BF), vmem((seq, width), BF), vmem((seq, width), BF),
        vmem((2, seq, 6 * half), BF), vmem((2, seq, ffn), BF), vmem((2, 2, seq, width), BF), vmem((seq, CHUNK), BF), vmem((seq, 2 * half), BF),
        vmem((seq, 6 * half), BF), vmem((seq, width), F32), vmem((2, 8, width), F32), vmem((8, width), F32), vmem((8, 128), F32),
        vmem((2, width), F32), vmem((6, CHUNK, width), BF), vmem((DEPTH, width, CHUNK), BF), vmem((KDEPTH, CHUNK, width), BF),
        dma((4,)), dma((4,)), dma((4,)), dma((4,)), dma((12,)), dma((2,)), dma((2,)),
        dma((micro,)), dma((micro,)), dma((2,)), dma((2,)), dma((2,)), dma((2,)), dma((3,)), dma((DEPTH,)), dma((KDEPTH,)), dma((6,)), dma((2,)),
        dma((4, 2)), dma(()),
        dma(()), dma(()), dma(()), dma(()), dma(()), dma(()), dma(()), dma(()), dma((9,)), dma((2,)), dma((6,)), dma((7,)),
    ]
    return pl.pallas_call(
        functools.partial(step_kernel, dims),
        out_shape=tuple(out_shape),
        in_specs=[any_spec] * 6 + [pl.BlockSpec(memory_space=vmem)],
        out_specs=(any_spec,) * len(out_shape),
        scratch_shapes=scratch,
        compiler_params=pltpu.CompilerParams(collective_id=0, has_side_effects=True, vmem_limit_bytes=67043328),
        name='step_phase',
    )(x, y, *own, own_gains)


def attn_scores(query, key):
    seq_len = query.shape[-2]
    scores = dot('bhqe,bhke->bhqk', query, key) * (query.shape[-1] ** -0.5)
    q_pos = lax.broadcasted_iota(jnp.int32, (seq_len, seq_len), 0)
    k_pos = lax.broadcasted_iota(jnp.int32, (seq_len, seq_len), 1)
    return jax.nn.softmax(jnp.where(k_pos <= q_pos, scores, -1e30), axis=-1)


def attn_backward(qkv, probs, d_context):
    scale = qkv.shape[-1] ** -0.5
    d_probs = dot('bhqe,bhke->bhqk', d_context, qkv[2]).astype(BF).astype(F32)
    d_value = dot('bhqk,bhqe->bhke', probs.astype(BF), d_context).astype(BF)
    d_scores = probs * (d_probs - jnp.sum(d_probs * probs, axis=-1, keepdims=True)) * scale
    d_query = jnp.einsum('bhqk,bhke->bhqe', d_scores, qkv[1].astype(F32), precision=lax.Precision.HIGHEST).astype(BF)
    d_key = jnp.einsum('bhqk,bhqe->bhke', d_scores, qkv[0].astype(F32), precision=lax.Precision.HIGHEST).astype(BF)
    return jnp.stack([d_query, d_key, d_value])


def owner_grads(act, mid, d_mid, grad_out, weights):
    w_qkv, w_out, w_up, w_down, gain_attn, gain_mlp = weights
    normed_a = rms_core(act.astype(F32), gain_attn).astype(BF)
    qkv = dot('bsd,dkhe->kbhse', normed_a, w_qkv).astype(BF)
    probs = attn_scores(qkv[0], qkv[1])
    context = dot('bhqk,bhke->bhqe', probs.astype(BF), qkv[2]).astype(BF)
    d_w_out = dot('bhse,bsd->hed', context, d_mid)
    d_context = dot('bsd,hed->bhse', d_mid, w_out).astype(BF)
    d_qkv = attn_backward(qkv, probs, d_context)
    d_w_qkv = dot('bsd,kbhse->dkhe', normed_a, d_qkv)
    normed_m = rms_core(mid.astype(F32), gain_mlp).astype(BF)
    up_f32 = dot('bsd,df->bsf', normed_m, w_up).astype(BF).astype(F32)
    hidden = gelu_tanh(up_f32).astype(BF)
    d_w_down = dot('bsf,bsd->fd', hidden, grad_out)
    d_act = dot('bsd,fd->bsf', grad_out, w_down).astype(BF)
    _, pull = jax.vjp(gelu_tanh, up_f32)
    d_up = pull(d_act.astype(F32))[0].astype(BF)
    d_w_up = dot('bsd,bsf->df', normed_m, d_up)
    return d_w_qkv, d_w_out, d_w_up, d_w_down


def solution(mesh):
    act_spec = P('rep', None, None, None)
    weight_specs = (
        P(('rep', 'stage'), None, None, 'tp', None),
        P(('rep', 'stage'), 'tp', None, None),
        P(('rep', 'stage'), None, 'tp'),
        P(('rep', 'stage'), 'tp', None),
        P(('rep', 'stage'), None),
        P(('rep', 'stage'), None),
    )

    def device_fn(inputs, targets, w_qkv, w_out, w_up, w_down, gain_attn, gain_mlp):
        micro_count, _, seq_len, width = inputs.shape
        dims = (micro_count, seq_len, width, 2 * w_out.shape[1], w_out.shape[2], 2 * w_up.shape[2])
        norm_factor = 1.0 / (inputs.size)
        stage = lax.axis_index('stage')
        tp = lax.axis_index('tp')
        x_pos, core = stage // 2, stage % 2
        home = jnp.where(x_pos == 0, tp, 3 - tp)
        is_l = stage == home
        own = (w_qkv[0], w_out[0], w_up[0], w_down[0])
        own_gains = (gain_attn[0].astype(F32), gain_mlp[0].astype(F32))
        rows_of = (own[0].transpose(1, 2, 3, 0).reshape(-1, width), own[1].reshape(-1, width), own[2], own[3])

        results = step_phase(dims, inputs, targets, rows_of, jnp.stack(own_gains))
        dx, oh_same, oh_other, oa_same, oa_other, od_same, od_other, og_same, og_other, dg_same, dg_other, loss_all = results[5:17]

        x_core = lax.dynamic_index_in_dim(inputs, core, 1, keepdims=False)
        x_other = lax.dynamic_index_in_dim(inputs, 1 - core, 1, keepdims=False)
        is_4 = (home == 1) & jnp.logical_not(is_l)
        both = lambda same, other: jnp.concatenate([same, other], 0)
        rows_a = both(jnp.where(is_4, x_core, oa_same), jnp.where(is_4, x_other, oa_other))
        weight_grads = owner_grads(rows_a, both(oh_same, oh_other), both(od_same, od_other), both(og_same, og_other), own + own_gains)
        mine = jnp.sum(dg_same + dg_other, 1)
        loss = jnp.sum(loss_all) * (0.5 * norm_factor)

        dx = dx[:, None]
        at_b = move(dx, [(0, 4), (1, 5)])
        at_d = move(dx, [(0, 2), (1, 3)])
        at_c = move(at_b, [(4, 6), (5, 7)])
        dx = jnp.where(home == 0, dx, jnp.where(home == 1, at_b, jnp.where(home == 2, at_c, at_d)))
        other = move(dx, CORE_SWAP)
        d_inputs = jnp.concatenate([jnp.where(core == 0, dx, other), jnp.where(core == 0, other, dx)], 1)
        return (loss.reshape(1), d_inputs) + tuple(g[None] for g in weight_grads) + (mine[0][None], mine[1][None])

    return jax.shard_map(device_fn, mesh=mesh, in_specs=(act_spec, act_spec) + weight_specs, out_specs=(P('rep'), act_spec) + weight_specs, check_vma=False)
```

time: 1860 us -> 1660 us (0.89)
  the two profiles are of different devices: /device:TPU:3 before, /device:TPU:5 now
where the time goes in v3:
time: 1660 us
  Pallas kernels  1100 us (66%)
  matrix products  383 us (23%)
  other arithmetic  85.8 us (5%)
  waiting for transfers between devices  36 us (2%)
  local copies, waits for them, and re-layouts  25.7 us (2%)
  starting transfers between devices  21.5 us (1%)
    pallas_call x1, Pallas kernels, step_phase(): pl.pallas_call(functools.partial(step_kernel, dims), out_shape=tuple(out_...  1100 us
    dot_general x11, matrix products, dot(): return jnp.einsum(eq, a, b, preferred_element_type=F32)  319 us
    ppermute x4, waiting for transfers between devices, move(): return lax.ppermute(value, AX, perm)  36 us
    dot_general x1, matrix products, attn_backward(): jnp.einsum('bhqk,bhke->bhqe', d_scores, qkv[1].astype(F32), precision=lax...  34.6 us
  transfers between devices with their start and end apart: 4, of which 1 were waited for; matrix products, arithmetic and copies ran while one was open for 28% of the time, Pallas kernels for 0%

profile of v3, /device:TPU:5, one launch (start us, length us, event | category | flops | bytes accessed | tf_op | source)
XLA Modules:
  0.0 1655.6 jit_solution(12487197589317438315)
XLA Ops:
  0.6 1.3 maximum_convert_fusion.own_gains
  2.0 1100.1 %step_phase.1 = (bf16[8,192,1536]{2,1,0:T(8,128)(2,1)}, bf16[8,192,1536]{2,1,0:T(8,128)(2,1)}, bf16[8,192,1536]{2,1,0:T(8,128)(2,1)}, bf16[8,192,6144]{2,1,0:T(8...) custom-call(bf16[8,2,192,1536]{3,2,1,0:T(8,128)(2,1)} %x_ref.1, ...), custom_call_target="tpu_custom_call" | custom-call | tf_op jit(solution)/shard_map/step_phase/pallas_call | solution.py:817
  1102.1 1.4 collective-permute-start
  1103.5 2.8 collective-permute-start.2
  1108.4 5.0 constant_dynamic-update-slice_fusion.1
  1113.4 2.7 constant_dynamic-update-slice_fusion.3
  1116.1 9.6 bitcast_select_fusion.1
  1125.7 6.0 fusion.16
  1132.3 36.2 %convert_bitcast_fusion = bf16[3,16,8,192,96]{4,3,2,0,1:T(8,128)(2,1)} fusion(f32[1536]{0:T(1024)S(1)} %convert_reduce_fusion.1, f32[16,192]{1,0:T(8,128)S(1)} %add_rsqrt_fusion.1, bf16[1,1536,3,8,96]{1,4,3,2,0:T(8,128)(2,1)} %param.10, bf16[8,192,1536]{2,1,0:T(8,128)(2,1)} %get-tuple-element.43, bf16[8,192,1536]{2,1,0:T(8,128)(2,1)S(1)} %get-tuple-element.42), kind=kOutput, calls=%fused_computation.42 | convolution fusion | flops 21783379968 | bytes 30689280 | tf_op jit(solution)/shard_map/bsd,dkhe->kbhse/dot_general | solution.py:44
  1168.5 16.9 %fusion.75 = f32[16,8,192,192]{2,3,1,0:T(8,128)} fusion(bf16[3,16,8,192,96]{4,3,2,0,1:T(8,128)(2,1)} %convert_bitcast_fusion), kind=kOutput, calls=%fused_computation.86 | convolution fusion | flops 905969664 | bytes 31457280 | tf_op jit(solution)/shard_map/bhqe,bhke->bhqk/dot_general | solution.py:44
  1185.3 8.5 constant_dynamic-update-slice_fusion
  1193.8 13.4 fusion.81
  1207.2 25.2 %fusion.119 = (f32[16,8,192]{2,1,0:T(8,128)S(1)}, f32[16,8,192,192]{2,3,1,0:T(8,128)}) fusion(f32[16,8,192,192]{2,3,1,0:T(8,128)} %fusion.75, pred[192,192]{0,1:T(8,128)(4,1)S(1)} %iota_compare_fusion), kind=kOutput, calls=%fused_computation.126 | output fusion | flops 28311744 | bytes 37883904 | tf_op jit(solution)/shard_map/sub | solution.py:833
  1232.4 22.5 %fusion.12 = (f32[16,8,192]{2,1,0:T(8,128)S(1)}, bf16[16,8,192,192]{2,3,1,0:T(8,128)(2,1)}, bf16[16,8,192,192]{2,3,1,0:T(8,128)(2,1)}) fusion(f32[16,8,192,192]{2,3,1,0:T(8,128)} %get-tuple-element.49, f32[16,8,192]{2,1,0:T(8,128)S(1)} %get-tuple-element.48, bf16[3,16,8,192,96]{4,3,2,0,1:T(8,128)(2,1)} %convert_bitcast_fusion, ...), kind=kOutput, calls=%fused_computation.20 | convolution fusion | flops 934256640 | bytes 56819712 | tf_op jit(solution)/shard_map/bhqe,bhke->bhqk/dot_general | solution.py:44
  1254.9 34.6 %convert_bitcast_fusion.3 = bf16[1,16,8,192,96]{4,3,2,1,0:T(8,128)(2,1)} fusion(bf16[3,16,8,192,96]{4,3,2,0,1:T(8,128)(2,1)} %convert_bitcast_fusion, bf16[16,8,192,192]{2,3,1,0:T(8,128)(2,1)} %get-tuple-element.50, f32[16,8,192]{2,1,0:T(8,128)S(1)} %get-tuple-element.40, f32[16,8,192,192]{2,3,1,0:T(8,128)} %get-tuple-element.49, ...), kind=kOutput, calls=%fused_computation.85 | convolution fusion | flops 5461770240 | bytes 48955392 | tf_op jit(solution)/shard_map/bhqk,bhke->bhqe/dot_general | solution.py:841
  1289.5 30.2 %convert_bitcast_fusion.2 = bf16[1,16,8,192,96]{4,3,2,1,0:T(8,128)(2,1)} fusion(bf16[3,16,8,192,96]{4,3,2,0,1:T(8,128)(2,1)} %convert_bitcast_fusion, bf16[16,8,192,192]{2,3,1,0:T(8,128)(2,1)} %get-tuple-element.50, f32[16,8,192]{2,1,0:T(8,128)S(1)} %get-tuple-element.40, f32[16,8,192,192]{2,3,1,0:T(8,128)} %get-tuple-element.49, ...), kind=kOutput, calls=%fused_computation.84 | convolution fusion | flops 5461770240 | bytes 48955392 | tf_op jit(solution)/shard_map/bhqk,bhqe->bhke/dot_general | solution.py:842
  1319.7 5.7 fusion.19
  1325.4 37.0 %fusion.56 = bf16[16,192,3072]{2,1,0:T(8,128)(2,1)} fusion(bf16[16,192,1536]{2,1,0:T(8,128)(2,1)} %get-tuple-element.52, bf16[1,3072,1536]{2,1,0:T(8,128)(2,1)} %param.13), kind=kOutput, calls=%fused_computation.68 | convolution fusion | flops 28991029248 | bytes 37748736 | tf_op jit(solution)/shard_map/bsd,fd->bsf/dot_general | solution.py:44
  1362.4 12.4 convert_bitcast_fusion.1
  1374.8 10.8 fusion.132
  1385.7 34.9 %fusion.65 = f32[1,1536,3,8,96]{1,4,3,2,0:T(8,128)} fusion(bf16[1,16,8,192,96]{4,3,2,1,0:T(8,128)(2,1)} %convert_bitcast_fusion.1, bf16[1,16,8,192,96]{4,3,2,1,0:T(8,128)(2,1)} %convert_bitcast_fusion.2, bf16[1,16,8,192,96]{4,3,2,1,0:T(8,128)(2,1)} %convert_bitcast_fusion.3, f32[1536]{0:T(1024)S(1)} %copy-done.15, f32[16,192]{1,0:T(8,128)S(1)} %copy-done.13, ...), kind=kOutput, calls=%fused_computation.74 | convolution fusion | flops 21818769408 | bytes 37767168 | tf_op jit(solution)/shard_map/bsd,kbhse->dkhe/dot_general | solution.py:44
  1420.6 36.0 %convolution_convert_fusion = bf16[16,192,3072]{2,1,0:T(8,128)(2,1)} fusion(bf16[1,1536,3072]{2,1,0:T(8,128)(2,1)} %param.12, f32[1536]{0:T(1024)S(1)} %copy-done.11, f32[16,192]{1,0:T(8,128)S(1)} %copy-done.9, bf16[8,192,1536]{2,1,0:T(8,128)(2,1)S(1)} %copy-done.1, bf16[8,192,1536]{2,1,0:T(8,128)(2,1)S(1)} %copy-done), kind=kOutput, calls=%fused_computation.59 | convolution fusion | flops 29024059392 | bytes 37767168 | tf_op jit(solution)/shard_map/bsd,df->bsf/dot_general | solution.py:44
  1456.6 3.4 collective-permute-start.1
  1460.1 50.0 %fusion.36 = f32[1,1536,3072]{2,1,0:T(8,128)} fusion(bf16[16,192,3072]{2,1,0:T(8,128)(2,1)} %convolution_convert_fusion, bf16[16,192,3072]{2,1,0:T(8,128)(2,1)} %fusion.56, bf16[16,192,1536]{2,1,0:T(8,128)(2,1)} %fusion.132), kind=kOutput, calls=%fused_computation.47 | convolution fusion | flops 29198647296 | bytes 66060288 | tf_op jit(solution)/shard_map/bsd,bsf->df/dot_general | solution.py:44
  1510.1 36.0 %collective-permute-done.1 = bf16[8,1,192,1536]{3,2,0,1:T(8,128)(2,1)} collective-permute-done((bf16[8,1,192,1536]{3,2,0,1:T(8,128)(2,1)}, bf16[8,1,192,1536]{3,2,0,1:T(8,128)(2,1)}, u32[]{:S(2)}, u32[]{:S(2)}) %collective-permute-start.1) | collective-permute-done | bytes 4718624 | tf_op jit(solution)/shard_map/ppermute | solution.py:31
  1546.1 8.1 select_select_fusion
  1554.2 13.8 collective-permute-start.3
  1568.0 42.6 %fusion.39 = f32[1,3072,1536]{2,1,0:T(8,128)} fusion(bf16[16,192,1536]{2,1,0:T(8,128)(2,1)} %get-tuple-element.52, bf16[16,192,3072]{2,1,0:T(8,128)(2,1)} %convolution_convert_fusion), kind=kOutput, calls=%fused_computation.48 | convolution fusion | flops 29085401088 | bytes 47185920 | tf_op jit(solution)/shard_map/bsf,bsd->fd/dot_general | solution.py:44
  1612.6 16.8 %fusion.76 = f32[1,8,96,1536]{3,2,1,0:T(8,128)} fusion(bf16[16,192,1536]{2,1,0:T(8,128)(2,1)} %get-tuple-element.51, bf16[16,8,192,192]{2,3,1,0:T(8,128)(2,1)} %get-tuple-element.41, bf16[3,16,8,192,96]{4,3,2,0,1:T(8,128)(2,1)} %convert_bitcast_fusion), kind=kOutput, calls=%fused_computation.92 | convolution fusion | flops 8156086272 | bytes 33030144 | tf_op jit(solution)/shard_map/bhse,bsd->hed/dot_general | solution.py:44
  1629.4 8.1 broadcast_select_fusion.1
  1637.5 8.2 pad_maximum_fusion
  1645.8 8.3 copy.18
  (50 shorter events, 4.0 us)
Async XLA Ops:
  1102.1 11.3 slice-start
  1102.1 354.6 %collective-permute-start = (bf16[8,1,192,1536]{3,2,0,1:T(8,128)(2,1)}, bf16[8,1,192,1536]{3,2,0,1:T(8,128)(2,1)}, u32[]{:S(2)}, u32[]{:S(2)}) collective-permute-start(bf16[8,1,192,1536]{3,2,0,1:T(8,128)(2,1)} %bitcast.120), channel_id=1, source_target_pairs={{0,4},{1,5}} | collective-permute-start | bytes 14155784 | tf_op jit(solution)/shard_map/ppermute | solution.py:31
  1103.5 406.6 %collective-permute-start.2 = (bf16[8,1,192,1536]{3,2,0,1:T(8,128)(2,1)}, bf16[8,1,192,1536]{3,2,0,1:T(8,128)(2,1)}, u32[]{:S(2)}, u32[]{:S(2)}) collective-permute-start(bf16[8,1,192,1536]{3,2,0,1:T(8,128)(2,1)} %bitcast.121), channel_id=1, source_target_pairs={{0,2},{1,3}} | collective-permute-start | bytes 14155784 | tf_op jit(solution)/shard_map/ppermute | solution.py:31
  1108.3 23.3 %copy-start.14 = (f32[1536]{0:T(1024)}, f32[1536]{0:T(1024)S(1)}, u32[]{:S(2)}) copy-start(f32[1536]{0:T(1024)S(1)} %convert_reduce_fusion.1) | copy-start | bytes 18436
  1108.4 5.0 slice-start.1
  1125.7 6.0 copy-start.2
  1131.7 0.6 copy-start.12
  1185.3 8.5 copy-start.5
  1325.4 49.4 %copy-start.8 = (f32[16,192]{1,0:T(8,128)}, f32[16,192]{1,0:T(8,128)S(1)}, u32[]{:S(2)}) copy-start(f32[16,192]{1,0:T(8,128)S(1)} %add_rsqrt_fusion) | copy-start | bytes 36868
  1362.4 12.4 copy-start.10
  1374.8 10.9 copy-start.3
  1374.8 10.9 copy-start.4
  1374.8 10.9 copy-start.13
  1374.8 10.9 copy-start.15
  1385.7 34.9 %copy-start = (bf16[8,192,1536]{2,1,0:T(8,128)(2,1)S(1)}, bf16[8,192,1536]{2,1,0:T(8,128)(2,1)}, u32[]{:S(2)}) copy-start(bf16[8,192,1536]{2,1,0:T(8,128)(2,1)} %get-tuple-element.26) | copy-start | bytes 14155780
  1385.7 34.9 %copy-start.1 = (bf16[8,192,1536]{2,1,0:T(8,128)(2,1)S(1)}, bf16[8,192,1536]{2,1,0:T(8,128)(2,1)}, u32[]{:S(2)}) copy-start(bf16[8,192,1536]{2,1,0:T(8,128)(2,1)} %get-tuple-element.27) | copy-start | bytes 14155780
  1385.7 34.9 %copy-start.9 = (f32[16,192]{1,0:T(8,128)S(1)}, f32[16,192]{1,0:T(8,128)}, u32[]{:S(2)}) copy-start(f32[16,192]{1,0:T(8,128)} %copy-done.8) | copy-start | bytes 36868
  1385.7 34.9 %copy-start.11 = (f32[1536]{0:T(1024)S(1)}, f32[1536]{0:T(1024)}, u32[]{:S(2)}) copy-start(f32[1536]{0:T(1024)} %convert_reduce_fusion) | copy-start | bytes 18436
  1456.6 89.4 %collective-permute-start.1 = (bf16[8,1,192,1536]{3,2,0,1:T(8,128)(2,1)}, bf16[8,1,192,1536]{3,2,0,1:T(8,128)(2,1)}, u32[]{:S(2)}, u32[]{:S(2)}) collective-permute-start(bf16[8,1,192,1536]{3,2,0,1:T(8,128)(2,1)} %collective-permute-done), channel_id=1, source_target_pairs={{4,6},{5,7}} | collective-permute-start | bytes 14155784 | tf_op jit(solution)/shard_map/ppermute | solution.py:31
  1554.2 56.5 %copy-start.16 = (f32[2,8,128]{2,1,0:T(8,128)S(1)}, f32[2,8,128]{2,1,0:T(8,128)}, u32[]{:S(2)}) copy-start(f32[2,8,128]{2,1,0:T(8,128)} %get-tuple-element.20) | copy-start | bytes 24580
  1554.2 57.7 %copy-start.6 = (f32[2,8,1536]{2,1,0:T(8,128)S(1)}, f32[2,8,1536]{2,1,0:T(8,128)}, u32[]{:S(2)}) copy-start(f32[2,8,1536]{2,1,0:T(8,128)} %get-tuple-element.30) | copy-start | bytes 294916
  1554.2 57.8 %copy-start.7 = (f32[2,8,1536]{2,1,0:T(8,128)S(1)}, f32[2,8,1536]{2,1,0:T(8,128)}, u32[]{:S(2)}) copy-start(f32[2,8,1536]{2,1,0:T(8,128)} %get-tuple-element.31) | copy-start | bytes 294916
  1554.2 75.2 %collective-permute-start.3 = (bf16[8,1,192,1536]{3,2,0,1:T(8,128)(2,1)}, bf16[8,1,192,1536]{3,2,0,1:T(8,128)(2,1)}, u32[]{:S(2)}, u32[]{:S(2)}) collective-permute-start(bf16[8,1,192,1536]{3,2,0,1:T(8,128)(2,1)} %select_select_fusion), channel_id=1, source_target_pairs={{0,1},{1,0},{2,3},{3,2},{4,5},{5,4},{6,7},{7,6}} | collective-permute-start | bytes 14155784 | tf_op jit(solution)/shard_map/ppermute | solution.py:31

commit v4 on v3

v4 whole, which is shorter than its diff:
```python
import functools

import jax
import jax.numpy as jnp
from jax import lax
from jax.experimental import pallas as pl
from jax.experimental.pallas import tpu as pltpu
from jax.sharding import PartitionSpec as P

NORM_EPS = 1e-5
AX = ('tp', 'stage')
BF = jnp.bfloat16
F32 = jnp.float32
MESH = pl.DeviceIdType.MESH
ANY = pl.ANY

R_SWAP = [(1, 4), (4, 1), (2, 7), (7, 2)]
CORE_SWAP = [(0, 1), (1, 0), (2, 3), (3, 2), (4, 5), (5, 4), (6, 7), (7, 6)]
L_TO_R = [(0, 1), (5, 4), (6, 7), (3, 2)]

GELU_A = 0.7978845608028654
GELU_B = 0.044715
I0, I1, I2, I3, I4, I6, I8 = 0, 1, 2, 3, 4, 6, 8
CHUNK = 1024
SUB = 256
DEPTH = 3
KDEPTH = 2
HEAD_PAD = 128
VMEM_LIMIT = 67043328


def move(value, perm):
    return lax.ppermute(value, AX, perm)


def mm(a, b):
    return lax.dot_general(a, b, (((I1,), (I0,)), ((), ())), preferred_element_type=F32)


def mm_nt(a, b):
    return lax.dot_general(a, b, (((I1,), (I1,)), ((), ())), preferred_element_type=F32)


def mm_tn(a, b):
    return lax.dot_general(a, b, (((I0,), (I0,)), ((), ())), preferred_element_type=F32)


class Place:
    def __init__(self):
        self.tp = lax.axis_index('tp')
        self.stage = lax.axis_index('stage')
        self.core = self.stage % I2
        self.x_pos = self.stage // I2
        self.home = self.x_pos * (I3 - I2 * self.tp) + self.tp
        self.is_l = self.stage == self.home
        self.sib = self.stage + I1 - I2 * self.core

    def at(self, tp, stage):
        return {'tp': tp, 'stage': stage}

    @property
    def sibling(self):
        return self.at(self.tp, self.sib)

    @property
    def across(self):
        return self.at(I1 - self.tp, self.stage)

    @property
    def across_other(self):
        return self.at(I1 - self.tp, self.sib)

    def others(self, src, dst, send_sems, recv_sem):
        copies = []
        for d_tp in (I0, I1):
            for d_stage in range(I4):
                if d_tp or d_stage:
                    there = self.at(self.tp + d_tp - I2 * d_tp * self.tp, (self.stage + d_stage) % I4)
                    copies.append(remote(src, dst, send_sems.at[len(copies)], recv_sem, there))
        return copies

    def chain(self, delta):
        there = self.home + delta
        x_pos = there // I2
        tp = there % I2 + x_pos * (I1 - I2 * (there % I2))
        return self.at(tp, I2 * x_pos + self.core)


def entry_barrier(place):
    barrier = pltpu.get_barrier_semaphore()
    for d_tp in (I0, I1):
        for d_stage in range(I4):
            if d_tp or d_stage:
                tp = place.tp + d_tp - I2 * d_tp * place.tp
                stage = (place.stage + d_stage) % I4
                pl.semaphore_signal(barrier, inc=I1, device_id=place.at(tp, stage), device_id_type=MESH)
    pl.semaphore_wait(barrier, 7)


def remote(src, dst, send_sem, recv_sem, device_id):
    return pltpu.make_async_remote_copy(src_ref=src, dst_ref=dst, send_sem=send_sem, recv_sem=recv_sem, device_id=device_id, device_id_type=MESH)


def rows_loop(total, step, body):
    def run(i, carry):
        body(pl.ds(pl.multiple_of(i * step, step), step))
        return carry
    lax.fori_loop(I0, total // step, run, I0)


def norm_rows(src, gain_row, dst, total):
    def body(rows):
        v = src[rows, :].astype(F32)
        inv = lax.rsqrt(jnp.mean(v * v, axis=-I1, keepdims=True) + NORM_EPS)
        dst[rows, :] = (v * inv * gain_row).astype(BF)
    rows_loop(total, 32, body)


def gelu_gate(u):
    u2 = u * u
    t = jnp.tanh(u * (GELU_A + (GELU_A * GELU_B) * u2))
    return 0.5 * t + 0.5, u2


def gelu_slope(hidden, gate, u2):
    return gate + hidden * (1.0 - gate) * (2.0 * GELU_A + (6.0 * GELU_A * GELU_B) * u2)


def causal_probs(q, k, scale):
    s = mm_nt(q, k) * scale
    q_pos = lax.broadcasted_iota(jnp.int32, s.shape, I0)
    k_pos = lax.broadcasted_iota(jnp.int32, s.shape, I1)
    s = jnp.where(k_pos <= q_pos, s, -1e30)
    e = jnp.exp(s - jnp.max(s, axis=-I1, keepdims=True))
    return e * (1.0 / jnp.sum(e, axis=-I1, keepdims=True))


def attention_backward(q, k, v, d_ctx, scale):
    probs = causal_probs(q, k, scale)
    probs_bf = probs.astype(BF)
    dp = mm_nt(d_ctx, v).astype(BF).astype(F32)
    ds = probs * (dp - jnp.sum(dp * probs, axis=-I1, keepdims=True)) * scale
    dv = mm_tn(probs_bf, d_ctx)
    hi = ds.astype(BF)
    rest = ds - hi.astype(F32)
    lo = rest.astype(BF)
    tail = (rest - lo.astype(F32)).astype(BF)
    dq = mm(hi, k) + (mm(lo, k) + mm(tail, k))
    dk = mm_tn(hi, q) + (mm_tn(lo, q) + mm_tn(tail, q))
    return probs_bf, dq.astype(BF), dk.astype(BF), dv.astype(BF)


def lanes(offset, size):
    return pl.ds(pl.multiple_of(offset, 128), size)


class Stream:
    def __init__(self, buf, sem, depth, parts, total, by_heads):
        self.buf, self.sem, self.depth, self.parts, self.total, self.by_heads = buf, sem, depth, parts, total, by_heads
        self.per_tick = sum(p[I1] for p in parts)

    def copy_in(self, ref, index, slot):
        if not self.by_heads:
            where = pl.ds(pl.multiple_of(index * CHUNK, CHUNK), CHUNK)
            pltpu.make_async_copy(ref.at[:, where], self.buf.at[slot], self.sem.at[slot]).start()
            return
        for r in range(I8):
            rows = pl.ds(pl.multiple_of(index * 768 + r * 96, 96), 96)
            pltpu.make_async_copy(ref.at[rows, :], self.buf.at[slot, r * 128:r * 128 + 96, :], self.sem.at[slot]).start()

    def start(self, seq):
        @pl.when(seq < self.total)
        def _():
            j = seq % self.per_tick
            slot = seq % self.depth
            base = I0
            for choices, chunks in self.parts:
                for condition, ref in choices:
                    here = (j >= base) & (j < base + chunks)
                    here = here if condition is None else here & condition

                    @pl.when(here)
                    def _(ref=ref, low=base):
                        self.copy_in(ref, j - low, slot)
                base += chunks

    def prime(self):
        for seq in range(self.depth):
            self.start(jnp.int32(seq))

    def wait(self, seq):
        slot = seq % self.depth
        ref = self.parts[I0][I0][I0][I1]
        if self.by_heads:
            pltpu.make_async_copy(ref.at[I0:768, :], self.buf.at[slot, I0:768, :], self.sem.at[slot]).wait()
        else:
            pltpu.make_async_copy(ref.at[:, I0:CHUNK], self.buf.at[slot], self.sem.at[slot]).wait()
        return self.buf.at[slot]


PIECES = [(0, 0, 0), (0, 0, 1), (0, 0, 2), (1, 0, 0), (2, 1, 0), (2, 1, 1), (2, 1, 2), (2, 1, 3), (3, 0, 0), (3, 0, 1), (3, 0, 2), (3, 0, 3)]


def piece(ref, axis, index):
    return ref.at[index * 768:(index + I1) * 768, :] if axis == I0 else ref.at[:, index * 768:(index + I1) * 768]


def weight_phase(place, is_r, own, near, far, turned, wn, wk, send_sem, y_send, d_send, near_sem, far_sem, load_sem, store_sem):
    wk[...] = jnp.zeros_like(wk)

    @pl.when(place.is_l)
    def _():
        for i in range(I4):
            remote(own[i], near[i], send_sem.at[i], near_sem.at[i], place.sibling).start()

    @pl.when(is_r)
    def _():
        for c, (i, axis, index) in enumerate(PIECES):
            remote(piece(own[i], axis, index), piece(far[i], axis, index), y_send.at[i], far_sem.at[c], place.across_other).start()

    def load(i, refs, t, slot):
        for condition, ref in refs:
            def go(ref=ref):
                if i < I2:
                    for r in range(I2):
                        rows = pl.ds(pl.multiple_of(t * 192 + r * 96, 96), 96)
                        pltpu.make_async_copy(ref.at[rows, :], wk.at[I0, pl.ds(slot * SUB + r * 128, 96), :], load_sem.at[slot]).start()
                elif i == I2:
                    pltpu.make_async_copy(ref.at[:, lanes(t * SUB, SUB)], wn.at[slot, :, I0:SUB], load_sem.at[slot]).start()
                else:
                    rows = pl.ds(pl.multiple_of(t * SUB, SUB), SUB)
                    pltpu.make_async_copy(ref.at[rows, :], wk.at[I0, pl.ds(512 + slot * SUB, SUB), :], load_sem.at[slot]).start()
            if condition is None:
                go()
            else:
                pl.when(condition)(go)

    def loaded(i, refs, slot):
        ref = refs[I0][I1]
        if i < I2:
            pltpu.make_async_copy(ref.at[I0:192, :], wk.at[I0, I0:192, :], load_sem.at[slot]).wait()
        elif i == I2:
            pltpu.make_async_copy(ref.at[:, I0:SUB], wn.at[slot, :, I0:SUB], load_sem.at[slot]).wait()
        else:
            pltpu.make_async_copy(ref.at[I0:SUB, :], wk.at[I0, 512:768, :], load_sem.at[slot]).wait()

    def store(i, dst, t, slot):
        if i == I2:
            rows = pl.ds(pl.multiple_of(t * SUB, SUB), SUB)
            return pltpu.make_async_copy(wk.at[I1, pl.ds(slot * SUB, SUB), :], dst.at[rows, :], store_sem.at[slot])
        return pltpu.make_async_copy(wn.at[slot, :, SUB:512], dst.at[:, lanes(t * SUB, SUB)], store_sem.at[slot])

    def turn(i, refs, dst, first, count):
        load(i, refs, first, I0)

        def step(n, c):
            slot = n % I2

            @pl.when(n + I1 < count)
            def _():
                load(i, refs, first + n + I1, I1 - slot)
            loaded(i, refs, slot)

            @pl.when(n >= I2)
            def _():
                store(i, dst, first + n - I2, slot).wait()
            for b in range(I6):
                cut = slice(b * SUB, b * SUB + SUB)
                if i == I2:
                    wk[I1, pl.ds(pl.multiple_of(slot * SUB, SUB), SUB), cut] = wn[slot, cut, I0:SUB].T
                else:
                    base = I0 if i < I2 else 512
                    wn[slot, cut, SUB:512] = wk[I0, pl.ds(pl.multiple_of(base + slot * SUB, SUB), SUB), cut].T
            store(i, dst, first + n, slot).start()
            return c
        lax.fori_loop(I0, count, step, I0)
        for n in (count - I2, count - I1):
            store(i, dst, first + n, n % I2).wait()

    counts = (12, I4, 12, 12)
    for i in range(I4):
        @pl.when(is_r)
        def _(i=i):
            remote(near[i], near[i], send_sem.at[i], near_sem.at[i], place.sibling).wait_recv()
        turn(i, [(place.is_l, own[i]), (is_r, near[i])], turned[i][I0], I0, counts[i])
    done = [I0, I0, I0, I0]
    for c, (i, axis, index) in enumerate(PIECES):
        view = piece(far[i], axis, index)
        remote(view, view, d_send.at[i], far_sem.at[c], place.sibling).wait_recv()

        @pl.when(is_r)
        def _(i=i, c=c, view=view):
            remote(view, view, d_send.at[i], far_sem.at[c], place.sibling).start()
        count = I4 if i < I2 else I3
        turn(i, [(None, far[i])], turned[i][I1], done[i], count)
        done[i] += count

    @pl.when(place.is_l)
    def _():
        for i in range(I4):
            remote(own[i], near[i], send_sem.at[i], near_sem.at[i], place.sibling).wait_send()

    @pl.when(is_r)
    def _():
        for i in range(I4):
            remote(own[i], far[i], y_send.at[i], far_sem.at[I0], place.across_other).wait_send()
            remote(far[i], far[i], d_send.at[i], far_sem.at[I0], place.sibling).wait_send()


def step_kernel(dims, x_ref, y_ref, wq, wo, wu, wd, own_gains,
                a_s, h_s, m_s, qkv_s, u_s, dx_s, oh_same, oh_other, oa_same, oa_other, od_same, od_other, og_same, og_other,
                dg_same, dg_other, loss_all, nq, no, nu, nd, fq, fo, fu, fd, tq0, to0, tu0, td0, tq1, to1, tu1, td1,
                abuf, gbuf, hbuf, obuf, nbuf, ybuf, qkvbuf, ubuf, habuf, zbuf, ctxbuf, dqkvbuf, acc, accg, lossbuf, losstile, gains, wres, wn, wk,
                send_sem, y_send, d_send, near_sem, far_sem, t_load, t_store,
                act_sem, grad_sem, hop_f, hop_b, keep_sem, back_sem, save_sem, stream_n, stream_k, res_sem, big_sem, load_sem, y_sem,
                os_sem, oo_sem, as_sem, ao_sem, ds_sem, do_sem, gs_sem, go_sem, bulk, gain_sem, tiny, loss_send):
    micro, seq, width, heads, head_dim, ffn = dims
    place = Place()
    is_first, is_last = place.home == I0, place.home == I3
    home02 = (place.home == I0) | (place.home == I2)
    home13 = jnp.logical_not(home02)
    is_r = jnp.logical_not(place.is_l)
    half = heads // I2 * HEAD_PAD
    scale = head_dim ** -0.5
    norm_factor = 1.0 / (micro * I2 * seq * width)
    own, near, far = (wq, wo, wu, wd), (nq, no, nu, nd), (fq, fo, fu, fd)
    turned = ((tq0, tq1), (to0, to1), (tu0, tu1), (td0, td1))
    entry_barrier(place)

    @pl.when(place.is_l)
    def _():
        pltpu.make_async_copy(own_gains, gains, gain_sem.at[I0]).start()
        remote(own_gains, gains, gain_sem.at[I1], gain_sem.at[I0], place.sibling).start()

    @pl.when(is_first)
    def _():
        for m in range(micro):
            pltpu.make_async_copy(x_ref.at[m, place.core], abuf.at[m], act_sem.at[m]).start()
    weight_phase(place, is_r, own, near, far, turned, wn, wk, send_sem, y_send, d_send, near_sem, far_sem, t_load, t_store)
    pltpu.make_async_copy(own_gains, gains, gain_sem.at[I0]).wait()

    @pl.when(place.is_l)
    def _():
        remote(own_gains, gains, gain_sem.at[I1], gain_sem.at[I0], place.sibling).wait_send()

    def near_of(i):
        return [(place.is_l, own[i]), (is_r, near[i])]

    def resident(choices_of_half, start):
        for c in range(I6):
            for condition, ref in choices_of_half[c // I3]:
                copy = pltpu.make_async_copy(ref.at[(c % I3) * CHUNK:(c % I3 + I1) * CHUNK, :], wres.at[c], res_sem.at[c])
                if condition is None:
                    copy.start()
                else:
                    pl.when(condition)(copy.start)

    def resident_ready(j):
        pltpu.make_async_copy(wd.at[I0:CHUNK, :], wres.at[j], res_sem.at[j]).wait()

    def saved(dst, index):
        return pltpu.make_async_copy(hbuf, dst, save_sem.at[index])

    sn = Stream(wn, stream_n, DEPTH, [([(None, tq0)], I3), ([(None, tq1)], I3), (near_of(I2), I3), ([(None, fu)], I3)], micro * 12, False)
    sk = Stream(wk, stream_k, KDEPTH, [(near_of(I1), I1), ([(None, fo)], I1)], micro * I2, True)
    sn.prime()
    sk.prime()
    resident((near_of(I3), [(None, fd)]), True)
    lossbuf[...] = jnp.zeros_like(lossbuf)

    def qkv_out(m):
        return pltpu.make_async_copy(qkvbuf.at[I0], qkv_s.at[m], big_sem.at[I0])

    def up_out(m):
        return pltpu.make_async_copy(ubuf.at[I0], u_s.at[m], big_sem.at[I1])

    def act_out(m):
        return pltpu.make_async_copy(abuf.at[m], a_s.at[m], save_sem.at[I2])

    def hop_forward(m):
        return remote(obuf.at[m % I2], abuf.at[m], hop_f.at[m % I2], act_sem.at[m], place.chain(I1))

    def near_hand(src, dst_far, dst_own, sem, recv_sem):
        return (lambda: remote(src, dst_far, sem, recv_sem, place.sibling)), (lambda: pltpu.make_async_copy(src, dst_own, sem))

    def hand_out(m):
        return near_hand(obuf.at[m % I2], oa_other.at[m], oa_same.at[m], keep_sem.at[m % I2], ao_sem)

    def both_kinds(condition, copies, start):
        far_copy, own_copy = copies

        @pl.when(condition & place.is_l)
        def _():
            far_copy().start() if start else far_copy().wait_send()

        @pl.when(condition & is_r)
        def _():
            own_copy().start() if start else own_copy().wait()

    def forward_tick(m, carry):
        act, mid, out = abuf.at[m], hbuf, obuf.at[m % I2]
        pltpu.make_async_copy(x_ref.at[m, place.core], act, act_sem.at[m]).wait()
        act_out(m).start()

        @pl.when(place.is_l)
        def _():
            pltpu.make_async_copy(act, oa_same.at[m], as_sem).start()

        @pl.when(is_last)
        def _():
            pltpu.make_async_copy(y_ref.at[m, place.core], ybuf, y_sem).start()
        norm_rows(act, gains[I0:I1, :], nbuf, seq)

        @pl.when(m > I0)
        def _():
            qkv_out(m).wait()

        def qkv_step(j, c):
            w = sn.wait(m * 12 + j)
            for n in range(I0, CHUNK, SUB):
                qkvbuf[I0, :, lanes(j * CHUNK + n, SUB)] = mm(nbuf[...], w[:, n:n + SUB]).astype(BF)
            sn.start(m * 12 + j + DEPTH)
            return c
        lax.fori_loop(I0, I6, qkv_step, I0)
        qkv_out(m).start()
        act_out(m).wait()

        @pl.when(is_r)
        def _():
            remote(a_s.at[m], oa_other.at[m], bulk.at[I0], ao_sem, place.sibling).start()

        def head_step(i, c):
            for r in range(I4):
                base = (i // I2) * (I3 * half) + ((i % I2) * I4 + r) * HEAD_PAD
                q = qkvbuf[I0, :, lanes(base, HEAD_PAD)]
                k = qkvbuf[I0, :, lanes(base + half, HEAD_PAD)]
                v = qkvbuf[I0, :, lanes(base + I2 * half, HEAD_PAD)]
                probs = causal_probs(q, k, scale).astype(BF)
                ctxbuf[:, lanes((i * I4 + r) * HEAD_PAD, HEAD_PAD)] = mm(probs, v).astype(BF)
            return c
        lax.fori_loop(I0, heads // I4, head_step, I0)

        w0, w1 = sk.wait(m * I2), sk.wait(m * I2 + I1)
        for n in range(I0, width, SUB):
            total = mm(ctxbuf[:, I0:half], w0[:, n:n + SUB]) + mm(ctxbuf[:, half:I2 * half], w1[:, n:n + SUB])
            mid[:, n:n + SUB] = (act[:, n:n + SUB].astype(F32) + total).astype(BF)
        sk.start(m * I2 + KDEPTH)
        sk.start(m * I2 + I1 + KDEPTH)
        saved(h_s.at[m], I0).start()

        @pl.when(place.is_l)
        def _():
            saved(oh_same.at[m], I1).start()
        norm_rows(mid, gains[I1:I2, :], nbuf, seq)

        @pl.when(m > I0)
        def _():
            up_out(m).wait()
        acc[...] = jnp.zeros_like(acc)

        def mlp_step(j, c):
            w = sn.wait(m * 12 + I6 + j)
            for n in range(I0, CHUNK, SUB):
                u = mm(nbuf[...], w[:, n:n + SUB]).astype(BF)
                ubuf[I0, :, lanes(j * CHUNK + n, SUB)] = u
                uf = u.astype(F32)
                zbuf[:, n:n + SUB] = (uf * gelu_gate(uf)[I0]).astype(BF)
            sn.start(m * 12 + I6 + j + DEPTH)

            @pl.when(m == I0)
            def _():
                resident_ready(j)
            for n in range(I0, width, SUB):
                acc[:, n:n + SUB] += mm(zbuf[...], wres[j, :, n:n + SUB])
            return c
        lax.fori_loop(I0, I6, mlp_step, I0)
        up_out(m).start()

        @pl.when((m > I1) & jnp.logical_not(is_last))
        def _():
            hop_forward(m).wait_send()

        both_kinds((m > I1) & home02, hand_out(m), False)

        def finish(rows):
            out[rows, :] = (mid[rows, :].astype(F32) + acc[rows, :]).astype(BF)
        rows_loop(seq, 32, finish)

        @pl.when(jnp.logical_not(is_last))
        def _():
            hop_forward(m).start()

        both_kinds(home02, hand_out(m), True)

        @pl.when(is_last)
        def _():
            pltpu.make_async_copy(y_ref.at[m, place.core], ybuf, y_sem).wait()

            def seed(rows):
                error = out[rows, :].astype(F32) - ybuf[rows, :].astype(F32)
                gbuf[m, rows, :] = (error * norm_factor).astype(BF)
                lossbuf[...] += jnp.sum((error * error).reshape(I4, I8, width), axis=I0)
            rows_loop(seq, 32, seed)

        saved(h_s.at[m], I0).wait()

        @pl.when(place.is_l)
        def _():
            saved(oh_same.at[m], I1).wait()
            remote(h_s.at[m], oh_same.at[m], bulk.at[I2], os_sem, place.across).start()

        @pl.when(is_r)
        def _():
            remote(h_s.at[m], oh_other.at[m], bulk.at[I2], oo_sem, place.sibling).start()
            remote(h_s.at[m], oh_other.at[m], bulk.at[I3], oo_sem, place.across_other).start()

        @pl.when(is_last & place.is_l)
        def _():
            remote(gbuf.at[m], og_same.at[m], bulk.at[I4], gs_sem, place.across).start()

        @pl.when(is_last & is_r)
        def _():
            remote(gbuf.at[m], og_other.at[m], bulk.at[I4], go_sem, place.across_other).start()
        return carry

    lax.fori_loop(I0, micro, forward_tick, I0)

    @pl.when(is_last)
    def _():
        total = lossbuf[:, I0:128]
        for n in range(128, width, 128):
            total = total + lossbuf[:, n:n + 128]
        losstile[...] = total
        pltpu.make_async_copy(losstile, loss_all.at[place.core], tiny.at[5]).start()
        for index, copy in enumerate(place.others(losstile, loss_all.at[place.core], loss_send, tiny.at[5])):
            copy.start()
    for copy in (qkv_out(micro - I1), up_out(micro - I1)):
        copy.wait()

    @pl.when(jnp.logical_not(is_last))
    def _():
        for m in (micro - I2, micro - I1):
            hop_forward(m).wait_send()
    for m in (micro - I2, micro - I1):
        both_kinds(home02, hand_out(m), False)

    bn = Stream(wn, stream_n, DEPTH, [([(None, td0)], I3), ([(None, td1)], I3), ([(None, to0)], I1), ([(None, to1)], I1)], micro * I8, False)
    bk = Stream(wk, stream_k, KDEPTH, [(near_of(I0), I3), ([(None, fq)], I3)], micro * I6, True)
    bn.prime()
    bk.prime()
    resident(([(None, tu0)], [(None, tu1)]), True)

    def loads(i):
        m = micro - I1 - i
        slot = i % I2
        return (pltpu.make_async_copy(u_s.at[m], ubuf.at[slot], load_sem.at[I0, slot]),
                pltpu.make_async_copy(qkv_s.at[m], qkvbuf.at[slot], load_sem.at[I1, slot]),
                pltpu.make_async_copy(h_s.at[m], habuf.at[slot, I0], load_sem.at[I2, slot]),
                pltpu.make_async_copy(a_s.at[m], habuf.at[slot, I1], load_sem.at[I3, slot]))

    for copy in loads(I0):
        copy.start()
    accg[...] = jnp.zeros_like(accg)

    def norm_back(index, x, base, dst, gain_row):
        def body(rows):
            xf = x[rows, :].astype(F32)
            dy = acc[rows, :].astype(BF).astype(F32)
            inv = lax.rsqrt(jnp.mean(xf * xf, axis=-I1, keepdims=True) + NORM_EPS)
            xn = xf * inv
            accg[index] += jnp.sum((dy * xn).reshape(I4, I8, width), axis=I0)
            dyg = dy * gain_row
            dx = inv * (dyg - xn * jnp.mean(dyg * xn, axis=-I1, keepdims=True))
            dst[rows, :] = (base[rows, :].astype(F32) + dx).astype(BF)
        rows_loop(seq, 32, body)

    def hop_back(i):
        m = micro - I1 - i
        return remote(obuf.at[i % I2], gbuf.at[m], hop_b.at[i % I2], grad_sem.at[m], place.chain(-I1))

    def hand_back(i):
        m = micro - I1 - i
        return near_hand(obuf.at[i % I2], og_other.at[m], og_same.at[m], back_sem.at[i % I2], go_sem)

    def keep_dx(i):
        return pltpu.make_async_copy(obuf.at[i % I2], dx_s.at[micro - I1 - i], back_sem.at[i % I2])

    def back_ready(i):
        both_kinds((i > I1) & home13, hand_back(i), False)

        @pl.when((i > I1) & is_first)
        def _():
            keep_dx(i).wait()

        @pl.when((i > I1) & jnp.logical_not(is_first))
        def _():
            hop_back(i).wait_send()

    def backward_tick(i, carry):
        m = micro - I1 - i
        slot = i % I2
        grad, dmid, prev = gbuf.at[m], hbuf, obuf.at[slot]
        u_now, qkv_now, h_now, a_now = ubuf.at[slot], qkvbuf.at[slot], habuf.at[slot, I0], habuf.at[slot, I1]

        @pl.when(i + I1 < micro)
        def _():
            for copy in loads(i + I1):
                copy.start()

        @pl.when(jnp.logical_not(is_last))
        def _():
            remote(grad, grad, hop_b.at[slot], grad_sem.at[m], place.sibling).wait_recv()

        @pl.when(place.is_l)
        def _():
            pltpu.make_async_copy(grad, og_same.at[m], gs_sem).start()

        @pl.when(is_r)
        def _():
            remote(grad, og_other.at[m], bulk.at[5], go_sem, place.sibling).start()
        load_u, load_qkv, load_h, load_a = loads(i)
        load_u.wait()
        acc[...] = jnp.zeros_like(acc)

        def mlp_step(j, c):
            w = bn.wait(i * I8 + j)
            for n in range(I0, CHUNK, SUB):
                dz = mm(grad[...], w[:, n:n + SUB]).astype(BF).astype(F32)
                u = u_now[:, lanes(j * CHUNK + n, SUB)].astype(F32)
                gate, u2 = gelu_gate(u)
                zbuf[:, n:n + SUB] = (dz * gelu_slope(u * gate, gate, u2)).astype(BF)
            bn.start(i * I8 + j + DEPTH)

            @pl.when(i == I0)
            def _():
                resident_ready(j)
            for n in range(I0, width, SUB):
                acc[:, n:n + SUB] += mm(zbuf[...], wres[j, :, n:n + SUB])
            return c
        lax.fori_loop(I0, I6, mlp_step, I0)
        load_h.wait()
        norm_back(I1, h_now, grad, dmid, gains[I1:I2, :])

        @pl.when(place.is_l)
        def _():
            saved(od_same.at[m], I0).start()

        @pl.when(is_r)
        def _():
            saved(m_s.at[m], I0).start()
        for c in range(I2):
            w = bn.wait(i * I8 + I6 + c)
            for n in range(I0, CHUNK, SUB):
                ctxbuf[:, c * CHUNK + n:c * CHUNK + n + SUB] = mm(dmid[...], w[:, n:n + SUB]).astype(BF)
            bn.start(i * I8 + I6 + c + DEPTH)
        load_qkv.wait()

        def head_step(t, c):
            for r in range(I2):
                base = (t // I4) * (I3 * half) + ((t % I4) * I2 + r) * HEAD_PAD
                q = qkv_now[:, lanes(base, HEAD_PAD)]
                k = qkv_now[:, lanes(base + half, HEAD_PAD)]
                v = qkv_now[:, lanes(base + I2 * half, HEAD_PAD)]
                dc = ctxbuf[:, lanes((t * I2 + r) * HEAD_PAD, HEAD_PAD)]
                _, dq, dk, dv = attention_backward(q, k, v, dc, scale)
                dqkvbuf[:, lanes(base, HEAD_PAD)] = dq
                dqkvbuf[:, lanes(base + half, HEAD_PAD)] = dk
                dqkvbuf[:, lanes(base + I2 * half, HEAD_PAD)] = dv
            return c
        lax.fori_loop(I0, heads // I2, head_step, I0)
        acc[...] = jnp.zeros_like(acc)

        def qkv_step(j, c):
            w = bk.wait(i * I6 + j)
            for n in range(I0, width, SUB):
                acc[:, n:n + SUB] += mm(dqkvbuf[:, lanes(j * CHUNK, CHUNK)], w[:, n:n + SUB])
            bk.start(i * I6 + j + KDEPTH)
            return c
        lax.fori_loop(I0, I6, qkv_step, I0)
        load_a.wait()
        back_ready(i)
        norm_back(I0, a_now, dmid, prev, gains[I0:I1, :])

        @pl.when(jnp.logical_not(is_first))
        def _():
            hop_back(i).start()

        @pl.when(is_first)
        def _():
            keep_dx(i).start()
        both_kinds(home13, hand_back(i), True)

        @pl.when(place.is_l)
        def _():
            saved(od_same.at[m], I0).wait()
            remote(od_same.at[m], od_same.at[m], bulk.at[I6], ds_sem, place.across).start()

        @pl.when(is_r)
        def _():
            saved(m_s.at[m], I0).wait()
            remote(m_s.at[m], od_other.at[m], bulk.at[I6], do_sem, place.sibling).start()
            remote(m_s.at[m], od_other.at[m], bulk.at[7], do_sem, place.across_other).start()

        @pl.when((place.home == I2) & place.is_l)
        def _():
            remote(a_s.at[m], oa_same.at[m], bulk.at[I8], as_sem, place.across).start()

        @pl.when((place.home == I2) & is_r)
        def _():
            remote(a_s.at[m], oa_other.at[m], bulk.at[I8], ao_sem, place.across_other).start()
        return carry

    lax.fori_loop(I0, micro, backward_tick, I0)

    @pl.when((place.home == I1) & place.is_l)
    def _():
        for m in reversed(range(micro)):
            remote(gbuf.at[m], og_same.at[m], bulk.at[I4], gs_sem, place.across).start()

    @pl.when((place.home == I1) & is_r)
    def _():
        for m in reversed(range(micro)):
            remote(gbuf.at[m], og_other.at[m], bulk.at[I4], go_sem, place.across_other).start()

    @pl.when(place.is_l)
    def _():
        pltpu.make_async_copy(accg, dg_same, tiny.at[I0]).start()
        remote(accg, dg_same, tiny.at[I1], tiny.at[I0], place.across).start()

    @pl.when(is_r)
    def _():
        remote(accg, dg_other, tiny.at[I1], tiny.at[I4], place.sibling).start()
        remote(accg, dg_other, tiny.at[I2], tiny.at[I4], place.across_other).start()

    for i in (micro - I2, micro - I1):
        back_ready(jnp.int32(i))

    def sent(buf, sem):
        remote(buf, a_s, sem, ao_sem, place.sibling).wait_send()

    def got(dst, sem):
        pltpu.make_async_copy(dst, dst, sem).wait()

    sent(h_s, bulk.at[I2])
    sent(m_s, bulk.at[I6])

    @pl.when(is_r)
    def _():
        sent(a_s, bulk.at[I0])
        sent(h_s, bulk.at[I3])
        sent(gbuf, bulk.at[5])
        sent(m_s, bulk.at[7])
        remote(accg, dg_other, tiny.at[I2], tiny.at[I4], place.sibling).wait_send()

    @pl.when(home13)
    def _():
        sent(gbuf, bulk.at[I4])

    @pl.when(place.home == I2)
    def _():
        sent(a_s, bulk.at[I8])

    @pl.when(is_last)
    def _():
        for copy in place.others(losstile, loss_all.at[place.core], loss_send, tiny.at[5]):
            copy.wait_send()
    remote(accg, dg_other, tiny.at[I1], tiny.at[I4], place.sibling).wait_send()
    got(oh_other, oo_sem)
    got(od_other, do_sem)
    got(og_other, go_sem)
    got(dg_same, tiny.at[I0])
    got(dg_other, tiny.at[I4])
    got(loss_all, tiny.at[5])

    @pl.when(is_r)
    def _():
        got(oh_same, os_sem)
        got(od_same, ds_sem)

    @pl.when(place.is_l | home02)
    def _():
        got(og_same, gs_sem)

    @pl.when(place.is_l | (place.home == I3))
    def _():
        got(oa_same, as_sem)

    @pl.when(place.is_l | (place.home != I1))
    def _():
        got(oa_other, ao_sem)


def step_phase(dims, x, y, own, own_gains):
    micro, seq, width, heads, head_dim, ffn = dims
    half = heads // I2 * HEAD_PAD
    act = (micro, seq, width)
    raw = [(heads // I2 * I3 * head_dim, width), (heads // I2 * head_dim, width), (width, ffn // I2), (ffn // I2, width)]
    turned = [(width, I3 * half), (width, half), (ffn // I2, width), (width, ffn // I2)]
    outs = [act, act, act, (micro, seq, I6 * half), (micro, seq, ffn), act] + [act] * I8
    out_shape = [jax.ShapeDtypeStruct(s, BF) for s in outs]
    out_shape += [jax.ShapeDtypeStruct(s, F32) for s in ((I2, I8, width), (I2, I8, width), (I2, I8, 128))]
    out_shape += [jax.ShapeDtypeStruct(s, BF) for s in raw + raw + turned + turned]
    any_spec = pl.BlockSpec(memory_space=ANY)
    vmem, dma = pltpu.VMEM, pltpu.SemaphoreType.DMA
    scratch = [
        vmem(act, BF), vmem(act, BF), vmem((seq, width), BF), vmem((I2, seq, width), BF), vmem((seq, width), BF), vmem((seq, width), BF),
        vmem((I2, seq, I6 * half), BF), vmem((I2, seq, ffn), BF), vmem((I2, I2, seq, width), BF), vmem((seq, CHUNK), BF), vmem((seq, I2 * half), BF),
        vmem((seq, I6 * half), BF), vmem((seq, width), F32), vmem((I2, I8, width), F32), vmem((I8, width), F32), vmem((I8, 128), F32),
        vmem((I2, width), F32), vmem((I6, CHUNK, width), BF), vmem((DEPTH, width, CHUNK), BF), vmem((KDEPTH, CHUNK, width), BF),
        dma((I4,)), dma((I4,)), dma((I4,)), dma((I4,)), dma((12,)), dma((I2,)), dma((I2,)),
        dma((micro,)), dma((micro,)), dma((I2,)), dma((I2,)), dma((I2,)), dma((I2,)), dma((I3,)), dma((DEPTH,)), dma((KDEPTH,)), dma((I6,)), dma((I2,)),
        dma((I4, I2)), dma(()),
        dma(()), dma(()), dma(()), dma(()), dma(()), dma(()), dma(()), dma(()), dma((9,)), dma((I2,)), dma((I6,)), dma((7,)),
    ]
    return pl.pallas_call(
        functools.partial(step_kernel, dims),
        out_shape=tuple(out_shape),
        in_specs=[any_spec] * I6 + [pl.BlockSpec(memory_space=vmem)],
        out_specs=(any_spec,) * len(out_shape),
        scratch_shapes=scratch,
        compiler_params=pltpu.CompilerParams(collective_id=I0, has_side_effects=True, vmem_limit_bytes=VMEM_LIMIT),
        name='step_phase',
    )(x, y, *own, own_gains)


TOKENS = 512


def bring(pairs, sem):
    copies = [pltpu.make_async_copy(src, dst, sem.at[i]) for i, (src, dst) in enumerate(pairs)]
    for copy in copies:
        copy.start()
    return copies


def turn_into(dst, src, rows, cols):
    for r in range(I0, rows, SUB):
        for c in range(I0, cols, SUB):
            high, wide = min(SUB, rows - r), min(SUB, cols - c)
            dst[c:c + wide, r:r + high] = src[r:r + high, c:c + wide].T


def owner_mlp_kernel(hs, ho, gs, go, gain, wu, wd, dwu, dwd, n2, n2t, grad, wdt, z, zt, dup, sem):
    tokens, width = n2.shape
    part = tokens // I2

    @pl.when(pl.program_id(I0) == I0)
    def _():
        low, high = pl.ds(I0, part), pl.ds(part, part)
        for copy in bring([(hs, n2.at[low]), (ho, n2.at[high]), (gs, grad.at[low]), (go, grad.at[high])], sem):
            copy.wait()

        def prepare(rows):
            norm_rows(n2.at[rows], gain[...], n2.at[rows], SUB)
            for c in range(I0, width, SUB):
                n2t[c:c + SUB, rows] = n2[rows, c:c + SUB].T
        rows_loop(tokens, SUB, prepare)
    turn_into(wdt, wd, SUB, width)

    def front(rows):
        u = mm(n2[rows, :], wu[...]).astype(BF).astype(F32)
        dz = mm(grad[rows, :], wdt[...]).astype(BF).astype(F32)
        gate, u2 = gelu_gate(u)
        hidden = u * gate
        z[rows, :] = hidden.astype(BF)
        dup[rows, :] = (dz * gelu_slope(hidden, gate, u2)).astype(BF)
    rows_loop(tokens, TOKENS, front)
    turn_into(zt, z, tokens, SUB)
    for c in range(I0, width, TOKENS):
        dwu[c:c + TOKENS, :] = mm(n2t[c:c + TOKENS, :], dup[...])
    for c in range(I0, width, SUB):
        dwd[:, c:c + SUB] = mm(zt[...], grad[:, c:c + SUB])


def owner_mlp(h_rows, g_rows, gain, w_up, w_down):
    width, ffn = w_up.shape
    part = h_rows[I0].shape[I0]
    vmem = pltpu.VMEM
    any_spec = pl.BlockSpec(memory_space=ANY)
    up_spec = pl.BlockSpec((width, SUB), lambda i: (I0, i))
    down_spec = pl.BlockSpec((SUB, width), lambda i: (i, I0))
    rows = lambda n: vmem((I2 * part, n), BF)
    return pl.pallas_call(
        owner_mlp_kernel,
        grid=(ffn // SUB,),
        out_shape=(jax.ShapeDtypeStruct(w_up.shape, F32), jax.ShapeDtypeStruct(w_down.shape, F32)),
        in_specs=[any_spec] * I4 + [pl.BlockSpec(memory_space=vmem), up_spec, down_spec],
        out_specs=(up_spec, down_spec),
        scratch_shapes=[rows(width), vmem((width, I2 * part), BF), rows(width), vmem((width, SUB), BF), rows(SUB), vmem((SUB, I2 * part), BF), rows(SUB), pltpu.SemaphoreType.DMA((I4,))],
        compiler_params=pltpu.CompilerParams(vmem_limit_bytes=VMEM_LIMIT),
        cost_estimate=pl.CostEstimate(flops=16 * part * width * ffn, bytes_accessed=12 * width * ffn, transcendentals=I2 * part * ffn),
        name='owner_mlp',
    )(*h_rows, *g_rows, gain, w_up, w_down)


def owner_attn_kernel(seq, x_ref, rs, ro, ds, do, gain, wq, wo, dwq, dwo, n1, dmid, wpad, wqt, wot, qkv, dctx, dqkv, ctx, dqkvt, ctxt, sem):
    tokens, width = n1.shape
    part = tokens // I2
    head_dim = wo.shape[I1]
    scale = head_dim ** -0.5
    pair = I2 * HEAD_PAD

    @pl.when(pl.program_id(I0) == I0)
    def _():
        place = Place()
        from_x = (place.home == I1) & jnp.logical_not(place.is_l)
        low, high = pl.ds(I0, part), pl.ds(part, part)
        d_copies = bring([(ds, dmid.at[low]), (do, dmid.at[high])], sem)
        a_pairs = [(rs, n1.at[low]), (ro, n1.at[high])]
        a_sem = sem.at[I2:I4]

        @pl.when(from_x)
        def _():
            for m in range(part // seq):
                for first, core in ((I0, place.core), (part, I1 - place.core)):
                    pltpu.make_async_copy(x_ref.at[m, core], n1.at[pl.ds(first + m * seq, seq)], a_sem.at[min(first, I1)]).start()

        @pl.when(jnp.logical_not(from_x))
        def _():
            bring(a_pairs, a_sem)
        wpad[...] = jnp.zeros_like(wpad)
        for i, (src, dst) in enumerate(a_pairs):
            pltpu.make_async_copy(src, dst, a_sem.at[i]).wait()
        norm_rows(n1, gain[...], n1, tokens)
        for copy in d_copies:
            copy.wait()
    for r in range(I2):
        for t in range(I3):
            wpad[I0:head_dim, :] = wq[t, r]
            at = t * pair + r * HEAD_PAD
            turn_into(wqt.at[:, at:at + HEAD_PAD], wpad, HEAD_PAD, width)
        wpad[I0:head_dim, :] = wo[r]
        turn_into(wot.at[:, r * HEAD_PAD:(r + I1) * HEAD_PAD], wpad, HEAD_PAD, width)

    def front(rows):
        for n in range(I0, I3 * pair, pair):
            qkv[rows, n:n + pair] = mm(n1[rows, :], wqt[:, n:n + pair]).astype(BF)
        dctx[rows, :] = mm(dmid[rows, :], wot[...]).astype(BF)
    rows_loop(tokens, TOKENS, front)

    def sequence(rows):
        for r in range(I2):
            q_at, k_at, v_at = [slice(t * pair + r * HEAD_PAD, t * pair + (r + I1) * HEAD_PAD) for t in range(I3)]
            v, dc = qkv[rows, v_at], dctx[rows, q_at]
            probs, dq, dk, dv = attention_backward(qkv[rows, q_at], qkv[rows, k_at], v, dc, scale)
            ctx[rows, q_at] = mm(probs, v).astype(BF)
            dqkv[rows, q_at], dqkv[rows, k_at], dqkv[rows, v_at] = dq, dk, dv
    rows_loop(tokens, seq, sequence)

    def turn(rows):
        for t in range(I6):
            dqkvt[t * head_dim:(t + I1) * head_dim, rows] = dqkv[rows, t * HEAD_PAD:(t + I1) * HEAD_PAD].T[I0:head_dim]
        for t in range(I2):
            ctxt[t * head_dim:(t + I1) * head_dim, rows] = ctx[rows, t * HEAD_PAD:(t + I1) * HEAD_PAD].T[I0:head_dim]
    rows_loop(tokens, SUB, turn)
    for c in range(I0, width, SUB):
        cut = slice(c, c + SUB)
        dwq[:, :, :, cut] = mm(dqkvt[...], n1[:, cut]).reshape(I3, I2, head_dim, SUB)
        dwo[:, :, cut] = mm(ctxt[...], dmid[:, cut]).reshape(I2, head_dim, SUB)


def owner_attn(seq, x, a_rows, d_rows, gain, w_qkv, w_out):
    heads, head_dim, width = w_out.shape
    part = a_rows[I0].shape[I0]
    vmem = pltpu.VMEM
    any_spec = pl.BlockSpec(memory_space=ANY)
    q_spec = pl.BlockSpec((I3, I2, head_dim, width), lambda i: (I0, i, I0, I0))
    o_spec = pl.BlockSpec((I2, head_dim, width), lambda i: (i, I0, I0))
    rows = lambda n: vmem((I2 * part, n), BF)
    pair = I2 * HEAD_PAD
    return pl.pallas_call(
        functools.partial(owner_attn_kernel, seq),
        grid=(heads // I2,),
        out_shape=(jax.ShapeDtypeStruct(w_qkv.shape, F32), jax.ShapeDtypeStruct(w_out.shape, F32)),
        in_specs=[any_spec] * 5 + [pl.BlockSpec(memory_space=vmem), q_spec, o_spec],
        out_specs=(q_spec, o_spec),
        scratch_shapes=[
            rows(width), rows(width), vmem((HEAD_PAD, width), BF), vmem((width, I3 * pair), BF), vmem((width, pair), BF),
            rows(I3 * pair), rows(pair), rows(I3 * pair), rows(pair), vmem((I6 * head_dim, I2 * part), BF), vmem((I2 * head_dim, I2 * part), BF),
            pltpu.SemaphoreType.DMA((I4,)),
        ],
        compiler_params=pltpu.CompilerParams(vmem_limit_bytes=VMEM_LIMIT),
        cost_estimate=pl.CostEstimate(flops=36 * part * width * heads * head_dim, bytes_accessed=16 * width * width, transcendentals=part * heads * seq),
        name='owner_attn',
    )(x, *a_rows, *d_rows, gain, w_qkv, w_out)


def solution(mesh):
    act_spec = P('rep', None, None, None)
    weight_specs = (
        P(('rep', 'stage'), None, None, 'tp', None),
        P(('rep', 'stage'), 'tp', None, None),
        P(('rep', 'stage'), None, 'tp'),
        P(('rep', 'stage'), 'tp', None),
        P(('rep', 'stage'), None),
        P(('rep', 'stage'), None),
    )

    def device_fn(inputs, targets, w_qkv, w_out, w_up, w_down, gain_attn, gain_mlp):
        micro_count, _, seq_len, width = inputs.shape
        dims = (micro_count, seq_len, width, I2 * w_out.shape[I1], w_out.shape[I2], I2 * w_up.shape[I2])
        norm_factor = 1.0 / (inputs.size)
        stage = lax.axis_index('stage')
        tp = lax.axis_index('tp')
        x_pos, core = stage // I2, stage % I2
        home = jnp.where(x_pos == I0, tp, I3 - tp)
        is_l = stage == home
        own = (w_qkv[I0], w_out[I0], w_up[I0], w_down[I0])
        own_gains = jnp.concatenate([gain_attn, gain_mlp]).astype(F32)
        rows_of = (own[I0].transpose(I1, I2, I3, I0).reshape(-I1, width), own[I1].reshape(-I1, width), own[I2], own[I3])

        results = step_phase(dims, inputs, targets, rows_of, own_gains)
        dx, oh_same, oh_other, oa_same, oa_other, od_same, od_other, og_same, og_other, dg_same, dg_other, loss_all = results[5:17]

        flat = lambda *rows: [r.reshape(-I1, width) for r in rows]
        d_up, d_down = owner_mlp(flat(oh_same, oh_other), flat(og_same, og_other), own_gains[I1:], own[I2], own[I3])
        w_rows = own[I0].transpose(I1, I2, I3, I0)
        d_qkv, d_out = owner_attn(seq_len, inputs, flat(oa_same, oa_other), flat(od_same, od_other), own_gains[:I1], w_rows, own[I1])
        weight_grads = (d_qkv.transpose(I3, I0, I1, I2), d_out, d_up, d_down)
        mine = jnp.sum(dg_same + dg_other, I1)
        loss = jnp.sum(loss_all) * (0.5 * norm_factor)

        dx = dx[:, None]
        at_b = move(dx, [(I0, I4), (I1, 5)])
        at_d = move(dx, [(I0, I2), (I1, I3)])
        at_c = move(at_b, [(I4, I6), (5, 7)])
        dx = jnp.where(home == I0, dx, jnp.where(home == I1, at_b, jnp.where(home == I2, at_c, at_d)))
        other = move(dx, CORE_SWAP)
        d_inputs = jnp.concatenate([jnp.where(core == I0, dx, other), jnp.where(core == I0, other, dx)], I1)
        return (loss.reshape(I1), d_inputs) + tuple(g[None] for g in weight_grads) + (mine[I0][None], mine[I1][None])

    return jax.shard_map(device_fn, mesh=mesh, in_specs=(act_spec, act_spec) + weight_specs, out_specs=(P('rep'), act_spec) + weight_specs, check_vma=False)
```

time: 1660 us -> 1650 us (level)
  matrix products: 383 us -> 0 us
  Pallas kernels: 1100 us -> 1480 us
  waiting for transfers between devices: 36 us -> 114 us
  other arithmetic: 85.8 us -> 28.2 us
    dot_general x13 -> x0, matrix products: 383 us -> none  [the longest x11 319 us: dot(): return jnp.einsum(eq, a, b, preferred_element_type=F32)]
    pallas_call x0 -> x2, Pallas kernels: none -> 381 us  [the longest x1 208 us: owner_attn(): pl.pallas_call(functools.partial(owner_attn_kernel, seq), grid=(heads //...]
    ppermute x4, waiting for transfers between devices: 36 us -> 114 us  [move(): return lax.ppermute(value, AX, perm)]
    sub x1 -> x0, other arithmetic: 25.2 us -> none  [attn_scores(): return jax.nn.softmax(jnp.where(k_pos <= q_pos, scores, -1e+30), axis=-1)]
  transfers between devices with their start and end apart: 4 -> 4, of which waited for: 1 -> 1; matrix products, arithmetic and copies ran while one was open for 28% -> 0% of each run, Pallas kernels for 0% -> 23%
where the time goes in v4:
time: 1650 us
  Pallas kernels  1480 us (90%)
  waiting for transfers between devices  114 us (7%)
  other arithmetic  28.2 us (2%)
    pallas_call x1, Pallas kernels, step_phase(): pl.pallas_call(functools.partial(step_kernel, dims), out_shape=tuple(out_...  1100 us
    pallas_call x1, Pallas kernels, owner_attn(): pl.pallas_call(functools.partial(owner_attn_kernel, seq), grid=(heads //...  208 us
    pallas_call x1, Pallas kernels, owner_mlp(): pl.pallas_call(owner_mlp_kernel, grid=(ffn // SUB,), out_shape=(jax.Shape...  173 us
    ppermute x4, waiting for transfers between devices, move(): return lax.ppermute(value, AX, perm)  114 us
  transfers between devices with their start and end apart: 4, of which 1 were waited for; matrix products, arithmetic and copies ran while one was open for 0% of the time, Pallas kernels for 23%

profile of v4, /device:TPU:5, one launch (start us, length us, event | category | flops | bytes accessed | tf_op | source)
XLA Modules:
  0.0 1645.2 jit_solution(6585132895420625396)
XLA Ops:
  0.6 1.3 maximum_convert_fusion.own_gains
  2.0 1100.0 %step_phase.1 = (bf16[8,192,1536]{2,1,0:T(8,128)(2,1)}, bf16[8,192,1536]{2,1,0:T(8,128)(2,1)}, bf16[8,192,1536]{2,1,0:T(8,128)(2,1)}, bf16[8,192,6144]{2,1,0:T(8...) custom-call(bf16[8,2,192,1536]{3,2,1,0:T(8,128)(2,1)} %x_ref.3, ...), custom_call_target="tpu_custom_call" | custom-call | tf_op jit(solution)/shard_map/step_phase/pallas_call | solution.py:815
  1102.0 1.3 collective-permute-start
  1103.3 2.8 collective-permute-start.2
  1106.1 1.4 fusion.1
  1107.5 114.4 %collective-permute-done = bf16[8,1,192,1536]{3,2,0,1:T(8,128)(2,1)} collective-permute-done((bf16[8,1,192,1536]{3,2,0,1:T(8,128)(2,1)}, bf16[8,1,192,1536]{3,2,0,1:T(8,128)(2,1)}, u32[]{:S(2)}, u32[]{:S(2)}) %collective-permute-start) | collective-permute-done | bytes 4718624 | tf_op jit(solution)/shard_map/ppermute | solution.py:33
  1221.9 3.5 collective-permute-start.1
  1225.4 172.8 %owner_mlp.1 = (f32[1536,3072]{1,0:T(8,128)}, f32[3072,1536]{1,0:T(8,128)}) custom-call(bf16[1536,1536]{1,0:T(8,128)(2,1)} %bitcast.40, bf16[1536,1536]{1,0:T(8,128)(2,1)} %bitcast.41, bf16[1536,1536]{1,0:T(8,128)(2,1)} %bitcast.42, bf16[1536,1536]{1,0:T(8,128)(2,1)} %bitcast.43, f32[1,1536]{1,0:T(1,128)} %get-tuple-element.52.gain, ...), custom_call_target="tpu_custom_call" | custom-call | flops 115964116992 | bytes 56623104 | tf_op jit(solution)/shard_map/owner_mlp/pallas_call | solution.py:883
  1398.2 1.3 reduce_sum.18
  1400.2 1.0 add_reduce_fusion
  1401.2 0.6 fusion
  1401.8 0.0 collective-permute-done.2
  1401.8 0.0 collective-permute-done.1
  1401.8 8.1 select_select_fusion
  1409.9 1.3 collective-permute-start.3
  1411.2 208.2 %owner_attn.1 = (f32[3,8,96,1536]{3,2,1,0:T(8,128)}, f32[8,96,1536]{2,1,0:T(8,128)}) custom-call(bf16[8,2,192,1536]{3,2,1,0:T(8,128)(2,1)} %x_ref.3, bf16[1536,1536]{1,0:T(8,128)(2,1)} %bitcast.36, bf16[1536,1536]{1,0:T(8,128)(2,1)} %bitcast.37, bf16[1536,1536]{1,0:T(8,128)(2,1)} %bitcast.38, bf16[1536,1536]{1,0:T(8,128)(2,1)} %bitcast.39, ...), custom_call_target="tpu_custom_call" | custom-call | flops 65229815808 | bytes 37748736 | tf_op jit(solution)/shard_map/owner_attn/pallas_call | solution.py:971
  1619.4 0.0 collective-permute-done.3
  1619.4 8.2 broadcast_select_fusion.1
  1627.6 8.3 pad_maximum_fusion
  1635.8 8.3 copy.16
Async XLA Ops:
  1102.0 119.9 %collective-permute-start = (bf16[8,1,192,1536]{3,2,0,1:T(8,128)(2,1)}, bf16[8,1,192,1536]{3,2,0,1:T(8,128)(2,1)}, u32[]{:S(2)}, u32[]{:S(2)}) collective-permute-start(bf16[8,1,192,1536]{3,2,0,1:T(8,128)(2,1)} %bitcast.32), channel_id=1, source_target_pairs={{0,4},{1,5}} | collective-permute-start | bytes 14155784 | tf_op jit(solution)/shard_map/ppermute | solution.py:33
  1103.3 298.5 %collective-permute-start.2 = (bf16[8,1,192,1536]{3,2,0,1:T(8,128)(2,1)}, bf16[8,1,192,1536]{3,2,0,1:T(8,128)(2,1)}, u32[]{:S(2)}, u32[]{:S(2)}) collective-permute-start(bf16[8,1,192,1536]{3,2,0,1:T(8,128)(2,1)} %bitcast.33), channel_id=1, source_target_pairs={{0,2},{1,3}} | collective-permute-start | bytes 14155784 | tf_op jit(solution)/shard_map/ppermute | solution.py:33
  1221.9 179.9 %collective-permute-start.1 = (bf16[8,1,192,1536]{3,2,0,1:T(8,128)(2,1)}, bf16[8,1,192,1536]{3,2,0,1:T(8,128)(2,1)}, u32[]{:S(2)}, u32[]{:S(2)}) collective-permute-start(bf16[8,1,192,1536]{3,2,0,1:T(8,128)(2,1)} %collective-permute-done), channel_id=1, source_target_pairs={{4,6},{5,7}} | collective-permute-start | bytes 14155784 | tf_op jit(solution)/shard_map/ppermute | solution.py:33
  1409.9 209.5 %collective-permute-start.3 = (bf16[8,1,192,1536]{3,2,0,1:T(8,128)(2,1)}, bf16[8,1,192,1536]{3,2,0,1:T(8,128)(2,1)}, u32[]{:S(2)}, u32[]{:S(2)}) collective-permute-start(bf16[8,1,192,1536]{3,2,0,1:T(8,128)(2,1)} %select_select_fusion), channel_id=1, source_target_pairs={{0,1},{1,0},{2,3},{3,2},{4,5},{5,4},{6,7},{7,6}} | collective-permute-start | bytes 14155784 | tf_op jit(solution)/shard_map/ppermute | solution.py:33

commit v5 on v4

--- a/solution.py
+++ b/solution.py
@@ -8,15 +8,11 @@
 from jax.sharding import PartitionSpec as P
 
 NORM_EPS = 1e-5
-AX = ('tp', 'stage')
 BF = jnp.bfloat16
 F32 = jnp.float32
 MESH = pl.DeviceIdType.MESH
 ANY = pl.ANY
 
-R_SWAP = [(1, 4), (4, 1), (2, 7), (7, 2)]
-CORE_SWAP = [(0, 1), (1, 0), (2, 3), (3, 2), (4, 5), (5, 4), (6, 7), (7, 6)]
-L_TO_R = [(0, 1), (5, 4), (6, 7), (3, 2)]
 
 GELU_A = 0.7978845608028654
 GELU_B = 0.044715
@@ -27,10 +23,6 @@
 KDEPTH = 2
 HEAD_PAD = 128
 VMEM_LIMIT = 67043328
-
-
-def move(value, perm):
-    return lax.ppermute(value, AX, perm)
 
 
 def mm(a, b):
@@ -708,19 +700,21 @@
         @pl.when((place.home == I2) & is_r)
         def _():
             remote(a_s.at[m], oa_other.at[m], bulk.at[I8], ao_sem, place.across_other).start()
+        far_grad(m, (place.home == I1) & (i % I2 == I0))
         return carry
 
+    def far_grad(m, condition):
+        @pl.when(condition & place.is_l)
+        def _():
+            remote(gbuf.at[m], og_same.at[m], bulk.at[I4], gs_sem, place.across).start()
+
+        @pl.when(condition & is_r)
+        def _():
+            remote(gbuf.at[m], og_other.at[m], bulk.at[I4], go_sem, place.across_other).start()
+
     lax.fori_loop(I0, micro, backward_tick, I0)
-
-    @pl.when((place.home == I1) & place.is_l)
-    def _():
-        for m in reversed(range(micro)):
-            remote(gbuf.at[m], og_same.at[m], bulk.at[I4], gs_sem, place.across).start()
-
-    @pl.when((place.home == I1) & is_r)
-    def _():
-        for m in reversed(range(micro)):
-            remote(gbuf.at[m], og_other.at[m], bulk.at[I4], go_sem, place.across_other).start()
+    for i in range(I1, micro, I2):
+        far_grad(micro - I1 - i, place.home == I1)
 
     @pl.when(place.is_l)
     def _():
@@ -840,9 +834,85 @@
             dst[c:c + wide, r:r + high] = src[r:r + high, c:c + wide].T
 
 
-def owner_mlp_kernel(hs, ho, gs, go, gain, wu, wd, dwu, dwd, n2, n2t, grad, wdt, z, zt, dup, sem):
+def spread_dx(step, last, dx, d_in, here_sem, parent_sem, sib_sem, send_sems):
+    place = Place()
+    micro = dx.shape[I0]
+    below = place.at(place.tp, (place.stage + I2) % I4)
+    barrier = pltpu.get_barrier_semaphore()
+    is_a, is_b = place.home == I0, place.home == I1
+    is_leaf = place.home > I1
+
+    def block(m):
+        return d_in.at[m, place.core]
+
+    def hand(m, src, index, there):
+        remote(src, block(m), send_sems.at[index], sib_sem if index == I0 else parent_sem.at[m], there).start()
+
+    def arrived(m):
+        remote(block(m), block(m), send_sems.at[I0], parent_sem.at[m], place.sibling).wait_recv()
+
+    @pl.when(step == I0)
+    def _():
+        def tell(there):
+            pl.semaphore_signal(barrier, inc=I1, device_id=there, device_id_type=MESH)
+        tell(place.sibling)
+
+        @pl.when(is_b)
+        def _():
+            tell(place.across)
+
+        @pl.when(is_leaf)
+        def _():
+            tell(below)
+
+    @pl.when((step == I1) & is_a)
+    def _():
+        pl.semaphore_wait(barrier, I3)
+        for m in reversed(range(micro)):
+            hand(m, dx.at[m], I1, place.across)
+            hand(m, dx.at[m], I2, below)
+            hand(m, dx.at[m], I0, place.sibling)
+            pltpu.make_async_copy(dx.at[m], block(m), here_sem).start()
+
+    @pl.when((step == I2) & is_b)
+    def _():
+        pl.semaphore_wait(barrier, I2)
+
+    @pl.when((step > I2) & (step < I3 + micro) & is_b)
+    def _():
+        m = micro + I2 - step
+        arrived(m)
+        hand(m, block(m), I2, below)
+        hand(m, block(m), I0, place.sibling)
+
+    @pl.when((step == last) & is_leaf)
+    def _():
+        pl.semaphore_wait(barrier, I1)
+        for m in reversed(range(micro)):
+            arrived(m)
+            hand(m, block(m), I0, place.sibling)
+
+    @pl.when(step == last)
+    def _():
+        def sent(index):
+            remote(dx, dx, send_sems.at[index], sib_sem, place.sibling).wait_send()
+        sent(I0)
+
+        @pl.when(is_a)
+        def _():
+            sent(I1)
+            pltpu.make_async_copy(dx, dx, here_sem).wait()
+
+        @pl.when(jnp.logical_not(is_leaf))
+        def _():
+            sent(I2)
+        remote(dx, dx, send_sems.at[I0], sib_sem, place.sibling).wait_recv()
+
+
+def owner_mlp_kernel(dx, hs, ho, gs, go, gain, wu, wd, dwu, dwd, d_in, n2, n2t, grad, wdt, z, zt, dup, sem, here_sem, parent_sem, sib_sem, send_sems):
     tokens, width = n2.shape
     part = tokens // I2
+    spread_dx(pl.program_id(I0), pl.num_programs(I0) - I1, dx, d_in, here_sem, parent_sem, sib_sem, send_sems)
 
     @pl.when(pl.program_id(I0) == I0)
     def _():
@@ -872,10 +942,10 @@
         dwd[:, c:c + SUB] = mm(zt[...], grad[:, c:c + SUB])
 
 
-def owner_mlp(h_rows, g_rows, gain, w_up, w_down):
+def owner_mlp(dx, h_rows, g_rows, gain, w_up, w_down):
     width, ffn = w_up.shape
-    part = h_rows[I0].shape[I0]
-    vmem = pltpu.VMEM
+    part, micro = h_rows[I0].shape[I0], dx.shape[I0]
+    vmem, dma = pltpu.VMEM, pltpu.SemaphoreType.DMA
     any_spec = pl.BlockSpec(memory_space=ANY)
     up_spec = pl.BlockSpec((width, SUB), lambda i: (I0, i))
     down_spec = pl.BlockSpec((SUB, width), lambda i: (i, I0))
@@ -883,14 +953,14 @@
     return pl.pallas_call(
         owner_mlp_kernel,
         grid=(ffn // SUB,),
-        out_shape=(jax.ShapeDtypeStruct(w_up.shape, F32), jax.ShapeDtypeStruct(w_down.shape, F32)),
-        in_specs=[any_spec] * I4 + [pl.BlockSpec(memory_space=vmem), up_spec, down_spec],
-        out_specs=(up_spec, down_spec),
-        scratch_shapes=[rows(width), vmem((width, I2 * part), BF), rows(width), vmem((width, SUB), BF), rows(SUB), vmem((SUB, I2 * part), BF), rows(SUB), pltpu.SemaphoreType.DMA((I4,))],
-        compiler_params=pltpu.CompilerParams(vmem_limit_bytes=VMEM_LIMIT),
+        out_shape=(jax.ShapeDtypeStruct(w_up.shape, F32), jax.ShapeDtypeStruct(w_down.shape, F32), jax.ShapeDtypeStruct((micro, I2) + dx.shape[I1:], BF)),
+        in_specs=[any_spec] * 5 + [pl.BlockSpec(memory_space=vmem), up_spec, down_spec],
+        out_specs=(up_spec, down_spec, any_spec),
+        scratch_shapes=[rows(width), vmem((width, I2 * part), BF), rows(width), vmem((width, SUB), BF), rows(SUB), vmem((SUB, I2 * part), BF), rows(SUB), dma((I4,)), dma(()), dma((micro,)), dma(()), dma((I3,))],
+        compiler_params=pltpu.CompilerParams(collective_id=I1, has_side_effects=True, vmem_limit_bytes=VMEM_LIMIT),
         cost_estimate=pl.CostEstimate(flops=16 * part * width * ffn, bytes_accessed=12 * width * ffn, transcendentals=I2 * part * ffn),
         name='owner_mlp',
-    )(*h_rows, *g_rows, gain, w_up, w_down)
+    )(dx, *h_rows, *g_rows, gain, w_up, w_down)
 
 
 def owner_attn_kernel(seq, x_ref, rs, ro, ds, do, gain, wq, wo, dwq, dwo, n1, dmid, wpad, wqt, wot, qkv, dctx, dqkv, ctx, dqkvt, ctxt, sem):
@@ -1000,11 +1070,6 @@
         micro_count, _, seq_len, width = inputs.shape
         dims = (micro_count, seq_len, width, I2 * w_out.shape[I1], w_out.shape[I2], I2 * w_up.shape[I2])
         norm_factor = 1.0 / (inputs.size)
-        stage = lax.axis_index('stage')
-        tp = lax.axis_index('tp')
-        x_pos, core = stage // I2, stage % I2
-        home = jnp.where(x_pos == I0, tp, I3 - tp)
-        is_l = stage == home
         own = (w_qkv[I0], w_out[I0], w_up[I0], w_down[I0])
         own_gains = jnp.concatenate([gain_attn, gain_mlp]).astype(F32)
         rows_of = (own[I0].transpose(I1, I2, I3, I0).reshape(-I1, width), own[I1].reshape(-I1, width), own[I2], own[I3])
@@ -1013,20 +1078,13 @@
         dx, oh_same, oh_other, oa_same, oa_other, od_same, od_other, og_same, og_other, dg_same, dg_other, loss_all = results[5:17]
 
         flat = lambda *rows: [r.reshape(-I1, width) for r in rows]
-        d_up, d_down = owner_mlp(flat(oh_same, oh_other), flat(og_same, og_other), own_gains[I1:], own[I2], own[I3])
         w_rows = own[I0].transpose(I1, I2, I3, I0)
         d_qkv, d_out = owner_attn(seq_len, inputs, flat(oa_same, oa_other), flat(od_same, od_other), own_gains[:I1], w_rows, own[I1])
+        d_up, d_down, d_inputs = owner_mlp(dx, flat(oh_same, oh_other), flat(og_same, og_other), own_gains[I1:], own[I2], own[I3])
         weight_grads = (d_qkv.transpose(I3, I0, I1, I2), d_out, d_up, d_down)
         mine = jnp.sum(dg_same + dg_other, I1)
         loss = jnp.sum(loss_all) * (0.5 * norm_factor)
 
-        dx = dx[:, None]
-        at_b = move(dx, [(I0, I4), (I1, 5)])
-        at_d = move(dx, [(I0, I2), (I1, I3)])
-        at_c = move(at_b, [(I4, I6), (5, 7)])
-        dx = jnp.where(home == I0, dx, jnp.where(home == I1, at_b, jnp.where(home == I2, at_c, at_d)))
-        other = move(dx, CORE_SWAP)
-        d_inputs = jnp.concatenate([jnp.where(core == I0, dx, other), jnp.where(core == I0, other, dx)], I1)
         return (loss.reshape(I1), d_inputs) + tuple(g[None] for g in weight_grads) + (mine[I0][None], mine[I1][None])
 
     return jax.shard_map(device_fn, mesh=mesh, in_specs=(act_spec, act_spec) + weight_specs, out_specs=(P('rep'), act_spec) + weight_specs, check_vma=False)

time: 1650 us -> 1520 us (0.921)
  the two profiles are of different devices: /device:TPU:5 before, /device:TPU:1 now
where the time goes in v5:
time: 1520 us
  Pallas kernels  1470 us (97%)
  local copies, waits for them, and re-layouts  39.6 us (3%)
    pallas_call x1, Pallas kernels, step_phase(): pl.pallas_call(functools.partial(step_kernel, dims), out_shape=tuple(out_...  1070 us
    pallas_call x1, Pallas kernels, owner_attn(): pl.pallas_call(functools.partial(owner_attn_kernel, seq), grid=(heads //...  208 us
    pallas_call x1, Pallas kernels, owner_mlp(): pl.pallas_call(owner_mlp_kernel, grid=(ffn // SUB,), out_shape=(jax.Shape...  194 us
    unnamed x3, local copies, waits for them, and re-layouts  37.6 us

profile of v5, /device:TPU:1, one launch (start us, length us, event | category | flops | bytes accessed | tf_op | source)
XLA Modules:
  0.0 1519.3 jit_solution(16283613441606353269)
XLA Ops:
  0.6 1.3 maximum_convert_fusion.own_gains
  2.0 1071.7 %step_phase.1 = (bf16[8,192,1536]{2,1,0:T(8,128)(2,1)}, bf16[8,192,1536]{2,1,0:T(8,128)(2,1)}, bf16[8,192,1536]{2,1,0:T(8,128)(2,1)}, bf16[8,192,6144]{2,1,0:T(8...) custom-call(bf16[8,2,192,1536]{3,2,1,0:T(8,128)(2,1)} %x_ref.3, ...), custom_call_target="tpu_custom_call" | custom-call | tf_op jit(solution)/shard_map/step_phase/pallas_call | solution.py:809
  1073.7 1.4 fusion.1
  1075.1 193.6 %owner_mlp.1 = (f32[1536,3072]{1,0:T(8,128)}, f32[3072,1536]{1,0:T(8,128)}, bf16[8,2,192,1536]{3,2,1,0:T(8,128)(2,1)}) custom-call(bf16[8,192,1536]{2,1,0:T(8,128)(2,1)} %get-tuple-element.26.dx, bf16[1536,1536]{1,0:T(8,128)(2,1)} %bitcast.38, bf16[1536,1536]{1,0:T(8,128)(2,1)} %bitcast.39, bf16[1536,1536]{1,0:T(8,128)(2,1)} %bitcast.40, ...), custom_call_target="tpu_custom_call" | custom-call | flops 115964116992 | bytes 56623104 | tf_op jit(solution)/shard_map/owner_mlp/pallas_call | solution.py:953
  1268.6 208.4 %owner_attn.1 = (f32[3,8,96,1536]{3,2,1,0:T(8,128)}, f32[8,96,1536]{2,1,0:T(8,128)}) custom-call(bf16[8,2,192,1536]{3,2,1,0:T(8,128)(2,1)} %x_ref.3, bf16[1536,1536]{1,0:T(8,128)(2,1)} %bitcast.34, bf16[1536,1536]{1,0:T(8,128)(2,1)} %bitcast.35, bf16[1536,1536]{1,0:T(8,128)(2,1)} %bitcast.36, bf16[1536,1536]{1,0:T(8,128)(2,1)} %bitcast.37, ...), custom_call_target="tpu_custom_call" | custom-call | flops 65229815808 | bytes 37748736 | tf_op jit(solution)/shard_map/owner_attn/pallas_call | solution.py:1041
  1477.0 1.0 add_reduce_fusion
  1478.0 0.6 fusion
  1478.6 1.3 reduce_sum.18
  1480.6 8.3 copy.19
  1488.8 14.8 copy.20
  1503.6 14.6 copy.21

commit v6 on v5

--- a/solution.py
+++ b/solution.py
@@ -18,8 +18,10 @@
 GELU_B = 0.044715
 I0, I1, I2, I3, I4, I6, I8 = 0, 1, 2, 3, 4, 6, 8
 CHUNK = 1024
+BLOCK = 384
 SUB = 256
-DEPTH = 3
+DEPTH = 6
+BACK_DEPTH = 4
 KDEPTH = 2
 HEAD_PAD = 128
 VMEM_LIMIT = 67043328
@@ -118,32 +120,73 @@
     return gate + hidden * (1.0 - gate) * (2.0 * GELU_A + (6.0 * GELU_A * GELU_B) * u2)
 
 
-def causal_probs(q, k, scale):
-    s = mm_nt(q, k) * scale
-    q_pos = lax.broadcasted_iota(jnp.int32, s.shape, I0)
-    k_pos = lax.broadcasted_iota(jnp.int32, s.shape, I1)
-    s = jnp.where(k_pos <= q_pos, s, -1e30)
-    e = jnp.exp(s - jnp.max(s, axis=-I1, keepdims=True))
-    return e * (1.0 / jnp.sum(e, axis=-I1, keepdims=True))
-
-
-def attention_backward(q, k, v, d_ctx, scale):
-    probs = causal_probs(q, k, scale)
-    probs_bf = probs.astype(BF)
-    dp = mm_nt(d_ctx, v).astype(BF).astype(F32)
-    ds = probs * (dp - jnp.sum(dp * probs, axis=-I1, keepdims=True)) * scale
-    dv = mm_tn(probs_bf, d_ctx)
-    hi = ds.astype(BF)
-    rest = ds - hi.astype(F32)
-    lo = rest.astype(BF)
-    tail = (rest - lo.astype(F32)).astype(BF)
-    dq = mm(hi, k) + (mm(lo, k) + mm(tail, k))
-    dk = mm_tn(hi, q) + (mm_tn(lo, q) + mm_tn(tail, q))
-    return probs_bf, dq.astype(BF), dk.astype(BF), dv.astype(BF)
+def row_parts(heads, cut=128):
+    return [(*(x[low:high] for x in queries), *(x[:high] for x in keys), low)
+            for queries, keys in heads for low, high in ((I0, cut), (cut, queries[I0].shape[I0]))]
+
+
+def softmax_parts(scores, starts):
+    masked = []
+    for s, start in zip(scores, starts):
+        q_pos = lax.broadcasted_iota(jnp.int32, s.shape, I0) + start
+        k_pos = lax.broadcasted_iota(jnp.int32, s.shape, I1)
+        masked.append(jnp.where(k_pos <= q_pos, s, -1e30))
+    tops = [jnp.max(s, axis=-I1, keepdims=True) for s in masked]
+    powers = [jnp.exp(s - top) for s, top in zip(masked, tops)]
+    scales = [1.0 / jnp.sum(e, axis=-I1, keepdims=True) for e in powers]
+    return [e * r for e, r in zip(powers, scales)]
+
+
+def join_keys(top, low, cut=128):
+    return jnp.concatenate([top + low[:cut], low[cut:]], I0).astype(BF)
+
+
+def attention_forward(heads, scale):
+    units = row_parts([((q,), (k, v)) for q, k, v in heads])
+    probs = softmax_parts([mm_nt(q, k) * scale for q, k, _, _ in units], [u[-I1] for u in units])
+    parts = [mm(p.astype(BF), u[I2]) for p, u in zip(probs, units)]
+    return [jnp.concatenate([a, b], I0).astype(BF) for a, b in zip(parts[I0::I2], parts[I1::I2])]
+
+
+def attention_backward(heads, scale):
+    units = row_parts([((q, dc), (k, v)) for q, k, v, dc in heads])
+    scores = [mm_nt(q, k) * scale for q, _, k, _, _ in units]
+    dps = [mm_nt(dc, v) for _, dc, _, v, _ in units]
+    probs = softmax_parts(scores, [u[-I1] for u in units])
+    dps = [dp.astype(BF).astype(F32) for dp in dps]
+    deltas = [jnp.sum(dp * p, axis=-I1, keepdims=True) for dp, p in zip(dps, probs)]
+    dvs = [mm_tn(p.astype(BF), u[I1]) for p, u in zip(probs, units)]
+    dss = [p * (dp - delta) * scale for p, dp, delta in zip(probs, dps, deltas)]
+    terms = []
+    for ds in dss:
+        hi = ds.astype(BF)
+        rest = ds - hi.astype(F32)
+        lo = rest.astype(BF)
+        terms.append((hi, lo, (rest - lo.astype(F32)).astype(BF)))
+    dqs = [mm(hi, u[I2]) + (mm(lo, u[I2]) + mm(tail, u[I2])) for (hi, lo, tail), u in zip(terms, units)]
+    dks = [mm_tn(hi, u[I0]) + (mm_tn(lo, u[I0]) + mm_tn(tail, u[I0])) for (hi, lo, tail), u in zip(terms, units)]
+    return [(jnp.concatenate([dqs[i], dqs[i + I1]], I0).astype(BF), join_keys(dks[i], dks[i + I1]), join_keys(dvs[i], dvs[i + I1]))
+            for i in range(I0, len(units), I2)]
 
 
 def lanes(offset, size):
     return pl.ds(pl.multiple_of(offset, 128), size)
+
+
+def load_resident(buf, sem, halves):
+    for c in range(I6):
+        for condition, ref in halves[c // I3]:
+            copy = pltpu.make_async_copy(ref.at[(c % I3) * CHUNK:(c % I3 + I1) * CHUNK, :], buf.at[c], sem.at[c])
+            if condition is None:
+                copy.start()
+            else:
+                pl.when(condition)(copy.start)
+
+
+def load_heads(ref, index, dst, sem):
+    for r in range(I8):
+        rows = pl.ds(pl.multiple_of(index * 768 + r * 96, 96), 96)
+        pltpu.make_async_copy(ref.at[rows, :], dst.at[r * 128:r * 128 + 96, :], sem).start()
 
 
 class Stream:
@@ -156,9 +199,7 @@
             where = pl.ds(pl.multiple_of(index * CHUNK, CHUNK), CHUNK)
             pltpu.make_async_copy(ref.at[:, where], self.buf.at[slot], self.sem.at[slot]).start()
             return
-        for r in range(I8):
-            rows = pl.ds(pl.multiple_of(index * 768 + r * 96, 96), 96)
-            pltpu.make_async_copy(ref.at[rows, :], self.buf.at[slot, r * 128:r * 128 + 96, :], self.sem.at[slot]).start()
+        load_heads(ref, index, self.buf.at[slot], self.sem.at[slot])
 
     def start(self, seq):
         @pl.when(seq < self.total)
@@ -299,19 +340,23 @@
             remote(far[i], far[i], d_send.at[i], far_sem.at[I0], place.sibling).wait_send()
 
 
-def step_kernel(dims, x_ref, y_ref, wq, wo, wu, wd, own_gains,
-                a_s, h_s, m_s, qkv_s, u_s, dx_s, oh_same, oh_other, oa_same, oa_other, od_same, od_other, og_same, og_other,
-                dg_same, dg_other, loss_all, nq, no, nu, nd, fq, fo, fu, fd, tq0, to0, tu0, td0, tq1, to1, tu1, td1,
-                abuf, gbuf, hbuf, obuf, nbuf, ybuf, qkvbuf, ubuf, habuf, zbuf, ctxbuf, dqkvbuf, acc, accg, lossbuf, losstile, gains, wres, wn, wk,
-                send_sem, y_send, d_send, near_sem, far_sem, t_load, t_store,
-                act_sem, grad_sem, hop_f, hop_b, keep_sem, back_sem, save_sem, stream_n, stream_k, res_sem, big_sem, load_sem, y_sem,
-                os_sem, oo_sem, as_sem, ao_sem, ds_sem, do_sem, gs_sem, go_sem, bulk, gain_sem, tiny, loss_send):
+def near_choices(place, own, near):
+    return [(place.is_l, own), (jnp.logical_not(place.is_l), near)]
+
+
+def forward_kernel(dims, x_ref, y_ref, wq, wo, wu, wd, own_gains,
+                   a_s, h_s, qkv_s, u_s, g_s, oh_same, oh_other, oa_same, oa_other, loss_all, home_gains,
+                   nq, no, nu, nd, fq, fo, fu, fd, tq0, to0, tu0, td0, tq1, to1, tu1, td1,
+                   abuf, hbuf, obuf, nbuf, ybuf, sbuf, qkvbuf, ubuf, zbuf, ctxbuf, acc, lossbuf, losstile, gains, wres, wores, wn,
+                   send_sem, y_send, d_send, near_sem, far_sem, t_load, t_store,
+                   act_sem, hop_f, keep_sem, save_sem, stream_n, res_sem, out_sem, big_sem, y_sem, s_sem,
+                   os_sem, oo_sem, as_sem, ao_sem, bulk, gain_sem, tiny, loss_send):
     micro, seq, width, heads, head_dim, ffn = dims
     place = Place()
     is_first, is_last = place.home == I0, place.home == I3
     home02 = (place.home == I0) | (place.home == I2)
-    home13 = jnp.logical_not(home02)
     is_r = jnp.logical_not(place.is_l)
+    takes_x = (place.home == I1) & is_r
     half = heads // I2 * HEAD_PAD
     scale = head_dim ** -0.5
     norm_factor = 1.0 / (micro * I2 * seq * width)
@@ -328,43 +373,35 @@
     def _():
         for m in range(micro):
             pltpu.make_async_copy(x_ref.at[m, place.core], abuf.at[m], act_sem.at[m]).start()
-    weight_phase(place, is_r, own, near, far, turned, wn, wk, send_sem, y_send, d_send, near_sem, far_sem, t_load, t_store)
+    weight_phase(place, is_r, own, near, far, turned, wn, wores, send_sem, y_send, d_send, near_sem, far_sem, t_load, t_store)
     pltpu.make_async_copy(own_gains, gains, gain_sem.at[I0]).wait()
+    pltpu.make_async_copy(gains, home_gains, gain_sem.at[I0]).start()
 
     @pl.when(place.is_l)
     def _():
         remote(own_gains, gains, gain_sem.at[I1], gain_sem.at[I0], place.sibling).wait_send()
 
     def near_of(i):
-        return [(place.is_l, own[i]), (is_r, near[i])]
-
-    def resident(choices_of_half, start):
-        for c in range(I6):
-            for condition, ref in choices_of_half[c // I3]:
-                copy = pltpu.make_async_copy(ref.at[(c % I3) * CHUNK:(c % I3 + I1) * CHUNK, :], wres.at[c], res_sem.at[c])
-                if condition is None:
-                    copy.start()
-                else:
-                    pl.when(condition)(copy.start)
-
-    def resident_ready(j):
-        pltpu.make_async_copy(wd.at[I0:CHUNK, :], wres.at[j], res_sem.at[j]).wait()
+        return near_choices(place, own[i], near[i])
 
     def saved(dst, index):
         return pltpu.make_async_copy(hbuf, dst, save_sem.at[index])
 
     sn = Stream(wn, stream_n, DEPTH, [([(None, tq0)], I3), ([(None, tq1)], I3), (near_of(I2), I3), ([(None, fu)], I3)], micro * 12, False)
-    sk = Stream(wk, stream_k, KDEPTH, [(near_of(I1), I1), ([(None, fo)], I1)], micro * I2, True)
+    for c, choices in enumerate((near_of(I1), [(None, fo)])):
+        for condition, ref in choices:
+            def go(ref=ref, c=c):
+                load_heads(ref, I0, wores.at[c], out_sem.at[c])
+            go() if condition is None else pl.when(condition)(go)
     sn.prime()
-    sk.prime()
-    resident((near_of(I3), [(None, fd)]), True)
+    load_resident(wres, res_sem, (near_of(I3), [(None, fd)]))
     lossbuf[...] = jnp.zeros_like(lossbuf)
 
     def qkv_out(m):
-        return pltpu.make_async_copy(qkvbuf.at[I0], qkv_s.at[m], big_sem.at[I0])
+        return pltpu.make_async_copy(qkvbuf, qkv_s.at[m], big_sem.at[I0])
 
     def up_out(m):
-        return pltpu.make_async_copy(ubuf.at[I0], u_s.at[m], big_sem.at[I1])
+        return pltpu.make_async_copy(ubuf, u_s.at[m], big_sem.at[I1])
 
     def act_out(m):
         return pltpu.make_async_copy(abuf.at[m], a_s.at[m], save_sem.at[I2])
@@ -388,6 +425,12 @@
         @pl.when(condition & is_r)
         def _():
             own_copy().start() if start else own_copy().wait()
+
+    def x_out(m):
+        return pltpu.make_async_copy(ybuf, oa_same.at[m], y_sem), pltpu.make_async_copy(sbuf, oa_other.at[m], s_sem)
+
+    def seed_out(m):
+        return pltpu.make_async_copy(sbuf, g_s.at[m], s_sem)
 
     def forward_tick(m, carry):
         act, mid, out = abuf.at[m], hbuf, obuf.at[m % I2]
@@ -401,6 +444,15 @@
         @pl.when(is_last)
         def _():
             pltpu.make_async_copy(y_ref.at[m, place.core], ybuf, y_sem).start()
+
+        @pl.when(takes_x)
+        def _():
+            @pl.when(m > I0)
+            def _():
+                for copy in x_out(m):
+                    copy.wait()
+            for core, buf, sem in ((place.core, ybuf, y_sem), (I1 - place.core, sbuf, s_sem)):
+                pltpu.make_async_copy(x_ref.at[m, core], buf, sem).start()
         norm_rows(act, gains[I0:I1, :], nbuf, seq)
 
         @pl.when(m > I0)
@@ -410,7 +462,7 @@
         def qkv_step(j, c):
             w = sn.wait(m * 12 + j)
             for n in range(I0, CHUNK, SUB):
-                qkvbuf[I0, :, lanes(j * CHUNK + n, SUB)] = mm(nbuf[...], w[:, n:n + SUB]).astype(BF)
+                qkvbuf[:, lanes(j * CHUNK + n, SUB)] = mm(nbuf[...], w[:, n:n + SUB]).astype(BF)
             sn.start(m * 12 + j + DEPTH)
             return c
         lax.fori_loop(I0, I6, qkv_step, I0)
@@ -422,22 +474,20 @@
             remote(a_s.at[m], oa_other.at[m], bulk.at[I0], ao_sem, place.sibling).start()
 
         def head_step(i, c):
-            for r in range(I4):
-                base = (i // I2) * (I3 * half) + ((i % I2) * I4 + r) * HEAD_PAD
-                q = qkvbuf[I0, :, lanes(base, HEAD_PAD)]
-                k = qkvbuf[I0, :, lanes(base + half, HEAD_PAD)]
-                v = qkvbuf[I0, :, lanes(base + I2 * half, HEAD_PAD)]
-                probs = causal_probs(q, k, scale).astype(BF)
-                ctxbuf[:, lanes((i * I4 + r) * HEAD_PAD, HEAD_PAD)] = mm(probs, v).astype(BF)
+            base = i * (I3 * half)
+            views = [[qkvbuf[:, lanes(base + t * half + r * HEAD_PAD, HEAD_PAD)] for t in range(I3)] for r in range(I8)]
+            for r, context in enumerate(attention_forward(views, scale)):
+                ctxbuf[:, lanes(i * half + r * HEAD_PAD, HEAD_PAD)] = context
             return c
-        lax.fori_loop(I0, heads // I4, head_step, I0)
-
-        w0, w1 = sk.wait(m * I2), sk.wait(m * I2 + I1)
+        lax.fori_loop(I0, I2, head_step, I0)
+
+        @pl.when(m == I0)
+        def _():
+            for c in range(I2):
+                pltpu.make_async_copy(wo, wores.at[c, I0:768, :], out_sem.at[c]).wait()
         for n in range(I0, width, SUB):
-            total = mm(ctxbuf[:, I0:half], w0[:, n:n + SUB]) + mm(ctxbuf[:, half:I2 * half], w1[:, n:n + SUB])
+            total = mm(ctxbuf[:, I0:half], wores[I0, :, n:n + SUB]) + mm(ctxbuf[:, half:I2 * half], wores[I1, :, n:n + SUB])
             mid[:, n:n + SUB] = (act[:, n:n + SUB].astype(F32) + total).astype(BF)
-        sk.start(m * I2 + KDEPTH)
-        sk.start(m * I2 + I1 + KDEPTH)
         saved(h_s.at[m], I0).start()
 
         @pl.when(place.is_l)
@@ -454,14 +504,14 @@
             w = sn.wait(m * 12 + I6 + j)
             for n in range(I0, CHUNK, SUB):
                 u = mm(nbuf[...], w[:, n:n + SUB]).astype(BF)
-                ubuf[I0, :, lanes(j * CHUNK + n, SUB)] = u
+                ubuf[:, lanes(j * CHUNK + n, SUB)] = u
                 uf = u.astype(F32)
                 zbuf[:, n:n + SUB] = (uf * gelu_gate(uf)[I0]).astype(BF)
             sn.start(m * 12 + I6 + j + DEPTH)
 
             @pl.when(m == I0)
             def _():
-                resident_ready(j)
+                pltpu.make_async_copy(wd.at[I0:CHUNK, :], wres.at[j], res_sem.at[j]).wait()
             for n in range(I0, width, SUB):
                 acc[:, n:n + SUB] += mm(zbuf[...], wres[j, :, n:n + SUB])
             return c
@@ -488,11 +538,23 @@
         def _():
             pltpu.make_async_copy(y_ref.at[m, place.core], ybuf, y_sem).wait()
 
+            @pl.when(m > I0)
+            def _():
+                seed_out(m).wait()
+
             def seed(rows):
                 error = out[rows, :].astype(F32) - ybuf[rows, :].astype(F32)
-                gbuf[m, rows, :] = (error * norm_factor).astype(BF)
+                sbuf[rows, :] = (error * norm_factor).astype(BF)
                 lossbuf[...] += jnp.sum((error * error).reshape(I4, I8, width), axis=I0)
             rows_loop(seq, 32, seed)
+            seed_out(m).start()
+
+        @pl.when(takes_x)
+        def _():
+            for core, buf, sem in ((place.core, ybuf, y_sem), (I1 - place.core, sbuf, s_sem)):
+                pltpu.make_async_copy(x_ref.at[m, core], buf, sem).wait()
+            for copy in x_out(m):
+                copy.start()
 
         saved(h_s.at[m], I0).wait()
 
@@ -505,14 +567,6 @@
         def _():
             remote(h_s.at[m], oh_other.at[m], bulk.at[I2], oo_sem, place.sibling).start()
             remote(h_s.at[m], oh_other.at[m], bulk.at[I3], oo_sem, place.across_other).start()
-
-        @pl.when(is_last & place.is_l)
-        def _():
-            remote(gbuf.at[m], og_same.at[m], bulk.at[I4], gs_sem, place.across).start()
-
-        @pl.when(is_last & is_r)
-        def _():
-            remote(gbuf.at[m], og_other.at[m], bulk.at[I4], go_sem, place.across_other).start()
         return carry
 
     lax.fori_loop(I0, micro, forward_tick, I0)
@@ -523,8 +577,8 @@
         for n in range(128, width, 128):
             total = total + lossbuf[:, n:n + 128]
         losstile[...] = total
-        pltpu.make_async_copy(losstile, loss_all.at[place.core], tiny.at[5]).start()
-        for index, copy in enumerate(place.others(losstile, loss_all.at[place.core], loss_send, tiny.at[5])):
+        pltpu.make_async_copy(losstile, loss_all.at[place.core], tiny).start()
+        for index, copy in enumerate(place.others(losstile, loss_all.at[place.core], loss_send, tiny)):
             copy.start()
     for copy in (qkv_out(micro - I1), up_out(micro - I1)):
         copy.wait()
@@ -536,11 +590,95 @@
     for m in (micro - I2, micro - I1):
         both_kinds(home02, hand_out(m), False)
 
-    bn = Stream(wn, stream_n, DEPTH, [([(None, td0)], I3), ([(None, td1)], I3), ([(None, to0)], I1), ([(None, to1)], I1)], micro * I8, False)
-    bk = Stream(wk, stream_k, KDEPTH, [(near_of(I0), I3), ([(None, fq)], I3)], micro * I6, True)
+    @pl.when(is_last)
+    def _():
+        seed_out(micro - I1).wait()
+        for copy in place.others(losstile, loss_all.at[place.core], loss_send, tiny):
+            copy.wait_send()
+
+    @pl.when(takes_x)
+    def _():
+        for copy in x_out(micro - I1):
+            copy.wait()
+    pltpu.make_async_copy(gains, home_gains, gain_sem.at[I0]).wait()
+    sent, got = drain(place)
+    sent(h_s, bulk.at[I2])
+    got(oh_other, oo_sem)
+    got(loss_all, tiny)
+
+    @pl.when(is_r)
+    def _():
+        sent(a_s, bulk.at[I0])
+        sent(h_s, bulk.at[I3])
+        got(oh_same, os_sem)
+
+    @pl.when(place.is_l)
+    def _():
+        got(oa_same, as_sem)
+
+    @pl.when(place.is_l | home02)
+    def _():
+        got(oa_other, ao_sem)
+
+
+def drain(place):
+    def sent(buf, sem):
+        remote(buf, buf, sem, sem, place.sibling).wait_send()
+
+    def got(dst, sem):
+        pltpu.make_async_copy(dst, dst, sem).wait()
+    return sent, got
+
+
+def backward_kernel(dims, a_s, h_s, qkv_s, u_s, g_s, wq, nq, fq, td0, td1, to0, to1, tu0, tu1, gains, after, oa_in_same, oa_in_other,
+                    dx_s, m_s, od_same, od_other, og_same, og_other, oa_same, oa_other, dg_same, dg_other,
+                    gbuf, hbuf, obuf, qkvbuf, ubuf, habuf, zbuf, ctxbuf, dqkvbuf, acc, accg, wres, wn, wk,
+                    grad_sem, hop_b, back_sem, save_sem, stream_n, stream_k, res_sem, load_sem,
+                    ds_sem, do_sem, gs_sem, go_sem, as_sem, ao_sem, bulk, tiny):
+    micro, seq, width, heads, head_dim, ffn = dims
+    place = Place()
+    is_first, is_last = place.home == I0, place.home == I3
+    home13 = (place.home == I1) | is_last
+    is_r = jnp.logical_not(place.is_l)
+    half = heads // I2 * HEAD_PAD
+    scale = head_dim ** -0.5
+
+    barrier = pltpu.get_barrier_semaphore()
+    along_x = (place.home == I1) | (place.home == I2)
+    for there in (place.sibling, place.across, place.across_other):
+        pl.semaphore_signal(barrier, inc=I1, device_id=there, device_id_type=MESH)
+
+    @pl.when(along_x)
+    def _():
+        pl.semaphore_signal(barrier, inc=I1, device_id=place.at(place.tp, (place.stage + I2) % I4), device_id_type=MESH)
+
+    @pl.when(is_last)
+    def _():
+        for m in range(micro):
+            pltpu.make_async_copy(g_s.at[m], gbuf.at[m], grad_sem.at[m]).start()
+    wk[...] = jnp.zeros_like(wk)
+    bn = Stream(wn, stream_n, BACK_DEPTH, [([(None, td0)], I3), ([(None, td1)], I3), ([(None, to0)], I1), ([(None, to1)], I1)], micro * I8, False)
+    bk = Stream(wk, stream_k, KDEPTH, [(near_choices(place, wq, nq), I3), ([(None, fq)], I3)], micro * I6, True)
     bn.prime()
     bk.prime()
-    resident(([(None, tu0)], [(None, tu1)]), True)
+    load_resident(wres, res_sem, ([(None, tu0)], [(None, tu1)]))
+
+    def saved(dst, index):
+        return pltpu.make_async_copy(hbuf, dst, save_sem)
+
+    def both_kinds(condition, copies, start):
+        far_copy, own_copy = copies
+
+        @pl.when(condition & place.is_l)
+        def _():
+            far_copy().start() if start else far_copy().wait_send()
+
+        @pl.when(condition & is_r)
+        def _():
+            own_copy().start() if start else own_copy().wait()
+
+    def near_hand(src, dst_far, dst_own, sem, recv_sem):
+        return (lambda: remote(src, dst_far, sem, recv_sem, place.sibling)), (lambda: pltpu.make_async_copy(src, dst_own, sem))
 
     def loads(i):
         m = micro - I1 - i
@@ -599,17 +737,11 @@
             for copy in loads(i + I1):
                 copy.start()
 
-        @pl.when(jnp.logical_not(is_last))
-        def _():
-            remote(grad, grad, hop_b.at[slot], grad_sem.at[m], place.sibling).wait_recv()
+        pltpu.make_async_copy(g_s.at[m], grad, grad_sem.at[m]).wait()
 
         @pl.when(place.is_l)
         def _():
             pltpu.make_async_copy(grad, og_same.at[m], gs_sem).start()
-
-        @pl.when(is_r)
-        def _():
-            remote(grad, og_other.at[m], bulk.at[5], go_sem, place.sibling).start()
         load_u, load_qkv, load_h, load_a = loads(i)
         load_u.wait()
         acc[...] = jnp.zeros_like(acc)
@@ -621,11 +753,11 @@
                 u = u_now[:, lanes(j * CHUNK + n, SUB)].astype(F32)
                 gate, u2 = gelu_gate(u)
                 zbuf[:, n:n + SUB] = (dz * gelu_slope(u * gate, gate, u2)).astype(BF)
-            bn.start(i * I8 + j + DEPTH)
+            bn.start(i * I8 + j + BACK_DEPTH)
 
             @pl.when(i == I0)
             def _():
-                resident_ready(j)
+                pltpu.make_async_copy(tu0.at[I0:CHUNK, :], wres.at[j], res_sem.at[j]).wait()
             for n in range(I0, width, SUB):
                 acc[:, n:n + SUB] += mm(zbuf[...], wres[j, :, n:n + SUB])
             return c
@@ -644,22 +776,18 @@
             w = bn.wait(i * I8 + I6 + c)
             for n in range(I0, CHUNK, SUB):
                 ctxbuf[:, c * CHUNK + n:c * CHUNK + n + SUB] = mm(dmid[...], w[:, n:n + SUB]).astype(BF)
-            bn.start(i * I8 + I6 + c + DEPTH)
+            bn.start(i * I8 + I6 + c + BACK_DEPTH)
         load_qkv.wait()
 
         def head_step(t, c):
-            for r in range(I2):
-                base = (t // I4) * (I3 * half) + ((t % I4) * I2 + r) * HEAD_PAD
-                q = qkv_now[:, lanes(base, HEAD_PAD)]
-                k = qkv_now[:, lanes(base + half, HEAD_PAD)]
-                v = qkv_now[:, lanes(base + I2 * half, HEAD_PAD)]
-                dc = ctxbuf[:, lanes((t * I2 + r) * HEAD_PAD, HEAD_PAD)]
-                _, dq, dk, dv = attention_backward(q, k, v, dc, scale)
-                dqkvbuf[:, lanes(base, HEAD_PAD)] = dq
-                dqkvbuf[:, lanes(base + half, HEAD_PAD)] = dk
-                dqkvbuf[:, lanes(base + I2 * half, HEAD_PAD)] = dv
+            base = (t // I2) * (I3 * half) + (t % I2) * (I4 * HEAD_PAD)
+            at = [[lanes(base + part * half + r * HEAD_PAD, HEAD_PAD) for part in range(I3)] for r in range(I4)]
+            group = [(*(qkv_now[:, p] for p in at[r]), ctxbuf[:, lanes((t * I4 + r) * HEAD_PAD, HEAD_PAD)]) for r in range(I4)]
+            for r, grads in enumerate(attention_backward(group, scale)):
+                for p, value in zip(at[r], grads):
+                    dqkvbuf[:, p] = value
             return c
-        lax.fori_loop(I0, heads // I2, head_step, I0)
+        lax.fori_loop(I0, heads // I4, head_step, I0)
         acc[...] = jnp.zeros_like(acc)
 
         def qkv_step(j, c):
@@ -673,6 +801,10 @@
         back_ready(i)
         norm_back(I0, a_now, dmid, prev, gains[I0:I1, :])
 
+        @pl.when(i == I0)
+        def _():
+            pl.semaphore_wait(barrier, I3 + (place.home + I1) // I2 % I2)
+
         @pl.when(jnp.logical_not(is_first))
         def _():
             hop_back(i).start()
@@ -689,6 +821,7 @@
 
         @pl.when(is_r)
         def _():
+            remote(grad, og_other.at[m], bulk.at[5], go_sem, place.sibling).start()
             saved(m_s.at[m], I0).wait()
             remote(m_s.at[m], od_other.at[m], bulk.at[I6], do_sem, place.sibling).start()
             remote(m_s.at[m], od_other.at[m], bulk.at[7], do_sem, place.across_other).start()
@@ -713,8 +846,8 @@
             remote(gbuf.at[m], og_other.at[m], bulk.at[I4], go_sem, place.across_other).start()
 
     lax.fori_loop(I0, micro, backward_tick, I0)
-    for i in range(I1, micro, I2):
-        far_grad(micro - I1 - i, place.home == I1)
+    for i in range(micro):
+        far_grad(micro - I1 - i, is_last | (place.home == I1) if i % I2 else is_last)
 
     @pl.when(place.is_l)
     def _():
@@ -729,19 +862,11 @@
     for i in (micro - I2, micro - I1):
         back_ready(jnp.int32(i))
 
-    def sent(buf, sem):
-        remote(buf, a_s, sem, ao_sem, place.sibling).wait_send()
-
-    def got(dst, sem):
-        pltpu.make_async_copy(dst, dst, sem).wait()
-
-    sent(h_s, bulk.at[I2])
+    sent, got = drain(place)
     sent(m_s, bulk.at[I6])
 
     @pl.when(is_r)
     def _():
-        sent(a_s, bulk.at[I0])
-        sent(h_s, bulk.at[I3])
         sent(gbuf, bulk.at[5])
         sent(m_s, bulk.at[7])
         remote(accg, dg_other, tiny.at[I2], tiny.at[I4], place.sibling).wait_send()
@@ -754,87 +879,161 @@
     def _():
         sent(a_s, bulk.at[I8])
 
-    @pl.when(is_last)
-    def _():
-        for copy in place.others(losstile, loss_all.at[place.core], loss_send, tiny.at[5]):
-            copy.wait_send()
     remote(accg, dg_other, tiny.at[I1], tiny.at[I4], place.sibling).wait_send()
-    got(oh_other, oo_sem)
     got(od_other, do_sem)
     got(og_other, go_sem)
     got(dg_same, tiny.at[I0])
     got(dg_other, tiny.at[I4])
-    got(loss_all, tiny.at[5])
 
     @pl.when(is_r)
     def _():
-        got(oh_same, os_sem)
         got(od_same, ds_sem)
 
-    @pl.when(place.is_l | home02)
+    @pl.when(place.is_l | jnp.logical_not(home13))
     def _():
         got(og_same, gs_sem)
 
-    @pl.when(place.is_l | (place.home == I3))
+    @pl.when(is_last & is_r)
     def _():
         got(oa_same, as_sem)
-
-    @pl.when(place.is_l | (place.home != I1))
-    def _():
         got(oa_other, ao_sem)
 
 
-def step_phase(dims, x, y, own, own_gains):
+def shapes(*dims_list):
+    return [jax.ShapeDtypeStruct(d, BF) for d in dims_list]
+
+
+def forward_phase(dims, x, y, own, own_gains):
     micro, seq, width, heads, head_dim, ffn = dims
     half = heads // I2 * HEAD_PAD
     act = (micro, seq, width)
-    raw = [(heads // I2 * I3 * head_dim, width), (heads // I2 * head_dim, width), (width, ffn // I2), (ffn // I2, width)]
+    raw = [w.shape for w in own]
     turned = [(width, I3 * half), (width, half), (ffn // I2, width), (width, ffn // I2)]
-    outs = [act, act, act, (micro, seq, I6 * half), (micro, seq, ffn), act] + [act] * I8
-    out_shape = [jax.ShapeDtypeStruct(s, BF) for s in outs]
-    out_shape += [jax.ShapeDtypeStruct(s, F32) for s in ((I2, I8, width), (I2, I8, width), (I2, I8, 128))]
-    out_shape += [jax.ShapeDtypeStruct(s, BF) for s in raw + raw + turned + turned]
+    out_shape = shapes(act, act, (micro, seq, I6 * half), (micro, seq, ffn), *[act] * 5)
+    out_shape += [jax.ShapeDtypeStruct(s, F32) for s in ((I2, I8, 128), own_gains.shape)]
+    out_shape += shapes(*raw, *raw, *turned, *turned)
     any_spec = pl.BlockSpec(memory_space=ANY)
     vmem, dma = pltpu.VMEM, pltpu.SemaphoreType.DMA
+    row = vmem((seq, width), BF)
     scratch = [
-        vmem(act, BF), vmem(act, BF), vmem((seq, width), BF), vmem((I2, seq, width), BF), vmem((seq, width), BF), vmem((seq, width), BF),
-        vmem((I2, seq, I6 * half), BF), vmem((I2, seq, ffn), BF), vmem((I2, I2, seq, width), BF), vmem((seq, CHUNK), BF), vmem((seq, I2 * half), BF),
-        vmem((seq, I6 * half), BF), vmem((seq, width), F32), vmem((I2, I8, width), F32), vmem((I8, width), F32), vmem((I8, 128), F32),
-        vmem((I2, width), F32), vmem((I6, CHUNK, width), BF), vmem((DEPTH, width, CHUNK), BF), vmem((KDEPTH, CHUNK, width), BF),
+        vmem(act, BF), row, vmem((I2, seq, width), BF), row, row, row, vmem((seq, I6 * half), BF), vmem((seq, ffn), BF), vmem((seq, CHUNK), BF),
+        vmem((seq, I2 * half), BF), vmem((seq, width), F32), vmem((I8, width), F32), vmem((I8, 128), F32), vmem((I2, width), F32),
+        vmem((I6, CHUNK, width), BF), vmem((I2, CHUNK, width), BF), vmem((DEPTH, width, CHUNK), BF),
         dma((I4,)), dma((I4,)), dma((I4,)), dma((I4,)), dma((12,)), dma((I2,)), dma((I2,)),
-        dma((micro,)), dma((micro,)), dma((I2,)), dma((I2,)), dma((I2,)), dma((I2,)), dma((I3,)), dma((DEPTH,)), dma((KDEPTH,)), dma((I6,)), dma((I2,)),
-        dma((I4, I2)), dma(()),
-        dma(()), dma(()), dma(()), dma(()), dma(()), dma(()), dma(()), dma(()), dma((9,)), dma((I2,)), dma((I6,)), dma((7,)),
+        dma((micro,)), dma((I2,)), dma((I2,)), dma((I3,)), dma((DEPTH,)), dma((I6,)), dma((I2,)), dma((I2,)), dma(()), dma(()),
+        dma(()), dma(()), dma(()), dma(()), dma((I4,)), dma((I2,)), dma(()), dma((7,)),
     ]
     return pl.pallas_call(
-        functools.partial(step_kernel, dims),
+        functools.partial(forward_kernel, dims),
         out_shape=tuple(out_shape),
         in_specs=[any_spec] * I6 + [pl.BlockSpec(memory_space=vmem)],
         out_specs=(any_spec,) * len(out_shape),
         scratch_shapes=scratch,
         compiler_params=pltpu.CompilerParams(collective_id=I0, has_side_effects=True, vmem_limit_bytes=VMEM_LIMIT),
-        name='step_phase',
+        name='forward_phase',
     )(x, y, *own, own_gains)
 
 
-TOKENS = 512
-
-
-def bring(pairs, sem):
-    copies = [pltpu.make_async_copy(src, dst, sem.at[i]) for i, (src, dst) in enumerate(pairs)]
-    for copy in copies:
-        copy.start()
-    return copies
-
-
-def turn_into(dst, src, rows, cols):
-    for r in range(I0, rows, SUB):
-        for c in range(I0, cols, SUB):
-            high, wide = min(SUB, rows - r), min(SUB, cols - c)
-            dst[c:c + wide, r:r + high] = src[r:r + high, c:c + wide].T
-
-
-def spread_dx(step, last, dx, d_in, here_sem, parent_sem, sib_sem, send_sems):
+def backward_phase(dims, saved, weights, gains, after, oa_rows):
+    micro, seq, width, heads, head_dim, ffn = dims
+    half = heads // I2 * HEAD_PAD
+    act = (micro, seq, width)
+    out_shape = shapes(*[act] * I8) + [jax.ShapeDtypeStruct((I2, I8, width), F32)] * I2
+    any_spec = pl.BlockSpec(memory_space=ANY)
+    vmem, dma = pltpu.VMEM, pltpu.SemaphoreType.DMA
+    scratch = [
+        vmem(act, BF), vmem((seq, width), BF), vmem((I2, seq, width), BF), vmem((I2, seq, I6 * half), BF), vmem((I2, seq, ffn), BF),
+        vmem((I2, I2, seq, width), BF), vmem((seq, CHUNK), BF), vmem((seq, I2 * half), BF), vmem((seq, I6 * half), BF), vmem((seq, width), F32),
+        vmem((I2, I8, width), F32), vmem((I6, CHUNK, width), BF), vmem((BACK_DEPTH, width, CHUNK), BF), vmem((KDEPTH, CHUNK, width), BF),
+        dma((micro,)), dma((I2,)), dma((I2,)), dma(()), dma((BACK_DEPTH,)), dma((KDEPTH,)), dma((I6,)), dma((I4, I2)),
+        dma(()), dma(()), dma(()), dma(()), dma(()), dma(()), dma((9,)), dma((5,)),
+    ]
+    return pl.pallas_call(
+        functools.partial(backward_kernel, dims),
+        out_shape=tuple(out_shape),
+        in_specs=[any_spec] * 14 + [pl.BlockSpec(memory_space=vmem)] + [any_spec] * I3,
+        out_specs=(any_spec,) * len(out_shape),
+        scratch_shapes=scratch,
+        input_output_aliases={16: I6, 17: 7},
+        compiler_params=pltpu.CompilerParams(collective_id=I1, has_side_effects=True, vmem_limit_bytes=VMEM_LIMIT),
+        name='backward_phase',
+    )(*saved, *weights, gains, after, *oa_rows)
+
+
+def recompute_kernel(dims, early, h_same, h_other, a_same, a_other, gains, wq, wu, *refs):
+    (done, u_o, qkv_o, ctx_o, n1_o, n2_o), (wqbuf, wubuf, count, sem) = refs[-10:-I4], refs[-I4:]
+    micro, seq, width, heads, head_dim, ffn = dims
+    place = Place()
+    scale = head_dim ** -0.5
+    half = heads // I2 * HEAD_PAD
+    steps = I2 * micro * seq // BLOCK
+
+    def body(hs, ho, rs, ro, u, qkv, ctx, n1, n2):
+        step = count[I0]
+        count[I0] = step + I1
+        for low, high, gain, dst in ((hs, ho, gains[I1:I2, :], n2), (rs, ro, gains[I0:I1, :], n1)):
+            @pl.when(step < steps // I2)
+            def _(low=low, gain=gain, dst=dst):
+                norm_rows(low, gain, dst, BLOCK)
+
+            @pl.when(step >= steps // I2)
+            def _(high=high, gain=gain, dst=dst):
+                norm_rows(high, gain, dst, BLOCK)
+
+        def qkv_step(j, c):
+            rows = pl.ds(pl.multiple_of(j * SUB, SUB), SUB)
+            qkv[:, lanes(j * SUB, SUB)] = mm_nt(n1[...], wqbuf[rows, :]).astype(BF)
+            u[:, lanes(j * SUB, SUB)] = mm(n2[...], wubuf[:, lanes(j * SUB, SUB)]).astype(BF)
+            return c
+        lax.fori_loop(I0, I3 * half // SUB, qkv_step, I0)
+
+        def head_step(j, c):
+            at = [(pl.ds(s, seq), r * HEAD_PAD) for s in range(I0, BLOCK, seq) for r in range(I4)]
+            base = j * (I4 * HEAD_PAD)
+            views = [[qkv[rows, lanes(base + t * half + col, HEAD_PAD)] for t in range(I3)] for rows, col in at]
+            for (rows, col), context in zip(at, attention_forward(views, scale)):
+                ctx[rows, lanes(base + col, HEAD_PAD)] = context
+            return c
+        lax.fori_loop(I0, I2, head_step, I0)
+
+    @pl.when(place.home < I2 if early else place.home > I1)
+    def _():
+        wqbuf[...] = jnp.zeros_like(wqbuf)
+        for t in range(I3):
+            load_heads(wq, t, wqbuf.at[pl.ds(t * CHUNK, CHUNK)], sem.at[I0])
+        up = pltpu.make_async_copy(wu, wubuf, sem.at[I1])
+        up.start()
+        up.wait()
+        pltpu.make_async_copy(wq, wqbuf.at[I0:wq.shape[I0]], sem.at[I0]).wait()
+        count[I0] = I0
+        low = pl.BlockSpec((BLOCK, width), lambda i: (jnp.minimum(i, steps // I2 - I1), I0))
+        high = pl.BlockSpec((BLOCK, width), lambda i: (jnp.maximum(i - steps // I2, I0), I0))
+        block = lambda n: pl.BlockSpec((BLOCK, n), lambda i: (i, I0))
+        pltpu.emit_pipeline(body, grid=(steps,), in_specs=[low, high, low, high],
+                            out_specs=[block(ffn // I2), block(I3 * half), block(half), block(width), block(width)])(
+            h_same, h_other, a_same, a_other, u_o, qkv_o, ctx_o, n1_o, n2_o)
+
+
+def owner_recompute(dims, early, again, h_rows, a_rows, gains, own):
+    micro, seq, width, heads, head_dim, ffn = dims
+    half = heads // I2 * HEAD_PAD
+    tokens = I2 * micro * seq
+    any_spec = pl.BlockSpec(memory_space=ANY)
+    vmem = pltpu.VMEM
+    earlier = () if early else tuple(again)
+    return pl.pallas_call(
+        functools.partial(recompute_kernel, dims, early),
+        out_shape=(jax.ShapeDtypeStruct((I8, 128), F32), *shapes((tokens, ffn // I2), (tokens, I3 * half), (tokens, half), (tokens, width), (tokens, width))),
+        in_specs=[any_spec] * I4 + [pl.BlockSpec(memory_space=vmem)] + [any_spec] * (I2 + len(earlier)),
+        out_specs=(any_spec,) * I6,
+        scratch_shapes=[vmem((I3 * half, width), BF), vmem((width, ffn // I2), BF), pltpu.SMEM((I1,), jnp.int32), pltpu.SemaphoreType.DMA((I2,))],
+        input_output_aliases={7 + i: I1 + i for i in range(len(earlier))},
+        compiler_params=pltpu.CompilerParams(has_side_effects=True, vmem_limit_bytes=VMEM_LIMIT),
+        name='owner_recompute',
+    )(*h_rows, *a_rows, gains, own[I0], own[I2], *earlier)
+
+
+def spread_dx(step, last, dx, d_in, bounce, here_sem, parent_sem, sib_sem, send_sems):
     place = Place()
     micro = dx.shape[I0]
     below = place.at(place.tp, (place.stage + I2) % I4)
@@ -872,18 +1071,25 @@
             hand(m, dx.at[m], I1, place.across)
             hand(m, dx.at[m], I2, below)
             hand(m, dx.at[m], I0, place.sibling)
-            pltpu.make_async_copy(dx.at[m], block(m), here_sem).start()
+        pltpu.make_async_copy(dx, bounce, here_sem).start()
+
+    @pl.when((step == I2) & is_a)
+    def _():
+        pltpu.make_async_copy(dx, bounce, here_sem).wait()
+        for m in range(micro):
+            pltpu.make_async_copy(bounce.at[m], block(m), here_sem).start()
 
     @pl.when((step == I2) & is_b)
     def _():
         pl.semaphore_wait(barrier, I2)
 
-    @pl.when((step > I2) & (step < I3 + micro) & is_b)
-    def _():
-        m = micro + I2 - step
-        arrived(m)
-        hand(m, block(m), I2, below)
-        hand(m, block(m), I0, place.sibling)
+    @pl.when((step > I2) & (step < I3 + micro // I2) & is_b)
+    def _():
+        for r in (I1, I2):
+            m = micro + I6 - I2 * step - r
+            arrived(m)
+            hand(m, block(m), I2, below)
+            hand(m, block(m), I0, place.sibling)
 
     @pl.when((step == last) & is_leaf)
     def _():
@@ -909,119 +1115,104 @@
         remote(dx, dx, send_sems.at[I0], sib_sem, place.sibling).wait_recv()
 
 
-def owner_mlp_kernel(dx, hs, ho, gs, go, gain, wu, wd, dwu, dwd, d_in, n2, n2t, grad, wdt, z, zt, dup, sem, here_sem, parent_sem, sib_sem, send_sems):
-    tokens, width = n2.shape
-    part = tokens // I2
-    spread_dx(pl.program_id(I0), pl.num_programs(I0) - I1, dx, d_in, here_sem, parent_sem, sib_sem, send_sems)
-
-    @pl.when(pl.program_id(I0) == I0)
-    def _():
-        low, high = pl.ds(I0, part), pl.ds(part, part)
-        for copy in bring([(hs, n2.at[low]), (ho, n2.at[high]), (gs, grad.at[low]), (go, grad.at[high])], sem):
-            copy.wait()
-
-        def prepare(rows):
-            norm_rows(n2.at[rows], gain[...], n2.at[rows], SUB)
-            for c in range(I0, width, SUB):
-                n2t[c:c + SUB, rows] = n2[rows, c:c + SUB].T
-        rows_loop(tokens, SUB, prepare)
-    turn_into(wdt, wd, SUB, width)
-
-    def front(rows):
-        u = mm(n2[rows, :], wu[...]).astype(BF).astype(F32)
-        dz = mm(grad[rows, :], wdt[...]).astype(BF).astype(F32)
-        gate, u2 = gelu_gate(u)
-        hidden = u * gate
-        z[rows, :] = hidden.astype(BF)
-        dup[rows, :] = (dz * gelu_slope(hidden, gate, u2)).astype(BF)
-    rows_loop(tokens, TOKENS, front)
-    turn_into(zt, z, tokens, SUB)
-    for c in range(I0, width, TOKENS):
-        dwu[c:c + TOKENS, :] = mm(n2t[c:c + TOKENS, :], dup[...])
-    for c in range(I0, width, SUB):
-        dwd[:, c:c + SUB] = mm(zt[...], grad[:, c:c + SUB])
-
-
-def owner_mlp(dx, h_rows, g_rows, gain, w_up, w_down):
-    width, ffn = w_up.shape
-    part, micro = h_rows[I0].shape[I0], dx.shape[I0]
+def owner_backward_kernel(dims, dx, ds, do, gs, go, u, qkv, wo, wd, dqkv, dup, z, d_in,
+                          dmid, grad, dctx, wobuf, bounce, sem, here_sem, parent_sem, sib_sem, send_sems):
+    micro, seq, width, heads, head_dim, ffn = dims
+    half = heads // I2 * HEAD_PAD
+    scale = head_dim ** -0.5
+    step, steps = pl.program_id(I0), pl.num_programs(I0)
+    spread_dx(step, steps - I1, dx, d_in, bounce, here_sem, parent_sem, sib_sem, send_sems)
+
+    @pl.when(step == I0)
+    def _():
+        wobuf[...] = jnp.zeros_like(wobuf)
+        load_heads(wo, I0, wobuf, sem)
+        pltpu.make_async_copy(wo, wobuf.at[I0:wo.shape[I0]], sem).wait()
+    for near, far, dst in ((ds, do, dmid), (gs, go, grad)):
+        @pl.when(step < steps // I2)
+        def _(near=near, dst=dst):
+            dst[...] = near[...]
+
+        @pl.when(step >= steps // I2)
+        def _(far=far, dst=dst):
+            dst[...] = far[...]
+
+    def ctx_step(j, c):
+        rows = pl.ds(pl.multiple_of(j * SUB, SUB), SUB)
+        dctx[:, lanes(j * SUB, SUB)] = mm_nt(dmid[...], wobuf[rows, :]).astype(BF)
+        return c
+    lax.fori_loop(I0, half // SUB, ctx_step, I0)
+
+    def mlp_step(j, c):
+        rows = pl.ds(pl.multiple_of(j * SUB, SUB), SUB)
+        cols = lanes(j * SUB, SUB)
+        dz = mm_nt(grad[...], wd[rows, :]).astype(BF).astype(F32)
+        up = u[:, cols].astype(F32)
+        gate, up2 = gelu_gate(up)
+        hidden = up * gate
+        z[:, cols] = hidden.astype(BF)
+        dup[:, cols] = (dz * gelu_slope(hidden, gate, up2)).astype(BF)
+        return c
+    lax.fori_loop(I0, ffn // I2 // SUB, mlp_step, I0)
+
+    def head_step(j, c):
+        base = j * (I2 * HEAD_PAD)
+        at = [(pl.ds(s, seq), base + r * HEAD_PAD) for s in range(I0, BLOCK, seq) for r in range(I2)]
+        group = [(*(qkv[rows, lanes(t * half + col, HEAD_PAD)] for t in range(I3)), dctx[rows, lanes(col, HEAD_PAD)]) for rows, col in at]
+        for (rows, col), grads in zip(at, attention_backward(group, scale)):
+            for t, value in enumerate(grads):
+                dqkv[rows, lanes(t * half + col, HEAD_PAD)] = value
+        return c
+    lax.fori_loop(I0, heads // I4, head_step, I0)
+
+
+def owner_backward(dims, dx, d_rows, g_rows, ups, qkv, own):
+    micro, seq, width, heads, head_dim, ffn = dims
+    half = heads // I2 * HEAD_PAD
+    tokens = I2 * micro * seq
+    steps = tokens // BLOCK
     vmem, dma = pltpu.VMEM, pltpu.SemaphoreType.DMA
     any_spec = pl.BlockSpec(memory_space=ANY)
-    up_spec = pl.BlockSpec((width, SUB), lambda i: (I0, i))
-    down_spec = pl.BlockSpec((SUB, width), lambda i: (i, I0))
-    rows = lambda n: vmem((I2 * part, n), BF)
+    low = pl.BlockSpec((BLOCK, width), lambda i: (jnp.minimum(i, steps // I2 - I1), I0))
+    high = pl.BlockSpec((BLOCK, width), lambda i: (jnp.maximum(i - steps // I2, I0), I0))
+    block = lambda n: pl.BlockSpec((BLOCK, n), lambda i: (i, I0))
     return pl.pallas_call(
-        owner_mlp_kernel,
-        grid=(ffn // SUB,),
-        out_shape=(jax.ShapeDtypeStruct(w_up.shape, F32), jax.ShapeDtypeStruct(w_down.shape, F32), jax.ShapeDtypeStruct((micro, I2) + dx.shape[I1:], BF)),
-        in_specs=[any_spec] * 5 + [pl.BlockSpec(memory_space=vmem), up_spec, down_spec],
-        out_specs=(up_spec, down_spec, any_spec),
-        scratch_shapes=[rows(width), vmem((width, I2 * part), BF), rows(width), vmem((width, SUB), BF), rows(SUB), vmem((SUB, I2 * part), BF), rows(SUB), dma((I4,)), dma(()), dma((micro,)), dma(()), dma((I3,))],
-        compiler_params=pltpu.CompilerParams(collective_id=I1, has_side_effects=True, vmem_limit_bytes=VMEM_LIMIT),
-        cost_estimate=pl.CostEstimate(flops=16 * part * width * ffn, bytes_accessed=12 * width * ffn, transcendentals=I2 * part * ffn),
-        name='owner_mlp',
-    )(dx, *h_rows, *g_rows, gain, w_up, w_down)
-
-
-def owner_attn_kernel(seq, x_ref, rs, ro, ds, do, gain, wq, wo, dwq, dwo, n1, dmid, wpad, wqt, wot, qkv, dctx, dqkv, ctx, dqkvt, ctxt, sem):
+        functools.partial(owner_backward_kernel, dims),
+        grid=(steps,),
+        out_shape=tuple(shapes((tokens, I3 * half), (tokens, ffn // I2), (tokens, ffn // I2), (micro, I2, seq, width))),
+        in_specs=[any_spec, low, high, low, high, block(ffn // I2), block(I3 * half), any_spec, pl.BlockSpec((ffn // I2, width), lambda i: (I0, I0))],
+        out_specs=(block(I3 * half), block(ffn // I2), block(ffn // I2), any_spec),
+        scratch_shapes=[vmem((BLOCK, width), BF), vmem((BLOCK, width), BF), vmem((BLOCK, half), BF), vmem((half, width), BF), vmem((micro, seq, width), BF),
+                        dma(()), dma(()), dma((micro,)), dma(()), dma((I3,))],
+        compiler_params=pltpu.CompilerParams(collective_id=I2, has_side_effects=True, vmem_limit_bytes=VMEM_LIMIT),
+        name='owner_backward',
+    )(dx, *d_rows, *g_rows, ups, qkv, own[I1], own[I3])
+
+
+def bring(pairs, sem):
+    copies = [pltpu.make_async_copy(src, dst, sem.at[i]) for i, (src, dst) in enumerate(pairs)]
+    for copy in copies:
+        copy.start()
+    for copy in copies:
+        copy.wait()
+
+
+def attn_products_kernel(dq, dk, dv, ctx, n1_o, ds, do, dwq, dwo, n1, dmid, dqkvt, ctxt, sem):
     tokens, width = n1.shape
     part = tokens // I2
-    head_dim = wo.shape[I1]
-    scale = head_dim ** -0.5
-    pair = I2 * HEAD_PAD
+    head_dim = dwo.shape[I1]
 
     @pl.when(pl.program_id(I0) == I0)
     def _():
-        place = Place()
-        from_x = (place.home == I1) & jnp.logical_not(place.is_l)
-        low, high = pl.ds(I0, part), pl.ds(part, part)
-        d_copies = bring([(ds, dmid.at[low]), (do, dmid.at[high])], sem)
-        a_pairs = [(rs, n1.at[low]), (ro, n1.at[high])]
-        a_sem = sem.at[I2:I4]
-
-        @pl.when(from_x)
-        def _():
-            for m in range(part // seq):
-                for first, core in ((I0, place.core), (part, I1 - place.core)):
-                    pltpu.make_async_copy(x_ref.at[m, core], n1.at[pl.ds(first + m * seq, seq)], a_sem.at[min(first, I1)]).start()
-
-        @pl.when(jnp.logical_not(from_x))
-        def _():
-            bring(a_pairs, a_sem)
-        wpad[...] = jnp.zeros_like(wpad)
-        for i, (src, dst) in enumerate(a_pairs):
-            pltpu.make_async_copy(src, dst, a_sem.at[i]).wait()
-        norm_rows(n1, gain[...], n1, tokens)
-        for copy in d_copies:
-            copy.wait()
-    for r in range(I2):
-        for t in range(I3):
-            wpad[I0:head_dim, :] = wq[t, r]
-            at = t * pair + r * HEAD_PAD
-            turn_into(wqt.at[:, at:at + HEAD_PAD], wpad, HEAD_PAD, width)
-        wpad[I0:head_dim, :] = wo[r]
-        turn_into(wot.at[:, r * HEAD_PAD:(r + I1) * HEAD_PAD], wpad, HEAD_PAD, width)
-
-    def front(rows):
-        for n in range(I0, I3 * pair, pair):
-            qkv[rows, n:n + pair] = mm(n1[rows, :], wqt[:, n:n + pair]).astype(BF)
-        dctx[rows, :] = mm(dmid[rows, :], wot[...]).astype(BF)
-    rows_loop(tokens, TOKENS, front)
-
-    def sequence(rows):
+        bring([(n1_o, n1), (ds, dmid.at[pl.ds(I0, part)]), (do, dmid.at[pl.ds(part, part)])], sem)
+
+    def turn(rows):
+        for t, block in enumerate((dq, dk, dv)):
+            for r in range(I2):
+                at = (I2 * t + r) * head_dim
+                dqkvt[at:at + head_dim, rows] = block[rows, r * HEAD_PAD:(r + I1) * HEAD_PAD].T[I0:head_dim]
         for r in range(I2):
-            q_at, k_at, v_at = [slice(t * pair + r * HEAD_PAD, t * pair + (r + I1) * HEAD_PAD) for t in range(I3)]
-            v, dc = qkv[rows, v_at], dctx[rows, q_at]
-            probs, dq, dk, dv = attention_backward(qkv[rows, q_at], qkv[rows, k_at], v, dc, scale)
-            ctx[rows, q_at] = mm(probs, v).astype(BF)
-            dqkv[rows, q_at], dqkv[rows, k_at], dqkv[rows, v_at] = dq, dk, dv
-    rows_loop(tokens, seq, sequence)
-
-    def turn(rows):
-        for t in range(I6):
-            dqkvt[t * head_dim:(t + I1) * head_dim, rows] = dqkv[rows, t * HEAD_PAD:(t + I1) * HEAD_PAD].T[I0:head_dim]
-        for t in range(I2):
-            ctxt[t * head_dim:(t + I1) * head_dim, rows] = ctx[rows, t * HEAD_PAD:(t + I1) * HEAD_PAD].T[I0:head_dim]
+            ctxt[r * head_dim:(r + I1) * head_dim, rows] = ctx[rows, r * HEAD_PAD:(r + I1) * HEAD_PAD].T[I0:head_dim]
     rows_loop(tokens, SUB, turn)
     for c in range(I0, width, SUB):
         cut = slice(c, c + SUB)
@@ -1029,30 +1220,65 @@
         dwo[:, :, cut] = mm(ctxt[...], dmid[:, cut]).reshape(I2, head_dim, SUB)
 
 
-def owner_attn(seq, x, a_rows, d_rows, gain, w_qkv, w_out):
-    heads, head_dim, width = w_out.shape
-    part = a_rows[I0].shape[I0]
+def attn_products(dqkv, ctx, n1, d_rows, out_dims):
+    heads, head_dim, width = out_dims
+    tokens = n1.shape[I0]
     vmem = pltpu.VMEM
     any_spec = pl.BlockSpec(memory_space=ANY)
-    q_spec = pl.BlockSpec((I3, I2, head_dim, width), lambda i: (I0, i, I0, I0))
-    o_spec = pl.BlockSpec((I2, head_dim, width), lambda i: (i, I0, I0))
-    rows = lambda n: vmem((I2 * part, n), BF)
-    pair = I2 * HEAD_PAD
+    pairs = heads // I2
+    cols = lambda t: pl.BlockSpec((tokens, I2 * HEAD_PAD), lambda i: (I0, t * pairs + i))
     return pl.pallas_call(
-        functools.partial(owner_attn_kernel, seq),
-        grid=(heads // I2,),
-        out_shape=(jax.ShapeDtypeStruct(w_qkv.shape, F32), jax.ShapeDtypeStruct(w_out.shape, F32)),
-        in_specs=[any_spec] * 5 + [pl.BlockSpec(memory_space=vmem), q_spec, o_spec],
-        out_specs=(q_spec, o_spec),
-        scratch_shapes=[
-            rows(width), rows(width), vmem((HEAD_PAD, width), BF), vmem((width, I3 * pair), BF), vmem((width, pair), BF),
-            rows(I3 * pair), rows(pair), rows(I3 * pair), rows(pair), vmem((I6 * head_dim, I2 * part), BF), vmem((I2 * head_dim, I2 * part), BF),
-            pltpu.SemaphoreType.DMA((I4,)),
-        ],
+        attn_products_kernel,
+        grid=(pairs,),
+        out_shape=(jax.ShapeDtypeStruct((I3,) + out_dims, F32), jax.ShapeDtypeStruct(out_dims, F32)),
+        in_specs=[cols(I0), cols(I1), cols(I2), cols(I0), any_spec, any_spec, any_spec],
+        out_specs=(pl.BlockSpec((I3, I2, head_dim, width), lambda i: (I0, i, I0, I0)), pl.BlockSpec((I2, head_dim, width), lambda i: (i, I0, I0))),
+        scratch_shapes=[vmem((tokens, width), BF), vmem((tokens, width), BF), vmem((I6 * head_dim, tokens), BF), vmem((I2 * head_dim, tokens), BF),
+                        pltpu.SemaphoreType.DMA((I3,))],
         compiler_params=pltpu.CompilerParams(vmem_limit_bytes=VMEM_LIMIT),
-        cost_estimate=pl.CostEstimate(flops=36 * part * width * heads * head_dim, bytes_accessed=16 * width * width, transcendentals=part * heads * seq),
-        name='owner_attn',
-    )(x, *a_rows, *d_rows, gain, w_qkv, w_out)
+        name='attn_products',
+    )(dqkv, dqkv, dqkv, ctx, n1, *d_rows)
+
+
+def mlp_products_kernel(dup, z, n2_o, gs, go, dwu, dwd, n2t, grad, zt, stage, sem):
+    width, tokens = n2t.shape
+    part = tokens // I2
+
+    @pl.when(pl.program_id(I0) == I0)
+    def _():
+        bring([(n2_o, stage), (gs, grad.at[pl.ds(I0, part)]), (go, grad.at[pl.ds(part, part)])], sem)
+
+        def turn(rows):
+            for c in range(I0, width, SUB):
+                n2t[c:c + SUB, rows] = stage[rows, c:c + SUB].T
+        rows_loop(tokens, SUB, turn)
+
+    def turn_z(rows):
+        for c in range(I0, z.shape[I1], SUB):
+            zt[c:c + SUB, rows] = z[rows, c:c + SUB].T
+    rows_loop(tokens, SUB, turn_z)
+    for c in range(I0, width, I2 * SUB):
+        dwu[c:c + I2 * SUB, :] = mm(n2t[c:c + I2 * SUB, :], dup[...])
+    for c in range(I0, width, SUB):
+        dwd[:, c:c + SUB] = mm(zt[...], grad[:, c:c + SUB])
+
+
+def mlp_products(dup, hidden, n2, g_rows):
+    tokens, width = n2.shape
+    cols = dup.shape[I1]
+    vmem = pltpu.VMEM
+    any_spec = pl.BlockSpec(memory_space=ANY)
+    block = pl.BlockSpec((tokens, SUB), lambda i: (I0, i))
+    return pl.pallas_call(
+        mlp_products_kernel,
+        grid=(cols // SUB,),
+        out_shape=(jax.ShapeDtypeStruct((width, cols), F32), jax.ShapeDtypeStruct((cols, width), F32)),
+        in_specs=[block, block, any_spec, any_spec, any_spec],
+        out_specs=(pl.BlockSpec((width, SUB), lambda i: (I0, i)), pl.BlockSpec((SUB, width), lambda i: (i, I0))),
+        scratch_shapes=[vmem((width, tokens), BF), vmem((tokens, width), BF), vmem((SUB, tokens), BF), vmem((tokens, width), BF), pltpu.SemaphoreType.DMA((I3,))],
+        compiler_params=pltpu.CompilerParams(vmem_limit_bytes=VMEM_LIMIT),
+        name='mlp_products',
+    )(dup, hidden, n2, *g_rows)
 
 
 def solution(mesh):
@@ -1074,13 +1300,21 @@
         own_gains = jnp.concatenate([gain_attn, gain_mlp]).astype(F32)
         rows_of = (own[I0].transpose(I1, I2, I3, I0).reshape(-I1, width), own[I1].reshape(-I1, width), own[I2], own[I3])
 
-        results = step_phase(dims, inputs, targets, rows_of, own_gains)
-        dx, oh_same, oh_other, oa_same, oa_other, od_same, od_other, og_same, og_other, dg_same, dg_other, loss_all = results[5:17]
+        (acts, mids, qkv, ups, seeds, oh_same, oh_other, oa_same, oa_other, loss_all, home_gains, *weights) = forward_phase(dims, inputs, targets, rows_of, own_gains)
+        (nq, no, nu, nd), (fq, fo, fu, fd) = weights[I0:I4], weights[I4:I8]
+        (tq0, to0, tu0, td0), (tq1, to1, tu1, td1) = weights[I8:12], weights[12:16]
 
         flat = lambda *rows: [r.reshape(-I1, width) for r in rows]
-        w_rows = own[I0].transpose(I1, I2, I3, I0)
-        d_qkv, d_out = owner_attn(seq_len, inputs, flat(oa_same, oa_other), flat(od_same, od_other), own_gains[:I1], w_rows, own[I1])
-        d_up, d_down, d_inputs = owner_mlp(dx, flat(oh_same, oh_other), flat(og_same, og_other), own_gains[I1:], own[I2], own[I3])
+        h_rows = flat(oh_same, oh_other)
+        done, *again = owner_recompute(dims, True, None, h_rows, flat(oa_same, oa_other), own_gains, rows_of)
+        dx, _, od_same, od_other, og_same, og_other, oa_same, oa_other, dg_same, dg_other = backward_phase(
+            dims, (acts, mids, qkv, ups, seeds), (rows_of[I0], nq, fq, td0, td1, to0, to1, tu0, tu1), home_gains, done, (oa_same, oa_other))
+        _, *again = owner_recompute(dims, False, again, h_rows, flat(oa_same, oa_other), own_gains, rows_of)
+        ups_own, qkv_own, ctx_own, n1, n2 = again
+        d_rows, g_rows = flat(od_same, od_other), flat(og_same, og_other)
+        d_qkv_rows, d_up_rows, hidden, d_inputs = owner_backward(dims, dx, d_rows, g_rows, ups_own, qkv_own, rows_of)
+        d_qkv, d_out = attn_products(d_qkv_rows, ctx_own, n1, d_rows, w_out.shape[I1:])
+        d_up, d_down = mlp_products(d_up_rows, hidden, n2, g_rows)
         weight_grads = (d_qkv.transpose(I3, I0, I1, I2), d_out, d_up, d_down)
         mine = jnp.sum(dg_same + dg_other, I1)
         loss = jnp.sum(loss_all) * (0.5 * norm_factor)

time: 1520 us -> 1440 us (0.947)
  the two profiles are of different devices: /device:TPU:1 before, /device:TPU:3 now
where the time goes in v6:
time: 1440 us; the launch traced here: 1420 us
  Pallas kernels  1410 us (98%)
    pallas_call x1, Pallas kernels, forward_phase(): pl.pallas_call(functools.partial(forward_kernel, dims), out_shape=tuple(o...  622 us
    pallas_call x1, Pallas kernels, backward_phase(): pl.pallas_call(functools.partial(backward_kernel, dims), out_shape=tuple(...  368 us
    pallas_call x1, Pallas kernels, owner_backward(): pl.pallas_call(functools.partial(owner_backward_kernel, dims), grid=(step...  152 us
    pallas_call x2, Pallas kernels, owner_recompute(): pl.pallas_call(functools.partial(recompute_kernel, dims, early), out_shap...  128 us
    pallas_call x1, Pallas kernels, mlp_products(): pl.pallas_call(mlp_products_kernel, grid=(cols // SUB,), out_shape=(jax.S...  86.6 us
    pallas_call x1, Pallas kernels, attn_products(): pl.pallas_call(attn_products_kernel, grid=(pairs,), out_shape=(jax.ShapeD...  51.4 us

profile of v6, /device:TPU:3, one launch (start us, length us, event | category | flops | bytes accessed | tf_op | source)
XLA Modules:
  0.0 1422.9 jit_solution(11997212620645416629)
XLA Ops:
  0.6 1.3 maximum_convert_fusion.own_gains.gains
  2.0 622.2 %forward_phase.1 = (bf16[8,192,1536]{2,1,0:T(8,128)(2,1)}, bf16[8,192,1536]{2,1,0:T(8,128)(2,1)}, bf16[8,192,6144]{2,1,0:T(8,128)(2,1)}, bf16[8,192,6144]{2,1,0:...) custom-call(bf16[8,2,192,1536]{3,2,1,0:T(8,128)(2,1)} %x_ref.1, ...), custom_call_target="tpu_custom_call" | custom-call | tf_op jit(solution)/shard_map/forward_phase/pallas_call | solution.py:926
  624.1 1.3 reduce_sum.18
  626.1 0.7 owner_recompute.2
  626.8 367.8 %backward_phase.1 = (bf16[8,192,1536]{2,1,0:T(8,128)(2,1)}, bf16[8,192,1536]{2,1,0:T(8,128)(2,1)}, bf16[8,192,1536]{2,1,0:T(8,128)(2,1)}, bf16[8,192,1536]{2,1,0...) custom-call(bf16[8,192,1536]{2,1,0:T(8,128)(2,1)} %get-tuple-element, ...), custom_call_target="tpu_custom_call", output_to_operand_aliasing={{6}: (16, {}), {7}: (17, {})} | custom-call | tf_op jit(solution)/shard_map/backward_phase/pallas_call | solution.py:951
  994.6 127.4 %owner_recompute.3 = (f32[8,128]{1,0:T(8,128)}, bf16[3072,3072]{1,0:T(8,128)(2,1)}, bf16[3072,3072]{1,0:T(8,128)(2,1)}, bf16[3072,1024]{1,0:T(8,128)(2,1)}, bf16...) custom-call(bf16[1536,1536]{1,0:T(8,128)(2,1)} %bitcast.43, ...), custom_call_target="tpu_custom_call", output_to_operand_aliasing={{1}: (7, {}), {2}: (8, {}), {3}: (9, {}), {4}: (10, {}), {5... | custom-call | tf_op jit(solution)/shard_map/owner_recompute/pallas_call | solution.py:1024
  1122.0 1.0 add_reduce_fusion
  1123.0 0.6 fusion
  1123.6 151.8 %owner_backward.1 = (bf16[3072,3072]{1,0:T(8,128)(2,1)}, bf16[3072,3072]{1,0:T(8,128)(2,1)}, bf16[3072,3072]{1,0:T(8,128)(2,1)}, bf16[8,2,192,1536]{3,2,1,0:T(8,128)(2,1)}) custom-call(bf16[8,192,1536]{2,1,0:T(8,128)(2,1)} %get-tuple-element.75.dx, bf16[1536,1536]{1,0:T(8,128)(2,1)} %bitcast.46, bf16[1536,1536]{1,0:T(8,128)(2,1)} %bitcast.48, ...), custom_call_target="tpu_custom_call" | custom-call | tf_op jit(solution)/shard_map/owner_backward/pallas_call | solution.py:1179
  1275.4 51.4 %attn_products.1 = (f32[3,8,96,1536]{3,2,1,0:T(8,128)}, f32[8,96,1536]{2,1,0:T(8,128)}) custom-call(bf16[3072,3072]{1,0:T(8,128)(2,1)} %get-tuple-element.90.dq.dk.dv, bf16[3072,3072]{1,0:T(8,128)(2,1)} %get-tuple-element.90.dq.dk.dv, bf16[3072,3072]{1,0:T(8,128)(2,1)} %get-tuple-element.90.dq.dk.dv, bf16[3072,1024]{1,0:T(8,128)(2,1)} %get-tuple-element.91.ctx, ...), custom_call_target="tpu_custom_call" | custom-call | tf_op jit(solution)/shard_map/attn_products/pallas_call | solution.py:1230
  1326.8 86.6 %mlp_products.1 = (f32[1536,3072]{1,0:T(8,128)}, f32[3072,1536]{1,0:T(8,128)}) custom-call(bf16[3072,3072]{1,0:T(8,128)(2,1)} %get-tuple-element.95.dup, bf16[3072,3072]{1,0:T(8,128)(2,1)} %get-tuple-element.96.z, bf16[3072,1536]{1,0:T(8,128)(2,1)} %get-tuple-element.97.n2_o, bf16[1536,1536]{1,0:T(8,128)(2,1)} %bitcast.39, bf16[1536,1536]{1,0:T(8,128)(2,1)} %bitcast.41), custom_call_target="tpu_custom_call" | custom-call | tf_op jit(solution)/shard_map/mlp_products/pallas_call | solution.py:1272
  1413.5 8.3 copy.31

commit v7 on v6

--- a/solution.py
+++ b/solution.py
@@ -21,8 +21,8 @@
 BLOCK = 384
 SUB = 256
 DEPTH = 6
-BACK_DEPTH = 4
-KDEPTH = 2
+BACK_DEPTH = 6
+KDEPTH = 3
 HEAD_PAD = 128
 VMEM_LIMIT = 67043328
 
@@ -63,15 +63,6 @@
     @property
     def across_other(self):
         return self.at(I1 - self.tp, self.sib)
-
-    def others(self, src, dst, send_sems, recv_sem):
-        copies = []
-        for d_tp in (I0, I1):
-            for d_stage in range(I4):
-                if d_tp or d_stage:
-                    there = self.at(self.tp + d_tp - I2 * d_tp * self.tp, (self.stage + d_stage) % I4)
-                    copies.append(remote(src, dst, send_sems.at[len(copies)], recv_sem, there))
-        return copies
 
     def chain(self, delta):
         there = self.home + delta
@@ -196,8 +187,7 @@
 
     def copy_in(self, ref, index, slot):
         if not self.by_heads:
-            where = pl.ds(pl.multiple_of(index * CHUNK, CHUNK), CHUNK)
-            pltpu.make_async_copy(ref.at[:, where], self.buf.at[slot], self.sem.at[slot]).start()
+            pltpu.make_async_copy(ref.at[index], self.buf.at[slot], self.sem.at[slot]).start()
             return
         load_heads(ref, index, self.buf.at[slot], self.sem.at[slot])
 
@@ -227,7 +217,7 @@
         if self.by_heads:
             pltpu.make_async_copy(ref.at[I0:768, :], self.buf.at[slot, I0:768, :], self.sem.at[slot]).wait()
         else:
-            pltpu.make_async_copy(ref.at[:, I0:CHUNK], self.buf.at[slot], self.sem.at[slot]).wait()
+            pltpu.make_async_copy(ref.at[I0], self.buf.at[slot], self.sem.at[slot]).wait()
         return self.buf.at[slot]
 
 
@@ -238,7 +228,7 @@
     return ref.at[index * 768:(index + I1) * 768, :] if axis == I0 else ref.at[:, index * 768:(index + I1) * 768]
 
 
-def weight_phase(place, is_r, own, near, far, turned, wn, wk, send_sem, y_send, d_send, near_sem, far_sem, load_sem, store_sem):
+def weight_phase(place, is_r, own, near, far, turned, up_chunks, wn, wk, send_sem, y_send, d_send, near_sem, far_sem, load_sem, store_sem, chunk_sem):
     wk[...] = jnp.zeros_like(wk)
 
     @pl.when(place.is_l)
@@ -281,18 +271,29 @@
         if i == I2:
             rows = pl.ds(pl.multiple_of(t * SUB, SUB), SUB)
             return pltpu.make_async_copy(wk.at[I1, pl.ds(slot * SUB, SUB), :], dst.at[rows, :], store_sem.at[slot])
-        return pltpu.make_async_copy(wn.at[slot, :, SUB:512], dst.at[:, lanes(t * SUB, SUB)], store_sem.at[slot])
-
-    def turn(i, refs, dst, first, count):
+        return pltpu.make_async_copy(wn.at[slot, :, SUB:512], dst.at[t // I4, :, lanes(t % I4 * SUB, SUB)], store_sem.at[slot])
+
+    def keep(which, t, slot):
+        return pltpu.make_async_copy(wn.at[slot, :, I0:SUB], up_chunks[which].at[t // I4, :, lanes(t % I4 * SUB, SUB)], chunk_sem.at[slot])
+
+    def turn(i, refs, which, first, count):
+        dst = turned[i][which]
         load(i, refs, first, I0)
 
         def step(n, c):
             slot = n % I2
+
+            if i == I2:
+                @pl.when(n > I0)
+                def _():
+                    keep(which, first + n - I1, I1 - slot).wait()
 
             @pl.when(n + I1 < count)
             def _():
                 load(i, refs, first + n + I1, I1 - slot)
             loaded(i, refs, slot)
+            if i == I2:
+                keep(which, first + n, slot).start()
 
             @pl.when(n >= I2)
             def _():
@@ -309,13 +310,15 @@
         lax.fori_loop(I0, count, step, I0)
         for n in (count - I2, count - I1):
             store(i, dst, first + n, n % I2).wait()
+        if i == I2:
+            keep(which, first + count - I1, (count - I1) % I2).wait()
 
     counts = (12, I4, 12, 12)
     for i in range(I4):
         @pl.when(is_r)
         def _(i=i):
             remote(near[i], near[i], send_sem.at[i], near_sem.at[i], place.sibling).wait_recv()
-        turn(i, [(place.is_l, own[i]), (is_r, near[i])], turned[i][I0], I0, counts[i])
+        turn(i, [(place.is_l, own[i]), (is_r, near[i])], I0, I0, counts[i])
     done = [I0, I0, I0, I0]
     for c, (i, axis, index) in enumerate(PIECES):
         view = piece(far[i], axis, index)
@@ -325,7 +328,7 @@
         def _(i=i, c=c, view=view):
             remote(view, view, d_send.at[i], far_sem.at[c], place.sibling).start()
         count = I4 if i < I2 else I3
-        turn(i, [(None, far[i])], turned[i][I1], done[i], count)
+        turn(i, [(None, far[i])], I1, done[i], count)
         done[i] += count
 
     @pl.when(place.is_l)
@@ -345,12 +348,12 @@
 
 
 def forward_kernel(dims, x_ref, y_ref, wq, wo, wu, wd, own_gains,
-                   a_s, h_s, qkv_s, u_s, g_s, oh_same, oh_other, oa_same, oa_other, loss_all, home_gains,
-                   nq, no, nu, nd, fq, fo, fu, fd, tq0, to0, tu0, td0, tq1, to1, tu1, td1,
+                   a_s, h_s, qkv_s, u_s, g_s, oh_same, oh_other, oa_same, oa_other, og_same, og_other, loss_s, home_gains,
+                   nq, no, nu, nd, fq, fo, fu, fd, tq0, to0, tu0, td0, tq1, to1, tu1, td1, uc0, uc1,
                    abuf, hbuf, obuf, nbuf, ybuf, sbuf, qkvbuf, ubuf, zbuf, ctxbuf, acc, lossbuf, losstile, gains, wres, wores, wn,
-                   send_sem, y_send, d_send, near_sem, far_sem, t_load, t_store,
+                   send_sem, y_send, d_send, near_sem, far_sem, t_load, t_store, t_keep,
                    act_sem, hop_f, keep_sem, save_sem, stream_n, res_sem, out_sem, big_sem, y_sem, s_sem,
-                   os_sem, oo_sem, as_sem, ao_sem, bulk, gain_sem, tiny, loss_send):
+                   os_sem, oo_sem, as_sem, ao_sem, gs_sem, go_sem, bulk, gain_sem, tiny):
     micro, seq, width, heads, head_dim, ffn = dims
     place = Place()
     is_first, is_last = place.home == I0, place.home == I3
@@ -373,7 +376,7 @@
     def _():
         for m in range(micro):
             pltpu.make_async_copy(x_ref.at[m, place.core], abuf.at[m], act_sem.at[m]).start()
-    weight_phase(place, is_r, own, near, far, turned, wn, wores, send_sem, y_send, d_send, near_sem, far_sem, t_load, t_store)
+    weight_phase(place, is_r, own, near, far, turned, (uc0, uc1), wn, wores, send_sem, y_send, d_send, near_sem, far_sem, t_load, t_store, t_keep)
     pltpu.make_async_copy(own_gains, gains, gain_sem.at[I0]).wait()
     pltpu.make_async_copy(gains, home_gains, gain_sem.at[I0]).start()
 
@@ -387,7 +390,7 @@
     def saved(dst, index):
         return pltpu.make_async_copy(hbuf, dst, save_sem.at[index])
 
-    sn = Stream(wn, stream_n, DEPTH, [([(None, tq0)], I3), ([(None, tq1)], I3), (near_of(I2), I3), ([(None, fu)], I3)], micro * 12, False)
+    sn = Stream(wn, stream_n, DEPTH, [([(None, tq0)], I3), ([(None, tq1)], I3), ([(None, uc0)], I3), ([(None, uc1)], I3)], micro * 12, False)
     for c, choices in enumerate((near_of(I1), [(None, fo)])):
         for condition, ref in choices:
             def go(ref=ref, c=c):
@@ -431,6 +434,17 @@
 
     def seed_out(m):
         return pltpu.make_async_copy(sbuf, g_s.at[m], s_sem)
+
+    def send_seed(m):
+        seed_out(m).wait()
+
+        @pl.when(place.is_l)
+        def _():
+            remote(g_s.at[m], og_same.at[m], bulk.at[I1], gs_sem, place.across).start()
+
+        @pl.when(is_r)
+        def _():
+            remote(g_s.at[m], og_other.at[m], bulk.at[I1], go_sem, place.across_other).start()
 
     def forward_tick(m, carry):
         act, mid, out = abuf.at[m], hbuf, obuf.at[m % I2]
@@ -540,7 +554,7 @@
 
             @pl.when(m > I0)
             def _():
-                seed_out(m).wait()
+                send_seed(m - I1)
 
             def seed(rows):
                 error = out[rows, :].astype(F32) - ybuf[rows, :].astype(F32)
@@ -577,9 +591,7 @@
         for n in range(128, width, 128):
             total = total + lossbuf[:, n:n + 128]
         losstile[...] = total
-        pltpu.make_async_copy(losstile, loss_all.at[place.core], tiny).start()
-        for index, copy in enumerate(place.others(losstile, loss_all.at[place.core], loss_send, tiny)):
-            copy.start()
+        pltpu.make_async_copy(losstile, loss_s, tiny).start()
     for copy in (qkv_out(micro - I1), up_out(micro - I1)):
         copy.wait()
 
@@ -592,9 +604,8 @@
 
     @pl.when(is_last)
     def _():
-        seed_out(micro - I1).wait()
-        for copy in place.others(losstile, loss_all.at[place.core], loss_send, tiny):
-            copy.wait_send()
+        send_seed(micro - I1)
+        pltpu.make_async_copy(losstile, loss_s, tiny).wait()
 
     @pl.when(takes_x)
     def _():
@@ -604,7 +615,15 @@
     sent, got = drain(place)
     sent(h_s, bulk.at[I2])
     got(oh_other, oo_sem)
-    got(loss_all, tiny)
+
+    @pl.when(is_last)
+    def _():
+        sent(g_s, bulk.at[I1])
+
+    @pl.when((place.home == I2) & is_r)
+    def _():
+        got(og_same, gs_sem)
+        got(og_other, go_sem)
 
     @pl.when(is_r)
     def _():
@@ -630,11 +649,11 @@
     return sent, got
 
 
-def backward_kernel(dims, a_s, h_s, qkv_s, u_s, g_s, wq, nq, fq, td0, td1, to0, to1, tu0, tu1, gains, after, oa_in_same, oa_in_other,
-                    dx_s, m_s, od_same, od_other, og_same, og_other, oa_same, oa_other, dg_same, dg_other,
-                    gbuf, hbuf, obuf, qkvbuf, ubuf, habuf, zbuf, ctxbuf, dqkvbuf, acc, accg, wres, wn, wk,
-                    grad_sem, hop_b, back_sem, save_sem, stream_n, stream_k, res_sem, load_sem,
-                    ds_sem, do_sem, gs_sem, go_sem, as_sem, ao_sem, bulk, tiny):
+def backward_kernel(dims, a_s, h_s, qkv_s, u_s, g_s, wq, nq, fq, td0, td1, to0, to1, tu0, tu1, gains, loss_s, after, *refs):
+    (dx_s, m_s, od_same, od_other, og_same, og_other, oa_same, oa_other, dg_same, dg_other, loss_all,
+     gbuf, hbuf, obuf, qkvbuf, ubuf, habuf, zbuf, ctxbuf, dqkvbuf, acc, accg, wres, wn, wk,
+     grad_sem, hop_b, back_sem, dx_sem, dx_send, save_sem, stream_n, stream_k, res_sem, load_sem,
+     ds_sem, do_sem, gs_sem, go_sem, as_sem, ao_sem, bulk, tiny, loss_sem) = refs[I4:]
     micro, seq, width, heads, head_dim, ffn = dims
     place = Place()
     is_first, is_last = place.home == I0, place.home == I3
@@ -682,11 +701,13 @@
 
     def loads(i):
         m = micro - I1 - i
-        slot = i % I2
-        return (pltpu.make_async_copy(u_s.at[m], ubuf.at[slot], load_sem.at[I0, slot]),
-                pltpu.make_async_copy(qkv_s.at[m], qkvbuf.at[slot], load_sem.at[I1, slot]),
-                pltpu.make_async_copy(h_s.at[m], habuf.at[slot, I0], load_sem.at[I2, slot]),
-                pltpu.make_async_copy(a_s.at[m], habuf.at[slot, I1], load_sem.at[I3, slot]))
+        return [pltpu.make_async_copy(src.at[m], dst, load_sem.at[k])
+                for k, (src, dst) in enumerate(((u_s, ubuf), (qkv_s, qkvbuf), (h_s, habuf.at[I0]), (a_s, habuf.at[I1])))]
+
+    def load_next(i, k):
+        @pl.when(i + I1 < micro)
+        def _():
+            loads(i + I1)[k].start()
 
     for copy in loads(I0):
         copy.start()
@@ -721,21 +742,26 @@
         @pl.when((i > I1) & is_first)
         def _():
             keep_dx(i).wait()
+            dx_to_b(i).wait_send()
 
         @pl.when((i > I1) & jnp.logical_not(is_first))
         def _():
             hop_back(i).wait_send()
+
+    def pass_loss(tile):
+        @pl.when(jnp.logical_not(is_first))
+        def _():
+            remote(tile, loss_all.at[place.core], loss_sem.at[I0], loss_sem.at[I1], place.chain(-I1)).start()
+        remote(tile, loss_all.at[place.core], loss_sem.at[I2], loss_sem.at[I3], place.sibling).start()
+
+    def dx_to_b(i):
+        return remote(obuf.at[i % I2], dx_s.at[micro - I1 - i], dx_send.at[i % I2], dx_sem, place.across)
 
     def backward_tick(i, carry):
         m = micro - I1 - i
         slot = i % I2
         grad, dmid, prev = gbuf.at[m], hbuf, obuf.at[slot]
-        u_now, qkv_now, h_now, a_now = ubuf.at[slot], qkvbuf.at[slot], habuf.at[slot, I0], habuf.at[slot, I1]
-
-        @pl.when(i + I1 < micro)
-        def _():
-            for copy in loads(i + I1):
-                copy.start()
+        u_now, qkv_now, h_now, a_now = ubuf, qkvbuf, habuf.at[I0], habuf.at[I1]
 
         pltpu.make_async_copy(g_s.at[m], grad, grad_sem.at[m]).wait()
 
@@ -762,8 +788,10 @@
                 acc[:, n:n + SUB] += mm(zbuf[...], wres[j, :, n:n + SUB])
             return c
         lax.fori_loop(I0, I6, mlp_step, I0)
+        load_next(i, I0)
         load_h.wait()
         norm_back(I1, h_now, grad, dmid, gains[I1:I2, :])
+        load_next(i, I2)
 
         @pl.when(place.is_l)
         def _():
@@ -788,6 +816,7 @@
                     dqkvbuf[:, p] = value
             return c
         lax.fori_loop(I0, heads // I4, head_step, I0)
+        load_next(i, I1)
         acc[...] = jnp.zeros_like(acc)
 
         def qkv_step(j, c):
@@ -800,11 +829,26 @@
         load_a.wait()
         back_ready(i)
         norm_back(I0, a_now, dmid, prev, gains[I0:I1, :])
+        load_next(i, I3)
 
         @pl.when(i == I0)
         def _():
             pl.semaphore_wait(barrier, I3 + (place.home + I1) // I2 % I2)
 
+            @pl.when(is_last)
+            def _():
+                pass_loss(loss_s)
+
+            @pl.when((place.home == I2) & place.is_l)
+            def _():
+                for t in range(micro):
+                    remote(a_s.at[t], oa_same.at[t], bulk.at[I8], as_sem, place.across).start()
+
+            @pl.when((place.home == I2) & is_r)
+            def _():
+                for t in range(micro):
+                    remote(a_s.at[t], oa_other.at[t], bulk.at[I8], ao_sem, place.across_other).start()
+
         @pl.when(jnp.logical_not(is_first))
         def _():
             hop_back(i).start()
@@ -812,6 +856,7 @@
         @pl.when(is_first)
         def _():
             keep_dx(i).start()
+            dx_to_b(i).start()
         both_kinds(home13, hand_back(i), True)
 
         @pl.when(place.is_l)
@@ -826,13 +871,6 @@
             remote(m_s.at[m], od_other.at[m], bulk.at[I6], do_sem, place.sibling).start()
             remote(m_s.at[m], od_other.at[m], bulk.at[7], do_sem, place.across_other).start()
 
-        @pl.when((place.home == I2) & place.is_l)
-        def _():
-            remote(a_s.at[m], oa_same.at[m], bulk.at[I8], as_sem, place.across).start()
-
-        @pl.when((place.home == I2) & is_r)
-        def _():
-            remote(a_s.at[m], oa_other.at[m], bulk.at[I8], ao_sem, place.across_other).start()
         far_grad(m, (place.home == I1) & (i % I2 == I0))
         return carry
 
@@ -846,8 +884,20 @@
             remote(gbuf.at[m], og_other.at[m], bulk.at[I4], go_sem, place.across_other).start()
 
     lax.fori_loop(I0, micro, backward_tick, I0)
-    for i in range(micro):
-        far_grad(micro - I1 - i, is_last | (place.home == I1) if i % I2 else is_last)
+    for i in range(I1, micro, I2):
+        far_grad(micro - I1 - i, place.home == I1)
+    loss_mine = loss_all.at[place.core]
+
+    @pl.when(is_last)
+    def _():
+        own_loss = pltpu.make_async_copy(loss_s, loss_mine, loss_sem.at[I1])
+        own_loss.start()
+        own_loss.wait()
+
+    @pl.when(jnp.logical_not(is_last))
+    def _():
+        remote(loss_mine, loss_mine, loss_sem.at[I0], loss_sem.at[I1], place.sibling).wait_recv()
+        pass_loss(loss_mine)
 
     @pl.when(place.is_l)
     def _():
@@ -871,9 +921,16 @@
         sent(m_s, bulk.at[7])
         remote(accg, dg_other, tiny.at[I2], tiny.at[I4], place.sibling).wait_send()
 
-    @pl.when(home13)
+    @pl.when(place.home == I1)
     def _():
         sent(gbuf, bulk.at[I4])
+        got(dx_s, dx_sem)
+
+    @pl.when(jnp.logical_not(is_first))
+    def _():
+        remote(loss_mine, loss_mine, loss_sem.at[I0], loss_sem.at[I1], place.sibling).wait_send()
+    remote(loss_mine, loss_mine, loss_sem.at[I2], loss_sem.at[I3], place.sibling).wait_send()
+    remote(loss_mine, loss_mine, loss_sem.at[I2], loss_sem.at[I3], place.sibling).wait_recv()
 
     @pl.when(place.home == I2)
     def _():
@@ -881,7 +938,10 @@
 
     remote(accg, dg_other, tiny.at[I1], tiny.at[I4], place.sibling).wait_send()
     got(od_other, do_sem)
-    got(og_other, go_sem)
+
+    @pl.when(place.is_l | (place.home != I2))
+    def _():
+        got(og_other, go_sem)
     got(dg_same, tiny.at[I0])
     got(dg_other, tiny.at[I4])
 
@@ -889,7 +949,7 @@
     def _():
         got(od_same, ds_sem)
 
-    @pl.when(place.is_l | jnp.logical_not(home13))
+    @pl.when(place.is_l | is_first)
     def _():
         got(og_same, gs_sem)
 
@@ -908,10 +968,10 @@
     half = heads // I2 * HEAD_PAD
     act = (micro, seq, width)
     raw = [w.shape for w in own]
-    turned = [(width, I3 * half), (width, half), (ffn // I2, width), (width, ffn // I2)]
-    out_shape = shapes(act, act, (micro, seq, I6 * half), (micro, seq, ffn), *[act] * 5)
-    out_shape += [jax.ShapeDtypeStruct(s, F32) for s in ((I2, I8, 128), own_gains.shape)]
-    out_shape += shapes(*raw, *raw, *turned, *turned)
+    turned = [(I3, width, CHUNK), (I1, width, CHUNK), (ffn // I2, width), (I3, width, CHUNK)]
+    out_shape = shapes(act, act, (micro, seq, I6 * half), (micro, seq, ffn), *[act] * 7)
+    out_shape += [jax.ShapeDtypeStruct(s, F32) for s in ((I8, 128), own_gains.shape)]
+    out_shape += shapes(*raw, *raw, *turned, *turned, turned[I0], turned[I0])
     any_spec = pl.BlockSpec(memory_space=ANY)
     vmem, dma = pltpu.VMEM, pltpu.SemaphoreType.DMA
     row = vmem((seq, width), BF)
@@ -919,9 +979,9 @@
         vmem(act, BF), row, vmem((I2, seq, width), BF), row, row, row, vmem((seq, I6 * half), BF), vmem((seq, ffn), BF), vmem((seq, CHUNK), BF),
         vmem((seq, I2 * half), BF), vmem((seq, width), F32), vmem((I8, width), F32), vmem((I8, 128), F32), vmem((I2, width), F32),
         vmem((I6, CHUNK, width), BF), vmem((I2, CHUNK, width), BF), vmem((DEPTH, width, CHUNK), BF),
-        dma((I4,)), dma((I4,)), dma((I4,)), dma((I4,)), dma((12,)), dma((I2,)), dma((I2,)),
+        dma((I4,)), dma((I4,)), dma((I4,)), dma((I4,)), dma((12,)), dma((I2,)), dma((I2,)), dma((I2,)),
         dma((micro,)), dma((I2,)), dma((I2,)), dma((I3,)), dma((DEPTH,)), dma((I6,)), dma((I2,)), dma((I2,)), dma(()), dma(()),
-        dma(()), dma(()), dma(()), dma(()), dma((I4,)), dma((I2,)), dma(()), dma((7,)),
+        dma(()), dma(()), dma(()), dma(()), dma(()), dma(()), dma((I4,)), dma((I2,)), dma(()),
     ]
     return pl.pallas_call(
         functools.partial(forward_kernel, dims),
@@ -934,30 +994,30 @@
     )(x, y, *own, own_gains)
 
 
-def backward_phase(dims, saved, weights, gains, after, oa_rows):
+def backward_phase(dims, saved, weights, gains, loss, after, placed):
     micro, seq, width, heads, head_dim, ffn = dims
     half = heads // I2 * HEAD_PAD
     act = (micro, seq, width)
-    out_shape = shapes(*[act] * I8) + [jax.ShapeDtypeStruct((I2, I8, width), F32)] * I2
+    out_shape = shapes(*[act] * I8) + [jax.ShapeDtypeStruct((I2, I8, width), F32)] * I2 + [jax.ShapeDtypeStruct((I2, I8, 128), F32)]
     any_spec = pl.BlockSpec(memory_space=ANY)
     vmem, dma = pltpu.VMEM, pltpu.SemaphoreType.DMA
     scratch = [
-        vmem(act, BF), vmem((seq, width), BF), vmem((I2, seq, width), BF), vmem((I2, seq, I6 * half), BF), vmem((I2, seq, ffn), BF),
-        vmem((I2, I2, seq, width), BF), vmem((seq, CHUNK), BF), vmem((seq, I2 * half), BF), vmem((seq, I6 * half), BF), vmem((seq, width), F32),
+        vmem(act, BF), vmem((seq, width), BF), vmem((I2, seq, width), BF), vmem((seq, I6 * half), BF), vmem((seq, ffn), BF),
+        vmem((I2, seq, width), BF), vmem((seq, CHUNK), BF), vmem((seq, I2 * half), BF), vmem((seq, I6 * half), BF), vmem((seq, width), F32),
         vmem((I2, I8, width), F32), vmem((I6, CHUNK, width), BF), vmem((BACK_DEPTH, width, CHUNK), BF), vmem((KDEPTH, CHUNK, width), BF),
-        dma((micro,)), dma((I2,)), dma((I2,)), dma(()), dma((BACK_DEPTH,)), dma((KDEPTH,)), dma((I6,)), dma((I4, I2)),
-        dma(()), dma(()), dma(()), dma(()), dma(()), dma(()), dma((9,)), dma((5,)),
+        dma((micro,)), dma((I2,)), dma((I2,)), dma(()), dma((I2,)), dma(()), dma((BACK_DEPTH,)), dma((KDEPTH,)), dma((I6,)), dma((I4,)),
+        dma(()), dma(()), dma(()), dma(()), dma(()), dma(()), dma((9,)), dma((5,)), dma((I4,)),
     ]
     return pl.pallas_call(
         functools.partial(backward_kernel, dims),
         out_shape=tuple(out_shape),
-        in_specs=[any_spec] * 14 + [pl.BlockSpec(memory_space=vmem)] + [any_spec] * I3,
+        in_specs=[any_spec] * 14 + [pl.BlockSpec(memory_space=vmem)] * I2 + [any_spec] * 5,
         out_specs=(any_spec,) * len(out_shape),
         scratch_shapes=scratch,
-        input_output_aliases={16: I6, 17: 7},
+        input_output_aliases={17: I4, 18: 5, 19: I6, 20: 7},
         compiler_params=pltpu.CompilerParams(collective_id=I1, has_side_effects=True, vmem_limit_bytes=VMEM_LIMIT),
         name='backward_phase',
-    )(*saved, *weights, gains, after, *oa_rows)
+    )(*saved, *weights, gains, loss, after, *placed)
 
 
 def recompute_kernel(dims, early, h_same, h_other, a_same, a_other, gains, wq, wu, *refs):
@@ -1036,82 +1096,53 @@
 def spread_dx(step, last, dx, d_in, bounce, here_sem, parent_sem, sib_sem, send_sems):
     place = Place()
     micro = dx.shape[I0]
-    below = place.at(place.tp, (place.stage + I2) % I4)
+    along_x = place.at(place.tp, (place.stage + I2) % I4)
     barrier = pltpu.get_barrier_semaphore()
-    is_a, is_b = place.home == I0, place.home == I1
     is_leaf = place.home > I1
 
     def block(m):
         return d_in.at[m, place.core]
 
-    def hand(m, src, index, there):
-        remote(src, block(m), send_sems.at[index], sib_sem if index == I0 else parent_sem.at[m], there).start()
-
-    def arrived(m):
-        remote(block(m), block(m), send_sems.at[I0], parent_sem.at[m], place.sibling).wait_recv()
+    def to_sibling(m, src):
+        remote(src, block(m), send_sems.at[I0], sib_sem, place.sibling).start()
 
     @pl.when(step == I0)
     def _():
-        def tell(there):
-            pl.semaphore_signal(barrier, inc=I1, device_id=there, device_id_type=MESH)
-        tell(place.sibling)
-
-        @pl.when(is_b)
-        def _():
-            tell(place.across)
+        pl.semaphore_signal(barrier, inc=I1, device_id=place.sibling, device_id_type=MESH)
 
         @pl.when(is_leaf)
         def _():
-            tell(below)
-
-    @pl.when((step == I1) & is_a)
-    def _():
-        pl.semaphore_wait(barrier, I3)
+            pl.semaphore_signal(barrier, inc=I1, device_id=along_x, device_id_type=MESH)
+
+    @pl.when((step == I1) & jnp.logical_not(is_leaf))
+    def _():
+        pl.semaphore_wait(barrier, I2)
         for m in reversed(range(micro)):
-            hand(m, dx.at[m], I1, place.across)
-            hand(m, dx.at[m], I2, below)
-            hand(m, dx.at[m], I0, place.sibling)
+            remote(dx.at[m], block(m), send_sems.at[I1], parent_sem.at[m], along_x).start()
+            to_sibling(m, dx.at[m])
         pltpu.make_async_copy(dx, bounce, here_sem).start()
 
-    @pl.when((step == I2) & is_a)
+    @pl.when((step == I2) & jnp.logical_not(is_leaf))
     def _():
         pltpu.make_async_copy(dx, bounce, here_sem).wait()
         for m in range(micro):
             pltpu.make_async_copy(bounce.at[m], block(m), here_sem).start()
 
-    @pl.when((step == I2) & is_b)
-    def _():
-        pl.semaphore_wait(barrier, I2)
-
-    @pl.when((step > I2) & (step < I3 + micro // I2) & is_b)
-    def _():
-        for r in (I1, I2):
-            m = micro + I6 - I2 * step - r
-            arrived(m)
-            hand(m, block(m), I2, below)
-            hand(m, block(m), I0, place.sibling)
-
     @pl.when((step == last) & is_leaf)
     def _():
         pl.semaphore_wait(barrier, I1)
         for m in reversed(range(micro)):
-            arrived(m)
-            hand(m, block(m), I0, place.sibling)
+            remote(block(m), block(m), send_sems.at[I0], parent_sem.at[m], place.sibling).wait_recv()
+            to_sibling(m, block(m))
 
     @pl.when(step == last)
     def _():
-        def sent(index):
-            remote(dx, dx, send_sems.at[index], sib_sem, place.sibling).wait_send()
-        sent(I0)
-
-        @pl.when(is_a)
-        def _():
-            sent(I1)
+        remote(dx, dx, send_sems.at[I0], sib_sem, place.sibling).wait_send()
+
+        @pl.when(jnp.logical_not(is_leaf))
+        def _():
+            remote(dx, dx, send_sems.at[I1], sib_sem, place.sibling).wait_send()
             pltpu.make_async_copy(dx, dx, here_sem).wait()
-
-        @pl.when(jnp.logical_not(is_leaf))
-        def _():
-            sent(I2)
         remote(dx, dx, send_sems.at[I0], sib_sem, place.sibling).wait_recv()
 
 
@@ -1183,7 +1214,7 @@
         in_specs=[any_spec, low, high, low, high, block(ffn // I2), block(I3 * half), any_spec, pl.BlockSpec((ffn // I2, width), lambda i: (I0, I0))],
         out_specs=(block(I3 * half), block(ffn // I2), block(ffn // I2), any_spec),
         scratch_shapes=[vmem((BLOCK, width), BF), vmem((BLOCK, width), BF), vmem((BLOCK, half), BF), vmem((half, width), BF), vmem((micro, seq, width), BF),
-                        dma(()), dma(()), dma((micro,)), dma(()), dma((I3,))],
+                        dma(()), dma(()), dma((micro,)), dma(()), dma((I2,))],
         compiler_params=pltpu.CompilerParams(collective_id=I2, has_side_effects=True, vmem_limit_bytes=VMEM_LIMIT),
         name='owner_backward',
     )(dx, *d_rows, *g_rows, ups, qkv, own[I1], own[I3])
@@ -1300,15 +1331,15 @@
         own_gains = jnp.concatenate([gain_attn, gain_mlp]).astype(F32)
         rows_of = (own[I0].transpose(I1, I2, I3, I0).reshape(-I1, width), own[I1].reshape(-I1, width), own[I2], own[I3])
 
-        (acts, mids, qkv, ups, seeds, oh_same, oh_other, oa_same, oa_other, loss_all, home_gains, *weights) = forward_phase(dims, inputs, targets, rows_of, own_gains)
+        (acts, mids, qkv, ups, seeds, oh_same, oh_other, oa_same, oa_other, og_same, og_other, loss_tile, home_gains, *weights) = forward_phase(dims, inputs, targets, rows_of, own_gains)
         (nq, no, nu, nd), (fq, fo, fu, fd) = weights[I0:I4], weights[I4:I8]
         (tq0, to0, tu0, td0), (tq1, to1, tu1, td1) = weights[I8:12], weights[12:16]
 
         flat = lambda *rows: [r.reshape(-I1, width) for r in rows]
         h_rows = flat(oh_same, oh_other)
         done, *again = owner_recompute(dims, True, None, h_rows, flat(oa_same, oa_other), own_gains, rows_of)
-        dx, _, od_same, od_other, og_same, og_other, oa_same, oa_other, dg_same, dg_other = backward_phase(
-            dims, (acts, mids, qkv, ups, seeds), (rows_of[I0], nq, fq, td0, td1, to0, to1, tu0, tu1), home_gains, done, (oa_same, oa_other))
+        dx, _, od_same, od_other, og_same, og_other, oa_same, oa_other, dg_same, dg_other, loss_all = backward_phase(
+            dims, (acts, mids, qkv, ups, seeds), (rows_of[I0], nq, fq, td0, td1, to0, to1, tu0, tu1), home_gains, loss_tile, done, (og_same, og_other, oa_same, oa_other))
         _, *again = owner_recompute(dims, False, again, h_rows, flat(oa_same, oa_other), own_gains, rows_of)
         ups_own, qkv_own, ctx_own, n1, n2 = again
         d_rows, g_rows = flat(od_same, od_other), flat(og_same, og_other)

time: 1440 us -> 1360 us (0.944); the launches traced: 1420 us -> 1360 us
  Pallas kernels: 1410 us -> 1340 us
    pallas_call x1, Pallas kernels: 368 us -> 250 us  [backward_phase(): pl.pallas_call(functools.partial(backward_kernel, dims), out_shape=tuple(...]
    pallas_call x1, Pallas kernels: 152 us -> 194 us  [owner_backward(): pl.pallas_call(functools.partial(owner_backward_kernel, dims), grid=(step...]
where the time goes in v7:
time: 1360 us
  Pallas kernels  1340 us (99%)
    pallas_call x1, Pallas kernels, forward_phase(): pl.pallas_call(functools.partial(forward_kernel, dims), out_shape=tuple(o...  634 us
    pallas_call x1, Pallas kernels, backward_phase(): pl.pallas_call(functools.partial(backward_kernel, dims), out_shape=tuple(...  250 us
    pallas_call x1, Pallas kernels, owner_backward(): pl.pallas_call(functools.partial(owner_backward_kernel, dims), grid=(step...  194 us
    pallas_call x2, Pallas kernels, owner_recompute(): pl.pallas_call(functools.partial(recompute_kernel, dims, early), out_shap...  128 us
    pallas_call x1, Pallas kernels, mlp_products(): pl.pallas_call(mlp_products_kernel, grid=(cols // SUB,), out_shape=(jax.S...  86.6 us
    pallas_call x1, Pallas kernels, attn_products(): pl.pallas_call(attn_products_kernel, grid=(pairs,), out_shape=(jax.ShapeD...  51.4 us

profile of v7, /device:TPU:3, one launch (start us, length us, event | category | flops | bytes accessed | tf_op | source)
XLA Modules:
  0.0 1358.5 jit_solution(10470041523515155718)
XLA Ops:
  0.6 1.3 maximum_convert_fusion.own_gains.gains
  2.0 633.6 %forward_phase.1 = (bf16[8,192,1536]{2,1,0:T(8,128)(2,1)}, bf16[8,192,1536]{2,1,0:T(8,128)(2,1)}, bf16[8,192,6144]{2,1,0:T(8,128)(2,1)}, bf16[8,192,6144]{2,1,0:...) custom-call(bf16[8,2,192,1536]{3,2,1,0:T(8,128)(2,1)} %x_ref.1, ...), custom_call_target="tpu_custom_call" | custom-call | tf_op jit(solution)/shard_map/forward_phase/pallas_call | solution.py:986
  635.5 0.7 owner_recompute.2
  636.3 250.0 %backward_phase.1 = (bf16[8,192,1536]{2,1,0:T(8,128)(2,1)}, bf16[8,192,1536]{2,1,0:T(8,128)(2,1)}, bf16[8,192,1536]{2,1,0:T(8,128)(2,1)}, bf16[8,192,1536]{2,1,0...) custom-call(bf16[8,192,1536]{2,1,0:T(8,128)(2,1)} %get-tuple-element, ...), custom_call_target="tpu_custom_call", output_to_operand_aliasing={{4}: (17, {}), {5}: (18, {}), {6}: (19, {}), {7}: (20, {})} | custom-call | tf_op jit(solution)/shard_map/backward_phase/pallas_call | solution.py:1011
  886.3 127.4 %owner_recompute.3 = (f32[8,128]{1,0:T(8,128)}, bf16[3072,3072]{1,0:T(8,128)(2,1)}, bf16[3072,3072]{1,0:T(8,128)(2,1)}, bf16[3072,1024]{1,0:T(8,128)(2,1)}, bf16...) custom-call(bf16[1536,1536]{1,0:T(8,128)(2,1)} %bitcast.47, ...), custom_call_target="tpu_custom_call", output_to_operand_aliasing={{1}: (7, {}), {2}: (8, {}), {3}: (9, {}), {4}: (10, {}), {5... | custom-call | tf_op jit(solution)/shard_map/owner_recompute/pallas_call | solution.py:1084
  1013.7 1.3 reduce_sum.18
  1015.6 1.0 add_reduce_fusion
  1016.6 0.6 fusion
  1017.2 193.8 %owner_backward.1 = (bf16[3072,3072]{1,0:T(8,128)(2,1)}, bf16[3072,3072]{1,0:T(8,128)(2,1)}, bf16[3072,3072]{1,0:T(8,128)(2,1)}, bf16[8,2,192,1536]{3,2,1,0:T(8,128)(2,1)}) custom-call(bf16[8,192,1536]{2,1,0:T(8,128)(2,1)} %get-tuple-element.81.dx, bf16[1536,1536]{1,0:T(8,128)(2,1)} %bitcast.42, bf16[1536,1536]{1,0:T(8,128)(2,1)} %bitcast.44, ...), custom_call_target="tpu_custom_call" | custom-call | tf_op jit(solution)/shard_map/owner_backward/pallas_call | solution.py:1210
  1211.0 51.4 %attn_products.1 = (f32[3,8,96,1536]{3,2,1,0:T(8,128)}, f32[8,96,1536]{2,1,0:T(8,128)}) custom-call(bf16[3072,3072]{1,0:T(8,128)(2,1)} %get-tuple-element.96.dq.dk.dv, bf16[3072,3072]{1,0:T(8,128)(2,1)} %get-tuple-element.96.dq.dk.dv, bf16[3072,3072]{1,0:T(8,128)(2,1)} %get-tuple-element.96.dq.dk.dv, bf16[3072,1024]{1,0:T(8,128)(2,1)} %get-tuple-element.97.ctx, ...), custom_call_target="tpu_custom_call" | custom-call | tf_op jit(solution)/shard_map/attn_products/pallas_call | solution.py:1261
  1262.5 86.6 %mlp_products.1 = (f32[1536,3072]{1,0:T(8,128)}, f32[3072,1536]{1,0:T(8,128)}) custom-call(bf16[3072,3072]{1,0:T(8,128)(2,1)} %get-tuple-element.101.dup, bf16[3072,3072]{1,0:T(8,128)(2,1)} %get-tuple-element.102.z, bf16[3072,1536]{1,0:T(8,128)(2,1)} %get-tuple-element.103.n2_o, bf16[1536,1536]{1,0:T(8,128)(2,1)} %bitcast.37, bf16[1536,1536]{1,0:T(8,128)(2,1)} %bitcast.39), custom_call_target="tpu_custom_call" | custom-call | tf_op jit(solution)/shard_map/mlp_products/pallas_call | solution.py:1303
  1349.1 8.3 copy.35

commit v8 on v7

--- a/solution.py
+++ b/solution.py
@@ -23,6 +23,7 @@
 DEPTH = 6
 BACK_DEPTH = 6
 KDEPTH = 3
+EARLY_G = 3
 HEAD_PAD = 128
 VMEM_LIMIT = 67043328
 
@@ -358,6 +359,7 @@
     place = Place()
     is_first, is_last = place.home == I0, place.home == I3
     home02 = (place.home == I0) | (place.home == I2)
+    home13 = jnp.logical_not(home02)
     is_r = jnp.logical_not(place.is_l)
     takes_x = (place.home == I1) & is_r
     half = heads // I2 * HEAD_PAD
@@ -435,6 +437,15 @@
     def seed_out(m):
         return pltpu.make_async_copy(sbuf, g_s.at[m], s_sem)
 
+    def far_mid(m, condition):
+        @pl.when(condition & place.is_l)
+        def _():
+            remote(h_s.at[m], oh_same.at[m], bulk.at[I2], os_sem, place.across).start()
+
+        @pl.when(condition & is_r)
+        def _():
+            remote(h_s.at[m], oh_other.at[m], bulk.at[I2], oo_sem, place.across_other).start()
+
     def send_seed(m):
         seed_out(m).wait()
 
@@ -575,15 +586,17 @@
         @pl.when(place.is_l)
         def _():
             saved(oh_same.at[m], I1).wait()
-            remote(h_s.at[m], oh_same.at[m], bulk.at[I2], os_sem, place.across).start()
 
         @pl.when(is_r)
         def _():
-            remote(h_s.at[m], oh_other.at[m], bulk.at[I2], oo_sem, place.sibling).start()
-            remote(h_s.at[m], oh_other.at[m], bulk.at[I3], oo_sem, place.across_other).start()
+            remote(h_s.at[m], oh_other.at[m], bulk.at[I3], oo_sem, place.sibling).start()
+
+        far_mid(m, home13 | (m % I2 == I1))
         return carry
 
     lax.fori_loop(I0, micro, forward_tick, I0)
+    for m in range(I0, micro, I2):
+        far_mid(m, home02)
 
     @pl.when(is_last)
     def _():
@@ -871,7 +884,7 @@
             remote(m_s.at[m], od_other.at[m], bulk.at[I6], do_sem, place.sibling).start()
             remote(m_s.at[m], od_other.at[m], bulk.at[7], do_sem, place.across_other).start()
 
-        far_grad(m, (place.home == I1) & (i % I2 == I0))
+        far_grad(m, (place.home == I1) & (i % I2 == I1) & (i < I2 * EARLY_G))
         return carry
 
     def far_grad(m, condition):
@@ -884,8 +897,6 @@
             remote(gbuf.at[m], og_other.at[m], bulk.at[I4], go_sem, place.across_other).start()
 
     lax.fori_loop(I0, micro, backward_tick, I0)
-    for i in range(I1, micro, I2):
-        far_grad(micro - I1 - i, place.home == I1)
     loss_mine = loss_all.at[place.core]
 
     @pl.when(is_last)
@@ -923,7 +934,7 @@
 
     @pl.when(place.home == I1)
     def _():
-        sent(gbuf, bulk.at[I4])
+        sent(gbuf.at[I0:EARLY_G], bulk.at[I4])
         got(dx_s, dx_sem)
 
     @pl.when(jnp.logical_not(is_first))
@@ -939,9 +950,14 @@
     remote(accg, dg_other, tiny.at[I1], tiny.at[I4], place.sibling).wait_send()
     got(od_other, do_sem)
 
-    @pl.when(place.is_l | (place.home != I2))
+    @pl.when(place.is_l | home13)
     def _():
         got(og_other, go_sem)
+
+    @pl.when(is_first & is_r)
+    def _():
+        got(og_same.at[I0:EARLY_G], gs_sem)
+        got(og_other.at[I0:EARLY_G], go_sem)
     got(dg_same, tiny.at[I0])
     got(dg_other, tiny.at[I4])
 
@@ -949,7 +965,7 @@
     def _():
         got(od_same, ds_sem)
 
-    @pl.when(place.is_l | is_first)
+    @pl.when(place.is_l)
     def _():
         got(og_same, gs_sem)
 
@@ -1093,12 +1109,15 @@
     )(*h_rows, *a_rows, gains, own[I0], own[I2], *earlier)
 
 
-def spread_dx(step, last, dx, d_in, bounce, here_sem, parent_sem, sib_sem, send_sems):
+def spread_dx(step, last, dx, d_in, og_same, og_other, bounce, here_sem, parent_sem, sib_sem, send_sems, og_sems):
     place = Place()
     micro = dx.shape[I0]
     along_x = place.at(place.tp, (place.stage + I2) % I4)
     barrier = pltpu.get_barrier_semaphore()
     is_leaf = place.home > I1
+    gives_g = (place.home == I1) & place.is_l
+    takes_g = (place.home == I0) & jnp.logical_not(place.is_l)
+    late = [micro - I1 - i for i in range(micro) if i % I2 == I0 or i > I2 * EARLY_G]
 
     def block(m):
         return d_in.at[m, place.core]
@@ -1106,17 +1125,30 @@
     def to_sibling(m, src):
         remote(src, block(m), send_sems.at[I0], sib_sem, place.sibling).start()
 
+    def tell(there):
+        pl.semaphore_signal(barrier, inc=I1, device_id=there, device_id_type=MESH)
+
     @pl.when(step == I0)
     def _():
-        pl.semaphore_signal(barrier, inc=I1, device_id=place.sibling, device_id_type=MESH)
+        tell(place.sibling)
 
         @pl.when(is_leaf)
         def _():
-            pl.semaphore_signal(barrier, inc=I1, device_id=along_x, device_id_type=MESH)
+            tell(along_x)
+
+        @pl.when(takes_g)
+        def _():
+            tell(place.across)
 
     @pl.when((step == I1) & jnp.logical_not(is_leaf))
     def _():
-        pl.semaphore_wait(barrier, I2)
+        pl.semaphore_wait(barrier, I2 + gives_g.astype(jnp.int32))
+
+        @pl.when(gives_g)
+        def _():
+            for t, og in enumerate((og_same, og_other)):
+                for m in late:
+                    remote(og.at[m], og.at[m], og_sems.at[t], og_sems.at[I2 + t], place.across).start()
         for m in reversed(range(micro)):
             remote(dx.at[m], block(m), send_sems.at[I1], parent_sem.at[m], along_x).start()
             to_sibling(m, dx.at[m])
@@ -1128,6 +1160,12 @@
         for m in range(micro):
             pltpu.make_async_copy(bounce.at[m], block(m), here_sem).start()
 
+    @pl.when((step == (last + I1) // I2) & takes_g)
+    def _():
+        for t, og in enumerate((og_same, og_other)):
+            part = og.at[I0:len(late)]
+            remote(part, part, og_sems.at[t], og_sems.at[I2 + t], place.across).wait_recv()
+
     @pl.when((step == last) & is_leaf)
     def _():
         pl.semaphore_wait(barrier, I1)
@@ -1143,81 +1181,114 @@
         def _():
             remote(dx, dx, send_sems.at[I1], sib_sem, place.sibling).wait_send()
             pltpu.make_async_copy(dx, dx, here_sem).wait()
+
+        @pl.when(gives_g)
+        def _():
+            for t, og in enumerate((og_same, og_other)):
+                part = og.at[I0:len(late)]
+                remote(part, part, og_sems.at[t], og_sems.at[I2 + t], place.across).wait_send()
         remote(dx, dx, send_sems.at[I0], sib_sem, place.sibling).wait_recv()
 
 
-def owner_backward_kernel(dims, dx, ds, do, gs, go, u, qkv, wo, wd, dqkv, dup, z, d_in,
-                          dmid, grad, dctx, wobuf, bounce, sem, here_sem, parent_sem, sib_sem, send_sems):
+def owner_backward_kernel(dims, dx, ds, do, u, qkv, wo, wd, gs_in, go_in, dqkv, dup, z, d_in, og_same, og_other,
+                          dmid, gbuf, dctx, wobuf, bounce, sem, g_sem, here_sem, parent_sem, sib_sem, send_sems, og_sems):
     micro, seq, width, heads, head_dim, ffn = dims
     half = heads // I2 * HEAD_PAD
     scale = head_dim ** -0.5
     step, steps = pl.program_id(I0), pl.num_programs(I0)
-    spread_dx(step, steps - I1, dx, d_in, bounce, here_sem, parent_sem, sib_sem, send_sems)
+    blocks = steps // I2
+    spread_dx(step, steps - I1, dx, d_in, og_same, og_other, bounce, here_sem, parent_sem, sib_sem, send_sems, og_sems)
 
     @pl.when(step == I0)
     def _():
         wobuf[...] = jnp.zeros_like(wobuf)
         load_heads(wo, I0, wobuf, sem)
         pltpu.make_async_copy(wo, wobuf.at[I0:wo.shape[I0]], sem).wait()
-    for near, far, dst in ((ds, do, dmid), (gs, go, grad)):
-        @pl.when(step < steps // I2)
-        def _(near=near, dst=dst):
-            dst[...] = near[...]
-
-        @pl.when(step >= steps // I2)
-        def _(far=far, dst=dst):
-            dst[...] = far[...]
-
-    def ctx_step(j, c):
-        rows = pl.ds(pl.multiple_of(j * SUB, SUB), SUB)
-        dctx[:, lanes(j * SUB, SUB)] = mm_nt(dmid[...], wobuf[rows, :]).astype(BF)
-        return c
-    lax.fori_loop(I0, half // SUB, ctx_step, I0)
-
-    def mlp_step(j, c):
-        rows = pl.ds(pl.multiple_of(j * SUB, SUB), SUB)
-        cols = lanes(j * SUB, SUB)
-        dz = mm_nt(grad[...], wd[rows, :]).astype(BF).astype(F32)
-        up = u[:, cols].astype(F32)
-        gate, up2 = gelu_gate(up)
-        hidden = up * gate
-        z[:, cols] = hidden.astype(BF)
-        dup[:, cols] = (dz * gelu_slope(hidden, gate, up2)).astype(BF)
-        return c
-    lax.fori_loop(I0, ffn // I2 // SUB, mlp_step, I0)
-
-    def head_step(j, c):
-        base = j * (I2 * HEAD_PAD)
-        at = [(pl.ds(s, seq), base + r * HEAD_PAD) for s in range(I0, BLOCK, seq) for r in range(I2)]
-        group = [(*(qkv[rows, lanes(t * half + col, HEAD_PAD)] for t in range(I3)), dctx[rows, lanes(col, HEAD_PAD)]) for rows, col in at]
-        for (rows, col), grads in zip(at, attention_backward(group, scale)):
-            for t, value in enumerate(grads):
-                dqkv[rows, lanes(t * half + col, HEAD_PAD)] = value
-        return c
-    lax.fori_loop(I0, heads // I4, head_step, I0)
-
-
-def owner_backward(dims, dx, d_rows, g_rows, ups, qkv, own):
+
+    def g_load(n, start):
+        rows = BLOCK // seq
+        for og, low in ((og_same, I0), (og_other, blocks // I2)):
+            @pl.when((n >= low) & (n < low + blocks // I2))
+            def _(og=og, low=low):
+                copy = pltpu.make_async_copy(og.at[pl.ds((n - low) * rows, rows)], gbuf.at[n % I2], g_sem.at[n % I2])
+                copy.start() if start else copy.wait()
+
+    @pl.when(step < blocks)
+    def _():
+        @pl.when(step < blocks // I2)
+        def _():
+            dmid[...] = ds[...]
+
+        @pl.when(step >= blocks // I2)
+        def _():
+            dmid[...] = do[...]
+
+        def ctx_step(j, c):
+            rows = pl.ds(pl.multiple_of(j * SUB, SUB), SUB)
+            dctx[:, lanes(j * SUB, SUB)] = mm_nt(dmid[...], wobuf[rows, :]).astype(BF)
+            return c
+        lax.fori_loop(I0, half // SUB, ctx_step, I0)
+
+        def head_step(j, c):
+            base = j * (I2 * HEAD_PAD)
+            at = [(pl.ds(s, seq), base + r * HEAD_PAD) for s in range(I0, BLOCK, seq) for r in range(I2)]
+            group = [(*(qkv[rows, lanes(t * half + col, HEAD_PAD)] for t in range(I3)), dctx[rows, lanes(col, HEAD_PAD)]) for rows, col in at]
+            for (rows, col), grads in zip(at, attention_backward(group, scale)):
+                for t, value in enumerate(grads):
+                    dqkv[rows, lanes(t * half + col, HEAD_PAD)] = value
+            return c
+        lax.fori_loop(I0, heads // I4, head_step, I0)
+
+    @pl.when(step == blocks)
+    def _():
+        g_load(step - blocks, True)
+
+    @pl.when(step >= blocks)
+    def _():
+        n = step - blocks
+        g_load(n + I1, True)
+        g_load(n, False)
+        grad = gbuf.at[n % I2]
+
+        def mlp_step(j, c):
+            rows = pl.ds(pl.multiple_of(j * SUB, SUB), SUB)
+            cols = lanes(j * SUB, SUB)
+            dz = mm_nt(grad[...].reshape(BLOCK, width), wd[rows, :]).astype(BF).astype(F32)
+            up = u[:, cols].astype(F32)
+            gate, up2 = gelu_gate(up)
+            hidden = up * gate
+            z[:, cols] = hidden.astype(BF)
+            dup[:, cols] = (dz * gelu_slope(hidden, gate, up2)).astype(BF)
+            return c
+        lax.fori_loop(I0, ffn // I2 // SUB, mlp_step, I0)
+
+
+def owner_backward(dims, dx, d_rows, og, ups, qkv, own):
     micro, seq, width, heads, head_dim, ffn = dims
     half = heads // I2 * HEAD_PAD
     tokens = I2 * micro * seq
-    steps = tokens // BLOCK
+    blocks = tokens // BLOCK
     vmem, dma = pltpu.VMEM, pltpu.SemaphoreType.DMA
     any_spec = pl.BlockSpec(memory_space=ANY)
-    low = pl.BlockSpec((BLOCK, width), lambda i: (jnp.minimum(i, steps // I2 - I1), I0))
-    high = pl.BlockSpec((BLOCK, width), lambda i: (jnp.maximum(i - steps // I2, I0), I0))
-    block = lambda n: pl.BlockSpec((BLOCK, n), lambda i: (i, I0))
+    first = lambda i: jnp.minimum(i, blocks - I1)
+    second = lambda i: jnp.maximum(i - blocks, I0)
+    low = pl.BlockSpec((BLOCK, width), lambda i: (jnp.minimum(i, blocks // I2 - I1), I0))
+    high = pl.BlockSpec((BLOCK, width), lambda i: (jnp.maximum(first(i) - blocks // I2, I0), I0))
+    attn_block = pl.BlockSpec((BLOCK, I3 * half), lambda i: (first(i), I0))
+    mlp_block = pl.BlockSpec((BLOCK, ffn // I2), lambda i: (second(i), I0))
+    act = (micro, seq, width)
     return pl.pallas_call(
         functools.partial(owner_backward_kernel, dims),
-        grid=(steps,),
-        out_shape=tuple(shapes((tokens, I3 * half), (tokens, ffn // I2), (tokens, ffn // I2), (micro, I2, seq, width))),
-        in_specs=[any_spec, low, high, low, high, block(ffn // I2), block(I3 * half), any_spec, pl.BlockSpec((ffn // I2, width), lambda i: (I0, I0))],
-        out_specs=(block(I3 * half), block(ffn // I2), block(ffn // I2), any_spec),
-        scratch_shapes=[vmem((BLOCK, width), BF), vmem((BLOCK, width), BF), vmem((BLOCK, half), BF), vmem((half, width), BF), vmem((micro, seq, width), BF),
-                        dma(()), dma(()), dma((micro,)), dma(()), dma((I2,))],
+        grid=(I2 * blocks,),
+        out_shape=tuple(shapes((tokens, I3 * half), (tokens, ffn // I2), (tokens, ffn // I2), (micro, I2, seq, width), act, act)),
+        in_specs=[any_spec, low, high, mlp_block, attn_block, any_spec, pl.BlockSpec((ffn // I2, width), lambda i: (I0, I0)), any_spec, any_spec],
+        out_specs=(attn_block, mlp_block, mlp_block, any_spec, any_spec, any_spec),
+        scratch_shapes=[vmem((BLOCK, width), BF), vmem((I2, BLOCK // seq, seq, width), BF), vmem((BLOCK, half), BF), vmem((half, width), BF), vmem(act, BF),
+                        dma(()), dma((I2,)), dma(()), dma((micro,)), dma(()), dma((I2,)), dma((I4,))],
+        input_output_aliases={7: I4, I8: 5},
         compiler_params=pltpu.CompilerParams(collective_id=I2, has_side_effects=True, vmem_limit_bytes=VMEM_LIMIT),
         name='owner_backward',
-    )(dx, *d_rows, *g_rows, ups, qkv, own[I1], own[I3])
+    )(dx, *d_rows, ups, qkv, own[I1], own[I3], *og)
 
 
 def bring(pairs, sem):
@@ -1228,12 +1299,27 @@
         copy.wait()
 
 
-def attn_products_kernel(dq, dk, dv, ctx, n1_o, ds, do, dwq, dwo, n1, dmid, dqkvt, ctxt, sem):
+def attn_products_kernel(dq, dk, dv, ctx, n1_o, ds, do, dx_in, dwq, dwo, dx_out, n1, dmid, dqkvt, ctxt, bounce, sem, dx_sem):
     tokens, width = n1.shape
     part = tokens // I2
     head_dim = dwo.shape[I1]
-
-    @pl.when(pl.program_id(I0) == I0)
+    step, last = pl.program_id(I0), pl.num_programs(I0) - I1
+    into, out_of = pltpu.make_async_copy(dx_in, bounce, dx_sem), pltpu.make_async_copy(bounce, dx_out, dx_sem)
+
+    @pl.when(step == I1)
+    def _():
+        into.start()
+
+    @pl.when(step == I2)
+    def _():
+        into.wait()
+        out_of.start()
+
+    @pl.when(step == last)
+    def _():
+        out_of.wait()
+
+    @pl.when(step == I0)
     def _():
         bring([(n1_o, n1), (ds, dmid.at[pl.ds(I0, part)]), (do, dmid.at[pl.ds(part, part)])], sem)
 
@@ -1251,7 +1337,7 @@
         dwo[:, :, cut] = mm(ctxt[...], dmid[:, cut]).reshape(I2, head_dim, SUB)
 
 
-def attn_products(dqkv, ctx, n1, d_rows, out_dims):
+def attn_products(dqkv, ctx, n1, d_rows, dx, out_dims):
     heads, head_dim, width = out_dims
     tokens = n1.shape[I0]
     vmem = pltpu.VMEM
@@ -1261,14 +1347,14 @@
     return pl.pallas_call(
         attn_products_kernel,
         grid=(pairs,),
-        out_shape=(jax.ShapeDtypeStruct((I3,) + out_dims, F32), jax.ShapeDtypeStruct(out_dims, F32)),
-        in_specs=[cols(I0), cols(I1), cols(I2), cols(I0), any_spec, any_spec, any_spec],
-        out_specs=(pl.BlockSpec((I3, I2, head_dim, width), lambda i: (I0, i, I0, I0)), pl.BlockSpec((I2, head_dim, width), lambda i: (i, I0, I0))),
+        out_shape=(jax.ShapeDtypeStruct((I3,) + out_dims, F32), jax.ShapeDtypeStruct(out_dims, F32), jax.ShapeDtypeStruct(dx.shape, BF)),
+        in_specs=[cols(I0), cols(I1), cols(I2), cols(I0), any_spec, any_spec, any_spec, any_spec],
+        out_specs=(pl.BlockSpec((I3, I2, head_dim, width), lambda i: (I0, i, I0, I0)), pl.BlockSpec((I2, head_dim, width), lambda i: (i, I0, I0)), any_spec),
         scratch_shapes=[vmem((tokens, width), BF), vmem((tokens, width), BF), vmem((I6 * head_dim, tokens), BF), vmem((I2 * head_dim, tokens), BF),
-                        pltpu.SemaphoreType.DMA((I3,))],
+                        vmem(dx.shape, BF), pltpu.SemaphoreType.DMA((I3,)), pltpu.SemaphoreType.DMA(())],
         compiler_params=pltpu.CompilerParams(vmem_limit_bytes=VMEM_LIMIT),
         name='attn_products',
-    )(dqkv, dqkv, dqkv, ctx, n1, *d_rows)
+    )(dqkv, dqkv, dqkv, ctx, n1, *d_rows, dx)
 
 
 def mlp_products_kernel(dup, z, n2_o, gs, go, dwu, dwd, n2t, grad, zt, stage, sem):
@@ -1342,10 +1428,10 @@
             dims, (acts, mids, qkv, ups, seeds), (rows_of[I0], nq, fq, td0, td1, to0, to1, tu0, tu1), home_gains, loss_tile, done, (og_same, og_other, oa_same, oa_other))
         _, *again = owner_recompute(dims, False, again, h_rows, flat(oa_same, oa_other), own_gains, rows_of)
         ups_own, qkv_own, ctx_own, n1, n2 = again
-        d_rows, g_rows = flat(od_same, od_other), flat(og_same, og_other)
-        d_qkv_rows, d_up_rows, hidden, d_inputs = owner_backward(dims, dx, d_rows, g_rows, ups_own, qkv_own, rows_of)
-        d_qkv, d_out = attn_products(d_qkv_rows, ctx_own, n1, d_rows, w_out.shape[I1:])
-        d_up, d_down = mlp_products(d_up_rows, hidden, n2, g_rows)
+        d_rows = flat(od_same, od_other)
+        d_qkv_rows, d_up_rows, hidden, dx_all, og_same, og_other = owner_backward(dims, dx, d_rows, (og_same, og_other), ups_own, qkv_own, rows_of)
+        d_qkv, d_out, d_inputs = attn_products(d_qkv_rows, ctx_own, n1, d_rows, dx_all, w_out.shape[I1:])
+        d_up, d_down = mlp_products(d_up_rows, hidden, n2, flat(og_same, og_other))
         weight_grads = (d_qkv.transpose(I3, I0, I1, I2), d_out, d_up, d_down)
         mine = jnp.sum(dg_same + dg_other, I1)
         loss = jnp.sum(loss_all) * (0.5 * norm_factor)

time: 1360 us -> 1350 us (level)
  no operation moved by 1% of the time
where the time goes in v8:
time: 1350 us
  Pallas kernels  1340 us (99%)
    pallas_call x1, Pallas kernels, forward_phase(): pl.pallas_call(functools.partial(forward_kernel, dims), out_shape=tuple(o...  638 us
    pallas_call x1, Pallas kernels, backward_phase(): pl.pallas_call(functools.partial(backward_kernel, dims), out_shape=tuple(...  258 us
    pallas_call x1, Pallas kernels, owner_backward(): pl.pallas_call(functools.partial(owner_backward_kernel, dims), grid=(I2 *...  180 us
    pallas_call x2, Pallas kernels, owner_recompute(): pl.pallas_call(functools.partial(recompute_kernel, dims, early), out_shap...  128 us
    pallas_call x1, Pallas kernels, mlp_products(): pl.pallas_call(mlp_products_kernel, grid=(cols // SUB,), out_shape=(jax.S...  86.6 us
    pallas_call x1, Pallas kernels, attn_products(): pl.pallas_call(attn_products_kernel, grid=(pairs,), out_shape=(jax.ShapeD...  51.5 us

profile of v8, /device:TPU:3, one launch (start us, length us, event | category | flops | bytes accessed | tf_op | source)
XLA Modules:
  0.0 1349.0 jit_solution(18096109835538354631)
XLA Ops:
  0.6 1.3 maximum_convert_fusion.own_gains.gains
  2.0 638.0 %forward_phase.1 = (bf16[8,192,1536]{2,1,0:T(8,128)(2,1)}, bf16[8,192,1536]{2,1,0:T(8,128)(2,1)}, bf16[8,192,6144]{2,1,0:T(8,128)(2,1)}, bf16[8,192,6144]{2,1,0:...) custom-call(bf16[8,2,192,1536]{3,2,1,0:T(8,128)(2,1)} %x_ref.1, ...), custom_call_target="tpu_custom_call" | custom-call | tf_op jit(solution)/shard_map/forward_phase/pallas_call | solution.py:1002
  640.0 0.7 owner_recompute.2
  640.7 257.7 %backward_phase.1 = (bf16[8,192,1536]{2,1,0:T(8,128)(2,1)}, bf16[8,192,1536]{2,1,0:T(8,128)(2,1)}, bf16[8,192,1536]{2,1,0:T(8,128)(2,1)}, bf16[8,192,1536]{2,1,0...) custom-call(bf16[8,192,1536]{2,1,0:T(8,128)(2,1)} %get-tuple-element, ...), custom_call_target="tpu_custom_call", output_to_operand_aliasing={{4}: (17, {}), {5}: (18, {}), {6}: (19, {}), {7}: (20, {})} | custom-call | tf_op jit(solution)/shard_map/backward_phase/pallas_call | solution.py:1027
  898.4 127.4 %owner_recompute.3 = (f32[8,128]{1,0:T(8,128)}, bf16[3072,3072]{1,0:T(8,128)(2,1)}, bf16[3072,3072]{1,0:T(8,128)(2,1)}, bf16[3072,1024]{1,0:T(8,128)(2,1)}, bf16...) custom-call(bf16[1536,1536]{1,0:T(8,128)(2,1)} %bitcast.45, ...), custom_call_target="tpu_custom_call", output_to_operand_aliasing={{1}: (7, {}), {2}: (8, {}), {3}: (9, {}), {4}: (10, {}), {5... | custom-call | tf_op jit(solution)/shard_map/owner_recompute/pallas_call | solution.py:1100
  1025.8 1.3 reduce_sum.18
  1027.7 1.0 add_reduce_fusion
  1028.7 0.6 fusion
  1029.3 180.4 %owner_backward.1 = (bf16[3072,3072]{1,0:T(8,128)(2,1)}, bf16[3072,3072]{1,0:T(8,128)(2,1)}, bf16[3072,3072]{1,0:T(8,128)(2,1)}, bf16[8,2,192,1536]{3,2,1,0:T(8,...) custom-call(bf16[8,192,1536]{2,1,0:T(8,128)(2,1)} %get-tuple-element, ...), custom_call_target="tpu_custom_call", output_to_operand_aliasing={{4}: (7, {}), {5}: (8, {})} | custom-call | tf_op jit(solution)/shard_map/owner_backward/pallas_call | solution.py:1280
  1209.7 51.5 %attn_products.1 = (f32[3,8,96,1536]{3,2,1,0:T(8,128)}, f32[8,96,1536]{2,1,0:T(8,128)}, bf16[8,2,192,1536]{3,2,1,0:T(8,128)(2,1)}) custom-call(bf16[3072,3072]{1,0:T(8,128)(2,1)} %get-tuple-element.98.dq.dk.dv, bf16[3072,3072]{1,0:T(8,128)(2,1)} %get-tuple-element.98.dq.dk.dv, bf16[3072,3072]{1,0:T(8,128)(2,1)} %get-tuple-element.98.dq.dk.dv, ...), custom_call_target="tpu_custom_call" | custom-call | tf_op jit(solution)/shard_map/attn_products/pallas_call | solution.py:1347
  1261.2 86.6 %mlp_products.1 = (f32[1536,3072]{1,0:T(8,128)}, f32[3072,1536]{1,0:T(8,128)}) custom-call(bf16[3072,3072]{1,0:T(8,128)(2,1)} %get-tuple-element.105.dup, bf16[3072,3072]{1,0:T(8,128)(2,1)} %get-tuple-element.106.z, bf16[3072,1536]{1,0:T(8,128)(2,1)} %get-tuple-element.107.n2_o, bf16[1536,1536]{1,0:T(8,128)(2,1)} %bitcast.36, bf16[1536,1536]{1,0:T(8,128)(2,1)} %bitcast.37), custom_call_target="tpu_custom_call" | custom-call | tf_op jit(solution)/shard_map/mlp_products/pallas_call | solution.py:1389

commit v9 on v8

--- a/solution.py
+++ b/solution.py
@@ -24,6 +24,8 @@
 BACK_DEPTH = 6
 KDEPTH = 3
 EARLY_G = 3
+STAGGER_NS = 6000
+EARLY_SEEDS = 5
 HEAD_PAD = 128
 VMEM_LIMIT = 67043328
 
@@ -56,6 +58,10 @@
     @property
     def sibling(self):
         return self.at(self.tp, self.sib)
+
+    @property
+    def along_x(self):
+        return self.at(self.tp, (self.stage + I2) % I4)
 
     @property
     def across(self):
@@ -225,12 +231,22 @@
 PIECES = [(0, 0, 0), (0, 0, 1), (0, 0, 2), (1, 0, 0), (2, 1, 0), (2, 1, 1), (2, 1, 2), (2, 1, 3), (3, 0, 0), (3, 0, 1), (3, 0, 2), (3, 0, 3)]
 
 
+ROUND = (10, 11)
+ROUND_STEPS = (6, 8)
+
+
 def piece(ref, axis, index):
     return ref.at[index * 768:(index + I1) * 768, :] if axis == I0 else ref.at[:, index * 768:(index + I1) * 768]
 
 
-def weight_phase(place, is_r, own, near, far, turned, up_chunks, wn, wk, send_sem, y_send, d_send, near_sem, far_sem, load_sem, store_sem, chunk_sem):
+def weight_phase(place, is_r, own, near, far, turned, up_chunks, wn, wk, send_sem, y_send, d_send, near_sem, far_sem, load_sem, store_sem, chunk_sem,
+                 round_a, round_b, ra_sem, rb_sem, x_send, xd_send, rs_send):
     wk[...] = jnp.zeros_like(wk)
+    early = place.home < I2
+
+    def piece_of(arrays, c):
+        i, axis, index = PIECES[c]
+        return piece(arrays[i], axis, index)
 
     @pl.when(place.is_l)
     def _():
@@ -239,8 +255,17 @@
 
     @pl.when(is_r)
     def _():
+        for k, c in enumerate(ROUND):
+            @pl.when(early)
+            def _(k=k, c=c):
+                remote(piece_of(own, c), round_a.at[k], x_send.at[k], ra_sem.at[k], place.along_x).start()
         for c, (i, axis, index) in enumerate(PIECES):
-            remote(piece(own[i], axis, index), piece(far[i], axis, index), y_send.at[i], far_sem.at[c], place.across_other).start()
+            if c not in ROUND:
+                remote(piece_of(own, c), piece_of(far, c), y_send.at[i], far_sem.at[c], place.across_other).start()
+        for k, c in enumerate(ROUND):
+            @pl.when(jnp.logical_not(early))
+            def _(k=k, c=c):
+                remote(piece_of(own, c), piece_of(far, c), x_send.at[k], far_sem.at[c], place.across_other).start()
 
     def load(i, refs, t, slot):
         for condition, ref in refs:
@@ -321,13 +346,30 @@
             remote(near[i], near[i], send_sem.at[i], near_sem.at[i], place.sibling).wait_recv()
         turn(i, [(place.is_l, own[i]), (is_r, near[i])], I0, I0, counts[i])
     done = [I0, I0, I0, I0]
+
+    @pl.when(place.is_l & jnp.logical_not(early))
+    def _():
+        for k in range(len(ROUND)):
+            remote(round_a.at[k], round_a.at[k], rs_send.at[k], ra_sem.at[k], place.sibling).wait_recv()
+            remote(round_a.at[k], round_b.at[k], rs_send.at[k], rb_sem.at[k], place.across).start()
     for c, (i, axis, index) in enumerate(PIECES):
-        view = piece(far[i], axis, index)
+        view = piece_of(far, c)
+        for k, step in enumerate(ROUND_STEPS):
+            if c == step:
+                @pl.when(is_r & jnp.logical_not(early))
+                def _(k=k):
+                    remote(round_b.at[k], round_b.at[k], rs_send.at[k], rb_sem.at[k], place.sibling).wait_recv()
+                    remote(round_b.at[k], piece_of(far, ROUND[k]), rs_send.at[k], far_sem.at[ROUND[k]], place.along_x).start()
         remote(view, view, d_send.at[i], far_sem.at[c], place.sibling).wait_recv()
-
-        @pl.when(is_r)
-        def _(i=i, c=c, view=view):
-            remote(view, view, d_send.at[i], far_sem.at[c], place.sibling).start()
+        gives = is_r
+        sem = d_send.at[i]
+        if c in ROUND:
+            gives = (early & place.is_l) | (jnp.logical_not(early) & is_r)
+            sem = xd_send.at[ROUND.index(c)]
+
+        @pl.when(gives)
+        def _(c=c, view=view, sem=sem):
+            remote(view, view, sem, far_sem.at[c], place.sibling).start()
         count = I4 if i < I2 else I3
         turn(i, [(None, far[i])], I1, done[i], count)
         done[i] += count
@@ -340,8 +382,21 @@
     @pl.when(is_r)
     def _():
         for i in range(I4):
-            remote(own[i], far[i], y_send.at[i], far_sem.at[I0], place.across_other).wait_send()
-            remote(far[i], far[i], d_send.at[i], far_sem.at[I0], place.sibling).wait_send()
+            part = own[i] if i < I3 else own[i].at[I0:I2 * 768, :]
+            remote(part, part, y_send.at[i], far_sem.at[I0], place.across_other).wait_send()
+            remote(part, part, d_send.at[i], far_sem.at[I0], place.sibling).wait_send()
+        for k in range(len(ROUND)):
+            remote(round_a.at[k], round_a.at[k], x_send.at[k], far_sem.at[I0], place.sibling).wait_send()
+
+    @pl.when((early & place.is_l) | (jnp.logical_not(early) & is_r))
+    def _():
+        for k in range(len(ROUND)):
+            remote(round_a.at[k], round_a.at[k], xd_send.at[k], far_sem.at[I0], place.sibling).wait_send()
+
+    @pl.when(jnp.logical_not(early))
+    def _():
+        for k in range(len(ROUND)):
+            remote(round_a.at[k], round_a.at[k], rs_send.at[k], far_sem.at[I0], place.sibling).wait_send()
 
 
 def near_choices(place, own, near):
@@ -350,9 +405,9 @@
 
 def forward_kernel(dims, x_ref, y_ref, wq, wo, wu, wd, own_gains,
                    a_s, h_s, qkv_s, u_s, g_s, oh_same, oh_other, oa_same, oa_other, og_same, og_other, loss_s, home_gains,
-                   nq, no, nu, nd, fq, fo, fu, fd, tq0, to0, tu0, td0, tq1, to1, tu1, td1, uc0, uc1,
+                   nq, no, nu, nd, fq, fo, fu, fd, tq0, to0, tu0, td0, tq1, to1, tu1, td1, uc0, uc1, round_a, round_b,
                    abuf, hbuf, obuf, nbuf, ybuf, sbuf, qkvbuf, ubuf, zbuf, ctxbuf, acc, lossbuf, losstile, gains, wres, wores, wn,
-                   send_sem, y_send, d_send, near_sem, far_sem, t_load, t_store, t_keep,
+                   send_sem, y_send, d_send, near_sem, far_sem, t_load, t_store, t_keep, ra_sem, rb_sem, x_send, xd_send, rs_send,
                    act_sem, hop_f, keep_sem, save_sem, stream_n, res_sem, out_sem, big_sem, y_sem, s_sem,
                    os_sem, oo_sem, as_sem, ao_sem, gs_sem, go_sem, bulk, gain_sem, tiny):
     micro, seq, width, heads, head_dim, ffn = dims
@@ -378,7 +433,8 @@
     def _():
         for m in range(micro):
             pltpu.make_async_copy(x_ref.at[m, place.core], abuf.at[m], act_sem.at[m]).start()
-    weight_phase(place, is_r, own, near, far, turned, (uc0, uc1), wn, wores, send_sem, y_send, d_send, near_sem, far_sem, t_load, t_store, t_keep)
+    weight_phase(place, is_r, own, near, far, turned, (uc0, uc1), wn, wores, send_sem, y_send, d_send, near_sem, far_sem, t_load, t_store, t_keep,
+                 round_a, round_b, ra_sem, rb_sem, x_send, xd_send, rs_send)
     pltpu.make_async_copy(own_gains, gains, gain_sem.at[I0]).wait()
     pltpu.make_async_copy(gains, home_gains, gain_sem.at[I0]).start()
 
@@ -449,11 +505,11 @@
     def send_seed(m):
         seed_out(m).wait()
 
-        @pl.when(place.is_l)
+        @pl.when(place.is_l & (m < EARLY_SEEDS))
         def _():
             remote(g_s.at[m], og_same.at[m], bulk.at[I1], gs_sem, place.across).start()
 
-        @pl.when(is_r)
+        @pl.when(is_r & (m < EARLY_SEEDS))
         def _():
             remote(g_s.at[m], og_other.at[m], bulk.at[I1], go_sem, place.across_other).start()
 
@@ -594,6 +650,9 @@
         far_mid(m, home13 | (m % I2 == I1))
         return carry
 
+    @pl.when(is_first & (place.core == I0))
+    def _():
+        pl.delay(STAGGER_NS)
     lax.fori_loop(I0, micro, forward_tick, I0)
     for m in range(I0, micro, I2):
         far_mid(m, home02)
@@ -617,7 +676,7 @@
 
     @pl.when(is_last)
     def _():
-        send_seed(micro - I1)
+        seed_out(micro - I1).wait()
         pltpu.make_async_copy(losstile, loss_s, tiny).wait()
 
     @pl.when(takes_x)
@@ -631,12 +690,12 @@
 
     @pl.when(is_last)
     def _():
-        sent(g_s, bulk.at[I1])
+        sent(g_s.at[I0:EARLY_SEEDS], bulk.at[I1])
 
     @pl.when((place.home == I2) & is_r)
     def _():
-        got(og_same, gs_sem)
-        got(og_other, go_sem)
+        got(og_same.at[I0:EARLY_SEEDS], gs_sem)
+        got(og_other.at[I0:EARLY_SEEDS], go_sem)
 
     @pl.when(is_r)
     def _():
@@ -884,7 +943,9 @@
             remote(m_s.at[m], od_other.at[m], bulk.at[I6], do_sem, place.sibling).start()
             remote(m_s.at[m], od_other.at[m], bulk.at[7], do_sem, place.across_other).start()
 
-        far_grad(m, (place.home == I1) & (i % I2 == I1) & (i < I2 * EARLY_G))
+        now = (i % I2 == I1) & (i < I2 * EARLY_G)
+        far_grad(m, (place.home == I1) & now)
+        far_grad(micro - I1 - i // I2, is_last & now)
         return carry
 
     def far_grad(m, condition):
@@ -932,9 +993,12 @@
         sent(m_s, bulk.at[7])
         remote(accg, dg_other, tiny.at[I2], tiny.at[I4], place.sibling).wait_send()
 
+    @pl.when(home13)
+    def _():
+        sent(gbuf.at[I0:EARLY_G], bulk.at[I4])
+
     @pl.when(place.home == I1)
     def _():
-        sent(gbuf.at[I0:EARLY_G], bulk.at[I4])
         got(dx_s, dx_sem)
 
     @pl.when(jnp.logical_not(is_first))
@@ -954,7 +1018,7 @@
     def _():
         got(og_other, go_sem)
 
-    @pl.when(is_first & is_r)
+    @pl.when(jnp.logical_not(home13) & is_r)
     def _():
         got(og_same.at[I0:EARLY_G], gs_sem)
         got(og_other.at[I0:EARLY_G], go_sem)
@@ -987,7 +1051,7 @@
     turned = [(I3, width, CHUNK), (I1, width, CHUNK), (ffn // I2, width), (I3, width, CHUNK)]
     out_shape = shapes(act, act, (micro, seq, I6 * half), (micro, seq, ffn), *[act] * 7)
     out_shape += [jax.ShapeDtypeStruct(s, F32) for s in ((I8, 128), own_gains.shape)]
-    out_shape += shapes(*raw, *raw, *turned, *turned, turned[I0], turned[I0])
+    out_shape += shapes(*raw, *raw, *turned, *turned, turned[I0], turned[I0], *[(len(ROUND), 768, width)] * I2)
     any_spec = pl.BlockSpec(memory_space=ANY)
     vmem, dma = pltpu.VMEM, pltpu.SemaphoreType.DMA
     row = vmem((seq, width), BF)
@@ -995,7 +1059,7 @@
         vmem(act, BF), row, vmem((I2, seq, width), BF), row, row, row, vmem((seq, I6 * half), BF), vmem((seq, ffn), BF), vmem((seq, CHUNK), BF),
         vmem((seq, I2 * half), BF), vmem((seq, width), F32), vmem((I8, width), F32), vmem((I8, 128), F32), vmem((I2, width), F32),
         vmem((I6, CHUNK, width), BF), vmem((I2, CHUNK, width), BF), vmem((DEPTH, width, CHUNK), BF),
-        dma((I4,)), dma((I4,)), dma((I4,)), dma((I4,)), dma((12,)), dma((I2,)), dma((I2,)), dma((I2,)),
+        dma((I4,)), dma((I4,)), dma((I4,)), dma((I4,)), dma((12,)), dma((I2,)), dma((I2,)), dma((I2,)), *[dma((len(ROUND),))] * 5,
         dma((micro,)), dma((I2,)), dma((I2,)), dma((I3,)), dma((DEPTH,)), dma((I6,)), dma((I2,)), dma((I2,)), dma(()), dma(()),
         dma(()), dma(()), dma(()), dma(()), dma(()), dma(()), dma((I4,)), dma((I2,)), dma(()),
     ]

time: 1350 us -> 1360 us (level)
    pallas_call x1, Pallas kernels: 638 us -> 597 us  [forward_phase(): pl.pallas_call(functools.partial(forward_kernel, dims), out_shape=tuple(o...]
    pallas_call x1, Pallas kernels: 258 us -> 284 us  [backward_phase(): pl.pallas_call(functools.partial(backward_kernel, dims), out_shape=tuple(...]
    pallas_call x1, Pallas kernels: 180 us -> 202 us  [owner_backward(): pl.pallas_call(functools.partial(owner_backward_kernel, dims), grid=(I2 *...]
where the time goes in v9:
time: 1360 us
  Pallas kernels  1350 us (99%)
    pallas_call x1, Pallas kernels, forward_phase(): pl.pallas_call(functools.partial(forward_kernel, dims), out_shape=tuple(o...  597 us
    pallas_call x1, Pallas kernels, backward_phase(): pl.pallas_call(functools.partial(backward_kernel, dims), out_shape=tuple(...  284 us
    pallas_call x1, Pallas kernels, owner_backward(): pl.pallas_call(functools.partial(owner_backward_kernel, dims), grid=(I2 *...  202 us
    pallas_call x2, Pallas kernels, owner_recompute(): pl.pallas_call(functools.partial(recompute_kernel, dims, early), out_shap...  128 us
    pallas_call x1, Pallas kernels, mlp_products(): pl.pallas_call(mlp_products_kernel, grid=(cols // SUB,), out_shape=(jax.S...  86.6 us
    pallas_call x1, Pallas kernels, attn_products(): pl.pallas_call(attn_products_kernel, grid=(pairs,), out_shape=(jax.ShapeD...  51.5 us

profile of v9, /device:TPU:3, one launch (start us, length us, event | category | flops | bytes accessed | tf_op | source)
XLA Modules:
  0.0 1356.4 jit_solution(13649377268849966727)
XLA Ops:
  0.6 1.3 maximum_convert_fusion.own_gains.gains
  2.0 597.5 %forward_phase.1 = (bf16[8,192,1536]{2,1,0:T(8,128)(2,1)}, bf16[8,192,1536]{2,1,0:T(8,128)(2,1)}, bf16[8,192,6144]{2,1,0:T(8,128)(2,1)}, bf16[8,192,6144]{2,1,0:...) custom-call(bf16[8,2,192,1536]{3,2,1,0:T(8,128)(2,1)} %x_ref.1, ...), custom_call_target="tpu_custom_call" | custom-call | tf_op jit(solution)/shard_map/forward_phase/pallas_call | solution.py:1066
  599.4 0.7 owner_recompute.2
  600.2 284.4 %backward_phase.1 = (bf16[8,192,1536]{2,1,0:T(8,128)(2,1)}, bf16[8,192,1536]{2,1,0:T(8,128)(2,1)}, bf16[8,192,1536]{2,1,0:T(8,128)(2,1)}, bf16[8,192,1536]{2,1,0...) custom-call(bf16[8,192,1536]{2,1,0:T(8,128)(2,1)} %get-tuple-element, ...), custom_call_target="tpu_custom_call", output_to_operand_aliasing={{4}: (17, {}), {5}: (18, {}), {6}: (19, {}), {7}: (20, {})} | custom-call | tf_op jit(solution)/shard_map/backward_phase/pallas_call | solution.py:1091
  884.5 127.3 %owner_recompute.3 = (f32[8,128]{1,0:T(8,128)}, bf16[3072,3072]{1,0:T(8,128)(2,1)}, bf16[3072,3072]{1,0:T(8,128)(2,1)}, bf16[3072,1024]{1,0:T(8,128)(2,1)}, bf16...) custom-call(bf16[1536,1536]{1,0:T(8,128)(2,1)} %bitcast.45, ...), custom_call_target="tpu_custom_call", output_to_operand_aliasing={{1}: (7, {}), {2}: (8, {}), {3}: (9, {}), {4}: (10, {}), {5... | custom-call | tf_op jit(solution)/shard_map/owner_recompute/pallas_call | solution.py:1164
  1011.9 1.3 reduce_sum.18
  1013.8 1.0 add_reduce_fusion
  1014.8 0.6 fusion
  1015.4 201.7 %owner_backward.1 = (bf16[3072,3072]{1,0:T(8,128)(2,1)}, bf16[3072,3072]{1,0:T(8,128)(2,1)}, bf16[3072,3072]{1,0:T(8,128)(2,1)}, bf16[8,2,192,1536]{3,2,1,0:T(8,...) custom-call(bf16[8,192,1536]{2,1,0:T(8,128)(2,1)} %get-tuple-element, ...), custom_call_target="tpu_custom_call", output_to_operand_aliasing={{4}: (7, {}), {5}: (8, {})} | custom-call | tf_op jit(solution)/shard_map/owner_backward/pallas_call | solution.py:1344
  1217.1 51.5 %attn_products.1 = (f32[3,8,96,1536]{3,2,1,0:T(8,128)}, f32[8,96,1536]{2,1,0:T(8,128)}, bf16[8,2,192,1536]{3,2,1,0:T(8,128)(2,1)}) custom-call(bf16[3072,3072]{1,0:T(8,128)(2,1)} %get-tuple-element.98.dq.dk.dv, bf16[3072,3072]{1,0:T(8,128)(2,1)} %get-tuple-element.98.dq.dk.dv, bf16[3072,3072]{1,0:T(8,128)(2,1)} %get-tuple-element.98.dq.dk.dv, ...), custom_call_target="tpu_custom_call" | custom-call | tf_op jit(solution)/shard_map/attn_products/pallas_call | solution.py:1411
  1268.6 86.6 %mlp_products.1 = (f32[1536,3072]{1,0:T(8,128)}, f32[3072,1536]{1,0:T(8,128)}) custom-call(bf16[3072,3072]{1,0:T(8,128)(2,1)} %get-tuple-element.105.dup, bf16[3072,3072]{1,0:T(8,128)(2,1)} %get-tuple-element.106.z, bf16[3072,1536]{1,0:T(8,128)(2,1)} %get-tuple-element.107.n2_o, bf16[1536,1536]{1,0:T(8,128)(2,1)} %bitcast.36, bf16[1536,1536]{1,0:T(8,128)(2,1)} %bitcast.37), custom_call_target="tpu_custom_call" | custom-call | tf_op jit(solution)/shard_map/mlp_products/pallas_call | solution.py:1453

commit v10 on v9

--- a/solution.py
+++ b/solution.py
@@ -123,15 +123,15 @@
             for queries, keys in heads for low, high in ((I0, cut), (cut, queries[I0].shape[I0]))]
 
 
-def softmax_parts(scores, starts):
+def softmax_parts(scores, starts, keys_axis):
     masked = []
     for s, start in zip(scores, starts):
-        q_pos = lax.broadcasted_iota(jnp.int32, s.shape, I0) + start
-        k_pos = lax.broadcasted_iota(jnp.int32, s.shape, I1)
+        k_pos = lax.broadcasted_iota(jnp.int32, s.shape, keys_axis)
+        q_pos = lax.broadcasted_iota(jnp.int32, s.shape, I1 - keys_axis) + start
         masked.append(jnp.where(k_pos <= q_pos, s, -1e30))
-    tops = [jnp.max(s, axis=-I1, keepdims=True) for s in masked]
+    tops = [jnp.max(s, axis=keys_axis, keepdims=True) for s in masked]
     powers = [jnp.exp(s - top) for s, top in zip(masked, tops)]
-    scales = [1.0 / jnp.sum(e, axis=-I1, keepdims=True) for e in powers]
+    scales = [1.0 / jnp.sum(e, axis=keys_axis, keepdims=True) for e in powers]
     return [e * r for e, r in zip(powers, scales)]
 
 
@@ -141,19 +141,18 @@
 
 def attention_forward(heads, scale):
     units = row_parts([((q,), (k, v)) for q, k, v in heads])
-    probs = softmax_parts([mm_nt(q, k) * scale for q, k, _, _ in units], [u[-I1] for u in units])
+    probs = softmax_parts([mm_nt(q, k) * scale for q, k, _, _ in units], [u[-I1] for u in units], I1)
     parts = [mm(p.astype(BF), u[I2]) for p, u in zip(probs, units)]
     return [jnp.concatenate([a, b], I0).astype(BF) for a, b in zip(parts[I0::I2], parts[I1::I2])]
 
 
 def attention_backward(heads, scale):
     units = row_parts([((q, dc), (k, v)) for q, k, v, dc in heads])
-    scores = [mm_nt(q, k) * scale for q, _, k, _, _ in units]
-    dps = [mm_nt(dc, v) for _, dc, _, v, _ in units]
-    probs = softmax_parts(scores, [u[-I1] for u in units])
+    scores = [mm_nt(k, q) * scale for q, _, k, _, _ in units]
+    dps = [mm_nt(v, dc) for _, dc, _, v, _ in units]
+    probs = softmax_parts(scores, [u[-I1] for u in units], I0)
     dps = [dp.astype(BF).astype(F32) for dp in dps]
-    deltas = [jnp.sum(dp * p, axis=-I1, keepdims=True) for dp, p in zip(dps, probs)]
-    dvs = [mm_tn(p.astype(BF), u[I1]) for p, u in zip(probs, units)]
+    deltas = [jnp.sum(dp * p, axis=I0, keepdims=True) for dp, p in zip(dps, probs)]
     dss = [p * (dp - delta) * scale for p, dp, delta in zip(probs, dps, deltas)]
     terms = []
     for ds in dss:
@@ -161,9 +160,11 @@
         rest = ds - hi.astype(F32)
         lo = rest.astype(BF)
         terms.append((hi, lo, (rest - lo.astype(F32)).astype(BF)))
-    dqs = [mm(hi, u[I2]) + (mm(lo, u[I2]) + mm(tail, u[I2])) for (hi, lo, tail), u in zip(terms, units)]
-    dks = [mm_tn(hi, u[I0]) + (mm_tn(lo, u[I0]) + mm_tn(tail, u[I0])) for (hi, lo, tail), u in zip(terms, units)]
-    return [(jnp.concatenate([dqs[i], dqs[i + I1]], I0).astype(BF), join_keys(dks[i], dks[i + I1]), join_keys(dvs[i], dvs[i + I1]))
+    dvs = [mm(p.astype(BF), u[I1]) for p, u in zip(probs, units)]
+    dks = [mm(hi, u[I0]) + (mm(lo, u[I0]) + mm(tail, u[I0])) for (hi, lo, tail), u in zip(terms, units)]
+    k_turned = [u[I2].T for u in units]
+    dqs = [(mm(kt, hi) + (mm(kt, lo) + mm(kt, tail))).astype(BF) for (hi, lo, tail), kt in zip(terms, k_turned)]
+    return [(jnp.concatenate([dqs[i].T, dqs[i + I1].T], I0), join_keys(dks[i], dks[i + I1]), join_keys(dvs[i], dvs[i + I1]))
             for i in range(I0, len(units), I2)]
 
 
@@ -655,7 +656,7 @@
         pl.delay(STAGGER_NS)
     lax.fori_loop(I0, micro, forward_tick, I0)
     for m in range(I0, micro, I2):
-        far_mid(m, home02)
+        far_mid(m, is_first)
 
     @pl.when(is_last)
     def _():
@@ -685,8 +686,22 @@
             copy.wait()
     pltpu.make_async_copy(gains, home_gains, gain_sem.at[I0]).wait()
     sent, got = drain(place)
-    sent(h_s, bulk.at[I2])
-    got(oh_other, oo_sem)
+
+    @pl.when(place.home != I2)
+    def _():
+        sent(h_s, bulk.at[I2])
+
+    @pl.when(place.home == I2)
+    def _():
+        sent(h_s.at[I0:micro // I2], bulk.at[I2])
+
+    @pl.when(place.is_l | jnp.logical_not(is_last))
+    def _():
+        got(oh_other, oo_sem)
+
+    @pl.when(is_r & is_last)
+    def _():
+        got(oh_other.at[I0:micro // I2], oo_sem)
 
     @pl.when(is_last)
     def _():
@@ -701,7 +716,14 @@
     def _():
         sent(a_s, bulk.at[I0])
         sent(h_s, bulk.at[I3])
+
+    @pl.when(is_r & jnp.logical_not(is_last))
+    def _():
         got(oh_same, os_sem)
+
+    @pl.when(is_r & is_last)
+    def _():
+        got(oh_same.at[I0:micro // I2], os_sem)
 
     @pl.when(place.is_l)
     def _():
@@ -722,10 +744,10 @@
 
 
 def backward_kernel(dims, a_s, h_s, qkv_s, u_s, g_s, wq, nq, fq, td0, td1, to0, to1, tu0, tu1, gains, loss_s, after, *refs):
-    (dx_s, m_s, od_same, od_other, og_same, og_other, oa_same, oa_other, dg_same, dg_other, loss_all,
+    (dx_s, m_s, od_same, od_other, og_same, og_other, oa_same, oa_other, oh_same, oh_other, dg_same, dg_other, loss_all,
      gbuf, hbuf, obuf, qkvbuf, ubuf, habuf, zbuf, ctxbuf, dqkvbuf, acc, accg, wres, wn, wk,
      grad_sem, hop_b, back_sem, dx_sem, dx_send, save_sem, stream_n, stream_k, res_sem, load_sem,
-     ds_sem, do_sem, gs_sem, go_sem, as_sem, ao_sem, bulk, tiny, loss_sem) = refs[I4:]
+     ds_sem, do_sem, gs_sem, go_sem, as_sem, ao_sem, os_sem, oo_sem, bulk, tiny, loss_sem) = refs[I6:]
     micro, seq, width, heads, head_dim, ffn = dims
     place = Place()
     is_first, is_last = place.home == I0, place.home == I3
@@ -915,11 +937,15 @@
             def _():
                 for t in range(micro):
                     remote(a_s.at[t], oa_same.at[t], bulk.at[I8], as_sem, place.across).start()
+                for t in range(I0, micro, I2):
+                    remote(h_s.at[t], oh_same.at[t], bulk.at[9], os_sem, place.across).start()
 
             @pl.when((place.home == I2) & is_r)
             def _():
                 for t in range(micro):
                     remote(a_s.at[t], oa_other.at[t], bulk.at[I8], ao_sem, place.across_other).start()
+                for t in range(I0, micro, I2):
+                    remote(h_s.at[t], oh_other.at[t], bulk.at[9], oo_sem, place.across_other).start()
 
         @pl.when(jnp.logical_not(is_first))
         def _():
@@ -1010,6 +1036,7 @@
     @pl.when(place.home == I2)
     def _():
         sent(a_s, bulk.at[I8])
+        sent(h_s.at[I0:micro // I2], bulk.at[9])
 
     remote(accg, dg_other, tiny.at[I1], tiny.at[I4], place.sibling).wait_send()
     got(od_other, do_sem)
@@ -1037,6 +1064,8 @@
     def _():
         got(oa_same, as_sem)
         got(oa_other, ao_sem)
+        got(oh_same.at[I0:micro // I2], os_sem)
+        got(oh_other.at[I0:micro // I2], oo_sem)
 
 
 def shapes(*dims_list):
@@ -1078,7 +1107,7 @@
     micro, seq, width, heads, head_dim, ffn = dims
     half = heads // I2 * HEAD_PAD
     act = (micro, seq, width)
-    out_shape = shapes(*[act] * I8) + [jax.ShapeDtypeStruct((I2, I8, width), F32)] * I2 + [jax.ShapeDtypeStruct((I2, I8, 128), F32)]
+    out_shape = shapes(*[act] * 10) + [jax.ShapeDtypeStruct((I2, I8, width), F32)] * I2 + [jax.ShapeDtypeStruct((I2, I8, 128), F32)]
     any_spec = pl.BlockSpec(memory_space=ANY)
     vmem, dma = pltpu.VMEM, pltpu.SemaphoreType.DMA
     scratch = [
@@ -1086,15 +1115,15 @@
         vmem((I2, seq, width), BF), vmem((seq, CHUNK), BF), vmem((seq, I2 * half), BF), vmem((seq, I6 * half), BF), vmem((seq, width), F32),
         vmem((I2, I8, width), F32), vmem((I6, CHUNK, width), BF), vmem((BACK_DEPTH, width, CHUNK), BF), vmem((KDEPTH, CHUNK, width), BF),
         dma((micro,)), dma((I2,)), dma((I2,)), dma(()), dma((I2,)), dma(()), dma((BACK_DEPTH,)), dma((KDEPTH,)), dma((I6,)), dma((I4,)),
-        dma(()), dma(()), dma(()), dma(()), dma(()), dma(()), dma((9,)), dma((5,)), dma((I4,)),
+        *[dma(())] * I8, dma((10,)), dma((5,)), dma((I4,)),
     ]
     return pl.pallas_call(
         functools.partial(backward_kernel, dims),
         out_shape=tuple(out_shape),
-        in_specs=[any_spec] * 14 + [pl.BlockSpec(memory_space=vmem)] * I2 + [any_spec] * 5,
+        in_specs=[any_spec] * 14 + [pl.BlockSpec(memory_space=vmem)] * I2 + [any_spec] * 7,
         out_specs=(any_spec,) * len(out_shape),
         scratch_shapes=scratch,
-        input_output_aliases={17: I4, 18: 5, 19: I6, 20: 7},
+        input_output_aliases={17 + i: I4 + i for i in range(I6)},
         compiler_params=pltpu.CompilerParams(collective_id=I1, has_side_effects=True, vmem_limit_bytes=VMEM_LIMIT),
         name='backward_phase',
     )(*saved, *weights, gains, loss, after, *placed)
@@ -1486,11 +1515,11 @@
         (tq0, to0, tu0, td0), (tq1, to1, tu1, td1) = weights[I8:12], weights[12:16]
 
         flat = lambda *rows: [r.reshape(-I1, width) for r in rows]
-        h_rows = flat(oh_same, oh_other)
-        done, *again = owner_recompute(dims, True, None, h_rows, flat(oa_same, oa_other), own_gains, rows_of)
-        dx, _, od_same, od_other, og_same, og_other, oa_same, oa_other, dg_same, dg_other, loss_all = backward_phase(
-            dims, (acts, mids, qkv, ups, seeds), (rows_of[I0], nq, fq, td0, td1, to0, to1, tu0, tu1), home_gains, loss_tile, done, (og_same, og_other, oa_same, oa_other))
-        _, *again = owner_recompute(dims, False, again, h_rows, flat(oa_same, oa_other), own_gains, rows_of)
+        done, *again = owner_recompute(dims, True, None, flat(oh_same, oh_other), flat(oa_same, oa_other), own_gains, rows_of)
+        dx, _, od_same, od_other, og_same, og_other, oa_same, oa_other, oh_same, oh_other, dg_same, dg_other, loss_all = backward_phase(
+            dims, (acts, mids, qkv, ups, seeds), (rows_of[I0], nq, fq, td0, td1, to0, to1, tu0, tu1), home_gains, loss_tile, done,
+            (og_same, og_other, oa_same, oa_other, oh_same, oh_other))
+        _, *again = owner_recompute(dims, False, again, flat(oh_same, oh_other), flat(oa_same, oa_other), own_gains, rows_of)
         ups_own, qkv_own, ctx_own, n1, n2 = again
         d_rows = flat(od_same, od_other)
         d_qkv_rows, d_up_rows, hidden, dx_all, og_same, og_other = owner_backward(dims, dx, d_rows, (og_same, og_other), ups_own, qkv_own, rows_of)

time: 1360 us -> 1350 us (level)
  no operation moved by 1% of the time
where the time goes in v10:
time: 1350 us
  Pallas kernels  1350 us (100%)
    pallas_call x1, Pallas kernels, forward_phase(): pl.pallas_call(functools.partial(forward_kernel, dims), out_shape=tuple(o...  597 us
    pallas_call x1, Pallas kernels, backward_phase(): pl.pallas_call(functools.partial(backward_kernel, dims), out_shape=tuple(...  285 us
    pallas_call x1, Pallas kernels, owner_backward(): pl.pallas_call(functools.partial(owner_backward_kernel, dims), grid=(I2 *...  197 us
    pallas_call x2, Pallas kernels, owner_recompute(): pl.pallas_call(functools.partial(recompute_kernel, dims, early), out_shap...  128 us
    pallas_call x1, Pallas kernels, mlp_products(): pl.pallas_call(mlp_products_kernel, grid=(cols // SUB,), out_shape=(jax.S...  86.6 us
    pallas_call x1, Pallas kernels, attn_products(): pl.pallas_call(attn_products_kernel, grid=(pairs,), out_shape=(jax.ShapeD...  51.5 us

profile of v10, /device:TPU:3, one launch (start us, length us, event | category | flops | bytes accessed | tf_op | source)
XLA Modules:
  0.0 1351.9 jit_solution(599855768603867820)
XLA Ops:
  0.6 1.3 maximum_convert_fusion.own_gains.gains
  2.0 597.5 %forward_phase.1 = (bf16[8,192,1536]{2,1,0:T(8,128)(2,1)}, bf16[8,192,1536]{2,1,0:T(8,128)(2,1)}, bf16[8,192,6144]{2,1,0:T(8,128)(2,1)}, bf16[8,192,6144]{2,1,0:...) custom-call(bf16[8,2,192,1536]{3,2,1,0:T(8,128)(2,1)} %x_ref.1, ...), custom_call_target="tpu_custom_call" | custom-call | tf_op jit(solution)/shard_map/forward_phase/pallas_call | solution.py:1095
  599.4 0.7 owner_recompute.2
  600.2 284.6 %backward_phase.1 = (bf16[8,192,1536]{2,1,0:T(8,128)(2,1)}, bf16[8,192,1536]{2,1,0:T(8,128)(2,1)}, bf16[8,192,1536]{2,1,0:T(8,128)(2,1)}, bf16[8,192,1536]{2,1,0...) custom-call(bf16[8,192,1536]{2,1,0:T(8,128)(2,1)} %get-tuple-element, ...), custom_call_target="tpu_custom_call", output_to_operand_aliasing={{4}: (17, {}), {5}: (18, {}), {6}: (19, {}), {7}: (20, {}),... | custom-call | tf_op jit(solution)/shard_map/backward_phase/pallas_call | solution.py:1120
  884.8 127.3 %owner_recompute.3 = (f32[8,128]{1,0:T(8,128)}, bf16[3072,3072]{1,0:T(8,128)(2,1)}, bf16[3072,3072]{1,0:T(8,128)(2,1)}, bf16[3072,1024]{1,0:T(8,128)(2,1)}, bf16...) custom-call(bf16[1536,1536]{1,0:T(8,128)(2,1)} %bitcast.35, ...), custom_call_target="tpu_custom_call", output_to_operand_aliasing={{1}: (7, {}), {2}: (8, {}), {3}: (9, {}), {4}: (10, {}), {5... | custom-call | tf_op jit(solution)/shard_map/owner_recompute/pallas_call | solution.py:1193
  1012.1 1.3 reduce_sum.18
  1014.1 1.0 add_reduce_fusion
  1015.1 0.6 fusion
  1015.7 196.9 %owner_backward.1 = (bf16[3072,3072]{1,0:T(8,128)(2,1)}, bf16[3072,3072]{1,0:T(8,128)(2,1)}, bf16[3072,3072]{1,0:T(8,128)(2,1)}, bf16[8,2,192,1536]{3,2,1,0:T(8,...) custom-call(bf16[8,192,1536]{2,1,0:T(8,128)(2,1)} %get-tuple-element, ...), custom_call_target="tpu_custom_call", output_to_operand_aliasing={{4}: (7, {}), {5}: (8, {})} | custom-call | tf_op jit(solution)/shard_map/owner_backward/pallas_call | solution.py:1373
  1212.6 51.5 %attn_products.1 = (f32[3,8,96,1536]{3,2,1,0:T(8,128)}, f32[8,96,1536]{2,1,0:T(8,128)}, bf16[8,2,192,1536]{3,2,1,0:T(8,128)(2,1)}) custom-call(bf16[3072,3072]{1,0:T(8,128)(2,1)} %get-tuple-element.102.dq.dk.dv, bf16[3072,3072]{1,0:T(8,128)(2,1)} %get-tuple-element.102.dq.dk.dv, bf16[3072,3072]{1,0:T(8,128)(2,1)} %get-tuple-element.102.dq.dk.dv, ...), custom_call_target="tpu_custom_call" | custom-call | tf_op jit(solution)/shard_map/attn_products/pallas_call | solution.py:1440
  1264.1 86.6 %mlp_products.1 = (f32[1536,3072]{1,0:T(8,128)}, f32[3072,1536]{1,0:T(8,128)}) custom-call(bf16[3072,3072]{1,0:T(8,128)(2,1)} %get-tuple-element.109.dup, bf16[3072,3072]{1,0:T(8,128)(2,1)} %get-tuple-element.110.z, bf16[3072,1536]{1,0:T(8,128)(2,1)} %get-tuple-element.111.n2_o, bf16[1536,1536]{1,0:T(8,128)(2,1)} %bitcast.42, bf16[1536,1536]{1,0:T(8,128)(2,1)} %bitcast.43), custom_call_target="tpu_custom_call" | custom-call | tf_op jit(solution)/shard_map/mlp_products/pallas_call | solution.py:1482

commit v11 on v10

--- a/solution.py
+++ b/solution.py
@@ -21,7 +21,7 @@
 BLOCK = 384
 SUB = 256
 DEPTH = 6
-BACK_DEPTH = 6
+BACK_DEPTH = 5
 KDEPTH = 3
 EARLY_G = 3
 STAGGER_NS = 6000
@@ -168,6 +168,13 @@
             for i in range(I0, len(units), I2)]
 
 
+def blocked(rows, stack, cols):
+    total = mm(rows[:, I0:CHUNK], stack[I0, :, cols])
+    for j in range(I1, stack.shape[I0]):
+        total = total + mm(rows[:, j * CHUNK:(j + I1) * CHUNK], stack[j, :, cols])
+    return total
+
+
 def lanes(offset, size):
     return pl.ds(pl.multiple_of(offset, 128), size)
 
@@ -233,7 +240,7 @@
 
 
 ROUND = (10, 11)
-ROUND_STEPS = (6, 8)
+ROUND_STEPS = (1, 3)
 
 
 def piece(ref, axis, index):
@@ -346,13 +353,13 @@
         def _(i=i):
             remote(near[i], near[i], send_sem.at[i], near_sem.at[i], place.sibling).wait_recv()
         turn(i, [(place.is_l, own[i]), (is_r, near[i])], I0, I0, counts[i])
+        if i < len(ROUND):
+            @pl.when(place.is_l & jnp.logical_not(early))
+            def _(k=i):
+                remote(round_a.at[k], round_a.at[k], rs_send.at[k], ra_sem.at[k], place.sibling).wait_recv()
+                remote(round_a.at[k], round_b.at[k], rs_send.at[k], rb_sem.at[k], place.across).start()
     done = [I0, I0, I0, I0]
 
-    @pl.when(place.is_l & jnp.logical_not(early))
-    def _():
-        for k in range(len(ROUND)):
-            remote(round_a.at[k], round_a.at[k], rs_send.at[k], ra_sem.at[k], place.sibling).wait_recv()
-            remote(round_a.at[k], round_b.at[k], rs_send.at[k], rb_sem.at[k], place.across).start()
     for c, (i, axis, index) in enumerate(PIECES):
         view = piece_of(far, c)
         for k, step in enumerate(ROUND_STEPS):
@@ -407,7 +414,7 @@
 def forward_kernel(dims, x_ref, y_ref, wq, wo, wu, wd, own_gains,
                    a_s, h_s, qkv_s, u_s, g_s, oh_same, oh_other, oa_same, oa_other, og_same, og_other, loss_s, home_gains,
                    nq, no, nu, nd, fq, fo, fu, fd, tq0, to0, tu0, td0, tq1, to1, tu1, td1, uc0, uc1, round_a, round_b,
-                   abuf, hbuf, obuf, nbuf, ybuf, sbuf, qkvbuf, ubuf, zbuf, ctxbuf, acc, lossbuf, losstile, gains, wres, wores, wn,
+                   abuf, hbuf, obuf, nbuf, ybuf, sbuf, qkvbuf, ubuf, zbuf, ctxbuf, lossbuf, losstile, gains, wres, wores, wn,
                    send_sem, y_send, d_send, near_sem, far_sem, t_load, t_store, t_keep, ra_sem, rb_sem, x_send, xd_send, rs_send,
                    act_sem, hop_f, keep_sem, save_sem, stream_n, res_sem, out_sem, big_sem, y_sem, s_sem,
                    os_sem, oo_sem, as_sem, ao_sem, gs_sem, go_sem, bulk, gain_sem, tiny):
@@ -468,6 +475,10 @@
     def act_out(m):
         return pltpu.make_async_copy(abuf.at[m], a_s.at[m], save_sem.at[I2])
 
+    def hop_block(m, n):
+        cols = lanes(n * SUB, SUB)
+        return remote(obuf.at[m % I2, :, cols], abuf.at[m, :, cols], hop_f.at[m % I2], act_sem.at[m], place.chain(I1))
+
     def hop_forward(m):
         return remote(obuf.at[m % I2], abuf.at[m], hop_f.at[m % I2], act_sem.at[m], place.chain(I1))
 
@@ -580,39 +591,44 @@
         @pl.when(m > I0)
         def _():
             up_out(m).wait()
-        acc[...] = jnp.zeros_like(acc)
-
-        def mlp_step(j, c):
+
+        def up_step(j, c):
             w = sn.wait(m * 12 + I6 + j)
             for n in range(I0, CHUNK, SUB):
                 u = mm(nbuf[...], w[:, n:n + SUB]).astype(BF)
-                ubuf[:, lanes(j * CHUNK + n, SUB)] = u
+                at = lanes(j * CHUNK + n, SUB)
+                ubuf[:, at] = u
                 uf = u.astype(F32)
-                zbuf[:, n:n + SUB] = (uf * gelu_gate(uf)[I0]).astype(BF)
+                zbuf[:, at] = (uf * gelu_gate(uf)[I0]).astype(BF)
             sn.start(m * 12 + I6 + j + DEPTH)
-
-            @pl.when(m == I0)
+            return c
+        lax.fori_loop(I0, I6, up_step, I0)
+        up_out(m).start()
+
+        @pl.when((m > I1) & jnp.logical_not(is_last))
+        def _():
+            hop_forward(m).wait_send()
+
+        both_kinds((m > I1) & home02, hand_out(m), False)
+
+        @pl.when(m == I0)
+        def _():
+            for j in range(I6):
+                pltpu.make_async_copy(wd.at[I0:CHUNK, :], wres.at[j], res_sem.at[j]).wait()
+
+        def down_step(n, c):
+            cols = lanes(n * SUB, SUB)
+            out[:, cols] = (mid[:, cols].astype(F32) + blocked(zbuf, wres, cols)).astype(BF)
+
+            @pl.when((n > I0) & jnp.logical_not(is_last))
             def _():
-                pltpu.make_async_copy(wd.at[I0:CHUNK, :], wres.at[j], res_sem.at[j]).wait()
-            for n in range(I0, width, SUB):
-                acc[:, n:n + SUB] += mm(zbuf[...], wres[j, :, n:n + SUB])
+                hop_block(m, n - I1).start()
             return c
-        lax.fori_loop(I0, I6, mlp_step, I0)
-        up_out(m).start()
-
-        @pl.when((m > I1) & jnp.logical_not(is_last))
-        def _():
-            hop_forward(m).wait_send()
-
-        both_kinds((m > I1) & home02, hand_out(m), False)
-
-        def finish(rows):
-            out[rows, :] = (mid[rows, :].astype(F32) + acc[rows, :]).astype(BF)
-        rows_loop(seq, 32, finish)
+        lax.fori_loop(I0, width // SUB, down_step, I0)
 
         @pl.when(jnp.logical_not(is_last))
         def _():
-            hop_forward(m).start()
+            hop_block(m, width // SUB - I1).start()
 
         both_kinds(home02, hand_out(m), True)
 
@@ -747,7 +763,7 @@
     (dx_s, m_s, od_same, od_other, og_same, og_other, oa_same, oa_other, oh_same, oh_other, dg_same, dg_other, loss_all,
      gbuf, hbuf, obuf, qkvbuf, ubuf, habuf, zbuf, ctxbuf, dqkvbuf, acc, accg, wres, wn, wk,
      grad_sem, hop_b, back_sem, dx_sem, dx_send, save_sem, stream_n, stream_k, res_sem, load_sem,
-     ds_sem, do_sem, gs_sem, go_sem, as_sem, ao_sem, os_sem, oo_sem, bulk, tiny, loss_sem) = refs[I6:]
+     ds_sem, do_sem, gs_sem, go_sem, as_sem, ao_sem, os_sem, oo_sem, bulk, tiny, loss_sem, ready) = refs[I6:]
     micro, seq, width, heads, head_dim, ffn = dims
     place = Place()
     is_first, is_last = place.home == I0, place.home == I3
@@ -757,13 +773,13 @@
     scale = head_dim ** -0.5
 
     barrier = pltpu.get_barrier_semaphore()
-    along_x = (place.home == I1) | (place.home == I2)
+    is_b, is_c = place.home == I1, place.home == I2
     for there in (place.sibling, place.across, place.across_other):
         pl.semaphore_signal(barrier, inc=I1, device_id=there, device_id_type=MESH)
 
-    @pl.when(along_x)
-    def _():
-        pl.semaphore_signal(barrier, inc=I1, device_id=place.at(place.tp, (place.stage + I2) % I4), device_id_type=MESH)
+    @pl.when(is_c)
+    def _():
+        pl.semaphore_signal(barrier, inc=I1, device_id=place.along_x, device_id_type=MESH)
 
     @pl.when(is_last)
     def _():
@@ -864,24 +880,29 @@
             pltpu.make_async_copy(grad, og_same.at[m], gs_sem).start()
         load_u, load_qkv, load_h, load_a = loads(i)
         load_u.wait()
-        acc[...] = jnp.zeros_like(acc)
 
         def mlp_step(j, c):
             w = bn.wait(i * I8 + j)
             for n in range(I0, CHUNK, SUB):
+                at = lanes(j * CHUNK + n, SUB)
                 dz = mm(grad[...], w[:, n:n + SUB]).astype(BF).astype(F32)
-                u = u_now[:, lanes(j * CHUNK + n, SUB)].astype(F32)
+                u = u_now[:, at].astype(F32)
                 gate, u2 = gelu_gate(u)
-                zbuf[:, n:n + SUB] = (dz * gelu_slope(u * gate, gate, u2)).astype(BF)
+                zbuf[:, at] = (dz * gelu_slope(u * gate, gate, u2)).astype(BF)
             bn.start(i * I8 + j + BACK_DEPTH)
-
-            @pl.when(i == I0)
-            def _():
-                pltpu.make_async_copy(tu0.at[I0:CHUNK, :], wres.at[j], res_sem.at[j]).wait()
-            for n in range(I0, width, SUB):
-                acc[:, n:n + SUB] += mm(zbuf[...], wres[j, :, n:n + SUB])
             return c
         lax.fori_loop(I0, I6, mlp_step, I0)
+
+        @pl.when(i == I0)
+        def _():
+            for j in range(I6):
+                pltpu.make_async_copy(tu0.at[I0:CHUNK, :], wres.at[j], res_sem.at[j]).wait()
+
+        def turn_back(n, c):
+            cols = lanes(n * SUB, SUB)
+            acc[:, cols] = blocked(zbuf, wres, cols)
+            return c
+        lax.fori_loop(I0, width // SUB, turn_back, I0)
         load_next(i, I0)
         load_h.wait()
         norm_back(I1, h_now, grad, dmid, gains[I1:I2, :])
@@ -927,25 +948,17 @@
 
         @pl.when(i == I0)
         def _():
-            pl.semaphore_wait(barrier, I3 + (place.home + I1) // I2 % I2)
+            @pl.when(is_first | is_last)
+            def _():
+                pl.semaphore_wait(barrier, I3)
+
+            @pl.when(is_c)
+            def _():
+                pl.semaphore_wait(ready, I1)
 
             @pl.when(is_last)
             def _():
                 pass_loss(loss_s)
-
-            @pl.when((place.home == I2) & place.is_l)
-            def _():
-                for t in range(micro):
-                    remote(a_s.at[t], oa_same.at[t], bulk.at[I8], as_sem, place.across).start()
-                for t in range(I0, micro, I2):
-                    remote(h_s.at[t], oh_same.at[t], bulk.at[9], os_sem, place.across).start()
-
-            @pl.when((place.home == I2) & is_r)
-            def _():
-                for t in range(micro):
-                    remote(a_s.at[t], oa_other.at[t], bulk.at[I8], ao_sem, place.across_other).start()
-                for t in range(I0, micro, I2):
-                    remote(h_s.at[t], oh_other.at[t], bulk.at[9], oo_sem, place.across_other).start()
 
         @pl.when(jnp.logical_not(is_first))
         def _():
@@ -983,6 +996,27 @@
         def _():
             remote(gbuf.at[m], og_other.at[m], bulk.at[I4], go_sem, place.across_other).start()
 
+    @pl.when(is_b | is_c)
+    def _():
+        pl.semaphore_wait(barrier, 5 - place.home)
+
+    @pl.when(is_b)
+    def _():
+        pl.semaphore_signal(ready, inc=I1, device_id=place.along_x, device_id_type=MESH)
+
+    @pl.when(is_c & place.is_l)
+    def _():
+        for t in range(micro):
+            remote(a_s.at[t], oa_same.at[t], bulk.at[I8], as_sem, place.across).start()
+        for t in range(I0, micro, I2):
+            remote(h_s.at[t], oh_same.at[t], bulk.at[9], os_sem, place.across).start()
+
+    @pl.when(is_c & is_r)
+    def _():
+        for t in range(micro):
+            remote(a_s.at[t], oa_other.at[t], bulk.at[I8], ao_sem, place.across_other).start()
+        for t in range(I0, micro, I2):
+            remote(h_s.at[t], oh_other.at[t], bulk.at[9], oo_sem, place.across_other).start()
     lax.fori_loop(I0, micro, backward_tick, I0)
     loss_mine = loss_all.at[place.core]
 
@@ -1085,8 +1119,8 @@
     vmem, dma = pltpu.VMEM, pltpu.SemaphoreType.DMA
     row = vmem((seq, width), BF)
     scratch = [
-        vmem(act, BF), row, vmem((I2, seq, width), BF), row, row, row, vmem((seq, I6 * half), BF), vmem((seq, ffn), BF), vmem((seq, CHUNK), BF),
-        vmem((seq, I2 * half), BF), vmem((seq, width), F32), vmem((I8, width), F32), vmem((I8, 128), F32), vmem((I2, width), F32),
+        vmem(act, BF), row, vmem((I2, seq, width), BF), row, row, row, vmem((seq, I6 * half), BF), vmem((seq, ffn), BF), vmem((seq, ffn), BF),
+        vmem((seq, I2 * half), BF), vmem((I8, width), F32), vmem((I8, 128), F32), vmem((I2, width), F32),
         vmem((I6, CHUNK, width), BF), vmem((I2, CHUNK, width), BF), vmem((DEPTH, width, CHUNK), BF),
         dma((I4,)), dma((I4,)), dma((I4,)), dma((I4,)), dma((12,)), dma((I2,)), dma((I2,)), dma((I2,)), *[dma((len(ROUND),))] * 5,
         dma((micro,)), dma((I2,)), dma((I2,)), dma((I3,)), dma((DEPTH,)), dma((I6,)), dma((I2,)), dma((I2,)), dma(()), dma(()),
@@ -1112,10 +1146,10 @@
     vmem, dma = pltpu.VMEM, pltpu.SemaphoreType.DMA
     scratch = [
         vmem(act, BF), vmem((seq, width), BF), vmem((I2, seq, width), BF), vmem((seq, I6 * half), BF), vmem((seq, ffn), BF),
-        vmem((I2, seq, width), BF), vmem((seq, CHUNK), BF), vmem((seq, I2 * half), BF), vmem((seq, I6 * half), BF), vmem((seq, width), F32),
+        vmem((I2, seq, width), BF), vmem((seq, ffn), BF), vmem((seq, I2 * half), BF), vmem((seq, I6 * half), BF), vmem((seq, width), F32),
         vmem((I2, I8, width), F32), vmem((I6, CHUNK, width), BF), vmem((BACK_DEPTH, width, CHUNK), BF), vmem((KDEPTH, CHUNK, width), BF),
         dma((micro,)), dma((I2,)), dma((I2,)), dma(()), dma((I2,)), dma(()), dma((BACK_DEPTH,)), dma((KDEPTH,)), dma((I6,)), dma((I4,)),
-        *[dma(())] * I8, dma((10,)), dma((5,)), dma((I4,)),
+        *[dma(())] * I8, dma((10,)), dma((5,)), dma((I4,)), pltpu.SemaphoreType.REGULAR,
     ]
     return pl.pallas_call(
         functools.partial(backward_kernel, dims),

time: 1350 us -> 1320 us (0.978)
  Pallas kernels: 1350 us -> 1320 us
    pallas_call x1, Pallas kernels: 197 us -> 178 us  [owner_backward(): pl.pallas_call(functools.partial(owner_backward_kernel, dims), grid=(I2 *...]
where the time goes in v11:
time: 1320 us
  Pallas kernels  1320 us (100%)
    pallas_call x1, Pallas kernels, forward_phase(): pl.pallas_call(functools.partial(forward_kernel, dims), out_shape=tuple(o...  589 us
    pallas_call x1, Pallas kernels, backward_phase(): pl.pallas_call(functools.partial(backward_kernel, dims), out_shape=tuple(...  282 us
    pallas_call x1, Pallas kernels, owner_backward(): pl.pallas_call(functools.partial(owner_backward_kernel, dims), grid=(I2 *...  178 us
    pallas_call x2, Pallas kernels, owner_recompute(): pl.pallas_call(functools.partial(recompute_kernel, dims, early), out_shap...  128 us
    pallas_call x1, Pallas kernels, mlp_products(): pl.pallas_call(mlp_products_kernel, grid=(cols // SUB,), out_shape=(jax.S...  86.6 us
    pallas_call x1, Pallas kernels, attn_products(): pl.pallas_call(attn_products_kernel, grid=(pairs,), out_shape=(jax.ShapeD...  51.5 us

profile of v11, /device:TPU:3, one launch (start us, length us, event | category | flops | bytes accessed | tf_op | source)
XLA Modules:
  0.0 1322.3 jit_solution(14651748299399523431)
XLA Ops:
  0.6 1.3 maximum_convert_fusion.own_gains.gains
  2.0 589.4 %forward_phase.1 = (bf16[8,192,1536]{2,1,0:T(8,128)(2,1)}, bf16[8,192,1536]{2,1,0:T(8,128)(2,1)}, bf16[8,192,6144]{2,1,0:T(8,128)(2,1)}, bf16[8,192,6144]{2,1,0:...) custom-call(bf16[8,2,192,1536]{3,2,1,0:T(8,128)(2,1)} %x_ref.1, ...), custom_call_target="tpu_custom_call" | custom-call | tf_op jit(solution)/shard_map/forward_phase/pallas_call | solution.py:1129
  591.4 0.7 owner_recompute.2
  592.1 282.4 %backward_phase.1 = (bf16[8,192,1536]{2,1,0:T(8,128)(2,1)}, bf16[8,192,1536]{2,1,0:T(8,128)(2,1)}, bf16[8,192,1536]{2,1,0:T(8,128)(2,1)}, bf16[8,192,1536]{2,1,0...) custom-call(bf16[8,192,1536]{2,1,0:T(8,128)(2,1)} %get-tuple-element, ...), custom_call_target="tpu_custom_call", output_to_operand_aliasing={{4}: (17, {}), {5}: (18, {}), {6}: (19, {}), {7}: (20, {}),... | custom-call | tf_op jit(solution)/shard_map/backward_phase/pallas_call | solution.py:1154
  874.5 127.4 %owner_recompute.3 = (f32[8,128]{1,0:T(8,128)}, bf16[3072,3072]{1,0:T(8,128)(2,1)}, bf16[3072,3072]{1,0:T(8,128)(2,1)}, bf16[3072,1024]{1,0:T(8,128)(2,1)}, bf16...) custom-call(bf16[1536,1536]{1,0:T(8,128)(2,1)} %bitcast.35, ...), custom_call_target="tpu_custom_call", output_to_operand_aliasing={{1}: (7, {}), {2}: (8, {}), {3}: (9, {}), {4}: (10, {}), {5... | custom-call | tf_op jit(solution)/shard_map/owner_recompute/pallas_call | solution.py:1227
  1001.9 1.3 reduce_sum.18
  1003.8 1.0 add_reduce_fusion
  1004.8 0.6 fusion
  1005.4 177.6 %owner_backward.1 = (bf16[3072,3072]{1,0:T(8,128)(2,1)}, bf16[3072,3072]{1,0:T(8,128)(2,1)}, bf16[3072,3072]{1,0:T(8,128)(2,1)}, bf16[8,2,192,1536]{3,2,1,0:T(8,...) custom-call(bf16[8,192,1536]{2,1,0:T(8,128)(2,1)} %get-tuple-element, ...), custom_call_target="tpu_custom_call", output_to_operand_aliasing={{4}: (7, {}), {5}: (8, {})} | custom-call | tf_op jit(solution)/shard_map/owner_backward/pallas_call | solution.py:1407
  1183.0 51.5 %attn_products.1 = (f32[3,8,96,1536]{3,2,1,0:T(8,128)}, f32[8,96,1536]{2,1,0:T(8,128)}, bf16[8,2,192,1536]{3,2,1,0:T(8,128)(2,1)}) custom-call(bf16[3072,3072]{1,0:T(8,128)(2,1)} %get-tuple-element.102.dq.dk.dv, bf16[3072,3072]{1,0:T(8,128)(2,1)} %get-tuple-element.102.dq.dk.dv, bf16[3072,3072]{1,0:T(8,128)(2,1)} %get-tuple-element.102.dq.dk.dv, ...), custom_call_target="tpu_custom_call" | custom-call | tf_op jit(solution)/shard_map/attn_products/pallas_call | solution.py:1474
  1234.5 86.6 %mlp_products.1 = (f32[1536,3072]{1,0:T(8,128)}, f32[3072,1536]{1,0:T(8,128)}) custom-call(bf16[3072,3072]{1,0:T(8,128)(2,1)} %get-tuple-element.109.dup, bf16[3072,3072]{1,0:T(8,128)(2,1)} %get-tuple-element.110.z, bf16[3072,1536]{1,0:T(8,128)(2,1)} %get-tuple-element.111.n2_o, bf16[1536,1536]{1,0:T(8,128)(2,1)} %bitcast.42, bf16[1536,1536]{1,0:T(8,128)(2,1)} %bitcast.43), custom_call_target="tpu_custom_call" | custom-call | tf_op jit(solution)/shard_map/mlp_products/pallas_call | solution.py:1516

commit v12 on v11

--- a/solution.py
+++ b/solution.py
@@ -146,11 +146,18 @@
     return [jnp.concatenate([a, b], I0).astype(BF) for a, b in zip(parts[I0::I2], parts[I1::I2])]
 
 
-def attention_backward(heads, scale):
+def nothing():
+    pass
+
+
+def attention_backward(heads, scale, between=()):
+    work = iter(between)
     units = row_parts([((q, dc), (k, v)) for q, k, v, dc in heads])
     scores = [mm_nt(k, q) * scale for q, _, k, _, _ in units]
     dps = [mm_nt(v, dc) for _, dc, _, v, _ in units]
+    next(work, nothing)()
     probs = softmax_parts(scores, [u[-I1] for u in units], I0)
+    next(work, nothing)()
     dps = [dp.astype(BF).astype(F32) for dp in dps]
     deltas = [jnp.sum(dp * p, axis=I0, keepdims=True) for dp, p in zip(dps, probs)]
     dss = [p * (dp - delta) * scale for p, dp, delta in zip(probs, dps, deltas)]
@@ -160,6 +167,7 @@
         rest = ds - hi.astype(F32)
         lo = rest.astype(BF)
         terms.append((hi, lo, (rest - lo.astype(F32)).astype(BF)))
+    next(work, nothing)()
     dvs = [mm(p.astype(BF), u[I1]) for p, u in zip(probs, units)]
     dks = [mm(hi, u[I0]) + (mm(lo, u[I0]) + mm(tail, u[I0])) for (hi, lo, tail), u in zip(terms, units)]
     k_turned = [u[I2].T for u in units]
@@ -1171,6 +1179,14 @@
     half = heads // I2 * HEAD_PAD
     steps = I2 * micro * seq // BLOCK
 
+    def pieces(j):
+        copies = [pltpu.make_async_copy(wu.at[:, lanes(j * SUB, SUB)], wubuf.at[:, lanes(j * SUB, SUB)], sem.at[I0, j])]
+        for r in range(I2):
+            src = pl.ds(pl.multiple_of((I2 * j + r) * head_dim, head_dim), head_dim)
+            dst = pl.ds(pl.multiple_of((I2 * j + r) * HEAD_PAD, HEAD_PAD), head_dim)
+            copies.append(pltpu.make_async_copy(wq.at[src, :], wqbuf.at[dst, :], sem.at[I1 + r, j]))
+        return copies
+
     def body(hs, ho, rs, ro, u, qkv, ctx, n1, n2):
         step = count[I0]
         count[I0] = step + I1
@@ -1182,6 +1198,12 @@
             @pl.when(step >= steps // I2)
             def _(high=high, gain=gain, dst=dst):
                 norm_rows(high, gain, dst, BLOCK)
+
+        @pl.when(step == I0)
+        def _():
+            for j in range(I3 * half // SUB):
+                for copy in pieces(j):
+                    copy.wait()
 
         def qkv_step(j, c):
             rows = pl.ds(pl.multiple_of(j * SUB, SUB), SUB)
@@ -1201,13 +1223,12 @@
 
     @pl.when(place.home < I2 if early else place.home > I1)
     def _():
-        wqbuf[...] = jnp.zeros_like(wqbuf)
-        for t in range(I3):
-            load_heads(wq, t, wqbuf.at[pl.ds(t * CHUNK, CHUNK)], sem.at[I0])
-        up = pltpu.make_async_copy(wu, wubuf, sem.at[I1])
-        up.start()
-        up.wait()
-        pltpu.make_async_copy(wq, wqbuf.at[I0:wq.shape[I0]], sem.at[I0]).wait()
+        pads = jnp.zeros((HEAD_PAD - head_dim, width), BF)
+        for t in range(I3 * heads // I2):
+            wqbuf[t * HEAD_PAD + head_dim:(t + I1) * HEAD_PAD, :] = pads
+        for j in range(I3 * half // SUB):
+            for copy in pieces(j):
+                copy.start()
         count[I0] = I0
         low = pl.BlockSpec((BLOCK, width), lambda i: (jnp.minimum(i, steps // I2 - I1), I0))
         high = pl.BlockSpec((BLOCK, width), lambda i: (jnp.maximum(i - steps // I2, I0), I0))
@@ -1229,14 +1250,14 @@
         out_shape=(jax.ShapeDtypeStruct((I8, 128), F32), *shapes((tokens, ffn // I2), (tokens, I3 * half), (tokens, half), (tokens, width), (tokens, width))),
         in_specs=[any_spec] * I4 + [pl.BlockSpec(memory_space=vmem)] + [any_spec] * (I2 + len(earlier)),
         out_specs=(any_spec,) * I6,
-        scratch_shapes=[vmem((I3 * half, width), BF), vmem((width, ffn // I2), BF), pltpu.SMEM((I1,), jnp.int32), pltpu.SemaphoreType.DMA((I2,))],
+        scratch_shapes=[vmem((I3 * half, width), BF), vmem((width, ffn // I2), BF), pltpu.SMEM((I1,), jnp.int32), pltpu.SemaphoreType.DMA((I3, ffn // I2 // SUB))],
         input_output_aliases={7 + i: I1 + i for i in range(len(earlier))},
         compiler_params=pltpu.CompilerParams(has_side_effects=True, vmem_limit_bytes=VMEM_LIMIT),
         name='owner_recompute',
     )(*h_rows, *a_rows, gains, own[I0], own[I2], *earlier)
 
 
-def spread_dx(step, last, dx, d_in, og_same, og_other, bounce, here_sem, parent_sem, sib_sem, send_sems, og_sems):
+def spread_dx(step, last, dx, d_in, og_same, og_other, bounce, here_sem, parent_sem, sib_sem, send_sems, og_sems, ready):
     place = Place()
     micro = dx.shape[I0]
     along_x = place.at(place.tp, (place.stage + I2) % I4)
@@ -1259,43 +1280,48 @@
     def _():
         tell(place.sibling)
 
+        @pl.when(takes_g)
+        def _():
+            tell(place.across)
+
         @pl.when(is_leaf)
         def _():
+            pl.semaphore_wait(barrier, I2)
+            pl.semaphore_signal(ready, inc=I1, device_id=along_x, device_id_type=MESH)
+
+        @pl.when(jnp.logical_not(is_leaf))
+        def _():
             tell(along_x)
-
-        @pl.when(takes_g)
-        def _():
-            tell(place.across)
-
-    @pl.when((step == I1) & jnp.logical_not(is_leaf))
-    def _():
-        pl.semaphore_wait(barrier, I2 + gives_g.astype(jnp.int32))
+            pl.semaphore_wait(barrier, I1 + gives_g.astype(jnp.int32))
 
         @pl.when(gives_g)
         def _():
             for t, og in enumerate((og_same, og_other)):
                 for m in late:
                     remote(og.at[m], og.at[m], og_sems.at[t], og_sems.at[I2 + t], place.across).start()
+
+    @pl.when((step == I3) & jnp.logical_not(is_leaf))
+    def _():
+        pl.semaphore_wait(ready, I1)
         for m in reversed(range(micro)):
             remote(dx.at[m], block(m), send_sems.at[I1], parent_sem.at[m], along_x).start()
             to_sibling(m, dx.at[m])
         pltpu.make_async_copy(dx, bounce, here_sem).start()
 
-    @pl.when((step == I2) & jnp.logical_not(is_leaf))
+    @pl.when((step == I4) & jnp.logical_not(is_leaf))
     def _():
         pltpu.make_async_copy(dx, bounce, here_sem).wait()
         for m in range(micro):
             pltpu.make_async_copy(bounce.at[m], block(m), here_sem).start()
 
-    @pl.when((step == (last + I1) // I2) & takes_g)
-    def _():
-        for t, og in enumerate((og_same, og_other)):
+    for t, og in enumerate((og_same, og_other)):
+        @pl.when((step == I3 * t) & takes_g)
+        def _(t=t, og=og):
             part = og.at[I0:len(late)]
             remote(part, part, og_sems.at[t], og_sems.at[I2 + t], place.across).wait_recv()
 
     @pl.when((step == last) & is_leaf)
     def _():
-        pl.semaphore_wait(barrier, I1)
         for m in reversed(range(micro)):
             remote(block(m), block(m), send_sems.at[I0], parent_sem.at[m], place.sibling).wait_recv()
             to_sibling(m, block(m))
@@ -1318,76 +1344,65 @@
 
 
 def owner_backward_kernel(dims, dx, ds, do, u, qkv, wo, wd, gs_in, go_in, dqkv, dup, z, d_in, og_same, og_other,
-                          dmid, gbuf, dctx, wobuf, bounce, sem, g_sem, here_sem, parent_sem, sib_sem, send_sems, og_sems):
+                          dmid, gbuf, dctx, wobuf, bounce, sem, g_sem, here_sem, parent_sem, sib_sem, send_sems, og_sems, ready):
     micro, seq, width, heads, head_dim, ffn = dims
     half = heads // I2 * HEAD_PAD
     scale = head_dim ** -0.5
     step, steps = pl.program_id(I0), pl.num_programs(I0)
-    blocks = steps // I2
-    spread_dx(step, steps - I1, dx, d_in, og_same, og_other, bounce, here_sem, parent_sem, sib_sem, send_sems, og_sems)
+    spread_dx(step, steps - I1, dx, d_in, og_same, og_other, bounce, here_sem, parent_sem, sib_sem, send_sems, og_sems, ready)
+
+    def g_load(n, start):
+        rows = BLOCK // seq
+        for og, low in ((og_same, I0), (og_other, steps // I2)):
+            @pl.when((n >= low) & (n < low + steps // I2))
+            def _(og=og, low=low):
+                copy = pltpu.make_async_copy(og.at[pl.ds((n - low) * rows, rows)], gbuf.at[n % I2], g_sem.at[n % I2])
+                copy.start() if start else copy.wait()
 
     @pl.when(step == I0)
     def _():
+        g_load(step, True)
         wobuf[...] = jnp.zeros_like(wobuf)
         load_heads(wo, I0, wobuf, sem)
         pltpu.make_async_copy(wo, wobuf.at[I0:wo.shape[I0]], sem).wait()
-
-    def g_load(n, start):
-        rows = BLOCK // seq
-        for og, low in ((og_same, I0), (og_other, blocks // I2)):
-            @pl.when((n >= low) & (n < low + blocks // I2))
-            def _(og=og, low=low):
-                copy = pltpu.make_async_copy(og.at[pl.ds((n - low) * rows, rows)], gbuf.at[n % I2], g_sem.at[n % I2])
-                copy.start() if start else copy.wait()
-
-    @pl.when(step < blocks)
-    def _():
-        @pl.when(step < blocks // I2)
-        def _():
-            dmid[...] = ds[...]
-
-        @pl.when(step >= blocks // I2)
-        def _():
-            dmid[...] = do[...]
-
-        def ctx_step(j, c):
-            rows = pl.ds(pl.multiple_of(j * SUB, SUB), SUB)
-            dctx[:, lanes(j * SUB, SUB)] = mm_nt(dmid[...], wobuf[rows, :]).astype(BF)
-            return c
-        lax.fori_loop(I0, half // SUB, ctx_step, I0)
-
-        def head_step(j, c):
-            base = j * (I2 * HEAD_PAD)
-            at = [(pl.ds(s, seq), base + r * HEAD_PAD) for s in range(I0, BLOCK, seq) for r in range(I2)]
-            group = [(*(qkv[rows, lanes(t * half + col, HEAD_PAD)] for t in range(I3)), dctx[rows, lanes(col, HEAD_PAD)]) for rows, col in at]
-            for (rows, col), grads in zip(at, attention_backward(group, scale)):
-                for t, value in enumerate(grads):
-                    dqkv[rows, lanes(t * half + col, HEAD_PAD)] = value
-            return c
-        lax.fori_loop(I0, heads // I4, head_step, I0)
-
-    @pl.when(step == blocks)
-    def _():
-        g_load(step - blocks, True)
-
-    @pl.when(step >= blocks)
-    def _():
-        n = step - blocks
-        g_load(n + I1, True)
-        g_load(n, False)
-        grad = gbuf.at[n % I2]
-
-        def mlp_step(j, c):
-            rows = pl.ds(pl.multiple_of(j * SUB, SUB), SUB)
-            cols = lanes(j * SUB, SUB)
-            dz = mm_nt(grad[...].reshape(BLOCK, width), wd[rows, :]).astype(BF).astype(F32)
-            up = u[:, cols].astype(F32)
-            gate, up2 = gelu_gate(up)
-            hidden = up * gate
-            z[:, cols] = hidden.astype(BF)
-            dup[:, cols] = (dz * gelu_slope(hidden, gate, up2)).astype(BF)
-            return c
-        lax.fori_loop(I0, ffn // I2 // SUB, mlp_step, I0)
+    g_load(step + I1, True)
+
+    @pl.when(step < steps // I2)
+    def _():
+        dmid[...] = ds[...]
+
+    @pl.when(step >= steps // I2)
+    def _():
+        dmid[...] = do[...]
+
+    def ctx_step(j, c):
+        rows = pl.ds(pl.multiple_of(j * SUB, SUB), SUB)
+        dctx[:, lanes(j * SUB, SUB)] = mm_nt(dmid[...], wobuf[rows, :]).astype(BF)
+        return c
+    lax.fori_loop(I0, half // SUB, ctx_step, I0)
+    g_load(step, False)
+    grad = gbuf.at[step % I2]
+
+    def mlp_block(n):
+        rows = pl.ds(pl.multiple_of(n * SUB, SUB), SUB)
+        cols = lanes(n * SUB, SUB)
+        dz = mm_nt(grad[...].reshape(BLOCK, width), wd[rows, :]).astype(BF).astype(F32)
+        up = u[:, cols].astype(F32)
+        gate, up2 = gelu_gate(up)
+        hidden = up * gate
+        z[:, cols] = hidden.astype(BF)
+        dup[:, cols] = (dz * gelu_slope(hidden, gate, up2)).astype(BF)
+
+    def both_step(j, c):
+        base = j * (I2 * HEAD_PAD)
+        at = [(pl.ds(s, seq), base + r * HEAD_PAD) for s in range(I0, BLOCK, seq) for r in range(I2)]
+        group = [(*(qkv[rows, lanes(t * half + col, HEAD_PAD)] for t in range(I3)), dctx[rows, lanes(col, HEAD_PAD)]) for rows, col in at]
+        blocks = [functools.partial(mlp_block, j * I3 + r) for r in range(I3)]
+        for (rows, col), grads in zip(at, attention_backward(group, scale, blocks)):
+            for t, value in enumerate(grads):
+                dqkv[rows, lanes(t * half + col, HEAD_PAD)] = value
+        return c
+    lax.fori_loop(I0, heads // I4, both_step, I0)
 
 
 def owner_backward(dims, dx, d_rows, og, ups, qkv, own):
@@ -1397,21 +1412,19 @@
     blocks = tokens // BLOCK
     vmem, dma = pltpu.VMEM, pltpu.SemaphoreType.DMA
     any_spec = pl.BlockSpec(memory_space=ANY)
-    first = lambda i: jnp.minimum(i, blocks - I1)
-    second = lambda i: jnp.maximum(i - blocks, I0)
     low = pl.BlockSpec((BLOCK, width), lambda i: (jnp.minimum(i, blocks // I2 - I1), I0))
-    high = pl.BlockSpec((BLOCK, width), lambda i: (jnp.maximum(first(i) - blocks // I2, I0), I0))
-    attn_block = pl.BlockSpec((BLOCK, I3 * half), lambda i: (first(i), I0))
-    mlp_block = pl.BlockSpec((BLOCK, ffn // I2), lambda i: (second(i), I0))
+    high = pl.BlockSpec((BLOCK, width), lambda i: (jnp.maximum(i - blocks // I2, I0), I0))
+    attn_block = pl.BlockSpec((BLOCK, I3 * half), lambda i: (i, I0))
+    mlp_block = pl.BlockSpec((BLOCK, ffn // I2), lambda i: (i, I0))
     act = (micro, seq, width)
     return pl.pallas_call(
         functools.partial(owner_backward_kernel, dims),
-        grid=(I2 * blocks,),
+        grid=(blocks,),
         out_shape=tuple(shapes((tokens, I3 * half), (tokens, ffn // I2), (tokens, ffn // I2), (micro, I2, seq, width), act, act)),
         in_specs=[any_spec, low, high, mlp_block, attn_block, any_spec, pl.BlockSpec((ffn // I2, width), lambda i: (I0, I0)), any_spec, any_spec],
         out_specs=(attn_block, mlp_block, mlp_block, any_spec, any_spec, any_spec),
         scratch_shapes=[vmem((BLOCK, width), BF), vmem((I2, BLOCK // seq, seq, width), BF), vmem((BLOCK, half), BF), vmem((half, width), BF), vmem(act, BF),
-                        dma(()), dma((I2,)), dma(()), dma((micro,)), dma(()), dma((I2,)), dma((I4,))],
+                        dma(()), dma((I2,)), dma(()), dma((micro,)), dma(()), dma((I2,)), dma((I4,)), pltpu.SemaphoreType.REGULAR],
         input_output_aliases={7: I4, I8: 5},
         compiler_params=pltpu.CompilerParams(collective_id=I2, has_side_effects=True, vmem_limit_bytes=VMEM_LIMIT),
         name='owner_backward',

time: 1320 us -> 1310 us (level)
  Pallas kernels: 1320 us -> 1300 us
    pallas_call x1, Pallas kernels: 178 us -> 162 us  [owner_backward(): pl.pallas_call(functools.partial(owner_backward_kernel, dims), grid=(bloc...]
where the time goes in v12:
time: 1310 us
  Pallas kernels  1300 us (99%)
    pallas_call x1, Pallas kernels, forward_phase(): pl.pallas_call(functools.partial(forward_kernel, dims), out_shape=tuple(o...  589 us
    pallas_call x1, Pallas kernels, backward_phase(): pl.pallas_call(functools.partial(backward_kernel, dims), out_shape=tuple(...  282 us
    pallas_call x1, Pallas kernels, owner_backward(): pl.pallas_call(functools.partial(owner_backward_kernel, dims), grid=(bloc...  162 us
    pallas_call x2, Pallas kernels, owner_recompute(): pl.pallas_call(functools.partial(recompute_kernel, dims, early), out_shap...  128 us
    pallas_call x1, Pallas kernels, mlp_products(): pl.pallas_call(mlp_products_kernel, grid=(cols // SUB,), out_shape=(jax.S...  86.6 us
    pallas_call x1, Pallas kernels, attn_products(): pl.pallas_call(attn_products_kernel, grid=(pairs,), out_shape=(jax.ShapeD...  51.5 us

profile of v12, /device:TPU:3, one launch (start us, length us, event | category | flops | bytes accessed | tf_op | source)
XLA Modules:
  0.0 1306.5 jit_solution(10533737490400812565)
XLA Ops:
  0.6 1.3 maximum_convert_fusion.own_gains.gains
  2.0 589.4 %forward_phase.1 = (bf16[8,192,1536]{2,1,0:T(8,128)(2,1)}, bf16[8,192,1536]{2,1,0:T(8,128)(2,1)}, bf16[8,192,6144]{2,1,0:T(8,128)(2,1)}, bf16[8,192,6144]{2,1,0:...) custom-call(bf16[8,2,192,1536]{3,2,1,0:T(8,128)(2,1)} %x_ref.1, ...), custom_call_target="tpu_custom_call" | custom-call | tf_op jit(solution)/shard_map/forward_phase/pallas_call | solution.py:1137
  591.4 1.0 owner_recompute.2
  592.4 282.4 %backward_phase.1 = (bf16[8,192,1536]{2,1,0:T(8,128)(2,1)}, bf16[8,192,1536]{2,1,0:T(8,128)(2,1)}, bf16[8,192,1536]{2,1,0:T(8,128)(2,1)}, bf16[8,192,1536]{2,1,0...) custom-call(bf16[8,192,1536]{2,1,0:T(8,128)(2,1)} %get-tuple-element, ...), custom_call_target="tpu_custom_call", output_to_operand_aliasing={{4}: (17, {}), {5}: (18, {}), {6}: (19, {}), {7}: (20, {}),... | custom-call | tf_op jit(solution)/shard_map/backward_phase/pallas_call | solution.py:1162
  874.8 126.5 %owner_recompute.3 = (f32[8,128]{1,0:T(8,128)}, bf16[3072,3072]{1,0:T(8,128)(2,1)}, bf16[3072,3072]{1,0:T(8,128)(2,1)}, bf16[3072,1024]{1,0:T(8,128)(2,1)}, bf16...) custom-call(bf16[1536,1536]{1,0:T(8,128)(2,1)} %bitcast.35, ...), custom_call_target="tpu_custom_call", output_to_operand_aliasing={{1}: (7, {}), {2}: (8, {}), {3}: (9, {}), {4}: (10, {}), {5... | custom-call | tf_op jit(solution)/shard_map/owner_recompute/pallas_call | solution.py:1248
  1001.3 1.3 reduce_sum.18
  1003.3 1.0 add_reduce_fusion
  1004.3 0.6 fusion
  1004.9 162.3 %owner_backward.1 = (bf16[3072,3072]{1,0:T(8,128)(2,1)}, bf16[3072,3072]{1,0:T(8,128)(2,1)}, bf16[3072,3072]{1,0:T(8,128)(2,1)}, bf16[8,2,192,1536]{3,2,1,0:T(8,...) custom-call(bf16[8,192,1536]{2,1,0:T(8,128)(2,1)} %get-tuple-element, ...), custom_call_target="tpu_custom_call", output_to_operand_aliasing={{4}: (7, {}), {5}: (8, {})} | custom-call | tf_op jit(solution)/shard_map/owner_backward/pallas_call | solution.py:1420
  1167.2 51.5 %attn_products.1 = (f32[3,8,96,1536]{3,2,1,0:T(8,128)}, f32[8,96,1536]{2,1,0:T(8,128)}, bf16[8,2,192,1536]{3,2,1,0:T(8,128)(2,1)}) custom-call(bf16[3072,3072]{1,0:T(8,128)(2,1)} %get-tuple-element.102.dq.dk.dv, bf16[3072,3072]{1,0:T(8,128)(2,1)} %get-tuple-element.102.dq.dk.dv, bf16[3072,3072]{1,0:T(8,128)(2,1)} %get-tuple-element.102.dq.dk.dv, ...), custom_call_target="tpu_custom_call" | custom-call | tf_op jit(solution)/shard_map/attn_products/pallas_call | solution.py:1487
  1218.7 86.6 %mlp_products.1 = (f32[1536,3072]{1,0:T(8,128)}, f32[3072,1536]{1,0:T(8,128)}) custom-call(bf16[3072,3072]{1,0:T(8,128)(2,1)} %get-tuple-element.109.dup, bf16[3072,3072]{1,0:T(8,128)(2,1)} %get-tuple-element.110.z, bf16[3072,1536]{1,0:T(8,128)(2,1)} %get-tuple-element.111.n2_o, bf16[1536,1536]{1,0:T(8,128)(2,1)} %bitcast.42, bf16[1536,1536]{1,0:T(8,128)(2,1)} %bitcast.43), custom_call_target="tpu_custom_call" | custom-call | tf_op jit(solution)/shard_map/mlp_products/pallas_call | solution.py:1529

commit v13 on v12

--- a/solution.py
+++ b/solution.py
@@ -26,6 +26,7 @@
 EARLY_G = 3
 STAGGER_NS = 6000
 EARLY_SEEDS = 5
+EARLY_DX = 3
 HEAD_PAD = 128
 VMEM_LIMIT = 67043328
 
@@ -247,8 +248,9 @@
 PIECES = [(0, 0, 0), (0, 0, 1), (0, 0, 2), (1, 0, 0), (2, 1, 0), (2, 1, 1), (2, 1, 2), (2, 1, 3), (3, 0, 0), (3, 0, 1), (3, 0, 2), (3, 0, 3)]
 
 
-ROUND = (10, 11)
-ROUND_STEPS = (1, 3)
+ROUND = (11,)
+ROUND_STEPS = (1,)
+ORDER = (0, 1, 2, 3, 4, 5, 6, 7, 11, 8, 9, 10)
 
 
 def piece(ref, axis, index):
@@ -366,9 +368,8 @@
             def _(k=i):
                 remote(round_a.at[k], round_a.at[k], rs_send.at[k], ra_sem.at[k], place.sibling).wait_recv()
                 remote(round_a.at[k], round_b.at[k], rs_send.at[k], rb_sem.at[k], place.across).start()
-    done = [I0, I0, I0, I0]
-
-    for c, (i, axis, index) in enumerate(PIECES):
+    for c in ORDER:
+        i, axis, index = PIECES[c]
         view = piece_of(far, c)
         for k, step in enumerate(ROUND_STEPS):
             if c == step:
@@ -387,8 +388,7 @@
         def _(c=c, view=view, sem=sem):
             remote(view, view, sem, far_sem.at[c], place.sibling).start()
         count = I4 if i < I2 else I3
-        turn(i, [(None, far[i])], I1, done[i], count)
-        done[i] += count
+        turn(i, [(None, far[i])], I1, index * count, count)
 
     @pl.when(place.is_l)
     def _():
@@ -398,7 +398,7 @@
     @pl.when(is_r)
     def _():
         for i in range(I4):
-            part = own[i] if i < I3 else own[i].at[I0:I2 * 768, :]
+            part = own[i] if i < I3 else own[i].at[I0:(I4 - len(ROUND)) * 768, :]
             remote(part, part, y_send.at[i], far_sem.at[I0], place.across_other).wait_send()
             remote(part, part, d_send.at[i], far_sem.at[I0], place.sibling).wait_send()
         for k in range(len(ROUND)):
@@ -938,7 +938,8 @@
                 for p, value in zip(at[r], grads):
                     dqkvbuf[:, p] = value
             return c
-        lax.fori_loop(I0, heads // I4, head_step, I0)
+        for t in range(heads // I4):
+            head_step(t, I0)
         load_next(i, I1)
         acc[...] = jnp.zeros_like(acc)
 
@@ -1171,8 +1172,58 @@
     )(*saved, *weights, gains, loss, after, *placed)
 
 
+def late_rows(micro):
+    return [micro - I1 - i for i in range(micro) if i % I2 == I0 or i > I2 * EARLY_G]
+
+
+def hand_on(place, dx, d_in, og, sems):
+    micro = dx.shape[I0]
+    barrier = pltpu.get_barrier_semaphore()
+    late = late_rows(micro)
+    is_leaf = place.home > I1
+    gives_g = (place.home == I1) & place.is_l
+    takes_g = (place.home == I0) & jnp.logical_not(place.is_l)
+    part, g_part = dx.at[I0:EARLY_DX], og.at[I0:len(late)]
+
+    @pl.when(is_leaf)
+    def _():
+        pl.semaphore_signal(barrier, inc=I1, device_id=place.along_x, device_id_type=MESH)
+
+    @pl.when(takes_g)
+    def _():
+        pl.semaphore_signal(barrier, inc=I1, device_id=place.across, device_id_type=MESH)
+
+    @pl.when(jnp.logical_not(is_leaf))
+    def _():
+        pl.semaphore_wait(barrier, I1 + gives_g.astype(jnp.int32))
+
+        @pl.when(gives_g)
+        def _():
+            for m in late:
+                remote(og.at[m], og.at[m], sems.at[I2], sems.at[I3], place.across).start()
+        for m in range(micro - EARLY_DX, micro):
+            remote(dx.at[m], d_in.at[m, place.core], sems.at[I0], sems.at[I1], place.along_x).start()
+        remote(part, part, sems.at[I0], sems.at[I1], place.along_x).wait_send()
+
+        @pl.when(gives_g)
+        def _():
+            remote(g_part, g_part, sems.at[I2], sems.at[I3], place.across).wait_send()
+
+    def received():
+        @pl.when(is_leaf)
+        def _():
+            remote(part, part, sems.at[I0], sems.at[I1], place.along_x).wait_recv()
+
+        @pl.when(takes_g)
+        def _():
+            remote(g_part, g_part, sems.at[I2], sems.at[I3], place.across).wait_recv()
+    return received
+
+
 def recompute_kernel(dims, early, h_same, h_other, a_same, a_other, gains, wq, wu, *refs):
-    (done, u_o, qkv_o, ctx_o, n1_o, n2_o), (wqbuf, wubuf, count, sem) = refs[-10:-I4], refs[-I4:]
+    (wqbuf, wubuf, count, sem, sems) = refs[-5:]
+    outs = refs[:-5] if early else refs[7:-5]
+    (done, u_o, qkv_o, ctx_o, n1_o, n2_o) = outs[I0:I6]
     micro, seq, width, heads, head_dim, ffn = dims
     place = Place()
     scale = head_dim ** -0.5
@@ -1220,6 +1271,8 @@
                 ctx[rows, lanes(base + col, HEAD_PAD)] = context
             return c
         lax.fori_loop(I0, I2, head_step, I0)
+
+    received = nothing if early else hand_on(place, refs[I0], outs[I6], outs[7], sems)
 
     @pl.when(place.home < I2 if early else place.home > I1)
     def _():
@@ -1236,6 +1289,7 @@
         pltpu.emit_pipeline(body, grid=(steps,), in_specs=[low, high, low, high],
                             out_specs=[block(ffn // I2), block(I3 * half), block(half), block(width), block(width)])(
             h_same, h_other, a_same, a_other, u_o, qkv_o, ctx_o, n1_o, n2_o)
+    received()
 
 
 def owner_recompute(dims, early, again, h_rows, a_rows, gains, own):
@@ -1245,19 +1299,25 @@
     any_spec = pl.BlockSpec(memory_space=ANY)
     vmem = pltpu.VMEM
     earlier = () if early else tuple(again)
+    act = (micro, seq, width)
+    out_shape = [jax.ShapeDtypeStruct((I8, 128), F32), *shapes((tokens, ffn // I2), (tokens, I3 * half), (tokens, half), (tokens, width), (tokens, width))]
+    if not early:
+        out_shape += shapes((micro, I2, seq, width), act)
+    aliases = {} if early else {I8 + i: I1 + i for i in range(5)} | {13: 7}
+    comm = {} if early else dict(collective_id=I3)
     return pl.pallas_call(
         functools.partial(recompute_kernel, dims, early),
-        out_shape=(jax.ShapeDtypeStruct((I8, 128), F32), *shapes((tokens, ffn // I2), (tokens, I3 * half), (tokens, half), (tokens, width), (tokens, width))),
+        out_shape=tuple(out_shape),
         in_specs=[any_spec] * I4 + [pl.BlockSpec(memory_space=vmem)] + [any_spec] * (I2 + len(earlier)),
-        out_specs=(any_spec,) * I6,
-        scratch_shapes=[vmem((I3 * half, width), BF), vmem((width, ffn // I2), BF), pltpu.SMEM((I1,), jnp.int32), pltpu.SemaphoreType.DMA((I3, ffn // I2 // SUB))],
-        input_output_aliases={7 + i: I1 + i for i in range(len(earlier))},
-        compiler_params=pltpu.CompilerParams(has_side_effects=True, vmem_limit_bytes=VMEM_LIMIT),
+        out_specs=(any_spec,) * len(out_shape),
+        scratch_shapes=[vmem((I3 * half, width), BF), vmem((width, ffn // I2), BF), pltpu.SMEM((I1,), jnp.int32), pltpu.SemaphoreType.DMA((I3, ffn // I2 // SUB)), pltpu.SemaphoreType.DMA((I4,))],
+        input_output_aliases=aliases,
+        compiler_params=pltpu.CompilerParams(**comm, has_side_effects=True, vmem_limit_bytes=VMEM_LIMIT),
         name='owner_recompute',
     )(*h_rows, *a_rows, gains, own[I0], own[I2], *earlier)
 
 
-def spread_dx(step, last, dx, d_in, og_same, og_other, bounce, here_sem, parent_sem, sib_sem, send_sems, og_sems, ready):
+def spread_dx(step, last, dx, d_in, og_other, bounce, here_sem, parent_sem, sib_sem, send_sems, og_sems, ready):
     place = Place()
     micro = dx.shape[I0]
     along_x = place.at(place.tp, (place.stage + I2) % I4)
@@ -1265,7 +1325,7 @@
     is_leaf = place.home > I1
     gives_g = (place.home == I1) & place.is_l
     takes_g = (place.home == I0) & jnp.logical_not(place.is_l)
-    late = [micro - I1 - i for i in range(micro) if i % I2 == I0 or i > I2 * EARLY_G]
+    late = late_rows(micro)
 
     def block(m):
         return d_in.at[m, place.core]
@@ -1296,15 +1356,15 @@
 
         @pl.when(gives_g)
         def _():
-            for t, og in enumerate((og_same, og_other)):
-                for m in late:
-                    remote(og.at[m], og.at[m], og_sems.at[t], og_sems.at[I2 + t], place.across).start()
+            for m in late:
+                remote(og_other.at[m], og_other.at[m], og_sems.at[I0], og_sems.at[I1], place.across).start()
 
     @pl.when((step == I3) & jnp.logical_not(is_leaf))
     def _():
         pl.semaphore_wait(ready, I1)
         for m in reversed(range(micro)):
-            remote(dx.at[m], block(m), send_sems.at[I1], parent_sem.at[m], along_x).start()
+            if m < micro - EARLY_DX:
+                remote(dx.at[m], block(m), send_sems.at[I1], parent_sem.at[m], along_x).start()
             to_sibling(m, dx.at[m])
         pltpu.make_async_copy(dx, bounce, here_sem).start()
 
@@ -1314,16 +1374,17 @@
         for m in range(micro):
             pltpu.make_async_copy(bounce.at[m], block(m), here_sem).start()
 
-    for t, og in enumerate((og_same, og_other)):
-        @pl.when((step == I3 * t) & takes_g)
-        def _(t=t, og=og):
-            part = og.at[I0:len(late)]
-            remote(part, part, og_sems.at[t], og_sems.at[I2 + t], place.across).wait_recv()
+    part = og_other.at[I0:len(late)]
+
+    @pl.when((step == I3) & takes_g)
+    def _():
+        remote(part, part, og_sems.at[I0], og_sems.at[I1], place.across).wait_recv()
 
     @pl.when((step == last) & is_leaf)
     def _():
         for m in reversed(range(micro)):
-            remote(block(m), block(m), send_sems.at[I0], parent_sem.at[m], place.sibling).wait_recv()
+            if m < micro - EARLY_DX:
+                remote(block(m), block(m), send_sems.at[I0], parent_sem.at[m], place.sibling).wait_recv()
             to_sibling(m, block(m))
 
     @pl.when(step == last)
@@ -1332,24 +1393,23 @@
 
         @pl.when(jnp.logical_not(is_leaf))
         def _():
-            remote(dx, dx, send_sems.at[I1], sib_sem, place.sibling).wait_send()
+            rest = dx.at[I0:micro - EARLY_DX]
+            remote(rest, rest, send_sems.at[I1], sib_sem, place.sibling).wait_send()
             pltpu.make_async_copy(dx, dx, here_sem).wait()
 
         @pl.when(gives_g)
         def _():
-            for t, og in enumerate((og_same, og_other)):
-                part = og.at[I0:len(late)]
-                remote(part, part, og_sems.at[t], og_sems.at[I2 + t], place.across).wait_send()
+            remote(part, part, og_sems.at[I0], og_sems.at[I1], place.across).wait_send()
         remote(dx, dx, send_sems.at[I0], sib_sem, place.sibling).wait_recv()
 
 
-def owner_backward_kernel(dims, dx, ds, do, u, qkv, wo, wd, gs_in, go_in, dqkv, dup, z, d_in, og_same, og_other,
+def owner_backward_kernel(dims, dx, ds, do, u, qkv, wo, wd, og_same, go_in, d_first, dqkv, dup, z, d_in, og_other,
                           dmid, gbuf, dctx, wobuf, bounce, sem, g_sem, here_sem, parent_sem, sib_sem, send_sems, og_sems, ready):
     micro, seq, width, heads, head_dim, ffn = dims
     half = heads // I2 * HEAD_PAD
     scale = head_dim ** -0.5
     step, steps = pl.program_id(I0), pl.num_programs(I0)
-    spread_dx(step, steps - I1, dx, d_in, og_same, og_other, bounce, here_sem, parent_sem, sib_sem, send_sems, og_sems, ready)
+    spread_dx(step, steps - I1, dx, d_in, og_other, bounce, here_sem, parent_sem, sib_sem, send_sems, og_sems, ready)
 
     def g_load(n, start):
         rows = BLOCK // seq
@@ -1405,7 +1465,7 @@
     lax.fori_loop(I0, heads // I4, both_step, I0)
 
 
-def owner_backward(dims, dx, d_rows, og, ups, qkv, own):
+def owner_backward(dims, dx, d_in, d_rows, og, ups, qkv, own):
     micro, seq, width, heads, head_dim, ffn = dims
     half = heads // I2 * HEAD_PAD
     tokens = I2 * micro * seq
@@ -1420,15 +1480,15 @@
     return pl.pallas_call(
         functools.partial(owner_backward_kernel, dims),
         grid=(blocks,),
-        out_shape=tuple(shapes((tokens, I3 * half), (tokens, ffn // I2), (tokens, ffn // I2), (micro, I2, seq, width), act, act)),
-        in_specs=[any_spec, low, high, mlp_block, attn_block, any_spec, pl.BlockSpec((ffn // I2, width), lambda i: (I0, I0)), any_spec, any_spec],
-        out_specs=(attn_block, mlp_block, mlp_block, any_spec, any_spec, any_spec),
+        out_shape=tuple(shapes((tokens, I3 * half), (tokens, ffn // I2), (tokens, ffn // I2), (micro, I2, seq, width), act)),
+        in_specs=[any_spec, low, high, mlp_block, attn_block, any_spec, pl.BlockSpec((ffn // I2, width), lambda i: (I0, I0)), any_spec, any_spec, any_spec],
+        out_specs=(attn_block, mlp_block, mlp_block, any_spec, any_spec),
         scratch_shapes=[vmem((BLOCK, width), BF), vmem((I2, BLOCK // seq, seq, width), BF), vmem((BLOCK, half), BF), vmem((half, width), BF), vmem(act, BF),
-                        dma(()), dma((I2,)), dma(()), dma((micro,)), dma(()), dma((I2,)), dma((I4,)), pltpu.SemaphoreType.REGULAR],
-        input_output_aliases={7: I4, I8: 5},
+                        dma(()), dma((I2,)), dma(()), dma((micro,)), dma(()), dma((I2,)), dma((I2,)), pltpu.SemaphoreType.REGULAR],
+        input_output_aliases={I8: I4, 9: I3},
         compiler_params=pltpu.CompilerParams(collective_id=I2, has_side_effects=True, vmem_limit_bytes=VMEM_LIMIT),
         name='owner_backward',
-    )(dx, *d_rows, ups, qkv, own[I1], own[I3], *og)
+    )(dx, *d_rows, ups, qkv, own[I1], own[I3], *og, d_in)
 
 
 def bring(pairs, sem):
@@ -1566,10 +1626,10 @@
         dx, _, od_same, od_other, og_same, og_other, oa_same, oa_other, oh_same, oh_other, dg_same, dg_other, loss_all = backward_phase(
             dims, (acts, mids, qkv, ups, seeds), (rows_of[I0], nq, fq, td0, td1, to0, to1, tu0, tu1), home_gains, loss_tile, done,
             (og_same, og_other, oa_same, oa_other, oh_same, oh_other))
-        _, *again = owner_recompute(dims, False, again, flat(oh_same, oh_other), flat(oa_same, oa_other), own_gains, rows_of)
+        _, *again, d_first, og_same = owner_recompute(dims, False, (dx, *again, og_same), flat(oh_same, oh_other), flat(oa_same, oa_other), own_gains, rows_of)
         ups_own, qkv_own, ctx_own, n1, n2 = again
         d_rows = flat(od_same, od_other)
-        d_qkv_rows, d_up_rows, hidden, dx_all, og_same, og_other = owner_backward(dims, dx, d_rows, (og_same, og_other), ups_own, qkv_own, rows_of)
+        d_qkv_rows, d_up_rows, hidden, dx_all, og_other = owner_backward(dims, dx, d_first, d_rows, (og_same, og_other), ups_own, qkv_own, rows_of)
         d_qkv, d_out, d_inputs = attn_products(d_qkv_rows, ctx_own, n1, d_rows, dx_all, w_out.shape[I1:])
         d_up, d_down = mlp_products(d_up_rows, hidden, n2, flat(og_same, og_other))
         weight_grads = (d_qkv.transpose(I3, I0, I1, I2), d_out, d_up, d_down)

time: 1310 us -> 1300 us (level)
    pallas_call x2, Pallas kernels: 128 us -> 163 us  [owner_recompute(): pl.pallas_call(functools.partial(recompute_kernel, dims, early), out_shap...]
    pallas_call x1, Pallas kernels: 162 us -> 132 us  [owner_backward(): pl.pallas_call(functools.partial(owner_backward_kernel, dims), grid=(bloc...]
where the time goes in v13:
time: 1300 us
  Pallas kernels  1290 us (99%)
    pallas_call x1, Pallas kernels, forward_phase(): pl.pallas_call(functools.partial(forward_kernel, dims), out_shape=tuple(o...  577 us
    pallas_call x1, Pallas kernels, backward_phase(): pl.pallas_call(functools.partial(backward_kernel, dims), out_shape=tuple(...  281 us
    pallas_call x2, Pallas kernels, owner_recompute(): pl.pallas_call(functools.partial(recompute_kernel, dims, early), out_shap...  163 us
    pallas_call x1, Pallas kernels, owner_backward(): pl.pallas_call(functools.partial(owner_backward_kernel, dims), grid=(bloc...  132 us
    pallas_call x1, Pallas kernels, mlp_products(): pl.pallas_call(mlp_products_kernel, grid=(cols // SUB,), out_shape=(jax.S...  86.6 us
    pallas_call x1, Pallas kernels, attn_products(): pl.pallas_call(attn_products_kernel, grid=(pairs,), out_shape=(jax.ShapeD...  51.5 us

profile of v13, /device:TPU:3, one launch (start us, length us, event | category | flops | bytes accessed | tf_op | source)
XLA Modules:
  0.0 1297.5 jit_solution(8736404720176824784)
XLA Ops:
  0.6 1.3 maximum_convert_fusion.own_gains.gains
  2.0 576.7 %forward_phase.1 = (bf16[8,192,1536]{2,1,0:T(8,128)(2,1)}, bf16[8,192,1536]{2,1,0:T(8,128)(2,1)}, bf16[8,192,6144]{2,1,0:T(8,128)(2,1)}, bf16[8,192,6144]{2,1,0:...) custom-call(bf16[8,2,192,1536]{3,2,1,0:T(8,128)(2,1)} %x_ref.1, ...), custom_call_target="tpu_custom_call" | custom-call | tf_op jit(solution)/shard_map/forward_phase/pallas_call | solution.py:1138
  578.7 1.1 owner_recompute.2
  579.7 280.6 %backward_phase.1 = (bf16[8,192,1536]{2,1,0:T(8,128)(2,1)}, bf16[8,192,1536]{2,1,0:T(8,128)(2,1)}, bf16[8,192,1536]{2,1,0:T(8,128)(2,1)}, bf16[8,192,1536]{2,1,0...) custom-call(bf16[8,192,1536]{2,1,0:T(8,128)(2,1)} %get-tuple-element, ...), custom_call_target="tpu_custom_call", output_to_operand_aliasing={{4}: (17, {}), {5}: (18, {}), {6}: (19, {}), {7}: (20, {}),... | custom-call | tf_op jit(solution)/shard_map/backward_phase/pallas_call | solution.py:1163
  860.4 1.3 reduce_sum.18
  862.3 1.0 add_reduce_fusion
  863.3 0.6 fusion
  863.9 162.1 %owner_recompute.3 = (f32[8,128]{1,0:T(8,128)}, bf16[3072,3072]{1,0:T(8,128)(2,1)}, bf16[3072,3072]{1,0:T(8,128)(2,1)}, bf16[3072,1024]{1,0:T(8,128)(2,1)}, bf16...) custom-call(bf16[1536,1536]{1,0:T(8,128)(2,1)} %bitcast.36, ...), custom_call_target="tpu_custom_call", output_to_operand_aliasing={{1}: (8, {}), {2}: (9, {}), {3}: (10, {}), {4}: (11, {}), {... | custom-call | tf_op jit(solution)/shard_map/owner_recompute/pallas_call | solution.py:1308
  1026.1 132.2 %owner_backward.1 = (bf16[3072,3072]{1,0:T(8,128)(2,1)}, bf16[3072,3072]{1,0:T(8,128)(2,1)}, bf16[3072,3072]{1,0:T(8,128)(2,1)}, bf16[8,2,192,1536]{3,2,1,0:T(8,128)(2,1)}, bf16[8,192,1536]{2,1,0:T(8,128)(2,1)}) custom-call(bf16[8,192,1536]{2,1,0:T(8,128)(2,1)} %get-tuple-element.87.refs_0_.dx, ...), custom_call_target="tpu_custom_call", output_to_operand_aliasing={{4}: (8, {}), {3}: (9, {})} | custom-call | tf_op jit(solution)/shard_map/owner_backward/pallas_call | solution.py:1480
  1158.3 51.5 %attn_products.1 = (f32[3,8,96,1536]{3,2,1,0:T(8,128)}, f32[8,96,1536]{2,1,0:T(8,128)}, bf16[8,2,192,1536]{3,2,1,0:T(8,128)(2,1)}) custom-call(bf16[3072,3072]{1,0:T(8,128)(2,1)} %get-tuple-element.105.dq.dk.dv, bf16[3072,3072]{1,0:T(8,128)(2,1)} %get-tuple-element.105.dq.dk.dv, bf16[3072,3072]{1,0:T(8,128)(2,1)} %get-tuple-element.105.dq.dk.dv, ...), custom_call_target="tpu_custom_call" | custom-call | tf_op jit(solution)/shard_map/attn_products/pallas_call | solution.py:1547
  1209.7 86.6 %mlp_products.1 = (f32[1536,3072]{1,0:T(8,128)}, f32[3072,1536]{1,0:T(8,128)}) custom-call(bf16[3072,3072]{1,0:T(8,128)(2,1)} %get-tuple-element.112.dup, bf16[3072,3072]{1,0:T(8,128)(2,1)} %get-tuple-element.113.z, bf16[3072,1536]{1,0:T(8,128)(2,1)} %get-tuple-element.114.n2_o, bf16[1536,1536]{1,0:T(8,128)(2,1)} %bitcast.34, bf16[1536,1536]{1,0:T(8,128)(2,1)} %bitcast.43), custom_call_target="tpu_custom_call" | custom-call | tf_op jit(solution)/shard_map/mlp_products/pallas_call | solution.py:1589

commit v14 on v13

--- a/solution.py
+++ b/solution.py
@@ -26,7 +26,7 @@
 EARLY_G = 3
 STAGGER_NS = 6000
 EARLY_SEEDS = 5
-EARLY_DX = 3
+EARLY_DX = 2
 HEAD_PAD = 128
 VMEM_LIMIT = 67043328
 
@@ -140,15 +140,19 @@
     return jnp.concatenate([top + low[:cut], low[cut:]], I0).astype(BF)
 
 
-def attention_forward(heads, scale):
+def nothing():
+    pass
+
+
+def attention_forward(heads, scale, between=()):
+    work = iter(between)
     units = row_parts([((q,), (k, v)) for q, k, v in heads])
-    probs = softmax_parts([mm_nt(q, k) * scale for q, k, _, _ in units], [u[-I1] for u in units], I1)
+    scores = [mm_nt(q, k) * scale for q, k, _, _ in units]
+    next(work, nothing)()
+    probs = softmax_parts(scores, [u[-I1] for u in units], I1)
+    next(work, nothing)()
     parts = [mm(p.astype(BF), u[I2]) for p, u in zip(probs, units)]
     return [jnp.concatenate([a, b], I0).astype(BF) for a, b in zip(parts[I0::I2], parts[I1::I2])]
-
-
-def nothing():
-    pass
 
 
 def attention_backward(heads, scale, between=()):
@@ -782,8 +786,12 @@
 
     barrier = pltpu.get_barrier_semaphore()
     is_b, is_c = place.home == I1, place.home == I2
-    for there in (place.sibling, place.across, place.across_other):
-        pl.semaphore_signal(barrier, inc=I1, device_id=there, device_id_type=MESH)
+    pl.semaphore_signal(barrier, inc=I1, device_id=place.sibling, device_id_type=MESH)
+
+    @pl.when(jnp.logical_not(is_first))
+    def _():
+        for there in (place.across, place.across_other):
+            pl.semaphore_signal(barrier, inc=I1, device_id=there, device_id_type=MESH)
 
     @pl.when(is_c)
     def _():
@@ -938,8 +946,7 @@
                 for p, value in zip(at[r], grads):
                     dqkvbuf[:, p] = value
             return c
-        for t in range(heads // I4):
-            head_step(t, I0)
+        lax.fori_loop(I0, I2, lambda t, c: head_step(I2 * t + I1, head_step(I2 * t, c)), I0)
         load_next(i, I1)
         acc[...] = jnp.zeros_like(acc)
 
@@ -957,13 +964,17 @@
 
         @pl.when(i == I0)
         def _():
-            @pl.when(is_first | is_last)
+            @pl.when(is_last)
             def _():
                 pl.semaphore_wait(barrier, I3)
 
             @pl.when(is_c)
             def _():
                 pl.semaphore_wait(ready, I1)
+
+            @pl.when(is_b)
+            def _():
+                pl.semaphore_wait(ready, I2)
 
             @pl.when(is_last)
             def _():
@@ -1005,9 +1016,14 @@
         def _():
             remote(gbuf.at[m], og_other.at[m], bulk.at[I4], go_sem, place.across_other).start()
 
-    @pl.when(is_b | is_c)
-    def _():
-        pl.semaphore_wait(barrier, 5 - place.home)
+    @pl.when(jnp.logical_not(is_last))
+    def _():
+        pl.semaphore_wait(barrier, I3 - is_b.astype(jnp.int32))
+
+    @pl.when(is_first)
+    def _():
+        for there in (place.across, place.across_other):
+            pl.semaphore_signal(ready, inc=I1, device_id=there, device_id_type=MESH)
 
     @pl.when(is_b)
     def _():
@@ -1259,15 +1275,20 @@
         def qkv_step(j, c):
             rows = pl.ds(pl.multiple_of(j * SUB, SUB), SUB)
             qkv[:, lanes(j * SUB, SUB)] = mm_nt(n1[...], wqbuf[rows, :]).astype(BF)
-            u[:, lanes(j * SUB, SUB)] = mm(n2[...], wubuf[:, lanes(j * SUB, SUB)]).astype(BF)
             return c
         lax.fori_loop(I0, I3 * half // SUB, qkv_step, I0)
 
         def head_step(j, c):
             at = [(pl.ds(s, seq), r * HEAD_PAD) for s in range(I0, BLOCK, seq) for r in range(I4)]
             base = j * (I4 * HEAD_PAD)
+
+            def up_blocks(first):
+                for n in range(I3):
+                    cols = lanes((j * I6 + first + n) * SUB, SUB)
+                    u[:, cols] = mm(n2[...], wubuf[:, cols]).astype(BF)
             views = [[qkv[rows, lanes(base + t * half + col, HEAD_PAD)] for t in range(I3)] for rows, col in at]
-            for (rows, col), context in zip(at, attention_forward(views, scale)):
+            between = [functools.partial(up_blocks, I0), functools.partial(up_blocks, I3)]
+            for (rows, col), context in zip(at, attention_forward(views, scale, between)):
                 ctx[rows, lanes(base + col, HEAD_PAD)] = context
             return c
         lax.fori_loop(I0, I2, head_step, I0)
@@ -1359,7 +1380,7 @@
             for m in late:
                 remote(og_other.at[m], og_other.at[m], og_sems.at[I0], og_sems.at[I1], place.across).start()
 
-    @pl.when((step == I3) & jnp.logical_not(is_leaf))
+    @pl.when((step == I1) & jnp.logical_not(is_leaf))
     def _():
         pl.semaphore_wait(ready, I1)
         for m in reversed(range(micro)):
@@ -1368,7 +1389,7 @@
             to_sibling(m, dx.at[m])
         pltpu.make_async_copy(dx, bounce, here_sem).start()
 
-    @pl.when((step == I4) & jnp.logical_not(is_leaf))
+    @pl.when((step == I2) & jnp.logical_not(is_leaf))
     def _():
         pltpu.make_async_copy(dx, bounce, here_sem).wait()
         for m in range(micro):

time: 1300 us -> 1290 us (level)
    pallas_call x2, Pallas kernels: 163 us -> 150 us  [owner_recompute(): pl.pallas_call(functools.partial(recompute_kernel, dims, early), out_shap...]
where the time goes in v14:
time: 1290 us
  Pallas kernels  1280 us (99%)
    pallas_call x1, Pallas kernels, forward_phase(): pl.pallas_call(functools.partial(forward_kernel, dims), out_shape=tuple(o...  577 us
    pallas_call x1, Pallas kernels, backward_phase(): pl.pallas_call(functools.partial(backward_kernel, dims), out_shape=tuple(...  282 us
    pallas_call x2, Pallas kernels, owner_recompute(): pl.pallas_call(functools.partial(recompute_kernel, dims, early), out_shap...  150 us
    pallas_call x1, Pallas kernels, owner_backward(): pl.pallas_call(functools.partial(owner_backward_kernel, dims), grid=(bloc...  133 us
    pallas_call x1, Pallas kernels, mlp_products(): pl.pallas_call(mlp_products_kernel, grid=(cols // SUB,), out_shape=(jax.S...  86.6 us
    pallas_call x1, Pallas kernels, attn_products(): pl.pallas_call(attn_products_kernel, grid=(pairs,), out_shape=(jax.ShapeD...  51.5 us

profile of v14, /device:TPU:3, one launch (start us, length us, event | category | flops | bytes accessed | tf_op | source)
XLA Modules:
  0.0 1286.2 jit_solution(1881846921075716696)
XLA Ops:
  0.6 1.3 maximum_convert_fusion.own_gains.gains
  2.0 576.7 %forward_phase.1 = (bf16[8,192,1536]{2,1,0:T(8,128)(2,1)}, bf16[8,192,1536]{2,1,0:T(8,128)(2,1)}, bf16[8,192,6144]{2,1,0:T(8,128)(2,1)}, bf16[8,192,6144]{2,1,0:...) custom-call(bf16[8,2,192,1536]{3,2,1,0:T(8,128)(2,1)} %x_ref.1, ...), custom_call_target="tpu_custom_call" | custom-call | tf_op jit(solution)/shard_map/forward_phase/pallas_call | solution.py:1154
  578.7 1.1 owner_recompute.2
  579.7 282.2 %backward_phase.1 = (bf16[8,192,1536]{2,1,0:T(8,128)(2,1)}, bf16[8,192,1536]{2,1,0:T(8,128)(2,1)}, bf16[8,192,1536]{2,1,0:T(8,128)(2,1)}, bf16[8,192,1536]{2,1,0...) custom-call(bf16[8,192,1536]{2,1,0:T(8,128)(2,1)} %get-tuple-element, ...), custom_call_target="tpu_custom_call", output_to_operand_aliasing={{4}: (17, {}), {5}: (18, {}), {6}: (19, {}), {7}: (20, {}),... | custom-call | tf_op jit(solution)/shard_map/backward_phase/pallas_call | solution.py:1179
  861.9 1.3 reduce_sum.18
  863.9 1.0 add_reduce_fusion
  864.9 0.6 fusion
  865.5 148.5 %owner_recompute.3 = (f32[8,128]{1,0:T(8,128)}, bf16[3072,3072]{1,0:T(8,128)(2,1)}, bf16[3072,3072]{1,0:T(8,128)(2,1)}, bf16[3072,1024]{1,0:T(8,128)(2,1)}, bf16...) custom-call(bf16[1536,1536]{1,0:T(8,128)(2,1)} %bitcast.36, ...), custom_call_target="tpu_custom_call", output_to_operand_aliasing={{1}: (8, {}), {2}: (9, {}), {3}: (10, {}), {4}: (11, {}), {... | custom-call | tf_op jit(solution)/shard_map/owner_recompute/pallas_call | solution.py:1329
  1014.0 132.9 %owner_backward.1 = (bf16[3072,3072]{1,0:T(8,128)(2,1)}, bf16[3072,3072]{1,0:T(8,128)(2,1)}, bf16[3072,3072]{1,0:T(8,128)(2,1)}, bf16[8,2,192,1536]{3,2,1,0:T(8,128)(2,1)}, bf16[8,192,1536]{2,1,0:T(8,128)(2,1)}) custom-call(bf16[8,192,1536]{2,1,0:T(8,128)(2,1)} %get-tuple-element.87.refs_0_.dx, ...), custom_call_target="tpu_custom_call", output_to_operand_aliasing={{4}: (8, {}), {3}: (9, {})} | custom-call | tf_op jit(solution)/shard_map/owner_backward/pallas_call | solution.py:1501
  1146.9 51.5 %attn_products.1 = (f32[3,8,96,1536]{3,2,1,0:T(8,128)}, f32[8,96,1536]{2,1,0:T(8,128)}, bf16[8,2,192,1536]{3,2,1,0:T(8,128)(2,1)}) custom-call(bf16[3072,3072]{1,0:T(8,128)(2,1)} %get-tuple-element.105.dq.dk.dv, bf16[3072,3072]{1,0:T(8,128)(2,1)} %get-tuple-element.105.dq.dk.dv, bf16[3072,3072]{1,0:T(8,128)(2,1)} %get-tuple-element.105.dq.dk.dv, ...), custom_call_target="tpu_custom_call" | custom-call | tf_op jit(solution)/shard_map/attn_products/pallas_call | solution.py:1568
  1198.4 86.6 %mlp_products.1 = (f32[1536,3072]{1,0:T(8,128)}, f32[3072,1536]{1,0:T(8,128)}) custom-call(bf16[3072,3072]{1,0:T(8,128)(2,1)} %get-tuple-element.112.dup, bf16[3072,3072]{1,0:T(8,128)(2,1)} %get-tuple-element.113.z, bf16[3072,1536]{1,0:T(8,128)(2,1)} %get-tuple-element.114.n2_o, bf16[1536,1536]{1,0:T(8,128)(2,1)} %bitcast.34, bf16[1536,1536]{1,0:T(8,128)(2,1)} %bitcast.43), custom_call_target="tpu_custom_call" | custom-call | tf_op jit(solution)/shard_map/mlp_products/pallas_call | solution.py:1610

commit v15 on v14

--- a/solution.py
+++ b/solution.py
@@ -261,7 +261,7 @@
     return ref.at[index * 768:(index + I1) * 768, :] if axis == I0 else ref.at[:, index * 768:(index + I1) * 768]
 
 
-def weight_phase(place, is_r, own, near, far, turned, up_chunks, wn, wk, send_sem, y_send, d_send, near_sem, far_sem, load_sem, store_sem, chunk_sem,
+def weight_phase(place, is_r, own, near, far, turned, turned_own, up_chunks, wn, wk, send_sem, y_send, d_send, near_sem, far_sem, load_sem, store_sem, chunk_sem,
                  round_a, round_b, ra_sem, rb_sem, x_send, xd_send, rs_send):
     wk[...] = jnp.zeros_like(wk)
     early = place.home < I2
@@ -324,8 +324,8 @@
     def keep(which, t, slot):
         return pltpu.make_async_copy(wn.at[slot, :, I0:SUB], up_chunks[which].at[t // I4, :, lanes(t % I4 * SUB, SUB)], chunk_sem.at[slot])
 
-    def turn(i, refs, which, first, count):
-        dst = turned[i][which]
+    def turn(i, refs, which, first, count, dst=None):
+        dst = turned[i][which] if dst is None else dst
         load(i, refs, first, I0)
 
         def step(n, c):
@@ -372,6 +372,11 @@
             def _(k=i):
                 remote(round_a.at[k], round_a.at[k], rs_send.at[k], ra_sem.at[k], place.sibling).wait_recv()
                 remote(round_a.at[k], round_b.at[k], rs_send.at[k], rb_sem.at[k], place.across).start()
+
+    @pl.when(is_r)
+    def _():
+        for i, dst in zip((I0, I3), turned_own):
+            turn(i, [(None, own[i])], I0, I0, counts[i], dst)
     for c in ORDER:
         i, axis, index = PIECES[c]
         view = piece_of(far, c)
@@ -425,7 +430,7 @@
 
 def forward_kernel(dims, x_ref, y_ref, wq, wo, wu, wd, own_gains,
                    a_s, h_s, qkv_s, u_s, g_s, oh_same, oh_other, oa_same, oa_other, og_same, og_other, loss_s, home_gains,
-                   nq, no, nu, nd, fq, fo, fu, fd, tq0, to0, tu0, td0, tq1, to1, tu1, td1, uc0, uc1, round_a, round_b,
+                   nq, no, nu, nd, fq, fo, fu, fd, tq0, to0, tu0, td0, tq1, to1, tu1, td1, uc0, uc1, tqo, tdo, round_a, round_b,
                    abuf, hbuf, obuf, nbuf, ybuf, sbuf, qkvbuf, ubuf, zbuf, ctxbuf, lossbuf, losstile, gains, wres, wores, wn,
                    send_sem, y_send, d_send, near_sem, far_sem, t_load, t_store, t_keep, ra_sem, rb_sem, x_send, xd_send, rs_send,
                    act_sem, hop_f, keep_sem, save_sem, stream_n, res_sem, out_sem, big_sem, y_sem, s_sem,
@@ -453,7 +458,7 @@
     def _():
         for m in range(micro):
             pltpu.make_async_copy(x_ref.at[m, place.core], abuf.at[m], act_sem.at[m]).start()
-    weight_phase(place, is_r, own, near, far, turned, (uc0, uc1), wn, wores, send_sem, y_send, d_send, near_sem, far_sem, t_load, t_store, t_keep,
+    weight_phase(place, is_r, own, near, far, turned, (tqo, tdo), (uc0, uc1), wn, wores, send_sem, y_send, d_send, near_sem, far_sem, t_load, t_store, t_keep,
                  round_a, round_b, ra_sem, rb_sem, x_send, xd_send, rs_send)
     pltpu.make_async_copy(own_gains, gains, gain_sem.at[I0]).wait()
     pltpu.make_async_copy(gains, home_gains, gain_sem.at[I0]).start()
@@ -1139,7 +1144,7 @@
     turned = [(I3, width, CHUNK), (I1, width, CHUNK), (ffn // I2, width), (I3, width, CHUNK)]
     out_shape = shapes(act, act, (micro, seq, I6 * half), (micro, seq, ffn), *[act] * 7)
     out_shape += [jax.ShapeDtypeStruct(s, F32) for s in ((I8, 128), own_gains.shape)]
-    out_shape += shapes(*raw, *raw, *turned, *turned, turned[I0], turned[I0], *[(len(ROUND), 768, width)] * I2)
+    out_shape += shapes(*raw, *raw, *turned, *turned, *[turned[I0]] * I4, *[(len(ROUND), 768, width)] * I2)
     any_spec = pl.BlockSpec(memory_space=ANY)
     vmem, dma = pltpu.VMEM, pltpu.SemaphoreType.DMA
     row = vmem((seq, width), BF)
@@ -1195,7 +1200,7 @@
 def hand_on(place, dx, d_in, og, sems):
     micro = dx.shape[I0]
     barrier = pltpu.get_barrier_semaphore()
-    late = late_rows(micro)
+    late = [m for m in late_rows(micro) if m < I4]
     is_leaf = place.home > I1
     gives_g = (place.home == I1) & place.is_l
     takes_g = (place.home == I0) & jnp.logical_not(place.is_l)
@@ -1236,7 +1241,7 @@
     return received
 
 
-def recompute_kernel(dims, early, h_same, h_other, a_same, a_other, gains, wq, wu, *refs):
+def recompute_kernel(dims, early, h_same, h_other, a_same, a_other, gains, wq_near, wq_own, wu, *refs):
     (wqbuf, wubuf, count, sem, sems) = refs[-5:]
     outs = refs[:-5] if early else refs[7:-5]
     (done, u_o, qkv_o, ctx_o, n1_o, n2_o) = outs[I0:I6]
@@ -1247,12 +1252,9 @@
     steps = I2 * micro * seq // BLOCK
 
     def pieces(j):
-        copies = [pltpu.make_async_copy(wu.at[:, lanes(j * SUB, SUB)], wubuf.at[:, lanes(j * SUB, SUB)], sem.at[I0, j])]
-        for r in range(I2):
-            src = pl.ds(pl.multiple_of((I2 * j + r) * head_dim, head_dim), head_dim)
-            dst = pl.ds(pl.multiple_of((I2 * j + r) * HEAD_PAD, HEAD_PAD), head_dim)
-            copies.append(pltpu.make_async_copy(wq.at[src, :], wqbuf.at[dst, :], sem.at[I1 + r, j]))
-        return copies
+        cols = lanes(j * CHUNK, CHUNK)
+        up = pltpu.make_async_copy(wu.at[:, cols], wubuf.at[:, cols], sem.at[I0, j])
+        return up, [pltpu.make_async_copy(wq.at[j], wqbuf.at[j], sem.at[I1, j]) for wq in (wq_near, wq_own)]
 
     def body(hs, ho, rs, ro, u, qkv, ctx, n1, n2):
         step = count[I0]
@@ -1268,13 +1270,13 @@
 
         @pl.when(step == I0)
         def _():
-            for j in range(I3 * half // SUB):
-                for copy in pieces(j):
-                    copy.wait()
+            for j in range(I3):
+                up, (near, _) = pieces(j)
+                up.wait()
+                near.wait()
 
         def qkv_step(j, c):
-            rows = pl.ds(pl.multiple_of(j * SUB, SUB), SUB)
-            qkv[:, lanes(j * SUB, SUB)] = mm_nt(n1[...], wqbuf[rows, :]).astype(BF)
+            qkv[:, lanes(j * SUB, SUB)] = mm(n1[...], wqbuf[j // I4, :, lanes(j % I4 * SUB, SUB)]).astype(BF)
             return c
         lax.fori_loop(I0, I3 * half // SUB, qkv_step, I0)
 
@@ -1297,12 +1299,11 @@
 
     @pl.when(place.home < I2 if early else place.home > I1)
     def _():
-        pads = jnp.zeros((HEAD_PAD - head_dim, width), BF)
-        for t in range(I3 * heads // I2):
-            wqbuf[t * HEAD_PAD + head_dim:(t + I1) * HEAD_PAD, :] = pads
-        for j in range(I3 * half // SUB):
-            for copy in pieces(j):
-                copy.start()
+        for j in range(I3):
+            up, (near, mine) = pieces(j)
+            up.start()
+            pl.when(place.is_l)(near.start)
+            pl.when(jnp.logical_not(place.is_l))(mine.start)
         count[I0] = I0
         low = pl.BlockSpec((BLOCK, width), lambda i: (jnp.minimum(i, steps // I2 - I1), I0))
         high = pl.BlockSpec((BLOCK, width), lambda i: (jnp.maximum(i - steps // I2, I0), I0))
@@ -1313,7 +1314,7 @@
     received()
 
 
-def owner_recompute(dims, early, again, h_rows, a_rows, gains, own):
+def owner_recompute(dims, early, again, h_rows, a_rows, gains, w_qkv, w_up):
     micro, seq, width, heads, head_dim, ffn = dims
     half = heads // I2 * HEAD_PAD
     tokens = I2 * micro * seq
@@ -1324,21 +1325,21 @@
     out_shape = [jax.ShapeDtypeStruct((I8, 128), F32), *shapes((tokens, ffn // I2), (tokens, I3 * half), (tokens, half), (tokens, width), (tokens, width))]
     if not early:
         out_shape += shapes((micro, I2, seq, width), act)
-    aliases = {} if early else {I8 + i: I1 + i for i in range(5)} | {13: 7}
+    aliases = {} if early else {9 + i: I1 + i for i in range(5)} | {14: 7}
     comm = {} if early else dict(collective_id=I3)
     return pl.pallas_call(
         functools.partial(recompute_kernel, dims, early),
         out_shape=tuple(out_shape),
-        in_specs=[any_spec] * I4 + [pl.BlockSpec(memory_space=vmem)] + [any_spec] * (I2 + len(earlier)),
+        in_specs=[any_spec] * I4 + [pl.BlockSpec(memory_space=vmem)] + [any_spec] * (I3 + len(earlier)),
         out_specs=(any_spec,) * len(out_shape),
-        scratch_shapes=[vmem((I3 * half, width), BF), vmem((width, ffn // I2), BF), pltpu.SMEM((I1,), jnp.int32), pltpu.SemaphoreType.DMA((I3, ffn // I2 // SUB)), pltpu.SemaphoreType.DMA((I4,))],
+        scratch_shapes=[vmem((I3, width, CHUNK), BF), vmem((width, ffn // I2), BF), pltpu.SMEM((I1,), jnp.int32), pltpu.SemaphoreType.DMA((I2, I3)), pltpu.SemaphoreType.DMA((I4,))],
         input_output_aliases=aliases,
         compiler_params=pltpu.CompilerParams(**comm, has_side_effects=True, vmem_limit_bytes=VMEM_LIMIT),
         name='owner_recompute',
-    )(*h_rows, *a_rows, gains, own[I0], own[I2], *earlier)
-
-
-def spread_dx(step, last, dx, d_in, og_other, bounce, here_sem, parent_sem, sib_sem, send_sems, og_sems, ready):
+    )(*h_rows, *a_rows, gains, *w_qkv, w_up, *earlier)
+
+
+def spread_dx(step, last, dx, d_in, og_same, og_other, bounce, here_sem, parent_sem, sib_sem, send_sems, og_sems, ready):
     place = Place()
     micro = dx.shape[I0]
     along_x = place.at(place.tp, (place.stage + I2) % I4)
@@ -1347,6 +1348,7 @@
     gives_g = (place.home == I1) & place.is_l
     takes_g = (place.home == I0) & jnp.logical_not(place.is_l)
     late = late_rows(micro)
+    rest_same = [m for m in late if m >= I4]
 
     def block(m):
         return d_in.at[m, place.core]
@@ -1377,6 +1379,8 @@
 
         @pl.when(gives_g)
         def _():
+            for m in rest_same:
+                remote(og_same.at[m], og_same.at[m], og_sems.at[I2], og_sems.at[I3], place.across).start()
             for m in late:
                 remote(og_other.at[m], og_other.at[m], og_sems.at[I0], og_sems.at[I1], place.across).start()
 
@@ -1395,7 +1399,11 @@
         for m in range(micro):
             pltpu.make_async_copy(bounce.at[m], block(m), here_sem).start()
 
-    part = og_other.at[I0:len(late)]
+    part, part_same = og_other.at[I0:len(late)], og_same.at[I0:len(rest_same)]
+
+    @pl.when((step == I1) & takes_g)
+    def _():
+        remote(part_same, part_same, og_sems.at[I2], og_sems.at[I3], place.across).wait_recv()
 
     @pl.when((step == I3) & takes_g)
     def _():
@@ -1421,16 +1429,17 @@
         @pl.when(gives_g)
         def _():
             remote(part, part, og_sems.at[I0], og_sems.at[I1], place.across).wait_send()
+            remote(part_same, part_same, og_sems.at[I2], og_sems.at[I3], place.across).wait_send()
         remote(dx, dx, send_sems.at[I0], sib_sem, place.sibling).wait_recv()
 
 
-def owner_backward_kernel(dims, dx, ds, do, u, qkv, wo, wd, og_same, go_in, d_first, dqkv, dup, z, d_in, og_other,
-                          dmid, gbuf, dctx, wobuf, bounce, sem, g_sem, here_sem, parent_sem, sib_sem, send_sems, og_sems, ready):
+def owner_backward_kernel(dims, dx, ds, do, u, qkv, wo, wd_near, wd_own, gs_in, go_in, d_first, dqkv, dup, z, d_in, og_other, og_same,
+                          dmid, gbuf, dctx, wobuf, wdbuf, bounce, sem, wd_sem, g_sem, here_sem, parent_sem, sib_sem, send_sems, og_sems, ready):
     micro, seq, width, heads, head_dim, ffn = dims
     half = heads // I2 * HEAD_PAD
     scale = head_dim ** -0.5
     step, steps = pl.program_id(I0), pl.num_programs(I0)
-    spread_dx(step, steps - I1, dx, d_in, og_other, bounce, here_sem, parent_sem, sib_sem, send_sems, og_sems, ready)
+    spread_dx(step, steps - I1, dx, d_in, og_same, og_other, bounce, here_sem, parent_sem, sib_sem, send_sems, og_sems, ready)
 
     def g_load(n, start):
         rows = BLOCK // seq
@@ -1443,9 +1452,13 @@
     @pl.when(step == I0)
     def _():
         g_load(step, True)
+        is_l = Place().is_l
+        for condition, wd in ((is_l, wd_near), (jnp.logical_not(is_l), wd_own)):
+            pl.when(condition)(pltpu.make_async_copy(wd, wdbuf, wd_sem).start)
         wobuf[...] = jnp.zeros_like(wobuf)
         load_heads(wo, I0, wobuf, sem)
         pltpu.make_async_copy(wo, wobuf.at[I0:wo.shape[I0]], sem).wait()
+        pltpu.make_async_copy(wd_near, wdbuf, wd_sem).wait()
     g_load(step + I1, True)
 
     @pl.when(step < steps // I2)
@@ -1465,9 +1478,8 @@
     grad = gbuf.at[step % I2]
 
     def mlp_block(n):
-        rows = pl.ds(pl.multiple_of(n * SUB, SUB), SUB)
         cols = lanes(n * SUB, SUB)
-        dz = mm_nt(grad[...].reshape(BLOCK, width), wd[rows, :]).astype(BF).astype(F32)
+        dz = mm(grad[...].reshape(BLOCK, width), wdbuf[n // I4, :, lanes(n % I4 * SUB, SUB)]).astype(BF).astype(F32)
         up = u[:, cols].astype(F32)
         gate, up2 = gelu_gate(up)
         hidden = up * gate
@@ -1486,7 +1498,7 @@
     lax.fori_loop(I0, heads // I4, both_step, I0)
 
 
-def owner_backward(dims, dx, d_in, d_rows, og, ups, qkv, own):
+def owner_backward(dims, dx, d_in, d_rows, og, ups, qkv, w_out, w_down):
     micro, seq, width, heads, head_dim, ffn = dims
     half = heads // I2 * HEAD_PAD
     tokens = I2 * micro * seq
@@ -1501,15 +1513,15 @@
     return pl.pallas_call(
         functools.partial(owner_backward_kernel, dims),
         grid=(blocks,),
-        out_shape=tuple(shapes((tokens, I3 * half), (tokens, ffn // I2), (tokens, ffn // I2), (micro, I2, seq, width), act)),
-        in_specs=[any_spec, low, high, mlp_block, attn_block, any_spec, pl.BlockSpec((ffn // I2, width), lambda i: (I0, I0)), any_spec, any_spec, any_spec],
-        out_specs=(attn_block, mlp_block, mlp_block, any_spec, any_spec),
-        scratch_shapes=[vmem((BLOCK, width), BF), vmem((I2, BLOCK // seq, seq, width), BF), vmem((BLOCK, half), BF), vmem((half, width), BF), vmem(act, BF),
-                        dma(()), dma((I2,)), dma(()), dma((micro,)), dma(()), dma((I2,)), dma((I2,)), pltpu.SemaphoreType.REGULAR],
-        input_output_aliases={I8: I4, 9: I3},
+        out_shape=tuple(shapes((tokens, I3 * half), (tokens, ffn // I2), (tokens, ffn // I2), (micro, I2, seq, width), act, act)),
+        in_specs=[any_spec, low, high, mlp_block, attn_block, *[any_spec] * I6],
+        out_specs=(attn_block, mlp_block, mlp_block, any_spec, any_spec, any_spec),
+        scratch_shapes=[vmem((BLOCK, width), BF), vmem((I2, BLOCK // seq, seq, width), BF), vmem((BLOCK, half), BF), vmem((half, width), BF), vmem((I3, width, CHUNK), BF), vmem(act, BF),
+                        dma(()), dma(()), dma((I2,)), dma(()), dma((micro,)), dma(()), dma((I2,)), dma((I4,)), pltpu.SemaphoreType.REGULAR],
+        input_output_aliases={I8: 5, 9: I4, 10: I3},
         compiler_params=pltpu.CompilerParams(collective_id=I2, has_side_effects=True, vmem_limit_bytes=VMEM_LIMIT),
         name='owner_backward',
-    )(dx, *d_rows, ups, qkv, own[I1], own[I3], *og, d_in)
+    )(dx, *d_rows, ups, qkv, w_out, *w_down, *og, d_in)
 
 
 def bring(pairs, sem):
@@ -1640,17 +1652,18 @@
 
         (acts, mids, qkv, ups, seeds, oh_same, oh_other, oa_same, oa_other, og_same, og_other, loss_tile, home_gains, *weights) = forward_phase(dims, inputs, targets, rows_of, own_gains)
         (nq, no, nu, nd), (fq, fo, fu, fd) = weights[I0:I4], weights[I4:I8]
-        (tq0, to0, tu0, td0), (tq1, to1, tu1, td1) = weights[I8:12], weights[12:16]
+        (tq0, to0, tu0, td0), (tq1, to1, tu1, td1), (tqo, tdo) = weights[I8:12], weights[12:16], weights[18:20]
 
         flat = lambda *rows: [r.reshape(-I1, width) for r in rows]
-        done, *again = owner_recompute(dims, True, None, flat(oh_same, oh_other), flat(oa_same, oa_other), own_gains, rows_of)
+        done, *again = owner_recompute(dims, True, None, flat(oh_same, oh_other), flat(oa_same, oa_other), own_gains, (tq0, tqo), own[I2])
         dx, _, od_same, od_other, og_same, og_other, oa_same, oa_other, oh_same, oh_other, dg_same, dg_other, loss_all = backward_phase(
             dims, (acts, mids, qkv, ups, seeds), (rows_of[I0], nq, fq, td0, td1, to0, to1, tu0, tu1), home_gains, loss_tile, done,
             (og_same, og_other, oa_same, oa_other, oh_same, oh_other))
-        _, *again, d_first, og_same = owner_recompute(dims, False, (dx, *again, og_same), flat(oh_same, oh_other), flat(oa_same, oa_other), own_gains, rows_of)
+        _, *again, d_first, og_same = owner_recompute(dims, False, (dx, *again, og_same), flat(oh_same, oh_other), flat(oa_same, oa_other), own_gains, (tq0, tqo), own[I2])
         ups_own, qkv_own, ctx_own, n1, n2 = again
         d_rows = flat(od_same, od_other)
-        d_qkv_rows, d_up_rows, hidden, dx_all, og_other = owner_backward(dims, dx, d_first, d_rows, (og_same, og_other), ups_own, qkv_own, rows_of)
+        d_qkv_rows, d_up_rows, hidden, dx_all, og_other, og_same = owner_backward(
+            dims, dx, d_first, d_rows, (og_same, og_other), ups_own, qkv_own, rows_of[I1], (td0, tdo))
         d_qkv, d_out, d_inputs = attn_products(d_qkv_rows, ctx_own, n1, d_rows, dx_all, w_out.shape[I1:])
         d_up, d_down = mlp_products(d_up_rows, hidden, n2, flat(og_same, og_other))
         weight_grads = (d_qkv.transpose(I3, I0, I1, I2), d_out, d_up, d_down)

time: 1290 us -> 1290 us (level)
  no operation moved by 1% of the time
where the time goes in v15:
time: 1290 us
  Pallas kernels  1280 us (99%)
    pallas_call x1, Pallas kernels, forward_phase(): pl.pallas_call(functools.partial(forward_kernel, dims), out_shape=tuple(o...  577 us
    pallas_call x1, Pallas kernels, backward_phase(): pl.pallas_call(functools.partial(backward_kernel, dims), out_shape=tuple(...  282 us
    pallas_call x2, Pallas kernels, owner_recompute(): pl.pallas_call(functools.partial(recompute_kernel, dims, early), out_shap...  146 us
    pallas_call x1, Pallas kernels, owner_backward(): pl.pallas_call(functools.partial(owner_backward_kernel, dims), grid=(bloc...  137 us
    pallas_call x1, Pallas kernels, mlp_products(): pl.pallas_call(mlp_products_kernel, grid=(cols // SUB,), out_shape=(jax.S...  86.4 us
    pallas_call x1, Pallas kernels, attn_products(): pl.pallas_call(attn_products_kernel, grid=(pairs,), out_shape=(jax.ShapeD...  51.5 us

profile of v15, /device:TPU:3, one launch (start us, length us, event | category | flops | bytes accessed | tf_op | source)
XLA Modules:
  0.0 1285.6 jit_solution(3373440955323751722)
XLA Ops:
  0.6 1.3 maximum_convert_fusion.own_gains.gains
  2.0 576.7 %forward_phase.1 = (bf16[8,192,1536]{2,1,0:T(8,128)(2,1)}, bf16[8,192,1536]{2,1,0:T(8,128)(2,1)}, bf16[8,192,6144]{2,1,0:T(8,128)(2,1)}, bf16[8,192,6144]{2,1,0:...) custom-call(bf16[8,2,192,1536]{3,2,1,0:T(8,128)(2,1)} %x_ref.1, ...), custom_call_target="tpu_custom_call" | custom-call | tf_op jit(solution)/shard_map/forward_phase/pallas_call | solution.py:1159
  578.6 0.8 owner_recompute.2
  579.4 282.1 %backward_phase.1 = (bf16[8,192,1536]{2,1,0:T(8,128)(2,1)}, bf16[8,192,1536]{2,1,0:T(8,128)(2,1)}, bf16[8,192,1536]{2,1,0:T(8,128)(2,1)}, bf16[8,192,1536]{2,1,0...) custom-call(bf16[8,192,1536]{2,1,0:T(8,128)(2,1)} %get-tuple-element, ...), custom_call_target="tpu_custom_call", output_to_operand_aliasing={{4}: (17, {}), {5}: (18, {}), {6}: (19, {}), {7}: (20, {}),... | custom-call | tf_op jit(solution)/shard_map/backward_phase/pallas_call | solution.py:1184
  861.6 144.8 %owner_recompute.3 = (f32[8,128]{1,0:T(8,128)}, bf16[3072,3072]{1,0:T(8,128)(2,1)}, bf16[3072,3072]{1,0:T(8,128)(2,1)}, bf16[3072,1024]{1,0:T(8,128)(2,1)}, bf16...) custom-call(bf16[1536,1536]{1,0:T(8,128)(2,1)} %bitcast.32, ...), custom_call_target="tpu_custom_call", output_to_operand_aliasing={{1}: (9, {}), {2}: (10, {}), {3}: (11, {}), {4}: (12, {}), ... | custom-call | tf_op jit(solution)/shard_map/owner_recompute/pallas_call | solution.py:1330
  1006.4 1.3 reduce_sum.18
  1008.4 136.7 %owner_backward.1 = (bf16[3072,3072]{1,0:T(8,128)(2,1)}, bf16[3072,3072]{1,0:T(8,128)(2,1)}, bf16[3072,3072]{1,0:T(8,128)(2,1)}, bf16[8,2,192,1536]{3,2,1,0:T(8,...) custom-call(bf16[8,192,1536]{2,1,0:T(8,128)(2,1)} %get-tuple-element, ...), custom_call_target="tpu_custom_call", output_to_operand_aliasing={{5}: (8, {}), {4}: (9, {}), {3}: (10, {})} | custom-call | tf_op jit(solution)/shard_map/owner_backward/pallas_call | solution.py:1513
  1145.0 51.5 %attn_products.1 = (f32[3,8,96,1536]{3,2,1,0:T(8,128)}, f32[8,96,1536]{2,1,0:T(8,128)}, bf16[8,2,192,1536]{3,2,1,0:T(8,128)(2,1)}) custom-call(bf16[3072,3072]{1,0:T(8,128)(2,1)} %get-tuple-element.112.dq.dk.dv, bf16[3072,3072]{1,0:T(8,128)(2,1)} %get-tuple-element.112.dq.dk.dv, bf16[3072,3072]{1,0:T(8,128)(2,1)} %get-tuple-element.112.dq.dk.dv, ...), custom_call_target="tpu_custom_call" | custom-call | tf_op jit(solution)/shard_map/attn_products/pallas_call | solution.py:1580
  1196.5 1.0 add_reduce_fusion
  1197.5 0.6 fusion
  1198.1 86.4 %mlp_products.1 = (f32[1536,3072]{1,0:T(8,128)}, f32[3072,1536]{1,0:T(8,128)}) custom-call(bf16[3072,3072]{1,0:T(8,128)(2,1)} %get-tuple-element.119.dup, bf16[3072,3072]{1,0:T(8,128)(2,1)} %get-tuple-element.120.z, bf16[3072,1536]{1,0:T(8,128)(2,1)} %get-tuple-element.121.n2_o, bf16[1536,1536]{1,0:T(8,128)(2,1)} %bitcast.30, bf16[1536,1536]{1,0:T(8,128)(2,1)} %bitcast.39), custom_call_target="tpu_custom_call" | custom-call | tf_op jit(solution)/shard_map/mlp_products/pallas_call | solution.py:1622

commit v16 on v15

--- a/solution.py
+++ b/solution.py
@@ -1409,12 +1409,14 @@
     def _():
         remote(part, part, og_sems.at[I0], og_sems.at[I1], place.across).wait_recv()
 
-    @pl.when((step == last) & is_leaf)
-    def _():
-        for m in reversed(range(micro)):
-            if m < micro - EARLY_DX:
-                remote(block(m), block(m), send_sems.at[I0], parent_sem.at[m], place.sibling).wait_recv()
-            to_sibling(m, block(m))
+    first = micro - EARLY_DX
+    for when, rows in ((I1, range(first, micro)), (last - I2, range(first // I2, first)), (last, range(first // I2))):
+        @pl.when((step == when) & is_leaf)
+        def _(rows=rows):
+            for m in reversed(rows):
+                if m < first:
+                    remote(block(m), block(m), send_sems.at[I0], parent_sem.at[m], place.sibling).wait_recv()
+                to_sibling(m, block(m))
 
     @pl.when(step == last)
     def _():

time: 1290 us -> 1280 us (level)
  no operation moved by 1% of the time
where the time goes in v16:
time: 1280 us
  Pallas kernels  1270 us (99%)
    pallas_call x1, Pallas kernels, forward_phase(): pl.pallas_call(functools.partial(forward_kernel, dims), out_shape=tuple(o...  577 us
    pallas_call x1, Pallas kernels, backward_phase(): pl.pallas_call(functools.partial(backward_kernel, dims), out_shape=tuple(...  282 us
    pallas_call x2, Pallas kernels, owner_recompute(): pl.pallas_call(functools.partial(recompute_kernel, dims, early), out_shap...  146 us
    pallas_call x1, Pallas kernels, owner_backward(): pl.pallas_call(functools.partial(owner_backward_kernel, dims), grid=(bloc...  132 us
    pallas_call x1, Pallas kernels, mlp_products(): pl.pallas_call(mlp_products_kernel, grid=(cols // SUB,), out_shape=(jax.S...  86.4 us
    pallas_call x1, Pallas kernels, attn_products(): pl.pallas_call(attn_products_kernel, grid=(pairs,), out_shape=(jax.ShapeD...  51.5 us

profile of v16, /device:TPU:3, one launch (start us, length us, event | category | flops | bytes accessed | tf_op | source)
XLA Modules:
  0.0 1281.4 jit_solution(7721922884122732463)
XLA Ops:
  0.6 1.3 maximum_convert_fusion.own_gains.gains
  2.0 576.7 %forward_phase.1 = (bf16[8,192,1536]{2,1,0:T(8,128)(2,1)}, bf16[8,192,1536]{2,1,0:T(8,128)(2,1)}, bf16[8,192,6144]{2,1,0:T(8,128)(2,1)}, bf16[8,192,6144]{2,1,0:...) custom-call(bf16[8,2,192,1536]{3,2,1,0:T(8,128)(2,1)} %x_ref.1, ...), custom_call_target="tpu_custom_call" | custom-call | tf_op jit(solution)/shard_map/forward_phase/pallas_call | solution.py:1159
  578.6 0.8 owner_recompute.2
  579.4 282.1 %backward_phase.1 = (bf16[8,192,1536]{2,1,0:T(8,128)(2,1)}, bf16[8,192,1536]{2,1,0:T(8,128)(2,1)}, bf16[8,192,1536]{2,1,0:T(8,128)(2,1)}, bf16[8,192,1536]{2,1,0...) custom-call(bf16[8,192,1536]{2,1,0:T(8,128)(2,1)} %get-tuple-element, ...), custom_call_target="tpu_custom_call", output_to_operand_aliasing={{4}: (17, {}), {5}: (18, {}), {6}: (19, {}), {7}: (20, {}),... | custom-call | tf_op jit(solution)/shard_map/backward_phase/pallas_call | solution.py:1184
  861.6 144.8 %owner_recompute.3 = (f32[8,128]{1,0:T(8,128)}, bf16[3072,3072]{1,0:T(8,128)(2,1)}, bf16[3072,3072]{1,0:T(8,128)(2,1)}, bf16[3072,1024]{1,0:T(8,128)(2,1)}, bf16...) custom-call(bf16[1536,1536]{1,0:T(8,128)(2,1)} %bitcast.32, ...), custom_call_target="tpu_custom_call", output_to_operand_aliasing={{1}: (9, {}), {2}: (10, {}), {3}: (11, {}), {4}: (12, {}), ... | custom-call | tf_op jit(solution)/shard_map/owner_recompute/pallas_call | solution.py:1330
  1006.4 1.3 reduce_sum.18
  1008.4 132.5 %owner_backward.1 = (bf16[3072,3072]{1,0:T(8,128)(2,1)}, bf16[3072,3072]{1,0:T(8,128)(2,1)}, bf16[3072,3072]{1,0:T(8,128)(2,1)}, bf16[8,2,192,1536]{3,2,1,0:T(8,...) custom-call(bf16[8,192,1536]{2,1,0:T(8,128)(2,1)} %get-tuple-element, ...), custom_call_target="tpu_custom_call", output_to_operand_aliasing={{5}: (8, {}), {4}: (9, {}), {3}: (10, {})} | custom-call | tf_op jit(solution)/shard_map/owner_backward/pallas_call | solution.py:1515
  1140.8 51.5 %attn_products.1 = (f32[3,8,96,1536]{3,2,1,0:T(8,128)}, f32[8,96,1536]{2,1,0:T(8,128)}, bf16[8,2,192,1536]{3,2,1,0:T(8,128)(2,1)}) custom-call(bf16[3072,3072]{1,0:T(8,128)(2,1)} %get-tuple-element.112.dq.dk.dv, bf16[3072,3072]{1,0:T(8,128)(2,1)} %get-tuple-element.112.dq.dk.dv, bf16[3072,3072]{1,0:T(8,128)(2,1)} %get-tuple-element.112.dq.dk.dv, ...), custom_call_target="tpu_custom_call" | custom-call | tf_op jit(solution)/shard_map/attn_products/pallas_call | solution.py:1582
  1192.3 1.0 add_reduce_fusion
  1193.3 0.6 fusion
  1193.9 86.4 %mlp_products.1 = (f32[1536,3072]{1,0:T(8,128)}, f32[3072,1536]{1,0:T(8,128)}) custom-call(bf16[3072,3072]{1,0:T(8,128)(2,1)} %get-tuple-element.119.dup, bf16[3072,3072]{1,0:T(8,128)(2,1)} %get-tuple-element.120.z, bf16[3072,1536]{1,0:T(8,128)(2,1)} %get-tuple-element.121.n2_o, bf16[1536,1536]{1,0:T(8,128)(2,1)} %bitcast.30, bf16[1536,1536]{1,0:T(8,128)(2,1)} %bitcast.39), custom_call_target="tpu_custom_call" | custom-call | tf_op jit(solution)/shard_map/mlp_products/pallas_call | solution.py:1624
